TPU v7x, 32 devices: a whole 2x2x4 slice. The times are simulated.
32 devices in a mesh: groups: 1, expert: 32 (over z, y, x, core).
Axes of the slice: x: 2, y: 2, z: 4, core: 2. Of those that a mesh axis runs over, the one named last changes fastest.
Arguments:
- tokens: bfloat16 [256, 4096], P(('groups', 'expert')), may hold values from -400 to 400
- norm_gain: float32 [4096], replicated, may hold values from 0.1 to 1.9
- expert_ids: int32 [256, 8], P(('groups', 'expert')), may hold values from 0 to 15, all different within a row; in each aligned block of 8 rows (0 to 7, 8 to 15, ...) at most 5 rows name the same one
- route_score: float32 [256, 8], P(('groups', 'expert')), may hold values from 0.05 to 1
- expert_pair: int32 [16], P('groups'), may hold values from 0 to 15, each once
- w_in: bfloat16 [32, 4096, 768], P(('groups', 'expert')), may hold values from -0.09375 to 0.09375
- w_out: bfloat16 [32, 384, 4096], P(('groups', 'expert')), may hold values from -0.4375 to 0.4375
Outputs:
- mixed: bfloat16 [256, 4096], P(('groups', 'expert'))
Inputs may be any that keep to these rules, and one draw needn't show every extreme that they name: `expert_ids`: each token names 8 different experts; among the tokens of one device no expert is named by more than 5 tokens, and in some devices' tokens one expert is named by exactly 5. `expert_pair`: each value once.
All inputs are finite; a program needn't handle non-finite values.
Results may differ from a plain program's by a relative error of at most 0.0076.
Values may be sent and summed in bfloat16 or wider, within the bound.
No kernel may reach another device: no remote copies, remote signals or barrier semaphores. Data moves between devices by JAX's collectives and lax.ppermute only.
A program may use at most 64 MiB of HBM per device.

v0:
```python
import functools

import jax
import jax.numpy as jnp
from jax import lax
from jax.experimental import pallas as pl
from jax.experimental.pallas import tpu as pltpu
from jax.sharding import PartitionSpec as P


LANES = 128
BF16 = jnp.bfloat16
F32 = jnp.float32
HBM = pl.BlockSpec(memory_space=pltpu.HBM)
VMEM = pl.BlockSpec(memory_space=pltpu.VMEM)
SMEM = pl.BlockSpec(memory_space=pltpu.SMEM)


def swap(block, mask):
    count = lax.axis_size("expert")
    return lax.ppermute(block, "expert", [(i, i ^ mask) for i in range(count)])


def prepare_kernel(tokens, gain, ids, score, pair, payload, *, width):
    widened = tokens[...].astype(F32)
    meansq = jnp.mean(widened * widened, axis=-1, keepdims=True)
    normed = widened * lax.rsqrt(meansq + 1e-06) * gain[...]
    payload[:, :width] = normed.astype(BF16)
    rows, top = ids.shape
    stations = pair.shape[1]
    table = payload.shape[1] - width
    shares = score[...] / jnp.sum(score[...], axis=-1, keepdims=True)
    labels = lax.broadcasted_iota(jnp.int32, (rows, stations), 1)
    named = jnp.zeros((rows, stations), F32)
    for k in range(top):
        named = named + jnp.where(ids[:, k : k + 1] == labels, shares[:, k : k + 1], 0.0)
    place = lax.broadcasted_iota(jnp.int32, (table, stations), 0)
    moved = jnp.where(pair[...] == place, 1.0, 0.0).astype(BF16)
    payload[:, width:] = lax.dot_general(
        named.astype(BF16), moved, (((1,), (1,)), ((), ())), preferred_element_type=F32
    ).astype(BF16)


def select_kernel(station, *refs, blocks, peers, cap, slots, width):
    payloads = refs[:blocks]
    own, shares, weights = refs[blocks : blocks + 3]
    chosen = refs[blocks + 3 :]
    rows_each = payloads[0].shape[0]
    rows = blocks * rows_each
    gathered = jnp.concatenate([ref[...].astype(F32) for ref in payloads], axis=0)
    table = gathered[:, width:]
    body = gathered[:, :width].astype(BF16)
    own[...] = body
    named = jnp.where(table > 0.0, 1.0, 0.0)
    row = lax.broadcasted_iota(jnp.int32, (rows, rows), 0)
    col = lax.broadcasted_iota(jnp.int32, (rows, rows), 1)
    earlier = (col < row) & (row // rows_each == col // rows_each)
    rank = jnp.dot(
        jnp.where(earlier, 1.0, 0.0).astype(BF16), named.astype(BF16), preferred_element_type=F32
    )
    block = lax.broadcasted_iota(jnp.int32, (rows, 1), 0) // rows_each
    lane = lax.broadcasted_iota(jnp.int32, (rows, table.shape[1]), 1)
    total = weights.shape[1]
    target = lax.broadcasted_iota(jnp.int32, (rows, total), 1)
    shared = jnp.zeros((rows, total), F32)
    for j in range(peers + 1):
        pick = lane == (station[0] ^ j)
        share = jnp.sum(jnp.where(pick, table, 0.0), axis=1, keepdims=True)
        if j == 0:
            shares[...] = jnp.broadcast_to(share, shares.shape)
            continue
        ranked = jnp.sum(jnp.where(pick, rank, 0.0), axis=1, keepdims=True)
        slot = block * cap + ranked.astype(jnp.int32) + (j - 1) * slots
        shared = shared + jnp.where(target == slot, share, 0.0)
    weights[...] = shared.astype(BF16)
    placing = jnp.where(shared > 0.0, 1.0, 0.0).astype(BF16)
    picked = lax.dot_general(
        placing, body, (((0,), (0,)), ((), ())), preferred_element_type=F32
    )
    for j in range(peers):
        chosen[j][...] = picked[j * slots : (j + 1) * slots].astype(BF16)


def activate(projected):
    half = projected.shape[1] // 2
    gate = projected[:, :half]
    return (gate / (1.0 + jnp.exp(-gate)) * projected[:, half:]).astype(BF16)


def own_kernel(
    own, other, w_in, w_out, keep, give, inward, outward, stacked, acc, in_sem, out_sem, *, steps_in, steps_out
):
    rows, width = own.shape
    k_len = width // steps_in
    n_len = width // steps_out
    copies_in = [
        pltpu.make_async_copy(
            w_in.at[0, pl.ds(s * k_len, k_len)], inward.at[pl.ds(s * k_len, k_len)], in_sem.at[s]
        )
        for s in range(steps_in)
    ]
    copy_out = pltpu.make_async_copy(w_out.at[0], outward, out_sem)
    for copy in copies_in:
        copy.start()
    copy_out.start()
    stacked[:rows] = own[...]
    stacked[rows:] = other[...]
    for s in range(steps_in):
        span = slice(s * k_len, (s + 1) * k_len)
        copies_in[s].wait()
        part = jnp.dot(stacked[:, span], inward[span], preferred_element_type=F32)
        if s == 0:
            acc[...] = part
        else:
            acc[...] += part
    hidden = activate(acc[...])
    copy_out.wait()
    for s in range(steps_out):
        cols = slice(s * n_len, (s + 1) * n_len)
        value = jnp.dot(hidden, outward[:, cols], preferred_element_type=F32)
        keep[:, cols] = value[:rows]
        give[:, cols] = value[rows:].astype(BF16)


def peer_kernel(*refs, peers, steps_out):
    pieces = refs[: 2 * peers]
    inward, outward = refs[2 * peers : 2 * peers + 2]
    results = refs[2 * peers + 2 : 4 * peers + 2]
    stacked = refs[-1]
    slots, width = pieces[0].shape
    for p, ref in enumerate(pieces):
        stacked[p * slots : (p + 1) * slots] = ref[...]
    hidden = activate(jnp.dot(stacked[...], inward[...], preferred_element_type=F32))
    n_len = width // steps_out
    for s in range(steps_out):
        cols = slice(s * n_len, (s + 1) * n_len)
        value = jnp.dot(hidden, outward[:, cols], preferred_element_type=F32)
        for p, ref in enumerate(results):
            ref[:, cols] = value[p * slots : (p + 1) * slots].astype(ref.dtype)


def combine_kernel(shares, weights, keep, got, *refs, peers):
    back = refs[:peers]
    blocks = refs[peers:]
    stacked = jnp.concatenate([ref[...] for ref in back], axis=0)
    mixed = jnp.dot(weights[...], stacked, preferred_element_type=F32)
    mixed = mixed + shares[:, :1] * (keep[...] + got[...].astype(F32))
    rows = blocks[0].shape[0]
    for b, ref in enumerate(blocks):
        ref[...] = mixed[b * rows : (b + 1) * rows].astype(ref.dtype)


def call(kernel, ins, outs, scratch=(), limit=6, flops=0, moved=0):
    return pl.pallas_call(
        kernel,
        in_specs=list(ins),
        out_specs=[VMEM] * len(outs),
        out_shape=[jax.ShapeDtypeStruct(*out) for out in outs],
        scratch_shapes=list(scratch),
        cost_estimate=pl.CostEstimate(flops=flops, bytes_accessed=moved, transcendentals=0),
        compiler_params=pltpu.CompilerParams(vmem_limit_bytes=limit << 20),
    )


def layer(tokens, norm_gain, expert_ids, route_score, expert_pair, w_in, w_out):
    devices = lax.axis_size("expert")
    chips = devices // 2
    bits = chips.bit_length() - 1
    low = bits // 2
    plane = 1 << low
    blocks = chips // plane
    peers = plane - 1
    stations = expert_pair.shape[0]
    rows, top = expert_ids.shape
    width = tokens.shape[1]
    cap = min(rows, -(-rows * top // stations) + 1)
    slots = -(-blocks * cap // 8) * 8
    table = -(-stations // LANES) * LANES
    held = blocks * rows
    half = w_out.shape[1]
    steps_in, steps_out = 8, 4
    station = (lax.axis_index("expert") // 2).astype(jnp.int32).reshape(1)

    (payload,) = call(
        functools.partial(prepare_kernel, width=width),
        [VMEM] * 5,
        [((rows, width + table), BF16)],
    )(tokens, norm_gain.reshape(1, width), expert_ids, route_score, expert_pair.reshape(1, stations))

    column = [payload] + [swap(payload, k << (low + 1)) for k in range(1, blocks)]
    own, shares, weights, *chosen = call(
        functools.partial(
            select_kernel, blocks=blocks, peers=peers, cap=cap, slots=slots, width=width
        ),
        [SMEM] + [VMEM] * blocks,
        [((held, width), BF16), ((held, LANES), F32), ((held, peers * slots), BF16)]
        + [((slots, width), BF16)] * peers,
    )(station, *column)

    arrived = []
    for j in range(1, plane):
        arrived.append(swap(chosen[j - 1], j << 1))
    other = swap(own, 1)
    keep, give, inward, outward = call(
        functools.partial(own_kernel, steps_in=steps_in, steps_out=steps_out),
        [VMEM, VMEM, HBM, HBM],
        [
            ((held, width), F32),
            ((held, width), BF16),
            ((width, 2 * half), BF16),
            ((half, width), BF16),
        ],
        [
            pltpu.VMEM((2 * held, width), BF16),
            pltpu.VMEM((2 * held, 2 * half), F32),
            pltpu.SemaphoreType.DMA((steps_in,)),
            pltpu.SemaphoreType.DMA,
        ],
        flops=2400 * held * half * width,
    )(
        own,
        other,
        pltpu.with_memory_space_constraint(w_in, pltpu.HBM),
        pltpu.with_memory_space_constraint(w_out, pltpu.HBM),
    )
    got = swap(give, 1)

    pieces = arrived + [swap(block, 1) for block in arrived]
    results = call(
        functools.partial(peer_kernel, peers=peers, steps_out=steps_out),
        [VMEM] * (2 * peers + 2),
        [((slots, width), F32)] * peers + [((slots, width), BF16)] * peers,
        [pltpu.VMEM((2 * peers * slots, width), BF16)],
        limit=12,
    )(*pieces, inward, outward)
    back = []
    for j in range(peers):
        done = results[j] + swap(results[peers + j], 1).astype(F32)
        back.append(swap(done.astype(BF16), (j + 1) << 1))

    summed = call(
        functools.partial(combine_kernel, peers=peers),
        [VMEM] * (4 + peers),
        [((rows, width), F32)] + [((rows, width), BF16)] * (blocks - 1),
    )(shares, weights, keep, got, *back)
    mixed = summed[0]
    for k in range(1, blocks):
        mixed = mixed + swap(summed[k], k << (low + 1)).astype(F32)
    mixed = mixed.astype(BF16)
    return mixed


def solution(mesh):
    in_specs = (
        P(("groups", "expert"), None),
        P(),
        P(("groups", "expert"), None),
        P(("groups", "expert"), None),
        P("groups"),
        P(("groups", "expert"), None, None),
        P(("groups", "expert"), None, None),
    )
    out_specs = P(("groups", "expert"), None)
    return jax.shard_map(layer, mesh=mesh, in_specs=in_specs, out_specs=out_specs, check_vma=False)
```

profile of v0, /device:TPU:0, one launch (start us, length us, event | category | flops | bytes accessed | tf_op | source)
XLA Modules:
  0.0 59.9 jit_solution(17568180338246441834)
XLA Ops:
  0.0 0.0 copy-start
  0.0 0.8 %copy-done = bf16[8,4096]{1,0:T(8,128)(2,1)S(1)} copy-done((bf16[8,4096]{1,0:T(8,128)(2,1)S(1)}, bf16[8,4096]{1,0:T(8,128)(2,1)}, u32[]{:S(2)}) %copy-start) | copy-done | bytes 65560
  0.8 0.0 copy-start.1
  0.8 0.7 %copy-done.1 = f32[4096]{0:T(1024)S(1)} copy-done((f32[4096]{0:T(1024)S(1)}, f32[4096]{0:T(1024)}, u32[]{:S(2)}) %copy-start.1) | copy-done | bytes 16408
  1.6 0.0 copy-start.2
  1.6 0.7 %copy-done.2 = s32[8,8]{1,0:T(8,128)S(1)} copy-done((s32[8,8]{1,0:T(8,128)S(1)}, s32[8,8]{1,0:T(8,128)}, u32[]{:S(2)}) %copy-start.2) | copy-done | bytes 280
  2.2 0.0 copy-start.3
  2.2 0.7 %copy-done.3 = f32[8,8]{1,0:T(8,128)S(1)} copy-done((f32[8,8]{1,0:T(8,128)S(1)}, f32[8,8]{1,0:T(8,128)}, u32[]{:S(2)}) %copy-start.3) | copy-done | bytes 280
  2.9 0.0 copy-start.4
  2.9 0.7 %copy-done.4 = s32[16]{0:T(128)S(1)} copy-done((s32[16]{0:T(128)S(1)}, s32[16]{0:T(128)}, u32[]{:S(2)}) %copy-start.4) | copy-done | bytes 88
  3.6 0.3 shard_map.73.refs_0_
  3.9 5.1 %collective-permute-start.2 = (bf16[8,4224]{1,0:T(8,128)(2,1)S(1)}, bf16[8,4224]{1,0:T(8,128)(2,1)S(1)}, u32[]{:S(2)}, u32[]{:S(2)}) collective-permute-start(bf16[8,4224]{1,0:T(8,128)(2,1)S(1)} %shard_map.73.refs_0_), channel_id=1, source_target_pairs={{0,24},{1,25},{2,26},{3,27},{4,28},{5,29},{6,30},{7,31},{8,16},{9,... | collective-permute-start | bytes 202760 | tf_op jit(solution)/shard_map/ppermute | solution.py:21
  9.0 0.0 collective-permute-start.1
  9.0 0.6 %collective-permute-start = (bf16[8,4224]{1,0:T(8,128)(2,1)S(1)}, bf16[8,4224]{1,0:T(8,128)(2,1)S(1)}, u32[]{:S(2)}, u32[]{:S(2)}) collective-permute-start(bf16[8,4224]{1,0:T(8,128)(2,1)S(1)} %shard_map.73.refs_0_), channel_id=1, source_target_pairs={{0,8},{1,9},{2,10},{3,11},{4,12},{5,13},{6,14},{7,15},{8,0},{9,1},... | collective-permute-start | bytes 202760 | tf_op jit(solution)/shard_map/ppermute | solution.py:21
  9.6 1.9 %collective-permute-done.2.refs_3_ = bf16[8,4224]{1,0:T(8,128)(2,1)S(1)} collective-permute-done((bf16[8,4224]{1,0:T(8,128)(2,1)S(1)}, bf16[8,4224]{1,0:T(8,128)(2,1)S(1)}, u32[]{:S(2)}, u32[]{:S(2)}) %collective-permute-start.2) | collective-permute-done | bytes 67616 | tf_op jit(solution)/shard_map/ppermute | solution.py:21
  11.5 3.2 %collective-permute-done.1.refs_2_ = bf16[8,4224]{1,0:T(8,128)(2,1)S(1)} collective-permute-done((bf16[8,4224]{1,0:T(8,128)(2,1)S(1)}, bf16[8,4224]{1,0:T(8,128)(2,1)S(1)}, u32[]{:S(2)}, u32[]{:S(2)}) %collective-permute-start.1) | collective-permute-done | bytes 67616 | tf_op jit(solution)/shard_map/ppermute | solution.py:21
  14.7 0.0 collective-permute-done.refs_1_
  14.7 0.6 shard_map.74
  15.3 0.1 collective-permute-start.3
  15.4 1.5 %collective-permute-start.5 = (bf16[24,4096]{1,0:T(8,128)(2,1)S(1)}, bf16[24,4096]{1,0:T(8,128)(2,1)S(1)}, u32[]{:S(2)}, u32[]{:S(2)}) collective-permute-start(bf16[24,4096]{1,0:T(8,128)(2,1)S(1)} %get-tuple-element.30), channel_id=1, source_target_pairs={{0,2},{1,3},{2,0},{3,1},{4,6},{5,7},{6,4},{7,5},{8,10},{9,11},{10,... | collective-permute-start | bytes 589832 | tf_op jit(solution)/shard_map/ppermute | solution.py:21
  16.9 1.5 %collective-permute-start.6 = (bf16[24,4096]{1,0:T(8,128)(2,1)S(1)}, bf16[24,4096]{1,0:T(8,128)(2,1)S(1)}, u32[]{:S(2)}, u32[]{:S(2)}) collective-permute-start(bf16[24,4096]{1,0:T(8,128)(2,1)S(1)} %get-tuple-element.31), channel_id=1, source_target_pairs={{0,4},{1,5},{2,6},{3,7},{4,0},{5,1},{6,2},{7,3},{8,12},{9,13},{10,... | collective-permute-start | bytes 589832 | tf_op jit(solution)/shard_map/ppermute | solution.py:21
  18.5 0.5 collective-permute-start.7
  19.0 4.3 %collective-permute-done.5.refs_0_ = bf16[24,4096]{1,0:T(8,128)(2,1)S(1)} collective-permute-done((bf16[24,4096]{1,0:T(8,128)(2,1)S(1)}, bf16[24,4096]{1,0:T(8,128)(2,1)S(1)}, u32[]{:S(2)}, u32[]{:S(2)}) %collective-permute-start.5) | collective-permute-done | bytes 196640 | tf_op jit(solution)/shard_map/ppermute | solution.py:21
  23.2 0.0 collective-permute-start.8
  23.2 4.9 %collective-permute-done.6.refs_1_ = bf16[24,4096]{1,0:T(8,128)(2,1)S(1)} collective-permute-done((bf16[24,4096]{1,0:T(8,128)(2,1)S(1)}, bf16[24,4096]{1,0:T(8,128)(2,1)S(1)}, u32[]{:S(2)}, u32[]{:S(2)}) %collective-permute-start.6) | collective-permute-done | bytes 196640 | tf_op jit(solution)/shard_map/ppermute | solution.py:21
  28.1 0.0 collective-permute-start.9
  28.1 0.0 collective-permute-done.7.refs_2_
  28.1 0.5 collective-permute-start.10
  28.6 0.0 collective-permute-done.3.other
  28.6 4.7 %shard_map.75 = (f32[32,4096]{1,0:T(8,128)S(1)}, bf16[32,4096]{1,0:T(8,128)(2,1)S(1)}, bf16[4096,768]{1,0:T(8,128)(2,1)S(1)}, bf16[384,4096]{1,0:T(8,128)(2,1)S(1)}) custom-call(bf16[32,4096]{1,0:T(8,128)(2,1)S(1)} %get-tuple-element.27.own, bf16[32,4096]{1,0:T(8,128)(2,1)S(1)} %collective-permute-done.3.other, bf16[1,4096,768]{2,1,0:T(8,128)(2,1)} %w_in.1, ...), custom_call_target="tpu_custom_call" | custom-call | flops 120795955200 | tf_op jit(solution)/shard_map/pallas_call | solution.py:204
  33.4 0.0 collective-permute-done.8.refs_3_
  33.4 0.0 collective-permute-done.9.refs_4_
  33.4 0.0 collective-permute-done.10.refs_5_
  33.4 2.4 %shard_map.76 = (f32[24,4096]{1,0:T(8,128)S(1)}, f32[24,4096]{1,0:T(8,128)S(1)}, f32[24,4096]{1,0:T(8,128)S(1)}, bf16[24,4096]{1,0:T(8,128)(2,1)S(1)}, bf16[24,4...) custom-call(bf16[24,4096]{1,0:T(8,128)(2,1)S(1)} %collective-permute-done.5.refs_0_, ...), custom_call_target="tpu_custom_call" | custom-call | tf_op jit(solution)/shard_map/pallas_call | solution.py:229
  35.8 0.1 collective-permute-start.11
  35.9 0.5 collective-permute-start.4
  36.4 0.1 collective-permute-start.13
  36.5 0.4 collective-permute-start.15
  36.9 0.4 collective-permute-done.11
  37.4 0.9 %collective-permute-start.12 = (bf16[24,4096]{1,0:T(8,128)(2,1)S(1)}, bf16[24,4096]{1,0:T(8,128)(2,1)S(1)}, u32[]{:S(2)}, u32[]{:S(2)}) collective-permute-start(bf16[24,4096]{1,0:T(8,128)(2,1)S(1)} %add_convert_fusion.2), channel_id=1, source_target_pairs={{0,2},{1,3},{2,0},{3,1},{4,6},{5,7},{6,4},{7,5},{8,10},{9,11},{10,... | collective-permute-start | bytes 589832 | tf_op jit(solution)/shard_map/ppermute | solution.py:21
  38.3 0.0 collective-permute-done.13
  38.3 1.3 %collective-permute-start.14 = (bf16[24,4096]{1,0:T(8,128)(2,1)S(1)}, bf16[24,4096]{1,0:T(8,128)(2,1)S(1)}, u32[]{:S(2)}, u32[]{:S(2)}) collective-permute-start(bf16[24,4096]{1,0:T(8,128)(2,1)S(1)} %add_convert_fusion.1), channel_id=1, source_target_pairs={{0,4},{1,5},{2,6},{3,7},{4,0},{5,1},{6,2},{7,3},{8,12},{9,13},{10,... | collective-permute-start | bytes 589832 | tf_op jit(solution)/shard_map/ppermute | solution.py:21
  39.6 0.0 collective-permute-done.15
  39.6 1.5 %collective-permute-start.16 = (bf16[24,4096]{1,0:T(8,128)(2,1)S(1)}, bf16[24,4096]{1,0:T(8,128)(2,1)S(1)}, u32[]{:S(2)}, u32[]{:S(2)}) collective-permute-start(bf16[24,4096]{1,0:T(8,128)(2,1)S(1)} %add_convert_fusion), channel_id=1, source_target_pairs={{0,6},{1,7},{2,4},{3,5},{4,2},{5,3},{6,0},{7,1},{8,14},{9,15},{10,... | collective-permute-start | bytes 589832 | tf_op jit(solution)/shard_map/ppermute | solution.py:21
  41.1 0.0 collective-permute-done.4.got
  41.1 4.1 %collective-permute-done.12.refs_0_ = bf16[24,4096]{1,0:T(8,128)(2,1)S(1)} collective-permute-done((bf16[24,4096]{1,0:T(8,128)(2,1)S(1)}, bf16[24,4096]{1,0:T(8,128)(2,1)S(1)}, u32[]{:S(2)}, u32[]{:S(2)}) %collective-permute-start.12) | collective-permute-done | bytes 196640 | tf_op jit(solution)/shard_map/ppermute | solution.py:21
  45.2 3.2 %collective-permute-done.14.refs_1_ = bf16[24,4096]{1,0:T(8,128)(2,1)S(1)} collective-permute-done((bf16[24,4096]{1,0:T(8,128)(2,1)S(1)}, bf16[24,4096]{1,0:T(8,128)(2,1)S(1)}, u32[]{:S(2)}, u32[]{:S(2)}) %collective-permute-start.14) | collective-permute-done | bytes 196640 | tf_op jit(solution)/shard_map/ppermute | solution.py:21
  48.4 1.2 %collective-permute-done.16.refs_2_ = bf16[24,4096]{1,0:T(8,128)(2,1)S(1)} collective-permute-done((bf16[24,4096]{1,0:T(8,128)(2,1)S(1)}, bf16[24,4096]{1,0:T(8,128)(2,1)S(1)}, u32[]{:S(2)}, u32[]{:S(2)}) %collective-permute-start.16) | collective-permute-done | bytes 196640 | tf_op jit(solution)/shard_map/ppermute | solution.py:21
  49.5 0.2 shard_map.77
  49.8 1.1 %collective-permute-start.17 = (bf16[8,4096]{1,0:T(8,128)(2,1)S(1)}, bf16[8,4096]{1,0:T(8,128)(2,1)S(1)}, u32[]{:S(2)}, u32[]{:S(2)}) collective-permute-start(bf16[8,4096]{1,0:T(8,128)(2,1)S(1)} %get-tuple-element.42), channel_id=1, source_target_pairs={{0,8},{1,9},{2,10},{3,11},{4,12},{5,13},{6,14},{7,15},{8,0},{9,1},... | collective-permute-start | bytes 196616 | tf_op jit(solution)/shard_map/ppermute | solution.py:21
  50.9 2.2 %collective-permute-start.18 = (bf16[8,4096]{1,0:T(8,128)(2,1)S(1)}, bf16[8,4096]{1,0:T(8,128)(2,1)S(1)}, u32[]{:S(2)}, u32[]{:S(2)}) collective-permute-start(bf16[8,4096]{1,0:T(8,128)(2,1)S(1)} %get-tuple-element.43), channel_id=1, source_target_pairs={{0,16},{1,17},{2,18},{3,19},{4,20},{5,21},{6,22},{7,23},{8,24},{9,... | collective-permute-start | bytes 196616 | tf_op jit(solution)/shard_map/ppermute | solution.py:21
  53.1 1.1 %collective-permute-start.19 = (bf16[8,4096]{1,0:T(8,128)(2,1)S(1)}, bf16[8,4096]{1,0:T(8,128)(2,1)S(1)}, u32[]{:S(2)}, u32[]{:S(2)}) collective-permute-start(bf16[8,4096]{1,0:T(8,128)(2,1)S(1)} %get-tuple-element.44), channel_id=1, source_target_pairs={{0,24},{1,25},{2,26},{3,27},{4,28},{5,29},{6,30},{7,31},{8,16},{9,... | collective-permute-start | bytes 196616 | tf_op jit(solution)/shard_map/ppermute | solution.py:21
  54.2 0.5 collective-permute-done.17
  54.7 2.9 %collective-permute-done.18 = bf16[8,4096]{1,0:T(8,128)(2,1)S(1)} collective-permute-done((bf16[8,4096]{1,0:T(8,128)(2,1)S(1)}, bf16[8,4096]{1,0:T(8,128)(2,1)S(1)}, u32[]{:S(2)}, u32[]{:S(2)}) %collective-permute-start.18) | collective-permute-done | bytes 65568 | tf_op jit(solution)/shard_map/ppermute | solution.py:21
  57.6 1.6 %collective-permute-done.19 = bf16[8,4096]{1,0:T(8,128)(2,1)S(1)} collective-permute-done((bf16[8,4096]{1,0:T(8,128)(2,1)S(1)}, bf16[8,4096]{1,0:T(8,128)(2,1)S(1)}, u32[]{:S(2)}, u32[]{:S(2)}) %collective-permute-start.19) | collective-permute-done | bytes 65568 | tf_op jit(solution)/shard_map/ppermute | solution.py:21
  59.2 0.7 %add_convert_fusion.3 = bf16[8,4096]{1,0:T(8,128)(2,1)} fusion(bf16[8,4096]{1,0:T(8,128)(2,1)S(1)} %collective-permute-done.19, bf16[8,4096]{1,0:T(8,128)(2,1)S(1)} %collective-permute-done.18, f32[8,4096]{1,0:T(8,128)S(1)} %get-tuple-element.41, bf16[8,4096]{1,0:T(8,128)(2,1)S(1)} %collective-permute-done.17), kind=kLoop, calls=%fused_computation.3 | loop fusion | flops 229376 | bytes 393216 | tf_op jit(solution)/shard_map/convert_element_type | solution.py:249
  (3 shorter events, 0.1 us)
Async XLA Ops:
  0.0 0.8 %copy-start = (bf16[8,4096]{1,0:T(8,128)(2,1)S(1)}, bf16[8,4096]{1,0:T(8,128)(2,1)}, u32[]{:S(2)}) copy-start(bf16[8,4096]{1,0:T(8,128)(2,1)} %tokens.1) | copy-start | bytes 196612
  0.8 0.7 %copy-start.1 = (f32[4096]{0:T(1024)S(1)}, f32[4096]{0:T(1024)}, u32[]{:S(2)}) copy-start(f32[4096]{0:T(1024)} %param.8) | copy-start | bytes 49156
  1.6 0.7 %copy-start.2 = (s32[8,8]{1,0:T(8,128)S(1)}, s32[8,8]{1,0:T(8,128)}, u32[]{:S(2)}) copy-start(s32[8,8]{1,0:T(8,128)} %ids.1) | copy-start | bytes 772
  2.2 0.7 %copy-start.3 = (f32[8,8]{1,0:T(8,128)S(1)}, f32[8,8]{1,0:T(8,128)}, u32[]{:S(2)}) copy-start(f32[8,8]{1,0:T(8,128)} %score.1) | copy-start | bytes 772
  2.9 0.7 %copy-start.4 = (s32[16]{0:T(128)S(1)}, s32[16]{0:T(128)}, u32[]{:S(2)}) copy-start(s32[16]{0:T(128)} %param.11) | copy-start | bytes 196
  3.9 7.6 %collective-permute-start.2 = (bf16[8,4224]{1,0:T(8,128)(2,1)S(1)}, bf16[8,4224]{1,0:T(8,128)(2,1)S(1)}, u32[]{:S(2)}, u32[]{:S(2)}) collective-permute-start(bf16[8,4224]{1,0:T(8,128)(2,1)S(1)} %shard_map.73.refs_0_), channel_id=1, source_target_pairs={{0,24},{1,25},{2,26},{3,27},{4,28},{5,29},{6,30},{7,31},{8,16},{9,... | collective-permute-start | bytes 202760 | tf_op jit(solution)/shard_map/ppermute | solution.py:21
  9.0 5.8 %collective-permute-start.1 = (bf16[8,4224]{1,0:T(8,128)(2,1)S(1)}, bf16[8,4224]{1,0:T(8,128)(2,1)S(1)}, u32[]{:S(2)}, u32[]{:S(2)}) collective-permute-start(bf16[8,4224]{1,0:T(8,128)(2,1)S(1)} %shard_map.73.refs_0_), channel_id=1, source_target_pairs={{0,16},{1,17},{2,18},{3,19},{4,20},{5,21},{6,22},{7,23},{8,24},{9,... | collective-permute-start | bytes 202760 | tf_op jit(solution)/shard_map/ppermute | solution.py:21
  9.0 5.8 %collective-permute-start = (bf16[8,4224]{1,0:T(8,128)(2,1)S(1)}, bf16[8,4224]{1,0:T(8,128)(2,1)S(1)}, u32[]{:S(2)}, u32[]{:S(2)}) collective-permute-start(bf16[8,4224]{1,0:T(8,128)(2,1)S(1)} %shard_map.73.refs_0_), channel_id=1, source_target_pairs={{0,8},{1,9},{2,10},{3,11},{4,12},{5,13},{6,14},{7,15},{8,0},{9,1},... | collective-permute-start | bytes 202760 | tf_op jit(solution)/shard_map/ppermute | solution.py:21
  15.3 13.3 %collective-permute-start.3 = (bf16[32,4096]{1,0:T(8,128)(2,1)S(1)}, bf16[32,4096]{1,0:T(8,128)(2,1)S(1)}, u32[]{:S(2)}, u32[]{:S(2)}) collective-permute-start(bf16[32,4096]{1,0:T(8,128)(2,1)S(1)} %get-tuple-element.27.own), channel_id=1, source_target_pairs={{0,1},{1,0},{2,3},{3,2},{4,5},{5,4},{6,7},{7,6},{8,9},{9,8},{10,11... | collective-permute-start | bytes 786440 | tf_op jit(solution)/shard_map/ppermute | solution.py:21
  15.4 7.8 %collective-permute-start.5 = (bf16[24,4096]{1,0:T(8,128)(2,1)S(1)}, bf16[24,4096]{1,0:T(8,128)(2,1)S(1)}, u32[]{:S(2)}, u32[]{:S(2)}) collective-permute-start(bf16[24,4096]{1,0:T(8,128)(2,1)S(1)} %get-tuple-element.30), channel_id=1, source_target_pairs={{0,2},{1,3},{2,0},{3,1},{4,6},{5,7},{6,4},{7,5},{8,10},{9,11},{10,... | collective-permute-start | bytes 589832 | tf_op jit(solution)/shard_map/ppermute | solution.py:21
  16.9 11.2 %collective-permute-start.6 = (bf16[24,4096]{1,0:T(8,128)(2,1)S(1)}, bf16[24,4096]{1,0:T(8,128)(2,1)S(1)}, u32[]{:S(2)}, u32[]{:S(2)}) collective-permute-start(bf16[24,4096]{1,0:T(8,128)(2,1)S(1)} %get-tuple-element.31), channel_id=1, source_target_pairs={{0,4},{1,5},{2,6},{3,7},{4,0},{5,1},{6,2},{7,3},{8,12},{9,13},{10,... | collective-permute-start | bytes 589832 | tf_op jit(solution)/shard_map/ppermute | solution.py:21
  18.5 9.7 %collective-permute-start.7 = (bf16[24,4096]{1,0:T(8,128)(2,1)S(1)}, bf16[24,4096]{1,0:T(8,128)(2,1)S(1)}, u32[]{:S(2)}, u32[]{:S(2)}) collective-permute-start(bf16[24,4096]{1,0:T(8,128)(2,1)S(1)} %get-tuple-element.32), channel_id=1, source_target_pairs={{0,6},{1,7},{2,4},{3,5},{4,2},{5,3},{6,0},{7,1},{8,14},{9,15},{10,... | collective-permute-start | bytes 589832 | tf_op jit(solution)/shard_map/ppermute | solution.py:21
  23.2 10.1 %collective-permute-start.8 = (bf16[24,4096]{1,0:T(8,128)(2,1)S(1)}, bf16[24,4096]{1,0:T(8,128)(2,1)S(1)}, u32[]{:S(2)}, u32[]{:S(2)}) collective-permute-start(bf16[24,4096]{1,0:T(8,128)(2,1)S(1)} %collective-permute-done.5.refs_0_), channel_id=1, source_target_pairs={{0,1},{1,0},{2,3},{3,2},{4,5},{5,4},{6,7},{7,6},{8,9},{9,8},{10,11... | collective-permute-start | bytes 589832 | tf_op jit(solution)/shard_map/ppermute | solution.py:21
  28.1 5.3 %collective-permute-start.9 = (bf16[24,4096]{1,0:T(8,128)(2,1)S(1)}, bf16[24,4096]{1,0:T(8,128)(2,1)S(1)}, u32[]{:S(2)}, u32[]{:S(2)}) collective-permute-start(bf16[24,4096]{1,0:T(8,128)(2,1)S(1)} %collective-permute-done.6.refs_1_), channel_id=1, source_target_pairs={{0,1},{1,0},{2,3},{3,2},{4,5},{5,4},{6,7},{7,6},{8,9},{9,8},{10,11... | collective-permute-start | bytes 589832 | tf_op jit(solution)/shard_map/ppermute | solution.py:21
  28.1 5.3 %collective-permute-start.10 = (bf16[24,4096]{1,0:T(8,128)(2,1)S(1)}, bf16[24,4096]{1,0:T(8,128)(2,1)S(1)}, u32[]{:S(2)}, u32[]{:S(2)}) collective-permute-start(bf16[24,4096]{1,0:T(8,128)(2,1)S(1)} %collective-permute-done.7.refs_2_), channel_id=1, source_target_pairs={{0,1},{1,0},{2,3},{3,2},{4,5},{5,4},{6,7},{7,6},{8,9},{9,8},{10,11... | collective-permute-start | bytes 589832 | tf_op jit(solution)/shard_map/ppermute | solution.py:21
  35.8 1.5 %collective-permute-start.11 = (bf16[24,4096]{1,0:T(8,128)(2,1)S(1)}, bf16[24,4096]{1,0:T(8,128)(2,1)S(1)}, u32[]{:S(2)}, u32[]{:S(2)}) collective-permute-start(bf16[24,4096]{1,0:T(8,128)(2,1)S(1)} %get-tuple-element.36), channel_id=1, source_target_pairs={{0,1},{1,0},{2,3},{3,2},{4,5},{5,4},{6,7},{7,6},{8,9},{9,8},{10,11... | collective-permute-start | bytes 589832 | tf_op jit(solution)/shard_map/ppermute | solution.py:21
  35.9 5.2 %collective-permute-start.4 = (bf16[32,4096]{1,0:T(8,128)(2,1)S(1)}, bf16[32,4096]{1,0:T(8,128)(2,1)S(1)}, u32[]{:S(2)}, u32[]{:S(2)}) collective-permute-start(bf16[32,4096]{1,0:T(8,128)(2,1)S(1)} %get-tuple-element.29), channel_id=1, source_target_pairs={{0,1},{1,0},{2,3},{3,2},{4,5},{5,4},{6,7},{7,6},{8,9},{9,8},{10,11... | collective-permute-start | bytes 786440 | tf_op jit(solution)/shard_map/ppermute | solution.py:21
  36.4 1.9 %collective-permute-start.13 = (bf16[24,4096]{1,0:T(8,128)(2,1)S(1)}, bf16[24,4096]{1,0:T(8,128)(2,1)S(1)}, u32[]{:S(2)}, u32[]{:S(2)}) collective-permute-start(bf16[24,4096]{1,0:T(8,128)(2,1)S(1)} %get-tuple-element.38), channel_id=1, source_target_pairs={{0,1},{1,0},{2,3},{3,2},{4,5},{5,4},{6,7},{7,6},{8,9},{9,8},{10,11... | collective-permute-start | bytes 589832 | tf_op jit(solution)/shard_map/ppermute | solution.py:21
  36.5 3.1 %collective-permute-start.15 = (bf16[24,4096]{1,0:T(8,128)(2,1)S(1)}, bf16[24,4096]{1,0:T(8,128)(2,1)S(1)}, u32[]{:S(2)}, u32[]{:S(2)}) collective-permute-start(bf16[24,4096]{1,0:T(8,128)(2,1)S(1)} %get-tuple-element.40), channel_id=1, source_target_pairs={{0,1},{1,0},{2,3},{3,2},{4,5},{5,4},{6,7},{7,6},{8,9},{9,8},{10,11... | collective-permute-start | bytes 589832 | tf_op jit(solution)/shard_map/ppermute | solution.py:21
  37.4 7.8 %collective-permute-start.12 = (bf16[24,4096]{1,0:T(8,128)(2,1)S(1)}, bf16[24,4096]{1,0:T(8,128)(2,1)S(1)}, u32[]{:S(2)}, u32[]{:S(2)}) collective-permute-start(bf16[24,4096]{1,0:T(8,128)(2,1)S(1)} %add_convert_fusion.2), channel_id=1, source_target_pairs={{0,2},{1,3},{2,0},{3,1},{4,6},{5,7},{6,4},{7,5},{8,10},{9,11},{10,... | collective-permute-start | bytes 589832 | tf_op jit(solution)/shard_map/ppermute | solution.py:21
  38.3 10.0 %collective-permute-start.14 = (bf16[24,4096]{1,0:T(8,128)(2,1)S(1)}, bf16[24,4096]{1,0:T(8,128)(2,1)S(1)}, u32[]{:S(2)}, u32[]{:S(2)}) collective-permute-start(bf16[24,4096]{1,0:T(8,128)(2,1)S(1)} %add_convert_fusion.1), channel_id=1, source_target_pairs={{0,4},{1,5},{2,6},{3,7},{4,0},{5,1},{6,2},{7,3},{8,12},{9,13},{10,... | collective-permute-start | bytes 589832 | tf_op jit(solution)/shard_map/ppermute | solution.py:21
  39.6 9.9 %collective-permute-start.16 = (bf16[24,4096]{1,0:T(8,128)(2,1)S(1)}, bf16[24,4096]{1,0:T(8,128)(2,1)S(1)}, u32[]{:S(2)}, u32[]{:S(2)}) collective-permute-start(bf16[24,4096]{1,0:T(8,128)(2,1)S(1)} %add_convert_fusion), channel_id=1, source_target_pairs={{0,6},{1,7},{2,4},{3,5},{4,2},{5,3},{6,0},{7,1},{8,14},{9,15},{10,... | collective-permute-start | bytes 589832 | tf_op jit(solution)/shard_map/ppermute | solution.py:21
  49.8 4.9 %collective-permute-start.17 = (bf16[8,4096]{1,0:T(8,128)(2,1)S(1)}, bf16[8,4096]{1,0:T(8,128)(2,1)S(1)}, u32[]{:S(2)}, u32[]{:S(2)}) collective-permute-start(bf16[8,4096]{1,0:T(8,128)(2,1)S(1)} %get-tuple-element.42), channel_id=1, source_target_pairs={{0,8},{1,9},{2,10},{3,11},{4,12},{5,13},{6,14},{7,15},{8,0},{9,1},... | collective-permute-start | bytes 196616 | tf_op jit(solution)/shard_map/ppermute | solution.py:21
  50.9 6.7 %collective-permute-start.18 = (bf16[8,4096]{1,0:T(8,128)(2,1)S(1)}, bf16[8,4096]{1,0:T(8,128)(2,1)S(1)}, u32[]{:S(2)}, u32[]{:S(2)}) collective-permute-start(bf16[8,4096]{1,0:T(8,128)(2,1)S(1)} %get-tuple-element.43), channel_id=1, source_target_pairs={{0,16},{1,17},{2,18},{3,19},{4,20},{5,21},{6,22},{7,23},{8,24},{9,... | collective-permute-start | bytes 196616 | tf_op jit(solution)/shard_map/ppermute | solution.py:21
  53.1 6.1 %collective-permute-start.19 = (bf16[8,4096]{1,0:T(8,128)(2,1)S(1)}, bf16[8,4096]{1,0:T(8,128)(2,1)S(1)}, u32[]{:S(2)}, u32[]{:S(2)}) collective-permute-start(bf16[8,4096]{1,0:T(8,128)(2,1)S(1)} %get-tuple-element.44), channel_id=1, source_target_pairs={{0,24},{1,25},{2,26},{3,27},{4,28},{5,29},{6,30},{7,31},{8,16},{9,... | collective-permute-start | bytes 196616 | tf_op jit(solution)/shard_map/ppermute | solution.py:21
where the time goes:
time: 60.2 us; the launch traced here: 59.9 us
  waiting for transfers between devices  28.1 us (47%)
  starting transfers between devices  19.1 us (32%)
  Pallas kernels  8.24 us (14%)
  local copies, waits for them, and re-layouts  3.58 us (6%)
  other arithmetic  0.77 us (1%)
    ppermute x20, waiting for transfers between devices, swap(): return lax.ppermute(block, 'expert', [(i, i ^ mask) for i in range(count)])  28.1 us
    ppermute x20, starting transfers between devices, swap(): return lax.ppermute(block, 'expert', [(i, i ^ mask) for i in range(count)])  19.1 us
    pallas_call x1, Pallas kernels, layer(): call(functools.partial(own_kernel, steps_in=steps_in, steps_out=steps_out...  4.74 us
    unnamed x10, local copies, waits for them, and re-layouts  3.58 us
    pallas_call x1, Pallas kernels, layer(): call(functools.partial(peer_kernel, peers=peers, steps_out=steps_out), [V...  2.4 us
  transfers between devices with their start and end apart: 20, of which 11 were waited for; matrix products, arithmetic and copies ran while one was open for 0% of the time, Pallas kernels for 8%

commit v1 on v0

v1 whole, which is shorter than its diff:
```python
import functools

import jax
import jax.numpy as jnp
from jax import lax
from jax.experimental import pallas as pl
from jax.experimental.pallas import tpu as pltpu
from jax.sharding import PartitionSpec as P


LANES = 128
BF16 = jnp.bfloat16
F32 = jnp.float32
HBM = pl.BlockSpec(memory_space=pltpu.HBM)
VMEM = pl.BlockSpec(memory_space=pltpu.VMEM)
SMEM = pl.BlockSpec(memory_space=pltpu.SMEM)


def swap(block, mask):
    count = lax.axis_size("expert")
    return lax.ppermute(block, "expert", [(i, i ^ mask) for i in range(count)])


def picked_rows(placing, body):
    return lax.dot_general(placing, body, (((0,), (0,)), ((), ())), preferred_element_type=F32)


def slot_weights(table, station, peers, slots, cap, rows_each):
    rows = table.shape[0]
    row = lax.broadcasted_iota(jnp.int32, (rows, rows), 0)
    col = lax.broadcasted_iota(jnp.int32, (rows, rows), 1)
    earlier = (col < row) & (row // rows_each == col // rows_each)
    rank = jnp.dot(
        jnp.where(earlier, 1.0, 0.0).astype(BF16),
        jnp.where(table > 0.0, 1.0, 0.0).astype(BF16),
        preferred_element_type=F32,
    )
    base = lax.broadcasted_iota(jnp.int32, (rows, 1), 0) // rows_each * cap
    lane = lax.broadcasted_iota(jnp.int32, table.shape, 1)
    target = lax.broadcasted_iota(jnp.int32, (rows, peers * slots), 1)
    weights = jnp.zeros((rows, peers * slots), F32)
    for j in range(peers):
        pick = lane == (station ^ (j + 1))
        share = jnp.sum(jnp.where(pick, table, 0.0), axis=1, keepdims=True)
        ranked = jnp.sum(jnp.where(pick, rank, 0.0), axis=1, keepdims=True)
        slot = base + ranked.astype(jnp.int32) + j * slots
        weights = weights + jnp.where(target == slot, share, 0.0)
    return weights


def prepare_kernel(station, *refs, peers, cap, slots, width):
    sources = refs[:5]
    payload, weights = refs[5:7]
    chosen = refs[7 : 7 + peers]
    copied = refs[7 + peers : 12 + peers]
    sems = refs[-1]
    copies = [
        pltpu.make_async_copy(source, target, sems.at[n])
        for n, (source, target) in enumerate(zip(sources, copied))
    ]
    for copy in copies:
        copy.start()
    for copy in copies:
        copy.wait()
    tokens, gain, ids, score, pair = copied
    widened = tokens[...].astype(F32)
    meansq = jnp.mean(widened * widened, axis=-1, keepdims=True)
    normed = (widened * lax.rsqrt(meansq + 1e-06) * gain[...]).astype(BF16)
    payload[:, :width] = normed
    rows, top = ids.shape
    stations = pair.shape[1]
    shares = score[...] / jnp.sum(score[...], axis=-1, keepdims=True)
    labels = lax.broadcasted_iota(jnp.int32, (rows, stations), 1)
    named = jnp.zeros((rows, stations), F32)
    for k in range(top):
        named = named + jnp.where(ids[:, k : k + 1] == labels, shares[:, k : k + 1], 0.0)
    place = lax.broadcasted_iota(jnp.int32, (payload.shape[1] - width, stations), 0)
    moved = jnp.where(pair[...] == place, 1.0, 0.0).astype(BF16)
    table = lax.dot_general(
        named.astype(BF16), moved, (((1,), (1,)), ((), ())), preferred_element_type=F32
    )
    payload[:, width:] = table.astype(BF16)
    shared = slot_weights(table, station[0], peers, slots, cap, rows)
    weights[...] = shared.astype(BF16)
    placed = picked_rows(jnp.where(shared > 0.0, 1.0, 0.0).astype(BF16), normed)
    for j, ref in enumerate(chosen):
        ref[...] = placed[j * slots : (j + 1) * slots].astype(BF16)


def select_kernel(station, *refs, blocks, peers, cap, slots, width):
    payloads = refs[:blocks]
    own, shares, weights = refs[blocks : blocks + 3]
    chosen = refs[blocks + 3 :]
    rows = payloads[0].shape[0]
    gathered = jnp.concatenate([ref[...].astype(F32) for ref in payloads], axis=0)
    table = gathered[:, width:]
    body = gathered[:, :width].astype(BF16)
    own[...] = body
    lane = lax.broadcasted_iota(jnp.int32, table.shape, 1)
    share = jnp.sum(jnp.where(lane == station[0], table, 0.0), axis=1, keepdims=True)
    shares[...] = jnp.broadcast_to(share, shares.shape)
    shared = slot_weights(table[rows:], station[0], peers, slots, cap, rows)
    weights[...] = shared.astype(BF16)
    placed = picked_rows(jnp.where(shared > 0.0, 1.0, 0.0).astype(BF16), body[rows:])
    for j, ref in enumerate(chosen):
        ref[...] = placed[j * slots : (j + 1) * slots].astype(BF16)


def activate(projected):
    half = projected.shape[1] // 2
    gate = projected[:, :half]
    return (gate / (1.0 + jnp.exp(-gate)) * projected[:, half:]).astype(BF16)


def own_kernel(
    own, other, w_in, w_out, keep, give, inward, outward, stacked, acc, in_sem, out_sem, *, steps_in, steps_out
):
    rows, width = own.shape
    k_len = width // steps_in
    n_len = width // steps_out
    copies_in = [
        pltpu.make_async_copy(
            w_in.at[0, pl.ds(s * k_len, k_len)], inward.at[pl.ds(s * k_len, k_len)], in_sem.at[s]
        )
        for s in range(steps_in)
    ]
    copy_out = pltpu.make_async_copy(w_out.at[0], outward, out_sem)
    for copy in copies_in:
        copy.start()
    copy_out.start()
    stacked[:rows] = own[...]
    stacked[rows:] = other[...]
    for s in range(steps_in):
        span = slice(s * k_len, (s + 1) * k_len)
        copies_in[s].wait()
        part = jnp.dot(stacked[:, span], inward[span], preferred_element_type=F32)
        if s == 0:
            acc[...] = part
        else:
            acc[...] += part
    hidden = activate(acc[...])
    copy_out.wait()
    for s in range(steps_out):
        cols = slice(s * n_len, (s + 1) * n_len)
        value = jnp.dot(hidden, outward[:, cols], preferred_element_type=F32)
        keep[:, cols] = value[:rows]
        give[:, cols] = value[rows:].astype(BF16)


def peer_kernel(*refs, peers, steps_out):
    pieces = refs[: 2 * peers]
    inward, outward = refs[2 * peers : 2 * peers + 2]
    results = refs[2 * peers + 2 : 4 * peers + 2]
    stacked = refs[-1]
    slots, width = pieces[0].shape
    for p, ref in enumerate(pieces):
        stacked[p * slots : (p + 1) * slots] = ref[...]
    hidden = activate(jnp.dot(stacked[...], inward[...], preferred_element_type=F32))
    n_len = width // steps_out
    for s in range(steps_out):
        cols = slice(s * n_len, (s + 1) * n_len)
        value = jnp.dot(hidden, outward[:, cols], preferred_element_type=F32)
        for p, ref in enumerate(results):
            ref[:, cols] = value[p * slots : (p + 1) * slots].astype(ref.dtype)


def combine_kernel(shares, weights, keep, got, *refs, peers):
    back = refs[:peers]
    blocks = refs[peers:]
    stacked = jnp.concatenate([ref[...] for ref in back], axis=0)
    mixed = jnp.dot(weights[...], stacked, preferred_element_type=F32)
    held = shares.shape[0]
    local = shares[:, :1] * (keep[:held] + got[:held].astype(F32))
    rows = blocks[0].shape[0]
    blocks[0][...] = local[:rows]
    for b, ref in enumerate(blocks[1:]):
        span = slice(b * rows, (b + 1) * rows)
        ref[...] = (mixed[span] + local[rows:][span]).astype(BF16)


def total_kernel(local, weights, *refs, peers):
    back = refs[:peers]
    stacked = jnp.concatenate([ref[...] for ref in back], axis=0)
    total = local[...] + jnp.dot(weights[...], stacked, preferred_element_type=F32)
    for ref in refs[peers:-1]:
        total = total + ref[...].astype(F32)
    refs[-1][...] = total.astype(BF16)


def call(kernel, ins, outs, scratch=(), limit=6, flops=0, moved=0):
    return pl.pallas_call(
        kernel,
        in_specs=list(ins),
        out_specs=[VMEM] * len(outs),
        out_shape=[jax.ShapeDtypeStruct(*out) for out in outs],
        scratch_shapes=list(scratch),
        cost_estimate=pl.CostEstimate(flops=flops, bytes_accessed=moved, transcendentals=0),
        compiler_params=pltpu.CompilerParams(vmem_limit_bytes=limit << 20),
    )


def layer(tokens, norm_gain, expert_ids, route_score, expert_pair, w_in, w_out):
    devices = lax.axis_size("expert")
    blocks, plane, up = shape_of(devices)
    peers = plane - 1
    stations = expert_pair.shape[0]
    rows, top = expert_ids.shape
    width = tokens.shape[1]
    half = w_out.shape[1]
    cap = min(rows, -(-rows * top // stations) + 1)
    slots_first = -(-cap // 8) * 8
    slots = -(-(blocks - 1) * cap // 8) * 8
    table = -(-stations // LANES) * LANES
    held = blocks * rows
    early = held + peers * slots_first
    steps_in, steps_out = 8, 4
    station = (lax.axis_index("expert") // 2).astype(jnp.int32).reshape(1)
    hbm = functools.partial(pltpu.with_memory_space_constraint, memory_space=pltpu.HBM)

    inputs = (
        tokens,
        norm_gain.reshape(1, width),
        expert_ids,
        route_score,
        expert_pair.reshape(1, stations),
    )
    payload, weights_first, *first = call(
        functools.partial(prepare_kernel, peers=peers, cap=cap, slots=slots_first, width=width),
        [SMEM] + [HBM] * 5,
        [((rows, width + table), BF16), ((rows, peers * slots_first), BF16)]
        + [((slots_first, width), BF16)] * peers,
        [pltpu.VMEM(x.shape, x.dtype) for x in inputs] + [pltpu.SemaphoreType.DMA((5,))],
    )(station, *[hbm(x) for x in inputs])

    column = [payload] + [swap(payload, k << up) for k in range(1, blocks)]
    first = [swap(first[j], (j + 1) << 1) for j in range(peers)]
    own, shares, weights, *chosen = call(
        functools.partial(
            select_kernel, blocks=blocks, peers=peers, cap=cap, slots=slots, width=width
        ),
        [SMEM] + [VMEM] * blocks,
        [((held, width), BF16), ((held, LANES), F32), ((held - rows, peers * slots), BF16)]
        + [((slots, width), BF16)] * peers,
    )(station, *column)

    arrived = [swap(chosen[j], (j + 1) << 1) for j in range(peers)]
    own = jnp.concatenate([own] + first, axis=0)
    other = swap(own, 1)
    owned = call(
        functools.partial(own_kernel, steps_in=steps_in, steps_out=steps_out),
        [VMEM, VMEM, HBM, HBM],
        [
            ((early, width), F32),
            ((early, width), BF16),
            ((width, 2 * half), BF16),
            ((half, width), BF16),
        ],
        [
            pltpu.VMEM((2 * early, width), BF16),
            pltpu.VMEM((2 * early, 2 * half), F32),
            pltpu.SemaphoreType.DMA((steps_in,)),
            pltpu.SemaphoreType.DMA,
        ],
        limit=10,
        flops=2400 * held * half * width,
    )
    keep, give, inward, outward = owned(own, other, hbm(w_in), hbm(w_out))
    got = swap(give, 1)

    pieces = arrived + [swap(block, 1) for block in arrived]
    results = call(
        functools.partial(peer_kernel, peers=peers, steps_out=steps_out),
        [VMEM] * (2 * peers + 2),
        [((slots, width), F32)] * peers + [((slots, width), BF16)] * peers,
        [pltpu.VMEM((2 * peers * slots, width), BF16)],
        limit=10,
    )(*pieces, inward, outward)
    back, back_first = [], []
    for j in range(peers):
        halves = swap(results[peers + j], 1)
        done = (results[j] + halves.astype(F32)).astype(BF16)
        back.append(swap(done, (j + 1) << 1))
        span = slice(held + j * slots_first, held + (j + 1) * slots_first)
        done = (keep[span] + got[span].astype(F32)).astype(BF16)
        back_first.append(swap(done, (j + 1) << 1))

    summed = call(
        functools.partial(combine_kernel, peers=peers),
        [VMEM] * (4 + peers),
        [((rows, width), F32)] + [((rows, width), BF16)] * (blocks - 1),
    )(shares, weights, keep, got, *back)
    returned = [swap(summed[k], k << up) for k in range(1, blocks)]
    (mixed,) = call(
        functools.partial(total_kernel, peers=peers),
        [VMEM] * (1 + peers + blocks),
        [((rows, width), BF16)],
    )(summed[0], weights_first, *back_first, *returned)
    return mixed


def shape_of(devices):
    bits = (devices // 2).bit_length() - 1
    low = bits // 2
    return 1 << (bits - low), 1 << low, low + 1


def solution(mesh):
    in_specs = (
        P(("groups", "expert"), None),
        P(),
        P(("groups", "expert"), None),
        P(("groups", "expert"), None),
        P("groups"),
        P(("groups", "expert"), None, None),
        P(("groups", "expert"), None, None),
    )
    out_specs = P(("groups", "expert"), None)
    return jax.shard_map(layer, mesh=mesh, in_specs=in_specs, out_specs=out_specs, check_vma=False)
```

time: 60.2 us -> 56.1 us (0.932)
  waiting for transfers between devices: 28.1 us -> 17.9 us
  starting transfers between devices: 19.1 us -> 27.6 us
  local copies, waits for them, and re-layouts: 3.58 us -> 0.04 us
  Pallas kernels: 8.24 us -> 10.2 us
  other arithmetic: 0.77 us -> 0.12 us
    ppermute x20 -> x26, waiting for transfers between devices: 28.1 us -> 17.9 us  [swap(): return lax.ppermute(block, 'expert', [(i, i ^ mask) for i in range(count)])]
    ppermute x20 -> x26, starting transfers between devices: 19.1 us -> 27.6 us  [swap(): return lax.ppermute(block, 'expert', [(i, i ^ mask) for i in range(count)])]
    unnamed x10 -> x3, local copies, waits for them, and re-layouts: 3.58 us -> 0.03 us
    pallas_call x2 -> x3, Pallas kernels: 5.04 us -> 7.25 us  [the longest x1 4.8 us: layer(): keep, give, inward, outward = owned(own, other, hbm(w_in), hbm(w_out))]
    convert_element_type x4, other arithmetic: 0.77 us -> 0.12 us  [the longest x3 0.08 us: layer(): done = (results[j] + halves.astype(F32)).astype(BF16)]
  transfers between devices with their start and end apart: 20 -> 26, of which waited for: 11 -> 12; matrix products, arithmetic and copies ran while one was open for 0% -> 0% of each run, Pallas kernels for 8% -> 9%
where the time goes in v1:
time: 56.1 us; the launch traced here: 55.9 us
  starting transfers between devices  27.6 us (49%)
  waiting for transfers between devices  17.9 us (32%)
  Pallas kernels  10.2 us (18%)
    ppermute x26, starting transfers between devices, swap(): return lax.ppermute(block, 'expert', [(i, i ^ mask) for i in range(count)])  27.6 us
    ppermute x26, waiting for transfers between devices, swap(): return lax.ppermute(block, 'expert', [(i, i ^ mask) for i in range(count)])  17.9 us
    pallas_call x1, Pallas kernels, layer(): keep, give, inward, outward = owned(own, other, hbm(w_in), hbm(w_out))  4.8 us
    pallas_call x1, Pallas kernels, layer(): call(functools.partial(peer_kernel, peers=peers, steps_out=steps_out), [V...  2.22 us
    pallas_call x1, Pallas kernels, layer(): call(functools.partial(prepare_kernel, peers=peers, cap=cap, slots=slots_...  1.64 us
  transfers between devices with their start and end apart: 26, of which 12 were waited for; matrix products, arithmetic and copies ran while one was open for 0% of the time, Pallas kernels for 9%

profile of v1, /device:TPU:0, one launch (start us, length us, event | category | flops | bytes accessed | tf_op | source)
XLA Modules:
  0.0 55.9 jit_solution(419720988418111326)
XLA Ops:
  0.0 1.6 %shard_map.73 = (bf16[8,4224]{1,0:T(8,128)(2,1)S(1)}, bf16[8,24]{1,0:T(8,128)(2,1)S(1)}, bf16[8,4096]{1,0:T(8,128)(2,1)S(1)}, bf16[8,4096]{1,0:T(8,128)(2,1)S(1)}, bf16[8,4096]{1,0:T(8,128)(2,1)S(1)}) custom-call(s32[1]{0:T(128)} %bitcast.station, bf16[8,4096]{1,0:T(8,128)(2,1)} %refs_0_.1, f32[1,4096]{1,0:T(1,128)} %bitcast.3, s32[8,8]{1,0:T(8,128)} %refs_2_.1, ...), custom_call_target="tpu_custom_call" | custom-call | tf_op jit(solution)/shard_map/pallas_call | solution.py:227
  1.7 5.1 %collective-permute-start.2 = (bf16[8,4224]{1,0:T(8,128)(2,1)S(1)}, bf16[8,4224]{1,0:T(8,128)(2,1)S(1)}, u32[]{:S(2)}, u32[]{:S(2)}) collective-permute-start(bf16[8,4224]{1,0:T(8,128)(2,1)S(1)} %get-tuple-element.30.refs_0_), channel_id=1, source_target_pairs={{0,24},{1,25},{2,26},{3,27},{4,28},{5,29},{6,30},{7,31},{8,16},{9,... | collective-permute-start | bytes 202760 | tf_op jit(solution)/shard_map/ppermute | solution.py:21
  6.8 0.0 collective-permute-start.1
  6.8 0.6 %collective-permute-start = (bf16[8,4224]{1,0:T(8,128)(2,1)S(1)}, bf16[8,4224]{1,0:T(8,128)(2,1)S(1)}, u32[]{:S(2)}, u32[]{:S(2)}) collective-permute-start(bf16[8,4224]{1,0:T(8,128)(2,1)S(1)} %get-tuple-element.30.refs_0_), channel_id=1, source_target_pairs={{0,8},{1,9},{2,10},{3,11},{4,12},{5,13},{6,14},{7,15},{8,0},{9,1},... | collective-permute-start | bytes 202760 | tf_op jit(solution)/shard_map/ppermute | solution.py:21
  7.4 1.6 %collective-permute-start.3 = (bf16[8,4096]{1,0:T(8,128)(2,1)S(1)}, bf16[8,4096]{1,0:T(8,128)(2,1)S(1)}, u32[]{:S(2)}, u32[]{:S(2)}) collective-permute-start(bf16[8,4096]{1,0:T(8,128)(2,1)S(1)} %get-tuple-element.34), channel_id=1, source_target_pairs={{0,2},{1,3},{2,0},{3,1},{4,6},{5,7},{6,4},{7,5},{8,10},{9,11},{10,... | collective-permute-start | bytes 196616 | tf_op jit(solution)/shard_map/ppermute | solution.py:21
  9.1 1.5 %collective-permute-start.4 = (bf16[8,4096]{1,0:T(8,128)(2,1)S(1)}, bf16[8,4096]{1,0:T(8,128)(2,1)S(1)}, u32[]{:S(2)}, u32[]{:S(2)}) collective-permute-start(bf16[8,4096]{1,0:T(8,128)(2,1)S(1)} %get-tuple-element.35), channel_id=1, source_target_pairs={{0,4},{1,5},{2,6},{3,7},{4,0},{5,1},{6,2},{7,3},{8,12},{9,13},{10,... | collective-permute-start | bytes 196616 | tf_op jit(solution)/shard_map/ppermute | solution.py:21
  10.6 0.0 collective-permute-done.2.refs_3_
  10.6 1.6 %collective-permute-start.5 = (bf16[8,4096]{1,0:T(8,128)(2,1)S(1)}, bf16[8,4096]{1,0:T(8,128)(2,1)S(1)}, u32[]{:S(2)}, u32[]{:S(2)}) collective-permute-start(bf16[8,4096]{1,0:T(8,128)(2,1)S(1)} %get-tuple-element.36), channel_id=1, source_target_pairs={{0,6},{1,7},{2,4},{3,5},{4,2},{5,3},{6,0},{7,1},{8,14},{9,15},{10,... | collective-permute-start | bytes 196616 | tf_op jit(solution)/shard_map/ppermute | solution.py:21
  12.2 0.4 collective-permute-done.1.refs_2_
  12.6 0.0 collective-permute-done.refs_1_
  12.6 0.5 shard_map.74
  13.1 0.0 collective-permute-done.3
  13.1 0.9 %collective-permute-done.4 = bf16[8,4096]{1,0:T(8,128)(2,1)S(1)} collective-permute-done((bf16[8,4096]{1,0:T(8,128)(2,1)S(1)}, bf16[8,4096]{1,0:T(8,128)(2,1)S(1)}, u32[]{:S(2)}, u32[]{:S(2)}) %collective-permute-start.4) | collective-permute-done | bytes 65568 | tf_op jit(solution)/shard_map/ppermute | solution.py:21
  14.1 1.7 %collective-permute-done.5 = bf16[8,4096]{1,0:T(8,128)(2,1)S(1)} collective-permute-done((bf16[8,4096]{1,0:T(8,128)(2,1)S(1)}, bf16[8,4096]{1,0:T(8,128)(2,1)S(1)}, u32[]{:S(2)}, u32[]{:S(2)}) %collective-permute-start.5) | collective-permute-done | bytes 65568 | tf_op jit(solution)/shard_map/ppermute | solution.py:21
  15.8 0.0 collective-permute-start.6
  15.8 0.7 %collective-permute-start.8 = (bf16[16,4096]{1,0:T(8,128)(2,1)S(1)}, bf16[16,4096]{1,0:T(8,128)(2,1)S(1)}, u32[]{:S(2)}, u32[]{:S(2)}) collective-permute-start(bf16[16,4096]{1,0:T(8,128)(2,1)S(1)} %get-tuple-element.39), channel_id=1, source_target_pairs={{0,2},{1,3},{2,0},{3,1},{4,6},{5,7},{6,4},{7,5},{8,10},{9,11},{10,... | collective-permute-start | bytes 393224 | tf_op jit(solution)/shard_map/ppermute | solution.py:21
  16.5 1.5 %collective-permute-start.9 = (bf16[16,4096]{1,0:T(8,128)(2,1)S(1)}, bf16[16,4096]{1,0:T(8,128)(2,1)S(1)}, u32[]{:S(2)}, u32[]{:S(2)}) collective-permute-start(bf16[16,4096]{1,0:T(8,128)(2,1)S(1)} %get-tuple-element.40), channel_id=1, source_target_pairs={{0,4},{1,5},{2,6},{3,7},{4,0},{5,1},{6,2},{7,3},{8,12},{9,13},{10,... | collective-permute-start | bytes 393224 | tf_op jit(solution)/shard_map/ppermute | solution.py:21
  18.0 1.3 %collective-permute-start.10 = (bf16[16,4096]{1,0:T(8,128)(2,1)S(1)}, bf16[16,4096]{1,0:T(8,128)(2,1)S(1)}, u32[]{:S(2)}, u32[]{:S(2)}) collective-permute-start(bf16[16,4096]{1,0:T(8,128)(2,1)S(1)} %get-tuple-element.41), channel_id=1, source_target_pairs={{0,6},{1,7},{2,4},{3,5},{4,2},{5,3},{6,0},{7,1},{8,14},{9,15},{10,... | collective-permute-start | bytes 393224 | tf_op jit(solution)/shard_map/ppermute | solution.py:21
  19.3 2.9 %collective-permute-done.8.refs_0_ = bf16[16,4096]{1,0:T(8,128)(2,1)S(1)} collective-permute-done((bf16[16,4096]{1,0:T(8,128)(2,1)S(1)}, bf16[16,4096]{1,0:T(8,128)(2,1)S(1)}, u32[]{:S(2)}, u32[]{:S(2)}) %collective-permute-start.8) | collective-permute-done | bytes 131104 | tf_op jit(solution)/shard_map/ppermute | solution.py:21
  22.2 0.0 collective-permute-start.11
  22.2 2.6 %collective-permute-done.9.refs_1_ = bf16[16,4096]{1,0:T(8,128)(2,1)S(1)} collective-permute-done((bf16[16,4096]{1,0:T(8,128)(2,1)S(1)}, bf16[16,4096]{1,0:T(8,128)(2,1)S(1)}, u32[]{:S(2)}, u32[]{:S(2)}) %collective-permute-start.9) | collective-permute-done | bytes 131104 | tf_op jit(solution)/shard_map/ppermute | solution.py:21
  24.8 0.0 collective-permute-start.12
  24.8 0.0 collective-permute-done.10.refs_2_
  24.9 0.5 collective-permute-start.13
  25.4 0.0 collective-permute-done.6.other
  25.4 4.8 %shard_map.75 = (f32[56,4096]{1,0:T(8,128)S(1)}, bf16[56,4096]{1,0:T(8,128)(2,1)S(1)}, bf16[4096,768]{1,0:T(8,128)(2,1)S(1)}, bf16[384,4096]{1,0:T(8,128)(2,1)S(1)}) custom-call(bf16[56,4096]{1,0:T(8,128)(2,1)S(1)} %constant_dynamic-update-slice_fusion.own, bf16[56,4096]{1,0:T(8,128)(2,1)S(1)} %collective-permute-done.6.other, bf16[1,4096,768]{2,1,0:T(8,128)(2,1)} %w_in.1, ...), custom_call_target="tpu_custom_call" | custom-call | flops 120795955200 | tf_op jit(solution)/shard_map/pallas_call | solution.py:267
  30.2 0.0 collective-permute-done.11.refs_3_
  30.2 0.0 collective-permute-done.12.refs_4_
  30.2 0.0 collective-permute-done.13.refs_5_
  30.2 2.2 %shard_map.76 = (f32[16,4096]{1,0:T(8,128)S(1)}, f32[16,4096]{1,0:T(8,128)S(1)}, f32[16,4096]{1,0:T(8,128)S(1)}, bf16[16,4096]{1,0:T(8,128)(2,1)S(1)}, bf16[16,4...) custom-call(bf16[16,4096]{1,0:T(8,128)(2,1)S(1)} %collective-permute-done.8.refs_0_, ...), custom_call_target="tpu_custom_call" | custom-call | tf_op jit(solution)/shard_map/pallas_call | solution.py:271
  32.4 0.1 collective-permute-start.14
  32.5 0.5 collective-permute-start.16
  33.0 0.1 collective-permute-start.18
  33.1 0.4 collective-permute-start.7
  33.5 0.3 collective-permute-done.14
  33.9 1.5 %collective-permute-start.15 = (bf16[16,4096]{1,0:T(8,128)(2,1)S(1)}, bf16[16,4096]{1,0:T(8,128)(2,1)S(1)}, u32[]{:S(2)}, u32[]{:S(2)}) collective-permute-start(bf16[16,4096]{1,0:T(8,128)(2,1)S(1)} %add_convert_fusion.2), channel_id=1, source_target_pairs={{0,2},{1,3},{2,0},{3,1},{4,6},{5,7},{6,4},{7,5},{8,10},{9,11},{10,... | collective-permute-start | bytes 393224 | tf_op jit(solution)/shard_map/ppermute | solution.py:21
  35.3 0.0 collective-permute-done.16
  35.4 0.7 %collective-permute-start.17 = (bf16[16,4096]{1,0:T(8,128)(2,1)S(1)}, bf16[16,4096]{1,0:T(8,128)(2,1)S(1)}, u32[]{:S(2)}, u32[]{:S(2)}) collective-permute-start(bf16[16,4096]{1,0:T(8,128)(2,1)S(1)} %add_convert_fusion.1), channel_id=1, source_target_pairs={{0,4},{1,5},{2,6},{3,7},{4,0},{5,1},{6,2},{7,3},{8,12},{9,13},{10,... | collective-permute-start | bytes 393224 | tf_op jit(solution)/shard_map/ppermute | solution.py:21
  36.1 0.0 collective-permute-done.18
  36.1 1.5 %collective-permute-start.19 = (bf16[16,4096]{1,0:T(8,128)(2,1)S(1)}, bf16[16,4096]{1,0:T(8,128)(2,1)S(1)}, u32[]{:S(2)}, u32[]{:S(2)}) collective-permute-start(bf16[16,4096]{1,0:T(8,128)(2,1)S(1)} %add_convert_fusion), channel_id=1, source_target_pairs={{0,6},{1,7},{2,4},{3,5},{4,2},{5,3},{6,0},{7,1},{8,14},{9,15},{10,... | collective-permute-start | bytes 393224 | tf_op jit(solution)/shard_map/ppermute | solution.py:21
  37.6 2.2 %collective-permute-done.15.refs_0_ = bf16[16,4096]{1,0:T(8,128)(2,1)S(1)} collective-permute-done((bf16[16,4096]{1,0:T(8,128)(2,1)S(1)}, bf16[16,4096]{1,0:T(8,128)(2,1)S(1)}, u32[]{:S(2)}, u32[]{:S(2)}) %collective-permute-start.15) | collective-permute-done | bytes 131104 | tf_op jit(solution)/shard_map/ppermute | solution.py:21
  39.8 3.7 %collective-permute-done.17.refs_1_ = bf16[16,4096]{1,0:T(8,128)(2,1)S(1)} collective-permute-done((bf16[16,4096]{1,0:T(8,128)(2,1)S(1)}, bf16[16,4096]{1,0:T(8,128)(2,1)S(1)}, u32[]{:S(2)}, u32[]{:S(2)}) %collective-permute-start.17) | collective-permute-done | bytes 131104 | tf_op jit(solution)/shard_map/ppermute | solution.py:21
  43.5 0.0 collective-permute-done.19.refs_2_
  43.5 0.0 collective-permute-done.7.got
  43.5 0.2 shard_map.77
  43.7 2.1 %collective-permute-start.23 = (bf16[8,4096]{1,0:T(8,128)(2,1)S(1)}, bf16[8,4096]{1,0:T(8,128)(2,1)S(1)}, u32[]{:S(2)}, u32[]{:S(2)}) collective-permute-start(bf16[8,4096]{1,0:T(8,128)(2,1)S(1)} %get-tuple-element.52), channel_id=1, source_target_pairs={{0,8},{1,9},{2,10},{3,11},{4,12},{5,13},{6,14},{7,15},{8,0},{9,1},... | collective-permute-start | bytes 196616 | tf_op jit(solution)/shard_map/ppermute | solution.py:21
  45.8 2.1 %collective-permute-start.24 = (bf16[8,4096]{1,0:T(8,128)(2,1)S(1)}, bf16[8,4096]{1,0:T(8,128)(2,1)S(1)}, u32[]{:S(2)}, u32[]{:S(2)}) collective-permute-start(bf16[8,4096]{1,0:T(8,128)(2,1)S(1)} %get-tuple-element.53), channel_id=1, source_target_pairs={{0,16},{1,17},{2,18},{3,19},{4,20},{5,21},{6,22},{7,23},{8,24},{9,... | collective-permute-start | bytes 196616 | tf_op jit(solution)/shard_map/ppermute | solution.py:21
  48.0 0.4 collective-permute-start.25
  48.5 1.9 %collective-permute-start.22 = (bf16[8,4096]{1,0:T(8,128)(2,1)S(1)}, bf16[8,4096]{1,0:T(8,128)(2,1)S(1)}, u32[]{:S(2)}, u32[]{:S(2)}) collective-permute-start(bf16[8,4096]{1,0:T(8,128)(2,1)S(1)} %get-tuple-element.55), channel_id=1, source_target_pairs={{0,6},{1,7},{2,4},{3,5},{4,2},{5,3},{6,0},{7,1},{8,14},{9,15},{10,... | collective-permute-start | bytes 196616 | tf_op jit(solution)/shard_map/ppermute | solution.py:21
  50.4 0.5 collective-permute-start.21
  50.9 0.0 collective-permute-done.23.refs_3_
  50.9 1.1 %collective-permute-start.20 = (bf16[8,4096]{1,0:T(8,128)(2,1)S(1)}, bf16[8,4096]{1,0:T(8,128)(2,1)S(1)}, u32[]{:S(2)}, u32[]{:S(2)}) collective-permute-start(bf16[8,4096]{1,0:T(8,128)(2,1)S(1)} %get-tuple-element.57), channel_id=1, source_target_pairs={{0,2},{1,3},{2,0},{3,1},{4,6},{5,7},{6,4},{7,5},{8,10},{9,11},{10,... | collective-permute-start | bytes 196616 | tf_op jit(solution)/shard_map/ppermute | solution.py:21
  52.0 0.5 collective-permute-done.24.refs_4_
  52.6 1.5 %collective-permute-done.25.refs_5_ = bf16[8,4096]{1,0:T(8,128)(2,1)S(1)} collective-permute-done((bf16[8,4096]{1,0:T(8,128)(2,1)S(1)}, bf16[8,4096]{1,0:T(8,128)(2,1)S(1)}, u32[]{:S(2)}, u32[]{:S(2)}) %collective-permute-start.25) | collective-permute-done | bytes 65568 | tf_op jit(solution)/shard_map/ppermute | solution.py:21
  54.0 0.0 collective-permute-done.22.refs_2_
  54.0 0.6 %collective-permute-done.21.refs_1_ = bf16[8,4096]{1,0:T(8,128)(2,1)S(1)} collective-permute-done((bf16[8,4096]{1,0:T(8,128)(2,1)S(1)}, bf16[8,4096]{1,0:T(8,128)(2,1)S(1)}, u32[]{:S(2)}, u32[]{:S(2)}) %collective-permute-start.21) | collective-permute-done | bytes 65568 | tf_op jit(solution)/shard_map/ppermute | solution.py:21
  54.6 0.5 collective-permute-done.20.refs_0_
  55.1 0.8 %shard_map.78 = bf16[8,4096]{1,0:T(8,128)(2,1)} custom-call(f32[8,4096]{1,0:T(8,128)S(1)} %get-tuple-element.50.local, bf16[8,24]{1,0:T(8,128)(2,1)S(1)} %get-tuple-element.51.weights, bf16[8,4096]{1,0:T(8,128)(2,1)S(1)} %collective-permute-done.20.refs_0_, bf16[8,4096]{1,0:T(8,128)(2,1)S(1)} %collective-permute-done.21.refs_1_, ...), custom_call_target="tpu_custom_call" | custom-call | tf_op jit(solution)/shard_map/pallas_call | solution.py:293
  (8 shorter events, 0.2 us)
Async XLA Ops:
  1.7 9.0 %collective-permute-start.2 = (bf16[8,4224]{1,0:T(8,128)(2,1)S(1)}, bf16[8,4224]{1,0:T(8,128)(2,1)S(1)}, u32[]{:S(2)}, u32[]{:S(2)}) collective-permute-start(bf16[8,4224]{1,0:T(8,128)(2,1)S(1)} %get-tuple-element.30.refs_0_), channel_id=1, source_target_pairs={{0,24},{1,25},{2,26},{3,27},{4,28},{5,29},{6,30},{7,31},{8,16},{9,... | collective-permute-start | bytes 202760 | tf_op jit(solution)/shard_map/ppermute | solution.py:21
  6.8 5.8 %collective-permute-start.1 = (bf16[8,4224]{1,0:T(8,128)(2,1)S(1)}, bf16[8,4224]{1,0:T(8,128)(2,1)S(1)}, u32[]{:S(2)}, u32[]{:S(2)}) collective-permute-start(bf16[8,4224]{1,0:T(8,128)(2,1)S(1)} %get-tuple-element.30.refs_0_), channel_id=1, source_target_pairs={{0,16},{1,17},{2,18},{3,19},{4,20},{5,21},{6,22},{7,23},{8,24},{9,... | collective-permute-start | bytes 202760 | tf_op jit(solution)/shard_map/ppermute | solution.py:21
  6.8 5.8 %collective-permute-start = (bf16[8,4224]{1,0:T(8,128)(2,1)S(1)}, bf16[8,4224]{1,0:T(8,128)(2,1)S(1)}, u32[]{:S(2)}, u32[]{:S(2)}) collective-permute-start(bf16[8,4224]{1,0:T(8,128)(2,1)S(1)} %get-tuple-element.30.refs_0_), channel_id=1, source_target_pairs={{0,8},{1,9},{2,10},{3,11},{4,12},{5,13},{6,14},{7,15},{8,0},{9,1},... | collective-permute-start | bytes 202760 | tf_op jit(solution)/shard_map/ppermute | solution.py:21
  7.4 5.7 %collective-permute-start.3 = (bf16[8,4096]{1,0:T(8,128)(2,1)S(1)}, bf16[8,4096]{1,0:T(8,128)(2,1)S(1)}, u32[]{:S(2)}, u32[]{:S(2)}) collective-permute-start(bf16[8,4096]{1,0:T(8,128)(2,1)S(1)} %get-tuple-element.34), channel_id=1, source_target_pairs={{0,2},{1,3},{2,0},{3,1},{4,6},{5,7},{6,4},{7,5},{8,10},{9,11},{10,... | collective-permute-start | bytes 196616 | tf_op jit(solution)/shard_map/ppermute | solution.py:21
  9.1 5.0 %collective-permute-start.4 = (bf16[8,4096]{1,0:T(8,128)(2,1)S(1)}, bf16[8,4096]{1,0:T(8,128)(2,1)S(1)}, u32[]{:S(2)}, u32[]{:S(2)}) collective-permute-start(bf16[8,4096]{1,0:T(8,128)(2,1)S(1)} %get-tuple-element.35), channel_id=1, source_target_pairs={{0,4},{1,5},{2,6},{3,7},{4,0},{5,1},{6,2},{7,3},{8,12},{9,13},{10,... | collective-permute-start | bytes 196616 | tf_op jit(solution)/shard_map/ppermute | solution.py:21
  10.6 5.2 %collective-permute-start.5 = (bf16[8,4096]{1,0:T(8,128)(2,1)S(1)}, bf16[8,4096]{1,0:T(8,128)(2,1)S(1)}, u32[]{:S(2)}, u32[]{:S(2)}) collective-permute-start(bf16[8,4096]{1,0:T(8,128)(2,1)S(1)} %get-tuple-element.36), channel_id=1, source_target_pairs={{0,6},{1,7},{2,4},{3,5},{4,2},{5,3},{6,0},{7,1},{8,14},{9,15},{10,... | collective-permute-start | bytes 196616 | tf_op jit(solution)/shard_map/ppermute | solution.py:21
  15.8 9.6 %collective-permute-start.6 = (bf16[56,4096]{1,0:T(8,128)(2,1)S(1)}, bf16[56,4096]{1,0:T(8,128)(2,1)S(1)}, u32[]{:S(2)}, u32[]{:S(2)}) collective-permute-start(bf16[56,4096]{1,0:T(8,128)(2,1)S(1)} %constant_dynamic-update-slice_fusion.own), channel_id=1, source_target_pairs={{0,1},{1,0},{2,3},{3,2},{4,5},{5,4},{6,7},{7,6},{8,9},{9,8},{10,11... | collective-permute-start | bytes 1376264 | tf_op jit(solution)/shard_map/ppermute | solution.py:21
  15.8 6.4 %collective-permute-start.8 = (bf16[16,4096]{1,0:T(8,128)(2,1)S(1)}, bf16[16,4096]{1,0:T(8,128)(2,1)S(1)}, u32[]{:S(2)}, u32[]{:S(2)}) collective-permute-start(bf16[16,4096]{1,0:T(8,128)(2,1)S(1)} %get-tuple-element.39), channel_id=1, source_target_pairs={{0,2},{1,3},{2,0},{3,1},{4,6},{5,7},{6,4},{7,5},{8,10},{9,11},{10,... | collective-permute-start | bytes 393224 | tf_op jit(solution)/shard_map/ppermute | solution.py:21
  16.5 8.4 %collective-permute-start.9 = (bf16[16,4096]{1,0:T(8,128)(2,1)S(1)}, bf16[16,4096]{1,0:T(8,128)(2,1)S(1)}, u32[]{:S(2)}, u32[]{:S(2)}) collective-permute-start(bf16[16,4096]{1,0:T(8,128)(2,1)S(1)} %get-tuple-element.40), channel_id=1, source_target_pairs={{0,4},{1,5},{2,6},{3,7},{4,0},{5,1},{6,2},{7,3},{8,12},{9,13},{10,... | collective-permute-start | bytes 393224 | tf_op jit(solution)/shard_map/ppermute | solution.py:21
  18.0 6.8 %collective-permute-start.10 = (bf16[16,4096]{1,0:T(8,128)(2,1)S(1)}, bf16[16,4096]{1,0:T(8,128)(2,1)S(1)}, u32[]{:S(2)}, u32[]{:S(2)}) collective-permute-start(bf16[16,4096]{1,0:T(8,128)(2,1)S(1)} %get-tuple-element.41), channel_id=1, source_target_pairs={{0,6},{1,7},{2,4},{3,5},{4,2},{5,3},{6,0},{7,1},{8,14},{9,15},{10,... | collective-permute-start | bytes 393224 | tf_op jit(solution)/shard_map/ppermute | solution.py:21
  22.2 8.0 %collective-permute-start.11 = (bf16[16,4096]{1,0:T(8,128)(2,1)S(1)}, bf16[16,4096]{1,0:T(8,128)(2,1)S(1)}, u32[]{:S(2)}, u32[]{:S(2)}) collective-permute-start(bf16[16,4096]{1,0:T(8,128)(2,1)S(1)} %collective-permute-done.8.refs_0_), channel_id=1, source_target_pairs={{0,1},{1,0},{2,3},{3,2},{4,5},{5,4},{6,7},{7,6},{8,9},{9,8},{10,11... | collective-permute-start | bytes 393224 | tf_op jit(solution)/shard_map/ppermute | solution.py:21
  24.8 5.3 %collective-permute-start.12 = (bf16[16,4096]{1,0:T(8,128)(2,1)S(1)}, bf16[16,4096]{1,0:T(8,128)(2,1)S(1)}, u32[]{:S(2)}, u32[]{:S(2)}) collective-permute-start(bf16[16,4096]{1,0:T(8,128)(2,1)S(1)} %collective-permute-done.9.refs_1_), channel_id=1, source_target_pairs={{0,1},{1,0},{2,3},{3,2},{4,5},{5,4},{6,7},{7,6},{8,9},{9,8},{10,11... | collective-permute-start | bytes 393224 | tf_op jit(solution)/shard_map/ppermute | solution.py:21
  24.9 5.3 %collective-permute-start.13 = (bf16[16,4096]{1,0:T(8,128)(2,1)S(1)}, bf16[16,4096]{1,0:T(8,128)(2,1)S(1)}, u32[]{:S(2)}, u32[]{:S(2)}) collective-permute-start(bf16[16,4096]{1,0:T(8,128)(2,1)S(1)} %collective-permute-done.10.refs_2_), channel_id=1, source_target_pairs={{0,1},{1,0},{2,3},{3,2},{4,5},{5,4},{6,7},{7,6},{8,9},{9,8},{10,11... | collective-permute-start | bytes 393224 | tf_op jit(solution)/shard_map/ppermute | solution.py:21
  32.4 1.4 %collective-permute-start.14 = (bf16[16,4096]{1,0:T(8,128)(2,1)S(1)}, bf16[16,4096]{1,0:T(8,128)(2,1)S(1)}, u32[]{:S(2)}, u32[]{:S(2)}) collective-permute-start(bf16[16,4096]{1,0:T(8,128)(2,1)S(1)} %get-tuple-element.45), channel_id=1, source_target_pairs={{0,1},{1,0},{2,3},{3,2},{4,5},{5,4},{6,7},{7,6},{8,9},{9,8},{10,11... | collective-permute-start | bytes 393224 | tf_op jit(solution)/shard_map/ppermute | solution.py:21
  32.5 2.8 %collective-permute-start.16 = (bf16[16,4096]{1,0:T(8,128)(2,1)S(1)}, bf16[16,4096]{1,0:T(8,128)(2,1)S(1)}, u32[]{:S(2)}, u32[]{:S(2)}) collective-permute-start(bf16[16,4096]{1,0:T(8,128)(2,1)S(1)} %get-tuple-element.47), channel_id=1, source_target_pairs={{0,1},{1,0},{2,3},{3,2},{4,5},{5,4},{6,7},{7,6},{8,9},{9,8},{10,11... | collective-permute-start | bytes 393224 | tf_op jit(solution)/shard_map/ppermute | solution.py:21
  33.0 3.1 %collective-permute-start.18 = (bf16[16,4096]{1,0:T(8,128)(2,1)S(1)}, bf16[16,4096]{1,0:T(8,128)(2,1)S(1)}, u32[]{:S(2)}, u32[]{:S(2)}) collective-permute-start(bf16[16,4096]{1,0:T(8,128)(2,1)S(1)} %get-tuple-element.49), channel_id=1, source_target_pairs={{0,1},{1,0},{2,3},{3,2},{4,5},{5,4},{6,7},{7,6},{8,9},{9,8},{10,11... | collective-permute-start | bytes 393224 | tf_op jit(solution)/shard_map/ppermute | solution.py:21
  33.1 10.4 %collective-permute-start.7 = (bf16[56,4096]{1,0:T(8,128)(2,1)S(1)}, bf16[56,4096]{1,0:T(8,128)(2,1)S(1)}, u32[]{:S(2)}, u32[]{:S(2)}) collective-permute-start(bf16[56,4096]{1,0:T(8,128)(2,1)S(1)} %get-tuple-element.38), channel_id=1, source_target_pairs={{0,1},{1,0},{2,3},{3,2},{4,5},{5,4},{6,7},{7,6},{8,9},{9,8},{10,11... | collective-permute-start | bytes 1376264 | tf_op jit(solution)/shard_map/ppermute | solution.py:21
  33.9 5.9 %collective-permute-start.15 = (bf16[16,4096]{1,0:T(8,128)(2,1)S(1)}, bf16[16,4096]{1,0:T(8,128)(2,1)S(1)}, u32[]{:S(2)}, u32[]{:S(2)}) collective-permute-start(bf16[16,4096]{1,0:T(8,128)(2,1)S(1)} %add_convert_fusion.2), channel_id=1, source_target_pairs={{0,2},{1,3},{2,0},{3,1},{4,6},{5,7},{6,4},{7,5},{8,10},{9,11},{10,... | collective-permute-start | bytes 393224 | tf_op jit(solution)/shard_map/ppermute | solution.py:21
  35.4 8.1 %collective-permute-start.17 = (bf16[16,4096]{1,0:T(8,128)(2,1)S(1)}, bf16[16,4096]{1,0:T(8,128)(2,1)S(1)}, u32[]{:S(2)}, u32[]{:S(2)}) collective-permute-start(bf16[16,4096]{1,0:T(8,128)(2,1)S(1)} %add_convert_fusion.1), channel_id=1, source_target_pairs={{0,4},{1,5},{2,6},{3,7},{4,0},{5,1},{6,2},{7,3},{8,12},{9,13},{10,... | collective-permute-start | bytes 393224 | tf_op jit(solution)/shard_map/ppermute | solution.py:21
  36.1 7.4 %collective-permute-start.19 = (bf16[16,4096]{1,0:T(8,128)(2,1)S(1)}, bf16[16,4096]{1,0:T(8,128)(2,1)S(1)}, u32[]{:S(2)}, u32[]{:S(2)}) collective-permute-start(bf16[16,4096]{1,0:T(8,128)(2,1)S(1)} %add_convert_fusion), channel_id=1, source_target_pairs={{0,6},{1,7},{2,4},{3,5},{4,2},{5,3},{6,0},{7,1},{8,14},{9,15},{10,... | collective-permute-start | bytes 393224 | tf_op jit(solution)/shard_map/ppermute | solution.py:21
  43.7 7.1 %collective-permute-start.23 = (bf16[8,4096]{1,0:T(8,128)(2,1)S(1)}, bf16[8,4096]{1,0:T(8,128)(2,1)S(1)}, u32[]{:S(2)}, u32[]{:S(2)}) collective-permute-start(bf16[8,4096]{1,0:T(8,128)(2,1)S(1)} %get-tuple-element.52), channel_id=1, source_target_pairs={{0,8},{1,9},{2,10},{3,11},{4,12},{5,13},{6,14},{7,15},{8,0},{9,1},... | collective-permute-start | bytes 196616 | tf_op jit(solution)/shard_map/ppermute | solution.py:21
  45.8 6.7 %collective-permute-start.24 = (bf16[8,4096]{1,0:T(8,128)(2,1)S(1)}, bf16[8,4096]{1,0:T(8,128)(2,1)S(1)}, u32[]{:S(2)}, u32[]{:S(2)}) collective-permute-start(bf16[8,4096]{1,0:T(8,128)(2,1)S(1)} %get-tuple-element.53), channel_id=1, source_target_pairs={{0,16},{1,17},{2,18},{3,19},{4,20},{5,21},{6,22},{7,23},{8,24},{9,... | collective-permute-start | bytes 196616 | tf_op jit(solution)/shard_map/ppermute | solution.py:21
  48.0 6.1 %collective-permute-start.25 = (bf16[8,4096]{1,0:T(8,128)(2,1)S(1)}, bf16[8,4096]{1,0:T(8,128)(2,1)S(1)}, u32[]{:S(2)}, u32[]{:S(2)}) collective-permute-start(bf16[8,4096]{1,0:T(8,128)(2,1)S(1)} %get-tuple-element.54), channel_id=1, source_target_pairs={{0,24},{1,25},{2,26},{3,27},{4,28},{5,29},{6,30},{7,31},{8,16},{9,... | collective-permute-start | bytes 196616 | tf_op jit(solution)/shard_map/ppermute | solution.py:21
  48.5 5.6 %collective-permute-start.22 = (bf16[8,4096]{1,0:T(8,128)(2,1)S(1)}, bf16[8,4096]{1,0:T(8,128)(2,1)S(1)}, u32[]{:S(2)}, u32[]{:S(2)}) collective-permute-start(bf16[8,4096]{1,0:T(8,128)(2,1)S(1)} %get-tuple-element.55), channel_id=1, source_target_pairs={{0,6},{1,7},{2,4},{3,5},{4,2},{5,3},{6,0},{7,1},{8,14},{9,15},{10,... | collective-permute-start | bytes 196616 | tf_op jit(solution)/shard_map/ppermute | solution.py:21
  50.4 4.3 %collective-permute-start.21 = (bf16[8,4096]{1,0:T(8,128)(2,1)S(1)}, bf16[8,4096]{1,0:T(8,128)(2,1)S(1)}, u32[]{:S(2)}, u32[]{:S(2)}) collective-permute-start(bf16[8,4096]{1,0:T(8,128)(2,1)S(1)} %get-tuple-element.56), channel_id=1, source_target_pairs={{0,4},{1,5},{2,6},{3,7},{4,0},{5,1},{6,2},{7,3},{8,12},{9,13},{10,... | collective-permute-start | bytes 196616 | tf_op jit(solution)/shard_map/ppermute | solution.py:21
  50.9 4.3 %collective-permute-start.20 = (bf16[8,4096]{1,0:T(8,128)(2,1)S(1)}, bf16[8,4096]{1,0:T(8,128)(2,1)S(1)}, u32[]{:S(2)}, u32[]{:S(2)}) collective-permute-start(bf16[8,4096]{1,0:T(8,128)(2,1)S(1)} %get-tuple-element.57), channel_id=1, source_target_pairs={{0,2},{1,3},{2,0},{3,1},{4,6},{5,7},{6,4},{7,5},{8,10},{9,11},{10,... | collective-permute-start | bytes 196616 | tf_op jit(solution)/shard_map/ppermute | solution.py:21

commit v2 on v1

--- a/solution.py
+++ b/solution.py
@@ -113,9 +113,10 @@
 
 
 def own_kernel(
-    own, other, w_in, w_out, keep, give, inward, outward, stacked, acc, in_sem, out_sem, *, steps_in, steps_out
+    own, first, other, w_in, w_out, keep, keep_first, give_first, inward, outward, stacked, acc, in_sem, out_sem, *, steps_in, steps_out
 ):
-    rows, width = own.shape
+    held, width = own.shape
+    extra = first.shape[0]
     k_len = width // steps_in
     n_len = width // steps_out
     copies_in = [
@@ -128,8 +129,9 @@
     for copy in copies_in:
         copy.start()
     copy_out.start()
-    stacked[:rows] = own[...]
-    stacked[rows:] = other[...]
+    stacked[:held] = own[...]
+    stacked[held : held + extra] = first[...]
+    stacked[held + extra :] = other[...]
     for s in range(steps_in):
         span = slice(s * k_len, (s + 1) * k_len)
         copies_in[s].wait()
@@ -143,25 +145,28 @@
     for s in range(steps_out):
         cols = slice(s * n_len, (s + 1) * n_len)
         value = jnp.dot(hidden, outward[:, cols], preferred_element_type=F32)
-        keep[:, cols] = value[:rows]
-        give[:, cols] = value[rows:].astype(BF16)
+        keep[:, cols] = value[:held]
+        keep_first[:, cols] = value[held : held + extra]
+        give_first[:, cols] = value[held + extra :].astype(BF16)
 
 
 def peer_kernel(*refs, peers, steps_out):
-    pieces = refs[: 2 * peers]
-    inward, outward = refs[2 * peers : 2 * peers + 2]
-    results = refs[2 * peers + 2 : 4 * peers + 2]
+    pieces = refs[: 2 * peers + 1]
+    inward, outward = refs[2 * peers + 1 : 2 * peers + 3]
+    results = refs[2 * peers + 3 : 4 * peers + 4]
     stacked = refs[-1]
-    slots, width = pieces[0].shape
-    for p, ref in enumerate(pieces):
-        stacked[p * slots : (p + 1) * slots] = ref[...]
+    width = pieces[0].shape[1]
+    ends = [0]
+    for ref in pieces:
+        ends.append(ends[-1] + ref.shape[0])
+        stacked[ends[-2] : ends[-1]] = ref[...]
     hidden = activate(jnp.dot(stacked[...], inward[...], preferred_element_type=F32))
     n_len = width // steps_out
     for s in range(steps_out):
         cols = slice(s * n_len, (s + 1) * n_len)
         value = jnp.dot(hidden, outward[:, cols], preferred_element_type=F32)
         for p, ref in enumerate(results):
-            ref[:, cols] = value[p * slots : (p + 1) * slots].astype(ref.dtype)
+            ref[:, cols] = value[ends[p] : ends[p + 1]].astype(ref.dtype)
 
 
 def combine_kernel(shares, weights, keep, got, *refs, peers):
@@ -169,8 +174,7 @@
     blocks = refs[peers:]
     stacked = jnp.concatenate([ref[...] for ref in back], axis=0)
     mixed = jnp.dot(weights[...], stacked, preferred_element_type=F32)
-    held = shares.shape[0]
-    local = shares[:, :1] * (keep[:held] + got[:held].astype(F32))
+    local = shares[:, :1] * (keep[...] + got[...].astype(F32))
     rows = blocks[0].shape[0]
     blocks[0][...] = local[:rows]
     for b, ref in enumerate(blocks[1:]):
@@ -212,7 +216,6 @@
     slots = -(-(blocks - 1) * cap // 8) * 8
     table = -(-stations // LANES) * LANES
     held = blocks * rows
-    early = held + peers * slots_first
     steps_in, steps_out = 8, 4
     station = (lax.axis_index("expert") // 2).astype(jnp.int32).reshape(1)
     hbm = functools.partial(pltpu.with_memory_space_constraint, memory_space=pltpu.HBM)
@@ -244,44 +247,54 @@
     )(station, *column)
 
     arrived = [swap(chosen[j], (j + 1) << 1) for j in range(peers)]
-    own = jnp.concatenate([own] + first, axis=0)
     other = swap(own, 1)
+    first = jnp.concatenate(first, axis=0)
+    other_first = swap(first, 1)
+    extra = peers * slots_first
+    total = held + 2 * extra
     owned = call(
         functools.partial(own_kernel, steps_in=steps_in, steps_out=steps_out),
-        [VMEM, VMEM, HBM, HBM],
+        [VMEM] * 3 + [HBM] * 2,
         [
-            ((early, width), F32),
-            ((early, width), BF16),
+            ((held, width), F32),
+            ((extra, width), F32),
+            ((extra, width), BF16),
             ((width, 2 * half), BF16),
             ((half, width), BF16),
         ],
         [
-            pltpu.VMEM((2 * early, width), BF16),
-            pltpu.VMEM((2 * early, 2 * half), F32),
+            pltpu.VMEM((total, width), BF16),
+            pltpu.VMEM((total, 2 * half), F32),
             pltpu.SemaphoreType.DMA((steps_in,)),
             pltpu.SemaphoreType.DMA,
         ],
         limit=10,
         flops=2400 * held * half * width,
     )
-    keep, give, inward, outward = owned(own, other, hbm(w_in), hbm(w_out))
-    got = swap(give, 1)
-
-    pieces = arrived + [swap(block, 1) for block in arrived]
-    results = call(
+    keep, keep_first, give_first, inward, outward = owned(
+        own, first, other_first, hbm(w_in), hbm(w_out)
+    )
+    got_first = swap(give_first, 1)
+
+    swapped = [swap(block, 1) for block in arrived]
+    peer_call = call(
         functools.partial(peer_kernel, peers=peers, steps_out=steps_out),
-        [VMEM] * (2 * peers + 2),
-        [((slots, width), F32)] * peers + [((slots, width), BF16)] * peers,
-        [pltpu.VMEM((2 * peers * slots, width), BF16)],
-        limit=10,
-    )(*pieces, inward, outward)
+        [VMEM] * (2 * peers + 3),
+        [((slots, width), F32)] * peers
+        + [((slots, width), BF16)] * peers
+        + [((held, width), BF16)],
+        [pltpu.VMEM((2 * peers * slots + held, width), BF16)],
+        limit=12,
+    )
+    results = peer_call(*arrived, *swapped, other, inward, outward)
+    got = swap(results[-1], 1)
     back, back_first = [], []
     for j in range(peers):
         halves = swap(results[peers + j], 1)
         done = (results[j] + halves.astype(F32)).astype(BF16)
         back.append(swap(done, (j + 1) << 1))
-        span = slice(held + j * slots_first, held + (j + 1) * slots_first)
-        done = (keep[span] + got[span].astype(F32)).astype(BF16)
+        span = slice(j * slots_first, (j + 1) * slots_first)
+        done = (keep_first[span] + got_first[span].astype(F32)).astype(BF16)
         back_first.append(swap(done, (j + 1) << 1))
 
     summed = call(

time: 56.1 us -> 58.3 us (1.039)
  waiting for transfers between devices: 17.9 us -> 21.6 us
  starting transfers between devices: 27.6 us -> 26.2 us
    ppermute x26 -> x28, waiting for transfers between devices: 17.9 us -> 21.6 us  [swap(): return lax.ppermute(block, 'expert', [(i, i ^ mask) for i in range(count)])]
    ppermute x26 -> x28, starting transfers between devices: 27.6 us -> 26.2 us  [swap(): return lax.ppermute(block, 'expert', [(i, i ^ mask) for i in range(count)])]
  transfers between devices with their start and end apart: 26 -> 28, of which waited for: 12 -> 10; matrix products, arithmetic and copies ran while one was open for 0% -> 0% of each run, Pallas kernels for 9% -> 9%
where the time goes in v2:
time: 58.3 us; the launch traced here: 58.1 us
  starting transfers between devices  26.2 us (45%)
  waiting for transfers between devices  21.6 us (37%)
  Pallas kernels  10.1 us (17%)
    ppermute x28, starting transfers between devices, swap(): return lax.ppermute(block, 'expert', [(i, i ^ mask) for i in range(count)])  26.2 us
    ppermute x28, waiting for transfers between devices, swap(): return lax.ppermute(block, 'expert', [(i, i ^ mask) for i in range(count)])  21.6 us
    pallas_call x1, Pallas kernels, layer(): owned(own, first, other_first, hbm(w_in), hbm(w_out))  4.76 us
    pallas_call x1, Pallas kernels, layer(): results = peer_call(*arrived, *swapped, other, inward, outward)  2.17 us
    pallas_call x1, Pallas kernels, layer(): call(functools.partial(prepare_kernel, peers=peers, cap=cap, slots=slots_...  1.64 us
  transfers between devices with their start and end apart: 28, of which 10 were waited for; matrix products, arithmetic and copies ran while one was open for 0% of the time, Pallas kernels for 9%

profile of v2, /device:TPU:0, one launch (start us, length us, event | category | flops | bytes accessed | tf_op | source)
XLA Modules:
  0.0 58.1 jit_solution(10549367357716078506)
XLA Ops:
  0.0 1.6 %shard_map.73 = (bf16[8,4224]{1,0:T(8,128)(2,1)S(1)}, bf16[8,24]{1,0:T(8,128)(2,1)S(1)}, bf16[8,4096]{1,0:T(8,128)(2,1)S(1)}, bf16[8,4096]{1,0:T(8,128)(2,1)S(1)}, bf16[8,4096]{1,0:T(8,128)(2,1)S(1)}) custom-call(s32[1]{0:T(128)} %bitcast.station, bf16[8,4096]{1,0:T(8,128)(2,1)} %refs_0_.1, f32[1,4096]{1,0:T(1,128)} %bitcast.3, s32[8,8]{1,0:T(8,128)} %refs_2_.1, ...), custom_call_target="tpu_custom_call" | custom-call | tf_op jit(solution)/shard_map/pallas_call | solution.py:230
  1.7 3.0 %collective-permute-start.3 = (bf16[8,4096]{1,0:T(8,128)(2,1)S(1)}, bf16[8,4096]{1,0:T(8,128)(2,1)S(1)}, u32[]{:S(2)}, u32[]{:S(2)}) collective-permute-start(bf16[8,4096]{1,0:T(8,128)(2,1)S(1)} %get-tuple-element.36), channel_id=1, source_target_pairs={{0,2},{1,3},{2,0},{3,1},{4,6},{5,7},{6,4},{7,5},{8,10},{9,11},{10,... | collective-permute-start | bytes 196616 | tf_op jit(solution)/shard_map/ppermute | solution.py:21
  4.7 3.6 %collective-permute-start.2 = (bf16[8,4224]{1,0:T(8,128)(2,1)S(1)}, bf16[8,4224]{1,0:T(8,128)(2,1)S(1)}, u32[]{:S(2)}, u32[]{:S(2)}) collective-permute-start(bf16[8,4224]{1,0:T(8,128)(2,1)S(1)} %get-tuple-element.32.refs_0_), channel_id=1, source_target_pairs={{0,24},{1,25},{2,26},{3,27},{4,28},{5,29},{6,30},{7,31},{8,16},{9,... | collective-permute-start | bytes 202760 | tf_op jit(solution)/shard_map/ppermute | solution.py:21
  8.3 0.0 collective-permute-start.1
  8.3 0.8 %collective-permute-start = (bf16[8,4224]{1,0:T(8,128)(2,1)S(1)}, bf16[8,4224]{1,0:T(8,128)(2,1)S(1)}, u32[]{:S(2)}, u32[]{:S(2)}) collective-permute-start(bf16[8,4224]{1,0:T(8,128)(2,1)S(1)} %get-tuple-element.32.refs_0_), channel_id=1, source_target_pairs={{0,8},{1,9},{2,10},{3,11},{4,12},{5,13},{6,14},{7,15},{8,0},{9,1},... | collective-permute-start | bytes 202760 | tf_op jit(solution)/shard_map/ppermute | solution.py:21
  9.1 1.5 %collective-permute-start.4 = (bf16[8,4096]{1,0:T(8,128)(2,1)S(1)}, bf16[8,4096]{1,0:T(8,128)(2,1)S(1)}, u32[]{:S(2)}, u32[]{:S(2)}) collective-permute-start(bf16[8,4096]{1,0:T(8,128)(2,1)S(1)} %get-tuple-element.37), channel_id=1, source_target_pairs={{0,4},{1,5},{2,6},{3,7},{4,0},{5,1},{6,2},{7,3},{8,12},{9,13},{10,... | collective-permute-start | bytes 196616 | tf_op jit(solution)/shard_map/ppermute | solution.py:21
  10.6 0.0 collective-permute-done.3
  10.6 0.3 collective-permute-start.5
  10.9 3.1 %collective-permute-done.4 = bf16[8,4096]{1,0:T(8,128)(2,1)S(1)} collective-permute-done((bf16[8,4096]{1,0:T(8,128)(2,1)S(1)}, bf16[8,4096]{1,0:T(8,128)(2,1)S(1)}, u32[]{:S(2)}, u32[]{:S(2)}) %collective-permute-start.4) | collective-permute-done | bytes 65568 | tf_op jit(solution)/shard_map/ppermute | solution.py:21
  14.0 1.8 %collective-permute-done.5 = bf16[8,4096]{1,0:T(8,128)(2,1)S(1)} collective-permute-done((bf16[8,4096]{1,0:T(8,128)(2,1)S(1)}, bf16[8,4096]{1,0:T(8,128)(2,1)S(1)}, u32[]{:S(2)}, u32[]{:S(2)}) %collective-permute-start.5) | collective-permute-done | bytes 65568 | tf_op jit(solution)/shard_map/ppermute | solution.py:21
  15.8 0.0 collective-permute-start.6
  15.8 0.0 collective-permute-done.2.refs_3_
  15.8 0.0 collective-permute-done.1.refs_2_
  15.8 0.0 collective-permute-done.refs_1_
  15.8 0.5 shard_map.74
  16.3 0.6 %collective-permute-start.7 = (bf16[16,4096]{1,0:T(8,128)(2,1)S(1)}, bf16[16,4096]{1,0:T(8,128)(2,1)S(1)}, u32[]{:S(2)}, u32[]{:S(2)}) collective-permute-start(bf16[16,4096]{1,0:T(8,128)(2,1)S(1)} %get-tuple-element.40), channel_id=1, source_target_pairs={{0,2},{1,3},{2,0},{3,1},{4,6},{5,7},{6,4},{7,5},{8,10},{9,11},{10,... | collective-permute-start | bytes 393224 | tf_op jit(solution)/shard_map/ppermute | solution.py:21
  16.9 0.3 collective-permute-start.8
  17.2 2.7 %collective-permute-start.9 = (bf16[16,4096]{1,0:T(8,128)(2,1)S(1)}, bf16[16,4096]{1,0:T(8,128)(2,1)S(1)}, u32[]{:S(2)}, u32[]{:S(2)}) collective-permute-start(bf16[16,4096]{1,0:T(8,128)(2,1)S(1)} %get-tuple-element.42), channel_id=1, source_target_pairs={{0,6},{1,7},{2,4},{3,5},{4,2},{5,3},{6,0},{7,1},{8,14},{9,15},{10,... | collective-permute-start | bytes 393224 | tf_op jit(solution)/shard_map/ppermute | solution.py:21
  19.9 0.0 collective-permute-start.13
  19.9 2.9 %collective-permute-done.7.refs_0_ = bf16[16,4096]{1,0:T(8,128)(2,1)S(1)} collective-permute-done((bf16[16,4096]{1,0:T(8,128)(2,1)S(1)}, bf16[16,4096]{1,0:T(8,128)(2,1)S(1)}, u32[]{:S(2)}, u32[]{:S(2)}) %collective-permute-start.7) | collective-permute-done | bytes 131104 | tf_op jit(solution)/shard_map/ppermute | solution.py:21
  22.8 0.0 collective-permute-start.10
  22.8 2.6 %collective-permute-done.8.refs_1_ = bf16[16,4096]{1,0:T(8,128)(2,1)S(1)} collective-permute-done((bf16[16,4096]{1,0:T(8,128)(2,1)S(1)}, bf16[16,4096]{1,0:T(8,128)(2,1)S(1)}, u32[]{:S(2)}, u32[]{:S(2)}) %collective-permute-start.8) | collective-permute-done | bytes 131104 | tf_op jit(solution)/shard_map/ppermute | solution.py:21
  25.3 0.0 collective-permute-start.11
  25.3 0.0 collective-permute-done.9.refs_2_
  25.3 0.5 collective-permute-start.12
  25.9 0.0 collective-permute-done.6.other
  25.9 4.8 %shard_map.75 = (f32[32,4096]{1,0:T(8,128)S(1)}, f32[24,4096]{1,0:T(8,128)S(1)}, bf16[24,4096]{1,0:T(8,128)(2,1)S(1)}, bf16[4096,768]{1,0:T(8,128)(2,1)S(1)}, bf16[384,4096]{1,0:T(8,128)(2,1)S(1)}) custom-call(bf16[32,4096]{1,0:T(8,128)(2,1)S(1)} %get-tuple-element.35.own, bf16[24,4096]{1,0:T(8,128)(2,1)S(1)} %constant_dynamic-update-slice_fusion.first, ...), custom_call_target="tpu_custom_call" | custom-call | flops 120795955200 | tf_op jit(solution)/shard_map/pallas_call | solution.py:274
  30.6 0.0 collective-permute-done.10.refs_3_
  30.6 0.0 collective-permute-done.11.refs_4_
  30.6 0.0 collective-permute-done.12.refs_5_
  30.7 0.0 collective-permute-done.13.refs_6_
  30.7 2.2 %shard_map.76 = (f32[16,4096]{1,0:T(8,128)S(1)}, f32[16,4096]{1,0:T(8,128)S(1)}, f32[16,4096]{1,0:T(8,128)S(1)}, bf16[16,4096]{1,0:T(8,128)(2,1)S(1)}, bf16[16,4...) custom-call(bf16[16,4096]{1,0:T(8,128)(2,1)S(1)} %collective-permute-done.7.refs_0_, ...), custom_call_target="tpu_custom_call" | custom-call | tf_op jit(solution)/shard_map/pallas_call | solution.py:289
  32.8 0.1 collective-permute-start.15
  32.9 0.5 collective-permute-start.21
  33.4 0.1 collective-permute-start.17
  33.5 0.4 collective-permute-start.19
  33.9 0.1 collective-permute-start.14
  34.0 0.2 collective-permute-done.15
  34.3 1.6 %collective-permute-start.16 = (bf16[16,4096]{1,0:T(8,128)(2,1)S(1)}, bf16[16,4096]{1,0:T(8,128)(2,1)S(1)}, u32[]{:S(2)}, u32[]{:S(2)}) collective-permute-start(bf16[16,4096]{1,0:T(8,128)(2,1)S(1)} %add_convert_fusion.2), channel_id=1, source_target_pairs={{0,2},{1,3},{2,0},{3,1},{4,6},{5,7},{6,4},{7,5},{8,10},{9,11},{10,... | collective-permute-start | bytes 393224 | tf_op jit(solution)/shard_map/ppermute | solution.py:21
  35.9 0.0 collective-permute-done.17
  35.9 0.5 collective-permute-start.18
  36.5 0.0 collective-permute-done.19
  36.5 1.6 %collective-permute-start.20 = (bf16[16,4096]{1,0:T(8,128)(2,1)S(1)}, bf16[16,4096]{1,0:T(8,128)(2,1)S(1)}, u32[]{:S(2)}, u32[]{:S(2)}) collective-permute-start(bf16[16,4096]{1,0:T(8,128)(2,1)S(1)} %add_convert_fusion), channel_id=1, source_target_pairs={{0,6},{1,7},{2,4},{3,5},{4,2},{5,3},{6,0},{7,1},{8,14},{9,15},{10,... | collective-permute-start | bytes 393224 | tf_op jit(solution)/shard_map/ppermute | solution.py:21
  38.0 0.0 collective-permute-done.21
  38.1 1.5 %collective-permute-start.24 = (bf16[8,4096]{1,0:T(8,128)(2,1)S(1)}, bf16[8,4096]{1,0:T(8,128)(2,1)S(1)}, u32[]{:S(2)}, u32[]{:S(2)}) collective-permute-start(bf16[8,4096]{1,0:T(8,128)(2,1)S(1)} %get-tuple-element.59), channel_id=1, source_target_pairs={{0,6},{1,7},{2,4},{3,5},{4,2},{5,3},{6,0},{7,1},{8,14},{9,15},{10,... | collective-permute-start | bytes 196616 | tf_op jit(solution)/shard_map/ppermute | solution.py:21
  39.6 0.6 collective-permute-done.16.refs_0_
  40.1 1.5 %collective-permute-start.23 = (bf16[8,4096]{1,0:T(8,128)(2,1)S(1)}, bf16[8,4096]{1,0:T(8,128)(2,1)S(1)}, u32[]{:S(2)}, u32[]{:S(2)}) collective-permute-start(bf16[8,4096]{1,0:T(8,128)(2,1)S(1)} %get-tuple-element.60), channel_id=1, source_target_pairs={{0,4},{1,5},{2,6},{3,7},{4,0},{5,1},{6,2},{7,3},{8,12},{9,13},{10,... | collective-permute-start | bytes 196616 | tf_op jit(solution)/shard_map/ppermute | solution.py:21
  41.6 4.6 %collective-permute-done.18.refs_1_ = bf16[16,4096]{1,0:T(8,128)(2,1)S(1)} collective-permute-done((bf16[16,4096]{1,0:T(8,128)(2,1)S(1)}, bf16[16,4096]{1,0:T(8,128)(2,1)S(1)}, u32[]{:S(2)}, u32[]{:S(2)}) %collective-permute-start.18) | collective-permute-done | bytes 131104 | tf_op jit(solution)/shard_map/ppermute | solution.py:21
  46.2 0.7 %collective-permute-start.22 = (bf16[8,4096]{1,0:T(8,128)(2,1)S(1)}, bf16[8,4096]{1,0:T(8,128)(2,1)S(1)}, u32[]{:S(2)}, u32[]{:S(2)}) collective-permute-start(bf16[8,4096]{1,0:T(8,128)(2,1)S(1)} %get-tuple-element.61), channel_id=1, source_target_pairs={{0,2},{1,3},{2,0},{3,1},{4,6},{5,7},{6,4},{7,5},{8,10},{9,11},{10,... | collective-permute-start | bytes 196616 | tf_op jit(solution)/shard_map/ppermute | solution.py:21
  46.9 0.0 collective-permute-done.20.refs_2_
  46.9 0.0 collective-permute-done.14.got
  46.9 0.2 shard_map.77
  47.1 1.3 %collective-permute-start.25 = (bf16[8,4096]{1,0:T(8,128)(2,1)S(1)}, bf16[8,4096]{1,0:T(8,128)(2,1)S(1)}, u32[]{:S(2)}, u32[]{:S(2)}) collective-permute-start(bf16[8,4096]{1,0:T(8,128)(2,1)S(1)} %get-tuple-element.56), channel_id=1, source_target_pairs={{0,8},{1,9},{2,10},{3,11},{4,12},{5,13},{6,14},{7,15},{8,0},{9,1},... | collective-permute-start | bytes 196616 | tf_op jit(solution)/shard_map/ppermute | solution.py:21
  48.4 2.9 %collective-permute-start.26 = (bf16[8,4096]{1,0:T(8,128)(2,1)S(1)}, bf16[8,4096]{1,0:T(8,128)(2,1)S(1)}, u32[]{:S(2)}, u32[]{:S(2)}) collective-permute-start(bf16[8,4096]{1,0:T(8,128)(2,1)S(1)} %get-tuple-element.57), channel_id=1, source_target_pairs={{0,16},{1,17},{2,18},{3,19},{4,20},{5,21},{6,22},{7,23},{8,24},{9,... | collective-permute-start | bytes 196616 | tf_op jit(solution)/shard_map/ppermute | solution.py:21
  51.3 0.0 collective-permute-done.24.refs_2_
  51.3 0.3 collective-permute-start.27
  51.5 0.0 collective-permute-done.23.refs_1_
  51.5 0.0 collective-permute-done.22.refs_0_
  51.5 0.6 collective-permute-done.25.refs_3_
  52.1 2.1 %collective-permute-done.26.refs_4_ = bf16[8,4096]{1,0:T(8,128)(2,1)S(1)} collective-permute-done((bf16[8,4096]{1,0:T(8,128)(2,1)S(1)}, bf16[8,4096]{1,0:T(8,128)(2,1)S(1)}, u32[]{:S(2)}, u32[]{:S(2)}) %collective-permute-start.26) | collective-permute-done | bytes 65568 | tf_op jit(solution)/shard_map/ppermute | solution.py:21
  54.2 3.1 %collective-permute-done.27.refs_5_ = bf16[8,4096]{1,0:T(8,128)(2,1)S(1)} collective-permute-done((bf16[8,4096]{1,0:T(8,128)(2,1)S(1)}, bf16[8,4096]{1,0:T(8,128)(2,1)S(1)}, u32[]{:S(2)}, u32[]{:S(2)}) %collective-permute-start.27) | collective-permute-done | bytes 65568 | tf_op jit(solution)/shard_map/ppermute | solution.py:21
  57.3 0.8 %shard_map.78 = bf16[8,4096]{1,0:T(8,128)(2,1)} custom-call(f32[8,4096]{1,0:T(8,128)S(1)} %get-tuple-element.52.local, bf16[8,24]{1,0:T(8,128)(2,1)S(1)} %get-tuple-element.53.weights, bf16[8,4096]{1,0:T(8,128)(2,1)S(1)} %collective-permute-done.22.refs_0_, bf16[8,4096]{1,0:T(8,128)(2,1)S(1)} %collective-permute-done.23.refs_1_, ...), custom_call_target="tpu_custom_call" | custom-call | tf_op jit(solution)/shard_map/pallas_call | solution.py:306
  (7 shorter events, 0.1 us)
Async XLA Ops:
  1.7 9.0 %collective-permute-start.3 = (bf16[8,4096]{1,0:T(8,128)(2,1)S(1)}, bf16[8,4096]{1,0:T(8,128)(2,1)S(1)}, u32[]{:S(2)}, u32[]{:S(2)}) collective-permute-start(bf16[8,4096]{1,0:T(8,128)(2,1)S(1)} %get-tuple-element.36), channel_id=1, source_target_pairs={{0,2},{1,3},{2,0},{3,1},{4,6},{5,7},{6,4},{7,5},{8,10},{9,11},{10,... | collective-permute-start | bytes 196616 | tf_op jit(solution)/shard_map/ppermute | solution.py:21
  4.7 11.1 %collective-permute-start.2 = (bf16[8,4224]{1,0:T(8,128)(2,1)S(1)}, bf16[8,4224]{1,0:T(8,128)(2,1)S(1)}, u32[]{:S(2)}, u32[]{:S(2)}) collective-permute-start(bf16[8,4224]{1,0:T(8,128)(2,1)S(1)} %get-tuple-element.32.refs_0_), channel_id=1, source_target_pairs={{0,24},{1,25},{2,26},{3,27},{4,28},{5,29},{6,30},{7,31},{8,16},{9,... | collective-permute-start | bytes 202760 | tf_op jit(solution)/shard_map/ppermute | solution.py:21
  8.3 7.5 %collective-permute-start.1 = (bf16[8,4224]{1,0:T(8,128)(2,1)S(1)}, bf16[8,4224]{1,0:T(8,128)(2,1)S(1)}, u32[]{:S(2)}, u32[]{:S(2)}) collective-permute-start(bf16[8,4224]{1,0:T(8,128)(2,1)S(1)} %get-tuple-element.32.refs_0_), channel_id=1, source_target_pairs={{0,16},{1,17},{2,18},{3,19},{4,20},{5,21},{6,22},{7,23},{8,24},{9,... | collective-permute-start | bytes 202760 | tf_op jit(solution)/shard_map/ppermute | solution.py:21
  8.3 7.5 %collective-permute-start = (bf16[8,4224]{1,0:T(8,128)(2,1)S(1)}, bf16[8,4224]{1,0:T(8,128)(2,1)S(1)}, u32[]{:S(2)}, u32[]{:S(2)}) collective-permute-start(bf16[8,4224]{1,0:T(8,128)(2,1)S(1)} %get-tuple-element.32.refs_0_), channel_id=1, source_target_pairs={{0,8},{1,9},{2,10},{3,11},{4,12},{5,13},{6,14},{7,15},{8,0},{9,1},... | collective-permute-start | bytes 202760 | tf_op jit(solution)/shard_map/ppermute | solution.py:21
  9.1 4.9 %collective-permute-start.4 = (bf16[8,4096]{1,0:T(8,128)(2,1)S(1)}, bf16[8,4096]{1,0:T(8,128)(2,1)S(1)}, u32[]{:S(2)}, u32[]{:S(2)}) collective-permute-start(bf16[8,4096]{1,0:T(8,128)(2,1)S(1)} %get-tuple-element.37), channel_id=1, source_target_pairs={{0,4},{1,5},{2,6},{3,7},{4,0},{5,1},{6,2},{7,3},{8,12},{9,13},{10,... | collective-permute-start | bytes 196616 | tf_op jit(solution)/shard_map/ppermute | solution.py:21
  10.6 5.2 %collective-permute-start.5 = (bf16[8,4096]{1,0:T(8,128)(2,1)S(1)}, bf16[8,4096]{1,0:T(8,128)(2,1)S(1)}, u32[]{:S(2)}, u32[]{:S(2)}) collective-permute-start(bf16[8,4096]{1,0:T(8,128)(2,1)S(1)} %get-tuple-element.38), channel_id=1, source_target_pairs={{0,6},{1,7},{2,4},{3,5},{4,2},{5,3},{6,0},{7,1},{8,14},{9,15},{10,... | collective-permute-start | bytes 196616 | tf_op jit(solution)/shard_map/ppermute | solution.py:21
  15.8 10.1 %collective-permute-start.6 = (bf16[24,4096]{1,0:T(8,128)(2,1)S(1)}, bf16[24,4096]{1,0:T(8,128)(2,1)S(1)}, u32[]{:S(2)}, u32[]{:S(2)}) collective-permute-start(bf16[24,4096]{1,0:T(8,128)(2,1)S(1)} %constant_dynamic-update-slice_fusion.first), channel_id=1, source_target_pairs={{0,1},{1,0},{2,3},{3,2},{4,5},{5,4},{6,7},{7,6},{8,9},{9,8},{10,11... | collective-permute-start | bytes 589832 | tf_op jit(solution)/shard_map/ppermute | solution.py:21
  16.3 6.4 %collective-permute-start.7 = (bf16[16,4096]{1,0:T(8,128)(2,1)S(1)}, bf16[16,4096]{1,0:T(8,128)(2,1)S(1)}, u32[]{:S(2)}, u32[]{:S(2)}) collective-permute-start(bf16[16,4096]{1,0:T(8,128)(2,1)S(1)} %get-tuple-element.40), channel_id=1, source_target_pairs={{0,2},{1,3},{2,0},{3,1},{4,6},{5,7},{6,4},{7,5},{8,10},{9,11},{10,... | collective-permute-start | bytes 393224 | tf_op jit(solution)/shard_map/ppermute | solution.py:21
  16.9 8.4 %collective-permute-start.8 = (bf16[16,4096]{1,0:T(8,128)(2,1)S(1)}, bf16[16,4096]{1,0:T(8,128)(2,1)S(1)}, u32[]{:S(2)}, u32[]{:S(2)}) collective-permute-start(bf16[16,4096]{1,0:T(8,128)(2,1)S(1)} %get-tuple-element.41), channel_id=1, source_target_pairs={{0,4},{1,5},{2,6},{3,7},{4,0},{5,1},{6,2},{7,3},{8,12},{9,13},{10,... | collective-permute-start | bytes 393224 | tf_op jit(solution)/shard_map/ppermute | solution.py:21
  17.2 8.1 %collective-permute-start.9 = (bf16[16,4096]{1,0:T(8,128)(2,1)S(1)}, bf16[16,4096]{1,0:T(8,128)(2,1)S(1)}, u32[]{:S(2)}, u32[]{:S(2)}) collective-permute-start(bf16[16,4096]{1,0:T(8,128)(2,1)S(1)} %get-tuple-element.42), channel_id=1, source_target_pairs={{0,6},{1,7},{2,4},{3,5},{4,2},{5,3},{6,0},{7,1},{8,14},{9,15},{10,... | collective-permute-start | bytes 393224 | tf_op jit(solution)/shard_map/ppermute | solution.py:21
  19.9 10.8 %collective-permute-start.13 = (bf16[32,4096]{1,0:T(8,128)(2,1)S(1)}, bf16[32,4096]{1,0:T(8,128)(2,1)S(1)}, u32[]{:S(2)}, u32[]{:S(2)}) collective-permute-start(bf16[32,4096]{1,0:T(8,128)(2,1)S(1)} %get-tuple-element.35.own), channel_id=1, source_target_pairs={{0,1},{1,0},{2,3},{3,2},{4,5},{5,4},{6,7},{7,6},{8,9},{9,8},{10,11... | collective-permute-start | bytes 786440 | tf_op jit(solution)/shard_map/ppermute | solution.py:21
  22.8 7.9 %collective-permute-start.10 = (bf16[16,4096]{1,0:T(8,128)(2,1)S(1)}, bf16[16,4096]{1,0:T(8,128)(2,1)S(1)}, u32[]{:S(2)}, u32[]{:S(2)}) collective-permute-start(bf16[16,4096]{1,0:T(8,128)(2,1)S(1)} %collective-permute-done.7.refs_0_), channel_id=1, source_target_pairs={{0,1},{1,0},{2,3},{3,2},{4,5},{5,4},{6,7},{7,6},{8,9},{9,8},{10,11... | collective-permute-start | bytes 393224 | tf_op jit(solution)/shard_map/ppermute | solution.py:21
  25.3 5.3 %collective-permute-start.11 = (bf16[16,4096]{1,0:T(8,128)(2,1)S(1)}, bf16[16,4096]{1,0:T(8,128)(2,1)S(1)}, u32[]{:S(2)}, u32[]{:S(2)}) collective-permute-start(bf16[16,4096]{1,0:T(8,128)(2,1)S(1)} %collective-permute-done.8.refs_1_), channel_id=1, source_target_pairs={{0,1},{1,0},{2,3},{3,2},{4,5},{5,4},{6,7},{7,6},{8,9},{9,8},{10,11... | collective-permute-start | bytes 393224 | tf_op jit(solution)/shard_map/ppermute | solution.py:21
  25.3 5.3 %collective-permute-start.12 = (bf16[16,4096]{1,0:T(8,128)(2,1)S(1)}, bf16[16,4096]{1,0:T(8,128)(2,1)S(1)}, u32[]{:S(2)}, u32[]{:S(2)}) collective-permute-start(bf16[16,4096]{1,0:T(8,128)(2,1)S(1)} %collective-permute-done.9.refs_2_), channel_id=1, source_target_pairs={{0,1},{1,0},{2,3},{3,2},{4,5},{5,4},{6,7},{7,6},{8,9},{9,8},{10,11... | collective-permute-start | bytes 393224 | tf_op jit(solution)/shard_map/ppermute | solution.py:21
  32.8 1.4 %collective-permute-start.15 = (bf16[16,4096]{1,0:T(8,128)(2,1)S(1)}, bf16[16,4096]{1,0:T(8,128)(2,1)S(1)}, u32[]{:S(2)}, u32[]{:S(2)}) collective-permute-start(bf16[16,4096]{1,0:T(8,128)(2,1)S(1)} %get-tuple-element.47), channel_id=1, source_target_pairs={{0,1},{1,0},{2,3},{3,2},{4,5},{5,4},{6,7},{7,6},{8,9},{9,8},{10,11... | collective-permute-start | bytes 393224 | tf_op jit(solution)/shard_map/ppermute | solution.py:21
  32.9 5.1 %collective-permute-start.21 = (bf16[24,4096]{1,0:T(8,128)(2,1)S(1)}, bf16[24,4096]{1,0:T(8,128)(2,1)S(1)}, u32[]{:S(2)}, u32[]{:S(2)}) collective-permute-start(bf16[24,4096]{1,0:T(8,128)(2,1)S(1)} %get-tuple-element.55), channel_id=1, source_target_pairs={{0,1},{1,0},{2,3},{3,2},{4,5},{5,4},{6,7},{7,6},{8,9},{9,8},{10,11... | collective-permute-start | bytes 589832 | tf_op jit(solution)/shard_map/ppermute | solution.py:21
  33.4 2.4 %collective-permute-start.17 = (bf16[16,4096]{1,0:T(8,128)(2,1)S(1)}, bf16[16,4096]{1,0:T(8,128)(2,1)S(1)}, u32[]{:S(2)}, u32[]{:S(2)}) collective-permute-start(bf16[16,4096]{1,0:T(8,128)(2,1)S(1)} %get-tuple-element.49), channel_id=1, source_target_pairs={{0,1},{1,0},{2,3},{3,2},{4,5},{5,4},{6,7},{7,6},{8,9},{9,8},{10,11... | collective-permute-start | bytes 393224 | tf_op jit(solution)/shard_map/ppermute | solution.py:21
  33.5 3.0 %collective-permute-start.19 = (bf16[16,4096]{1,0:T(8,128)(2,1)S(1)}, bf16[16,4096]{1,0:T(8,128)(2,1)S(1)}, u32[]{:S(2)}, u32[]{:S(2)}) collective-permute-start(bf16[16,4096]{1,0:T(8,128)(2,1)S(1)} %get-tuple-element.51), channel_id=1, source_target_pairs={{0,1},{1,0},{2,3},{3,2},{4,5},{5,4},{6,7},{7,6},{8,9},{9,8},{10,11... | collective-permute-start | bytes 393224 | tf_op jit(solution)/shard_map/ppermute | solution.py:21
  33.9 12.9 %collective-permute-start.14 = (bf16[32,4096]{1,0:T(8,128)(2,1)S(1)}, bf16[32,4096]{1,0:T(8,128)(2,1)S(1)}, u32[]{:S(2)}, u32[]{:S(2)}) collective-permute-start(bf16[32,4096]{1,0:T(8,128)(2,1)S(1)} %get-tuple-element.45), channel_id=1, source_target_pairs={{0,1},{1,0},{2,3},{3,2},{4,5},{5,4},{6,7},{7,6},{8,9},{9,8},{10,11... | collective-permute-start | bytes 786440 | tf_op jit(solution)/shard_map/ppermute | solution.py:21
  34.3 5.8 %collective-permute-start.16 = (bf16[16,4096]{1,0:T(8,128)(2,1)S(1)}, bf16[16,4096]{1,0:T(8,128)(2,1)S(1)}, u32[]{:S(2)}, u32[]{:S(2)}) collective-permute-start(bf16[16,4096]{1,0:T(8,128)(2,1)S(1)} %add_convert_fusion.2), channel_id=1, source_target_pairs={{0,2},{1,3},{2,0},{3,1},{4,6},{5,7},{6,4},{7,5},{8,10},{9,11},{10,... | collective-permute-start | bytes 393224 | tf_op jit(solution)/shard_map/ppermute | solution.py:21
  35.9 10.3 %collective-permute-start.18 = (bf16[16,4096]{1,0:T(8,128)(2,1)S(1)}, bf16[16,4096]{1,0:T(8,128)(2,1)S(1)}, u32[]{:S(2)}, u32[]{:S(2)}) collective-permute-start(bf16[16,4096]{1,0:T(8,128)(2,1)S(1)} %add_convert_fusion.1), channel_id=1, source_target_pairs={{0,4},{1,5},{2,6},{3,7},{4,0},{5,1},{6,2},{7,3},{8,12},{9,13},{10,... | collective-permute-start | bytes 393224 | tf_op jit(solution)/shard_map/ppermute | solution.py:21
  36.5 10.4 %collective-permute-start.20 = (bf16[16,4096]{1,0:T(8,128)(2,1)S(1)}, bf16[16,4096]{1,0:T(8,128)(2,1)S(1)}, u32[]{:S(2)}, u32[]{:S(2)}) collective-permute-start(bf16[16,4096]{1,0:T(8,128)(2,1)S(1)} %add_convert_fusion), channel_id=1, source_target_pairs={{0,6},{1,7},{2,4},{3,5},{4,2},{5,3},{6,0},{7,1},{8,14},{9,15},{10,... | collective-permute-start | bytes 393224 | tf_op jit(solution)/shard_map/ppermute | solution.py:21
  38.1 13.2 %collective-permute-start.24 = (bf16[8,4096]{1,0:T(8,128)(2,1)S(1)}, bf16[8,4096]{1,0:T(8,128)(2,1)S(1)}, u32[]{:S(2)}, u32[]{:S(2)}) collective-permute-start(bf16[8,4096]{1,0:T(8,128)(2,1)S(1)} %get-tuple-element.59), channel_id=1, source_target_pairs={{0,6},{1,7},{2,4},{3,5},{4,2},{5,3},{6,0},{7,1},{8,14},{9,15},{10,... | collective-permute-start | bytes 196616 | tf_op jit(solution)/shard_map/ppermute | solution.py:21
  40.1 11.4 %collective-permute-start.23 = (bf16[8,4096]{1,0:T(8,128)(2,1)S(1)}, bf16[8,4096]{1,0:T(8,128)(2,1)S(1)}, u32[]{:S(2)}, u32[]{:S(2)}) collective-permute-start(bf16[8,4096]{1,0:T(8,128)(2,1)S(1)} %get-tuple-element.60), channel_id=1, source_target_pairs={{0,4},{1,5},{2,6},{3,7},{4,0},{5,1},{6,2},{7,3},{8,12},{9,13},{10,... | collective-permute-start | bytes 196616 | tf_op jit(solution)/shard_map/ppermute | solution.py:21
  46.2 5.4 %collective-permute-start.22 = (bf16[8,4096]{1,0:T(8,128)(2,1)S(1)}, bf16[8,4096]{1,0:T(8,128)(2,1)S(1)}, u32[]{:S(2)}, u32[]{:S(2)}) collective-permute-start(bf16[8,4096]{1,0:T(8,128)(2,1)S(1)} %get-tuple-element.61), channel_id=1, source_target_pairs={{0,2},{1,3},{2,0},{3,1},{4,6},{5,7},{6,4},{7,5},{8,10},{9,11},{10,... | collective-permute-start | bytes 196616 | tf_op jit(solution)/shard_map/ppermute | solution.py:21
  47.1 5.0 %collective-permute-start.25 = (bf16[8,4096]{1,0:T(8,128)(2,1)S(1)}, bf16[8,4096]{1,0:T(8,128)(2,1)S(1)}, u32[]{:S(2)}, u32[]{:S(2)}) collective-permute-start(bf16[8,4096]{1,0:T(8,128)(2,1)S(1)} %get-tuple-element.56), channel_id=1, source_target_pairs={{0,8},{1,9},{2,10},{3,11},{4,12},{5,13},{6,14},{7,15},{8,0},{9,1},... | collective-permute-start | bytes 196616 | tf_op jit(solution)/shard_map/ppermute | solution.py:21
  48.4 5.9 %collective-permute-start.26 = (bf16[8,4096]{1,0:T(8,128)(2,1)S(1)}, bf16[8,4096]{1,0:T(8,128)(2,1)S(1)}, u32[]{:S(2)}, u32[]{:S(2)}) collective-permute-start(bf16[8,4096]{1,0:T(8,128)(2,1)S(1)} %get-tuple-element.57), channel_id=1, source_target_pairs={{0,16},{1,17},{2,18},{3,19},{4,20},{5,21},{6,22},{7,23},{8,24},{9,... | collective-permute-start | bytes 196616 | tf_op jit(solution)/shard_map/ppermute | solution.py:21
  51.3 6.1 %collective-permute-start.27 = (bf16[8,4096]{1,0:T(8,128)(2,1)S(1)}, bf16[8,4096]{1,0:T(8,128)(2,1)S(1)}, u32[]{:S(2)}, u32[]{:S(2)}) collective-permute-start(bf16[8,4096]{1,0:T(8,128)(2,1)S(1)} %get-tuple-element.58), channel_id=1, source_target_pairs={{0,24},{1,25},{2,26},{3,27},{4,28},{5,29},{6,30},{7,31},{8,16},{9,... | collective-permute-start | bytes 196616 | tf_op jit(solution)/shard_map/ppermute | solution.py:21

commit v3 on v1

--- a/solution.py
+++ b/solution.py
@@ -112,56 +112,38 @@
     return (gate / (1.0 + jnp.exp(-gate)) * projected[:, half:]).astype(BF16)
 
 
-def own_kernel(
-    own, other, w_in, w_out, keep, give, inward, outward, stacked, acc, in_sem, out_sem, *, steps_in, steps_out
-):
-    rows, width = own.shape
-    k_len = width // steps_in
-    n_len = width // steps_out
-    copies_in = [
+def load_kernel(weights, loaded, sems):
+    steps = sems.shape[0]
+    size = loaded.shape[0] // steps
+    copies = [
         pltpu.make_async_copy(
-            w_in.at[0, pl.ds(s * k_len, k_len)], inward.at[pl.ds(s * k_len, k_len)], in_sem.at[s]
+            weights.at[0, pl.ds(s * size, size)], loaded.at[pl.ds(s * size, size)], sems.at[s]
         )
-        for s in range(steps_in)
+        for s in range(steps)
     ]
-    copy_out = pltpu.make_async_copy(w_out.at[0], outward, out_sem)
-    for copy in copies_in:
+    for copy in copies:
         copy.start()
-    copy_out.start()
-    stacked[:rows] = own[...]
-    stacked[rows:] = other[...]
-    for s in range(steps_in):
-        span = slice(s * k_len, (s + 1) * k_len)
-        copies_in[s].wait()
-        part = jnp.dot(stacked[:, span], inward[span], preferred_element_type=F32)
-        if s == 0:
-            acc[...] = part
-        else:
-            acc[...] += part
-    hidden = activate(acc[...])
-    copy_out.wait()
-    for s in range(steps_out):
-        cols = slice(s * n_len, (s + 1) * n_len)
-        value = jnp.dot(hidden, outward[:, cols], preferred_element_type=F32)
-        keep[:, cols] = value[:rows]
-        give[:, cols] = value[rows:].astype(BF16)
-
-
-def peer_kernel(*refs, peers, steps_out):
-    pieces = refs[: 2 * peers]
-    inward, outward = refs[2 * peers : 2 * peers + 2]
-    results = refs[2 * peers + 2 : 4 * peers + 2]
+    for copy in copies:
+        copy.wait()
+
+
+def expert_kernel(*refs, pieces, steps_out):
+    inputs = refs[:pieces]
+    inward, outward = refs[pieces : pieces + 2]
+    results = refs[pieces + 2 : -1]
     stacked = refs[-1]
-    slots, width = pieces[0].shape
-    for p, ref in enumerate(pieces):
-        stacked[p * slots : (p + 1) * slots] = ref[...]
+    width = inputs[0].shape[1]
+    ends = [0]
+    for ref in inputs:
+        ends.append(ends[-1] + ref.shape[0])
+        stacked[ends[-2] : ends[-1]] = ref[...]
     hidden = activate(jnp.dot(stacked[...], inward[...], preferred_element_type=F32))
     n_len = width // steps_out
     for s in range(steps_out):
         cols = slice(s * n_len, (s + 1) * n_len)
         value = jnp.dot(hidden, outward[:, cols], preferred_element_type=F32)
         for p, ref in enumerate(results):
-            ref[:, cols] = value[p * slots : (p + 1) * slots].astype(ref.dtype)
+            ref[:, cols] = value[ends[p] : ends[p + 1]].astype(ref.dtype)
 
 
 def combine_kernel(shares, weights, keep, got, *refs, peers):
@@ -199,6 +181,13 @@
     )
 
 
+def load(weights, steps=8):
+    kernel = call(
+        load_kernel, [HBM], [(weights.shape[1:], weights.dtype)], [pltpu.SemaphoreType.DMA((steps,))]
+    )
+    return kernel(weights)[0]
+
+
 def layer(tokens, norm_gain, expert_ids, route_score, expert_pair, w_in, w_out):
     devices = lax.axis_size("expert")
     blocks, plane, up = shape_of(devices)
@@ -206,14 +195,12 @@
     stations = expert_pair.shape[0]
     rows, top = expert_ids.shape
     width = tokens.shape[1]
-    half = w_out.shape[1]
     cap = min(rows, -(-rows * top // stations) + 1)
     slots_first = -(-cap // 8) * 8
     slots = -(-(blocks - 1) * cap // 8) * 8
     table = -(-stations // LANES) * LANES
     held = blocks * rows
     early = held + peers * slots_first
-    steps_in, steps_out = 8, 4
     station = (lax.axis_index("expert") // 2).astype(jnp.int32).reshape(1)
     hbm = functools.partial(pltpu.with_memory_space_constraint, memory_space=pltpu.HBM)
 
@@ -232,6 +219,8 @@
         [pltpu.VMEM(x.shape, x.dtype) for x in inputs] + [pltpu.SemaphoreType.DMA((5,))],
     )(station, *[hbm(x) for x in inputs])
 
+    inward = load(hbm(w_in))
+    outward = load(hbm(w_out))
     column = [payload] + [swap(payload, k << up) for k in range(1, blocks)]
     first = [swap(first[j], (j + 1) << 1) for j in range(peers)]
     own, shares, weights, *chosen = call(
@@ -246,35 +235,19 @@
     arrived = [swap(chosen[j], (j + 1) << 1) for j in range(peers)]
     own = jnp.concatenate([own] + first, axis=0)
     other = swap(own, 1)
-    owned = call(
-        functools.partial(own_kernel, steps_in=steps_in, steps_out=steps_out),
-        [VMEM, VMEM, HBM, HBM],
-        [
-            ((early, width), F32),
-            ((early, width), BF16),
-            ((width, 2 * half), BF16),
-            ((half, width), BF16),
-        ],
-        [
-            pltpu.VMEM((2 * early, width), BF16),
-            pltpu.VMEM((2 * early, 2 * half), F32),
-            pltpu.SemaphoreType.DMA((steps_in,)),
-            pltpu.SemaphoreType.DMA,
-        ],
-        limit=10,
-        flops=2400 * held * half * width,
-    )
-    keep, give, inward, outward = owned(own, other, hbm(w_in), hbm(w_out))
+    swapped = [swap(block, 1) for block in arrived]
+    pieces = arrived + swapped + [own, other]
+    experts = call(
+        functools.partial(expert_kernel, pieces=len(pieces), steps_out=4),
+        [VMEM] * (len(pieces) + 2),
+        [((slots, width), F32)] * peers
+        + [((slots, width), BF16)] * peers
+        + [((early, width), F32), ((early, width), BF16)],
+        [pltpu.VMEM((2 * (peers * slots + early), width), BF16)],
+        limit=16,
+    )
+    *results, keep, give = experts(*pieces, inward, outward)
     got = swap(give, 1)
-
-    pieces = arrived + [swap(block, 1) for block in arrived]
-    results = call(
-        functools.partial(peer_kernel, peers=peers, steps_out=steps_out),
-        [VMEM] * (2 * peers + 2),
-        [((slots, width), F32)] * peers + [((slots, width), BF16)] * peers,
-        [pltpu.VMEM((2 * peers * slots, width), BF16)],
-        limit=10,
-    )(*pieces, inward, outward)
     back, back_first = [], []
     for j in range(peers):
         halves = swap(results[peers + j], 1)
@@ -284,11 +257,12 @@
         done = (keep[span] + got[span].astype(F32)).astype(BF16)
         back_first.append(swap(done, (j + 1) << 1))
 
-    summed = call(
+    combine = call(
         functools.partial(combine_kernel, peers=peers),
         [VMEM] * (4 + peers),
         [((rows, width), F32)] + [((rows, width), BF16)] * (blocks - 1),
-    )(shares, weights, keep, got, *back)
+    )
+    summed = combine(shares, weights, keep, got, *back)
     returned = [swap(summed[k], k << up) for k in range(1, blocks)]
     (mixed,) = call(
         functools.partial(total_kernel, peers=peers),

time: 56.1 us -> 57.2 us (1.020)
  Pallas kernels: 10.2 us -> 11.3 us
    pallas_call x3 -> x4, Pallas kernels: 7.24 us -> 8.32 us  [the longest x2 4.75 us: load(): return kernel(weights)[0]]
where the time goes in v3:
time: 57.2 us; the launch traced here: 57 us
  starting transfers between devices  27.6 us (48%)
  waiting for transfers between devices  17.9 us (31%)
  Pallas kernels  11.3 us (20%)
    ppermute x26, starting transfers between devices, swap(): return lax.ppermute(block, 'expert', [(i, i ^ mask) for i in range(count)])  27.6 us
    ppermute x26, waiting for transfers between devices, swap(): return lax.ppermute(block, 'expert', [(i, i ^ mask) for i in range(count)])  17.9 us
    pallas_call x2, Pallas kernels, load(): return kernel(weights)[0]  4.75 us
    pallas_call x1, Pallas kernels, layer(): *results, keep, give = experts(*pieces, inward, outward)  3.35 us
    pallas_call x1, Pallas kernels, layer(): call(functools.partial(prepare_kernel, peers=peers, cap=cap, slots=slots_...  1.64 us
  transfers between devices with their start and end apart: 26, of which 12 were waited for; matrix products, arithmetic and copies ran while one was open for 0% of the time, Pallas kernels for 9%

profile of v3, /device:TPU:0, one launch (start us, length us, event | category | flops | bytes accessed | tf_op | source)
XLA Modules:
  0.0 57.0 jit_solution(15533736244452942095)
XLA Ops:
  0.0 1.6 %shard_map.73 = (bf16[8,4224]{1,0:T(8,128)(2,1)S(1)}, bf16[8,24]{1,0:T(8,128)(2,1)S(1)}, bf16[8,4096]{1,0:T(8,128)(2,1)S(1)}, bf16[8,4096]{1,0:T(8,128)(2,1)S(1)}, bf16[8,4096]{1,0:T(8,128)(2,1)S(1)}) custom-call(s32[1]{0:T(128)} %bitcast.station, bf16[8,4096]{1,0:T(8,128)(2,1)} %refs_0_.1, f32[1,4096]{1,0:T(1,128)} %bitcast.3, s32[8,8]{1,0:T(8,128)} %refs_2_.1, ...), custom_call_target="tpu_custom_call" | custom-call | tf_op jit(solution)/shard_map/pallas_call | solution.py:214
  1.7 5.1 %collective-permute-start.2 = (bf16[8,4224]{1,0:T(8,128)(2,1)S(1)}, bf16[8,4224]{1,0:T(8,128)(2,1)S(1)}, u32[]{:S(2)}, u32[]{:S(2)}) collective-permute-start(bf16[8,4224]{1,0:T(8,128)(2,1)S(1)} %get-tuple-element.28.refs_0_), channel_id=1, source_target_pairs={{0,24},{1,25},{2,26},{3,27},{4,28},{5,29},{6,30},{7,31},{8,16},{9,... | collective-permute-start | bytes 202760 | tf_op jit(solution)/shard_map/ppermute | solution.py:21
  6.8 0.0 collective-permute-start.1
  6.8 0.6 %collective-permute-start = (bf16[8,4224]{1,0:T(8,128)(2,1)S(1)}, bf16[8,4224]{1,0:T(8,128)(2,1)S(1)}, u32[]{:S(2)}, u32[]{:S(2)}) collective-permute-start(bf16[8,4224]{1,0:T(8,128)(2,1)S(1)} %get-tuple-element.28.refs_0_), channel_id=1, source_target_pairs={{0,8},{1,9},{2,10},{3,11},{4,12},{5,13},{6,14},{7,15},{8,0},{9,1},... | collective-permute-start | bytes 202760 | tf_op jit(solution)/shard_map/ppermute | solution.py:21
  7.4 1.6 %collective-permute-start.9 = (bf16[8,4096]{1,0:T(8,128)(2,1)S(1)}, bf16[8,4096]{1,0:T(8,128)(2,1)S(1)}, u32[]{:S(2)}, u32[]{:S(2)}) collective-permute-start(bf16[8,4096]{1,0:T(8,128)(2,1)S(1)} %get-tuple-element.35), channel_id=1, source_target_pairs={{0,2},{1,3},{2,0},{3,1},{4,6},{5,7},{6,4},{7,5},{8,10},{9,11},{10,... | collective-permute-start | bytes 196616 | tf_op jit(solution)/shard_map/ppermute | solution.py:21
  9.1 1.5 %collective-permute-start.10 = (bf16[8,4096]{1,0:T(8,128)(2,1)S(1)}, bf16[8,4096]{1,0:T(8,128)(2,1)S(1)}, u32[]{:S(2)}, u32[]{:S(2)}) collective-permute-start(bf16[8,4096]{1,0:T(8,128)(2,1)S(1)} %get-tuple-element.36), channel_id=1, source_target_pairs={{0,4},{1,5},{2,6},{3,7},{4,0},{5,1},{6,2},{7,3},{8,12},{9,13},{10,... | collective-permute-start | bytes 196616 | tf_op jit(solution)/shard_map/ppermute | solution.py:21
  10.6 0.0 collective-permute-done.2.refs_3_
  10.6 1.6 %collective-permute-start.11 = (bf16[8,4096]{1,0:T(8,128)(2,1)S(1)}, bf16[8,4096]{1,0:T(8,128)(2,1)S(1)}, u32[]{:S(2)}, u32[]{:S(2)}) collective-permute-start(bf16[8,4096]{1,0:T(8,128)(2,1)S(1)} %get-tuple-element.37), channel_id=1, source_target_pairs={{0,6},{1,7},{2,4},{3,5},{4,2},{5,3},{6,0},{7,1},{8,14},{9,15},{10,... | collective-permute-start | bytes 196616 | tf_op jit(solution)/shard_map/ppermute | solution.py:21
  12.2 0.4 collective-permute-done.1.refs_2_
  12.6 0.0 collective-permute-done.refs_1_
  12.6 0.5 shard_map.74
  13.1 0.0 collective-permute-done.9
  13.1 0.9 %collective-permute-done.10 = bf16[8,4096]{1,0:T(8,128)(2,1)S(1)} collective-permute-done((bf16[8,4096]{1,0:T(8,128)(2,1)S(1)}, bf16[8,4096]{1,0:T(8,128)(2,1)S(1)}, u32[]{:S(2)}, u32[]{:S(2)}) %collective-permute-start.10) | collective-permute-done | bytes 65568 | tf_op jit(solution)/shard_map/ppermute | solution.py:21
  14.1 1.7 %collective-permute-done.11 = bf16[8,4096]{1,0:T(8,128)(2,1)S(1)} collective-permute-done((bf16[8,4096]{1,0:T(8,128)(2,1)S(1)}, bf16[8,4096]{1,0:T(8,128)(2,1)S(1)}, u32[]{:S(2)}, u32[]{:S(2)}) %collective-permute-start.11) | collective-permute-done | bytes 65568 | tf_op jit(solution)/shard_map/ppermute | solution.py:21
  15.8 0.0 collective-permute-start.12
  15.8 0.7 %collective-permute-start.3 = (bf16[16,4096]{1,0:T(8,128)(2,1)S(1)}, bf16[16,4096]{1,0:T(8,128)(2,1)S(1)}, u32[]{:S(2)}, u32[]{:S(2)}) collective-permute-start(bf16[16,4096]{1,0:T(8,128)(2,1)S(1)} %get-tuple-element.31), channel_id=1, source_target_pairs={{0,2},{1,3},{2,0},{3,1},{4,6},{5,7},{6,4},{7,5},{8,10},{9,11},{10,... | collective-permute-start | bytes 393224 | tf_op jit(solution)/shard_map/ppermute | solution.py:21
  16.5 1.5 %collective-permute-start.4 = (bf16[16,4096]{1,0:T(8,128)(2,1)S(1)}, bf16[16,4096]{1,0:T(8,128)(2,1)S(1)}, u32[]{:S(2)}, u32[]{:S(2)}) collective-permute-start(bf16[16,4096]{1,0:T(8,128)(2,1)S(1)} %get-tuple-element.32), channel_id=1, source_target_pairs={{0,4},{1,5},{2,6},{3,7},{4,0},{5,1},{6,2},{7,3},{8,12},{9,13},{10,... | collective-permute-start | bytes 393224 | tf_op jit(solution)/shard_map/ppermute | solution.py:21
  18.0 1.3 %collective-permute-start.5 = (bf16[16,4096]{1,0:T(8,128)(2,1)S(1)}, bf16[16,4096]{1,0:T(8,128)(2,1)S(1)}, u32[]{:S(2)}, u32[]{:S(2)}) collective-permute-start(bf16[16,4096]{1,0:T(8,128)(2,1)S(1)} %get-tuple-element.33), channel_id=1, source_target_pairs={{0,6},{1,7},{2,4},{3,5},{4,2},{5,3},{6,0},{7,1},{8,14},{9,15},{10,... | collective-permute-start | bytes 393224 | tf_op jit(solution)/shard_map/ppermute | solution.py:21
  19.3 2.9 %collective-permute-done.3.refs_0_ = bf16[16,4096]{1,0:T(8,128)(2,1)S(1)} collective-permute-done((bf16[16,4096]{1,0:T(8,128)(2,1)S(1)}, bf16[16,4096]{1,0:T(8,128)(2,1)S(1)}, u32[]{:S(2)}, u32[]{:S(2)}) %collective-permute-start.3) | collective-permute-done | bytes 131104 | tf_op jit(solution)/shard_map/ppermute | solution.py:21
  22.2 0.0 collective-permute-start.6
  22.2 2.6 %collective-permute-done.4.refs_1_ = bf16[16,4096]{1,0:T(8,128)(2,1)S(1)} collective-permute-done((bf16[16,4096]{1,0:T(8,128)(2,1)S(1)}, bf16[16,4096]{1,0:T(8,128)(2,1)S(1)}, u32[]{:S(2)}, u32[]{:S(2)}) %collective-permute-start.4) | collective-permute-done | bytes 131104 | tf_op jit(solution)/shard_map/ppermute | solution.py:21
  24.8 0.0 collective-permute-start.7
  24.8 0.0 collective-permute-done.5.refs_2_
  24.9 0.5 collective-permute-start.8
  25.4 1.9 %shard_map.76.refs_9_ = bf16[384,4096]{1,0:T(8,128)(2,1)S(1)} custom-call(bf16[1,384,4096]{2,1,0:T(8,128)(2,1)} %weights.3), custom_call_target="tpu_custom_call" | custom-call | tf_op jit(solution)/shard_map/pallas_call | solution.py:188
  27.3 2.9 %shard_map.75.refs_8_ = bf16[4096,768]{1,0:T(8,128)(2,1)S(1)} custom-call(bf16[1,4096,768]{2,1,0:T(8,128)(2,1)} %weights.2), custom_call_target="tpu_custom_call" | custom-call | tf_op jit(solution)/shard_map/pallas_call | solution.py:188
  30.1 0.0 collective-permute-done.6.refs_3_
  30.1 0.0 collective-permute-done.7.refs_4_
  30.1 0.0 collective-permute-done.8.refs_5_
  30.2 0.0 collective-permute-done.12.refs_7_
  30.2 3.3 %shard_map.77 = (f32[16,4096]{1,0:T(8,128)S(1)}, f32[16,4096]{1,0:T(8,128)S(1)}, f32[16,4096]{1,0:T(8,128)S(1)}, bf16[16,4096]{1,0:T(8,128)(2,1)S(1)}, bf16[16,4...) custom-call(bf16[16,4096]{1,0:T(8,128)(2,1)S(1)} %collective-permute-, ...), custom_call_target="tpu_custom_call" | custom-call | tf_op jit(solution)/shard_map/pallas_call | solution.py:249
  33.5 0.1 collective-permute-start.14
  33.6 0.5 collective-permute-start.16
  34.1 0.1 collective-permute-start.18
  34.2 0.4 collective-permute-start.13
  34.6 0.3 collective-permute-done.14
  35.0 1.5 %collective-permute-start.15 = (bf16[16,4096]{1,0:T(8,128)(2,1)S(1)}, bf16[16,4096]{1,0:T(8,128)(2,1)S(1)}, u32[]{:S(2)}, u32[]{:S(2)}) collective-permute-start(bf16[16,4096]{1,0:T(8,128)(2,1)S(1)} %add_convert_fusion.2), channel_id=1, source_target_pairs={{0,2},{1,3},{2,0},{3,1},{4,6},{5,7},{6,4},{7,5},{8,10},{9,11},{10,... | collective-permute-start | bytes 393224 | tf_op jit(solution)/shard_map/ppermute | solution.py:21
  36.4 0.0 collective-permute-done.16
  36.5 0.7 %collective-permute-start.17 = (bf16[16,4096]{1,0:T(8,128)(2,1)S(1)}, bf16[16,4096]{1,0:T(8,128)(2,1)S(1)}, u32[]{:S(2)}, u32[]{:S(2)}) collective-permute-start(bf16[16,4096]{1,0:T(8,128)(2,1)S(1)} %add_convert_fusion.1), channel_id=1, source_target_pairs={{0,4},{1,5},{2,6},{3,7},{4,0},{5,1},{6,2},{7,3},{8,12},{9,13},{10,... | collective-permute-start | bytes 393224 | tf_op jit(solution)/shard_map/ppermute | solution.py:21
  37.2 0.0 collective-permute-done.18
  37.2 1.5 %collective-permute-start.19 = (bf16[16,4096]{1,0:T(8,128)(2,1)S(1)}, bf16[16,4096]{1,0:T(8,128)(2,1)S(1)}, u32[]{:S(2)}, u32[]{:S(2)}) collective-permute-start(bf16[16,4096]{1,0:T(8,128)(2,1)S(1)} %add_convert_fusion), channel_id=1, source_target_pairs={{0,6},{1,7},{2,4},{3,5},{4,2},{5,3},{6,0},{7,1},{8,14},{9,15},{10,... | collective-permute-start | bytes 393224 | tf_op jit(solution)/shard_map/ppermute | solution.py:21
  38.7 2.2 %collective-permute-done.15.refs_0_ = bf16[16,4096]{1,0:T(8,128)(2,1)S(1)} collective-permute-done((bf16[16,4096]{1,0:T(8,128)(2,1)S(1)}, bf16[16,4096]{1,0:T(8,128)(2,1)S(1)}, u32[]{:S(2)}, u32[]{:S(2)}) %collective-permute-start.15) | collective-permute-done | bytes 131104 | tf_op jit(solution)/shard_map/ppermute | solution.py:21
  40.9 3.7 %collective-permute-done.17.refs_1_ = bf16[16,4096]{1,0:T(8,128)(2,1)S(1)} collective-permute-done((bf16[16,4096]{1,0:T(8,128)(2,1)S(1)}, bf16[16,4096]{1,0:T(8,128)(2,1)S(1)}, u32[]{:S(2)}, u32[]{:S(2)}) %collective-permute-start.17) | collective-permute-done | bytes 131104 | tf_op jit(solution)/shard_map/ppermute | solution.py:21
  44.6 0.0 collective-permute-done.19.refs_2_
  44.6 0.0 collective-permute-done.13.got
  44.6 0.2 shard_map.78
  44.8 2.1 %collective-permute-start.23 = (bf16[8,4096]{1,0:T(8,128)(2,1)S(1)}, bf16[8,4096]{1,0:T(8,128)(2,1)S(1)}, u32[]{:S(2)}, u32[]{:S(2)}) collective-permute-start(bf16[8,4096]{1,0:T(8,128)(2,1)S(1)} %get-tuple-element.48), channel_id=1, source_target_pairs={{0,8},{1,9},{2,10},{3,11},{4,12},{5,13},{6,14},{7,15},{8,0},{9,1},... | collective-permute-start | bytes 196616 | tf_op jit(solution)/shard_map/ppermute | solution.py:21
  46.9 2.1 %collective-permute-start.24 = (bf16[8,4096]{1,0:T(8,128)(2,1)S(1)}, bf16[8,4096]{1,0:T(8,128)(2,1)S(1)}, u32[]{:S(2)}, u32[]{:S(2)}) collective-permute-start(bf16[8,4096]{1,0:T(8,128)(2,1)S(1)} %get-tuple-element.49), channel_id=1, source_target_pairs={{0,16},{1,17},{2,18},{3,19},{4,20},{5,21},{6,22},{7,23},{8,24},{9,... | collective-permute-start | bytes 196616 | tf_op jit(solution)/shard_map/ppermute | solution.py:21
  49.1 0.4 collective-permute-start.25
  49.6 1.9 %collective-permute-start.22 = (bf16[8,4096]{1,0:T(8,128)(2,1)S(1)}, bf16[8,4096]{1,0:T(8,128)(2,1)S(1)}, u32[]{:S(2)}, u32[]{:S(2)}) collective-permute-start(bf16[8,4096]{1,0:T(8,128)(2,1)S(1)} %get-tuple-element.51), channel_id=1, source_target_pairs={{0,6},{1,7},{2,4},{3,5},{4,2},{5,3},{6,0},{7,1},{8,14},{9,15},{10,... | collective-permute-start | bytes 196616 | tf_op jit(solution)/shard_map/ppermute | solution.py:21
  51.5 0.5 collective-permute-start.21
  52.0 0.0 collective-permute-done.23.refs_3_
  52.0 1.1 %collective-permute-start.20 = (bf16[8,4096]{1,0:T(8,128)(2,1)S(1)}, bf16[8,4096]{1,0:T(8,128)(2,1)S(1)}, u32[]{:S(2)}, u32[]{:S(2)}) collective-permute-start(bf16[8,4096]{1,0:T(8,128)(2,1)S(1)} %get-tuple-element.53), channel_id=1, source_target_pairs={{0,2},{1,3},{2,0},{3,1},{4,6},{5,7},{6,4},{7,5},{8,10},{9,11},{10,... | collective-permute-start | bytes 196616 | tf_op jit(solution)/shard_map/ppermute | solution.py:21
  53.1 0.5 collective-permute-done.24.refs_4_
  53.7 1.5 %collective-permute-done.25.refs_5_ = bf16[8,4096]{1,0:T(8,128)(2,1)S(1)} collective-permute-done((bf16[8,4096]{1,0:T(8,128)(2,1)S(1)}, bf16[8,4096]{1,0:T(8,128)(2,1)S(1)}, u32[]{:S(2)}, u32[]{:S(2)}) %collective-permute-start.25) | collective-permute-done | bytes 65568 | tf_op jit(solution)/shard_map/ppermute | solution.py:21
  55.1 0.0 collective-permute-done.22.refs_2_
  55.1 0.6 %collective-permute-done.21.refs_1_ = bf16[8,4096]{1,0:T(8,128)(2,1)S(1)} collective-permute-done((bf16[8,4096]{1,0:T(8,128)(2,1)S(1)}, bf16[8,4096]{1,0:T(8,128)(2,1)S(1)}, u32[]{:S(2)}, u32[]{:S(2)}) %collective-permute-start.21) | collective-permute-done | bytes 65568 | tf_op jit(solution)/shard_map/ppermute | solution.py:21
  55.7 0.5 collective-permute-done.20.refs_0_
  56.2 0.8 %shard_map.79 = bf16[8,4096]{1,0:T(8,128)(2,1)} custom-call(f32[8,4096]{1,0:T(8,128)S(1)} %get-tuple-element.46.local, bf16[8,24]{1,0:T(8,128)(2,1)S(1)} %get-tuple-element.47.weights, bf16[8,4096]{1,0:T(8,128)(2,1)S(1)} %collective-permute-done.20.refs_0_, bf16[8,4096]{1,0:T(8,128)(2,1)S(1)} %collective-permute-done.21.refs_1_, ...), custom_call_target="tpu_custom_call" | custom-call | tf_op jit(solution)/shard_map/pallas_call | solution.py:267
  (8 shorter events, 0.2 us)
Async XLA Ops:
  1.7 9.0 %collective-permute-start.2 = (bf16[8,4224]{1,0:T(8,128)(2,1)S(1)}, bf16[8,4224]{1,0:T(8,128)(2,1)S(1)}, u32[]{:S(2)}, u32[]{:S(2)}) collective-permute-start(bf16[8,4224]{1,0:T(8,128)(2,1)S(1)} %get-tuple-element.28.refs_0_), channel_id=1, source_target_pairs={{0,24},{1,25},{2,26},{3,27},{4,28},{5,29},{6,30},{7,31},{8,16},{9,... | collective-permute-start | bytes 202760 | tf_op jit(solution)/shard_map/ppermute | solution.py:21
  6.8 5.8 %collective-permute-start.1 = (bf16[8,4224]{1,0:T(8,128)(2,1)S(1)}, bf16[8,4224]{1,0:T(8,128)(2,1)S(1)}, u32[]{:S(2)}, u32[]{:S(2)}) collective-permute-start(bf16[8,4224]{1,0:T(8,128)(2,1)S(1)} %get-tuple-element.28.refs_0_), channel_id=1, source_target_pairs={{0,16},{1,17},{2,18},{3,19},{4,20},{5,21},{6,22},{7,23},{8,24},{9,... | collective-permute-start | bytes 202760 | tf_op jit(solution)/shard_map/ppermute | solution.py:21
  6.8 5.8 %collective-permute-start = (bf16[8,4224]{1,0:T(8,128)(2,1)S(1)}, bf16[8,4224]{1,0:T(8,128)(2,1)S(1)}, u32[]{:S(2)}, u32[]{:S(2)}) collective-permute-start(bf16[8,4224]{1,0:T(8,128)(2,1)S(1)} %get-tuple-element.28.refs_0_), channel_id=1, source_target_pairs={{0,8},{1,9},{2,10},{3,11},{4,12},{5,13},{6,14},{7,15},{8,0},{9,1},... | collective-permute-start | bytes 202760 | tf_op jit(solution)/shard_map/ppermute | solution.py:21
  7.4 5.7 %collective-permute-start.9 = (bf16[8,4096]{1,0:T(8,128)(2,1)S(1)}, bf16[8,4096]{1,0:T(8,128)(2,1)S(1)}, u32[]{:S(2)}, u32[]{:S(2)}) collective-permute-start(bf16[8,4096]{1,0:T(8,128)(2,1)S(1)} %get-tuple-element.35), channel_id=1, source_target_pairs={{0,2},{1,3},{2,0},{3,1},{4,6},{5,7},{6,4},{7,5},{8,10},{9,11},{10,... | collective-permute-start | bytes 196616 | tf_op jit(solution)/shard_map/ppermute | solution.py:21
  9.1 5.0 %collective-permute-start.10 = (bf16[8,4096]{1,0:T(8,128)(2,1)S(1)}, bf16[8,4096]{1,0:T(8,128)(2,1)S(1)}, u32[]{:S(2)}, u32[]{:S(2)}) collective-permute-start(bf16[8,4096]{1,0:T(8,128)(2,1)S(1)} %get-tuple-element.36), channel_id=1, source_target_pairs={{0,4},{1,5},{2,6},{3,7},{4,0},{5,1},{6,2},{7,3},{8,12},{9,13},{10,... | collective-permute-start | bytes 196616 | tf_op jit(solution)/shard_map/ppermute | solution.py:21
  10.6 5.2 %collective-permute-start.11 = (bf16[8,4096]{1,0:T(8,128)(2,1)S(1)}, bf16[8,4096]{1,0:T(8,128)(2,1)S(1)}, u32[]{:S(2)}, u32[]{:S(2)}) collective-permute-start(bf16[8,4096]{1,0:T(8,128)(2,1)S(1)} %get-tuple-element.37), channel_id=1, source_target_pairs={{0,6},{1,7},{2,4},{3,5},{4,2},{5,3},{6,0},{7,1},{8,14},{9,15},{10,... | collective-permute-start | bytes 196616 | tf_op jit(solution)/shard_map/ppermute | solution.py:21
  15.8 14.4 %collective-permute-start.12 = (bf16[56,4096]{1,0:T(8,128)(2,1)S(1)}, bf16[56,4096]{1,0:T(8,128)(2,1)S(1)}, u32[]{:S(2)}, u32[]{:S(2)}) collective-permute-start(bf16[56,4096]{1,0:T(8,128)(2,1)S(1)} %constant_dynamic-update-slice_fusion.refs_6_), channel_id=1, source_target_pairs={{0,1},{1,0},{2,3},{3,2},{4,5},{5,4},{6,7},{7,6},{8,9},{9,8},{10,11... | collective-permute-start | bytes 1376264 | tf_op jit(solution)/shard_map/ppermute | solution.py:21
  15.8 6.4 %collective-permute-start.3 = (bf16[16,4096]{1,0:T(8,128)(2,1)S(1)}, bf16[16,4096]{1,0:T(8,128)(2,1)S(1)}, u32[]{:S(2)}, u32[]{:S(2)}) collective-permute-start(bf16[16,4096]{1,0:T(8,128)(2,1)S(1)} %get-tuple-element.31), channel_id=1, source_target_pairs={{0,2},{1,3},{2,0},{3,1},{4,6},{5,7},{6,4},{7,5},{8,10},{9,11},{10,... | collective-permute-start | bytes 393224 | tf_op jit(solution)/shard_map/ppermute | solution.py:21
  16.5 8.4 %collective-permute-start.4 = (bf16[16,4096]{1,0:T(8,128)(2,1)S(1)}, bf16[16,4096]{1,0:T(8,128)(2,1)S(1)}, u32[]{:S(2)}, u32[]{:S(2)}) collective-permute-start(bf16[16,4096]{1,0:T(8,128)(2,1)S(1)} %get-tuple-element.32), channel_id=1, source_target_pairs={{0,4},{1,5},{2,6},{3,7},{4,0},{5,1},{6,2},{7,3},{8,12},{9,13},{10,... | collective-permute-start | bytes 393224 | tf_op jit(solution)/shard_map/ppermute | solution.py:21
  18.0 6.8 %collective-permute-start.5 = (bf16[16,4096]{1,0:T(8,128)(2,1)S(1)}, bf16[16,4096]{1,0:T(8,128)(2,1)S(1)}, u32[]{:S(2)}, u32[]{:S(2)}) collective-permute-start(bf16[16,4096]{1,0:T(8,128)(2,1)S(1)} %get-tuple-element.33), channel_id=1, source_target_pairs={{0,6},{1,7},{2,4},{3,5},{4,2},{5,3},{6,0},{7,1},{8,14},{9,15},{10,... | collective-permute-start | bytes 393224 | tf_op jit(solution)/shard_map/ppermute | solution.py:21
  22.2 7.9 %collective-permute-start.6 = (bf16[16,4096]{1,0:T(8,128)(2,1)S(1)}, bf16[16,4096]{1,0:T(8,128)(2,1)S(1)}, u32[]{:S(2)}, u32[]{:S(2)}) collective-permute-start(bf16[16,4096]{1,0:T(8,128)(2,1)S(1)} %collective-permute-done.3.refs_0_), channel_id=1, source_target_pairs={{0,1},{1,0},{2,3},{3,2},{4,5},{5,4},{6,7},{7,6},{8,9},{9,8},{10,11... | collective-permute-start | bytes 393224 | tf_op jit(solution)/shard_map/ppermute | solution.py:21
  24.8 5.3 %collective-permute-start.7 = (bf16[16,4096]{1,0:T(8,128)(2,1)S(1)}, bf16[16,4096]{1,0:T(8,128)(2,1)S(1)}, u32[]{:S(2)}, u32[]{:S(2)}) collective-permute-start(bf16[16,4096]{1,0:T(8,128)(2,1)S(1)} %collective-permute-done.4.refs_1_), channel_id=1, source_target_pairs={{0,1},{1,0},{2,3},{3,2},{4,5},{5,4},{6,7},{7,6},{8,9},{9,8},{10,11... | collective-permute-start | bytes 393224 | tf_op jit(solution)/shard_map/ppermute | solution.py:21
  24.9 5.3 %collective-permute-start.8 = (bf16[16,4096]{1,0:T(8,128)(2,1)S(1)}, bf16[16,4096]{1,0:T(8,128)(2,1)S(1)}, u32[]{:S(2)}, u32[]{:S(2)}) collective-permute-start(bf16[16,4096]{1,0:T(8,128)(2,1)S(1)} %collective-permute-done.5.refs_2_), channel_id=1, source_target_pairs={{0,1},{1,0},{2,3},{3,2},{4,5},{5,4},{6,7},{7,6},{8,9},{9,8},{10,11... | collective-permute-start | bytes 393224 | tf_op jit(solution)/shard_map/ppermute | solution.py:21
  33.5 1.4 %collective-permute-start.14 = (bf16[16,4096]{1,0:T(8,128)(2,1)S(1)}, bf16[16,4096]{1,0:T(8,128)(2,1)S(1)}, u32[]{:S(2)}, u32[]{:S(2)}) collective-permute-start(bf16[16,4096]{1,0:T(8,128)(2,1)S(1)} %get-tuple-element.41), channel_id=1, source_target_pairs={{0,1},{1,0},{2,3},{3,2},{4,5},{5,4},{6,7},{7,6},{8,9},{9,8},{10,11... | collective-permute-start | bytes 393224 | tf_op jit(solution)/shard_map/ppermute | solution.py:21
  33.6 2.8 %collective-permute-start.16 = (bf16[16,4096]{1,0:T(8,128)(2,1)S(1)}, bf16[16,4096]{1,0:T(8,128)(2,1)S(1)}, u32[]{:S(2)}, u32[]{:S(2)}) collective-permute-start(bf16[16,4096]{1,0:T(8,128)(2,1)S(1)} %get-tuple-element.43), channel_id=1, source_target_pairs={{0,1},{1,0},{2,3},{3,2},{4,5},{5,4},{6,7},{7,6},{8,9},{9,8},{10,11... | collective-permute-start | bytes 393224 | tf_op jit(solution)/shard_map/ppermute | solution.py:21
  34.1 3.1 %collective-permute-start.18 = (bf16[16,4096]{1,0:T(8,128)(2,1)S(1)}, bf16[16,4096]{1,0:T(8,128)(2,1)S(1)}, u32[]{:S(2)}, u32[]{:S(2)}) collective-permute-start(bf16[16,4096]{1,0:T(8,128)(2,1)S(1)} %get-tuple-element.45), channel_id=1, source_target_pairs={{0,1},{1,0},{2,3},{3,2},{4,5},{5,4},{6,7},{7,6},{8,9},{9,8},{10,11... | collective-permute-start | bytes 393224 | tf_op jit(solution)/shard_map/ppermute | solution.py:21
  34.2 10.4 %collective-permute-start.13 = (bf16[56,4096]{1,0:T(8,128)(2,1)S(1)}, bf16[56,4096]{1,0:T(8,128)(2,1)S(1)}, u32[]{:S(2)}, u32[]{:S(2)}) collective-permute-start(bf16[56,4096]{1,0:T(8,128)(2,1)S(1)} %get-tuple-element.39), channel_id=1, source_target_pairs={{0,1},{1,0},{2,3},{3,2},{4,5},{5,4},{6,7},{7,6},{8,9},{9,8},{10,11... | collective-permute-start | bytes 1376264 | tf_op jit(solution)/shard_map/ppermute | solution.py:21
  35.0 5.9 %collective-permute-start.15 = (bf16[16,4096]{1,0:T(8,128)(2,1)S(1)}, bf16[16,4096]{1,0:T(8,128)(2,1)S(1)}, u32[]{:S(2)}, u32[]{:S(2)}) collective-permute-start(bf16[16,4096]{1,0:T(8,128)(2,1)S(1)} %add_convert_fusion.2), channel_id=1, source_target_pairs={{0,2},{1,3},{2,0},{3,1},{4,6},{5,7},{6,4},{7,5},{8,10},{9,11},{10,... | collective-permute-start | bytes 393224 | tf_op jit(solution)/shard_map/ppermute | solution.py:21
  36.5 8.1 %collective-permute-start.17 = (bf16[16,4096]{1,0:T(8,128)(2,1)S(1)}, bf16[16,4096]{1,0:T(8,128)(2,1)S(1)}, u32[]{:S(2)}, u32[]{:S(2)}) collective-permute-start(bf16[16,4096]{1,0:T(8,128)(2,1)S(1)} %add_convert_fusion.1), channel_id=1, source_target_pairs={{0,4},{1,5},{2,6},{3,7},{4,0},{5,1},{6,2},{7,3},{8,12},{9,13},{10,... | collective-permute-start | bytes 393224 | tf_op jit(solution)/shard_map/ppermute | solution.py:21
  37.2 7.4 %collective-permute-start.19 = (bf16[16,4096]{1,0:T(8,128)(2,1)S(1)}, bf16[16,4096]{1,0:T(8,128)(2,1)S(1)}, u32[]{:S(2)}, u32[]{:S(2)}) collective-permute-start(bf16[16,4096]{1,0:T(8,128)(2,1)S(1)} %add_convert_fusion), channel_id=1, source_target_pairs={{0,6},{1,7},{2,4},{3,5},{4,2},{5,3},{6,0},{7,1},{8,14},{9,15},{10,... | collective-permute-start | bytes 393224 | tf_op jit(solution)/shard_map/ppermute | solution.py:21
  44.8 7.1 %collective-permute-start.23 = (bf16[8,4096]{1,0:T(8,128)(2,1)S(1)}, bf16[8,4096]{1,0:T(8,128)(2,1)S(1)}, u32[]{:S(2)}, u32[]{:S(2)}) collective-permute-start(bf16[8,4096]{1,0:T(8,128)(2,1)S(1)} %get-tuple-element.48), channel_id=1, source_target_pairs={{0,8},{1,9},{2,10},{3,11},{4,12},{5,13},{6,14},{7,15},{8,0},{9,1},... | collective-permute-start | bytes 196616 | tf_op jit(solution)/shard_map/ppermute | solution.py:21
  46.9 6.7 %collective-permute-start.24 = (bf16[8,4096]{1,0:T(8,128)(2,1)S(1)}, bf16[8,4096]{1,0:T(8,128)(2,1)S(1)}, u32[]{:S(2)}, u32[]{:S(2)}) collective-permute-start(bf16[8,4096]{1,0:T(8,128)(2,1)S(1)} %get-tuple-element.49), channel_id=1, source_target_pairs={{0,16},{1,17},{2,18},{3,19},{4,20},{5,21},{6,22},{7,23},{8,24},{9,... | collective-permute-start | bytes 196616 | tf_op jit(solution)/shard_map/ppermute | solution.py:21
  49.1 6.1 %collective-permute-start.25 = (bf16[8,4096]{1,0:T(8,128)(2,1)S(1)}, bf16[8,4096]{1,0:T(8,128)(2,1)S(1)}, u32[]{:S(2)}, u32[]{:S(2)}) collective-permute-start(bf16[8,4096]{1,0:T(8,128)(2,1)S(1)} %get-tuple-element.50), channel_id=1, source_target_pairs={{0,24},{1,25},{2,26},{3,27},{4,28},{5,29},{6,30},{7,31},{8,16},{9,... | collective-permute-start | bytes 196616 | tf_op jit(solution)/shard_map/ppermute | solution.py:21
  49.6 5.6 %collective-permute-start.22 = (bf16[8,4096]{1,0:T(8,128)(2,1)S(1)}, bf16[8,4096]{1,0:T(8,128)(2,1)S(1)}, u32[]{:S(2)}, u32[]{:S(2)}) collective-permute-start(bf16[8,4096]{1,0:T(8,128)(2,1)S(1)} %get-tuple-element.51), channel_id=1, source_target_pairs={{0,6},{1,7},{2,4},{3,5},{4,2},{5,3},{6,0},{7,1},{8,14},{9,15},{10,... | collective-permute-start | bytes 196616 | tf_op jit(solution)/shard_map/ppermute | solution.py:21
  51.5 4.3 %collective-permute-start.21 = (bf16[8,4096]{1,0:T(8,128)(2,1)S(1)}, bf16[8,4096]{1,0:T(8,128)(2,1)S(1)}, u32[]{:S(2)}, u32[]{:S(2)}) collective-permute-start(bf16[8,4096]{1,0:T(8,128)(2,1)S(1)} %get-tuple-element.52), channel_id=1, source_target_pairs={{0,4},{1,5},{2,6},{3,7},{4,0},{5,1},{6,2},{7,3},{8,12},{9,13},{10,... | collective-permute-start | bytes 196616 | tf_op jit(solution)/shard_map/ppermute | solution.py:21
  52.0 4.3 %collective-permute-start.20 = (bf16[8,4096]{1,0:T(8,128)(2,1)S(1)}, bf16[8,4096]{1,0:T(8,128)(2,1)S(1)}, u32[]{:S(2)}, u32[]{:S(2)}) collective-permute-start(bf16[8,4096]{1,0:T(8,128)(2,1)S(1)} %get-tuple-element.53), channel_id=1, source_target_pairs={{0,2},{1,3},{2,0},{3,1},{4,6},{5,7},{6,4},{7,5},{8,10},{9,11},{10,... | collective-permute-start | bytes 196616 | tf_op jit(solution)/shard_map/ppermute | solution.py:21

commit v4 on v3

v4 whole, which is shorter than its diff:
```python
import functools

import jax
import jax.numpy as jnp
from jax import lax
from jax.experimental import pallas as pl
from jax.experimental.pallas import tpu as pltpu
from jax.sharding import PartitionSpec as P


LANES = 128
BF16 = jnp.bfloat16
F32 = jnp.float32
HBM = pl.BlockSpec(memory_space=pltpu.HBM)
VMEM = pl.BlockSpec(memory_space=pltpu.VMEM)
SMEM = pl.BlockSpec(memory_space=pltpu.SMEM)


def swap(block, mask):
    count = lax.axis_size("expert")
    return lax.ppermute(block, "expert", [(i, i ^ mask) for i in range(count)])


def picked_rows(placing, body):
    return lax.dot_general(placing, body, (((0,), (0,)), ((), ())), preferred_element_type=F32)


def slot_weights(table, station, peers, slots, cap, rows_each, first=0):
    rows = table.shape[0]
    row = lax.broadcasted_iota(jnp.int32, (rows, rows), 0)
    col = lax.broadcasted_iota(jnp.int32, (rows, rows), 1)
    earlier = (col < row) & (row // rows_each == col // rows_each)
    rank = jnp.dot(
        jnp.where(earlier, 1.0, 0.0).astype(BF16),
        jnp.where(table > 0.0, 1.0, 0.0).astype(BF16),
        preferred_element_type=F32,
    )
    block = lax.broadcasted_iota(jnp.int32, (rows, 1), 0) // rows_each
    base = jnp.where(block < first, block + rows // rows_each, block) * cap - first * cap
    lane = lax.broadcasted_iota(jnp.int32, table.shape, 1)
    target = lax.broadcasted_iota(jnp.int32, (rows, peers * slots), 1)
    weights = jnp.zeros((rows, peers * slots), F32)
    for j in range(peers):
        pick = lane == (station ^ (j + 1))
        share = jnp.sum(jnp.where(pick, table, 0.0), axis=1, keepdims=True)
        ranked = jnp.sum(jnp.where(pick, rank, 0.0), axis=1, keepdims=True)
        slot = base + ranked.astype(jnp.int32) + j * slots
        weights = weights + jnp.where(target == slot, share, 0.0)
    return weights


def prepare_kernel(station, *refs, peers, cap, slots, width):
    sources = refs[:5]
    heavy = refs[5]
    payload, loaded = refs[6:8]
    chosen = refs[8 : 8 + peers]
    copied = refs[8 + peers : 13 + peers]
    sems, heavy_sems = refs[-2:]
    copies = [
        pltpu.make_async_copy(source, target, sems.at[n])
        for n, (source, target) in enumerate(zip(sources, copied))
    ]
    for copy in copies:
        copy.start()
    weights = pieces_of(heavy, loaded, heavy_sems, 0)
    for copy in weights:
        copy.start()
    for copy in copies:
        copy.wait()
    tokens, gain, ids, score, pair = copied
    widened = tokens[...].astype(F32)
    meansq = jnp.mean(widened * widened, axis=-1, keepdims=True)
    normed = (widened * lax.rsqrt(meansq + 1e-06) * gain[...]).astype(BF16)
    payload[:, :width] = normed
    rows, top = ids.shape
    stations = pair.shape[1]
    shares = score[...] / jnp.sum(score[...], axis=-1, keepdims=True)
    labels = lax.broadcasted_iota(jnp.int32, (rows, stations), 1)
    named = jnp.zeros((rows, stations), F32)
    for k in range(top):
        named = named + jnp.where(ids[:, k : k + 1] == labels, shares[:, k : k + 1], 0.0)
    place = lax.broadcasted_iota(jnp.int32, (payload.shape[1] - width, stations), 0)
    moved = jnp.where(pair[...] == place, 1.0, 0.0).astype(BF16)
    table = lax.dot_general(
        named.astype(BF16), moved, (((1,), (1,)), ((), ())), preferred_element_type=F32
    )
    payload[:, width:] = table.astype(BF16)
    shared = slot_weights(table, station[0], peers, slots, cap, rows)
    placed = picked_rows(jnp.where(shared > 0.0, 1.0, 0.0).astype(BF16), normed)
    for j, ref in enumerate(chosen):
        ref[...] = placed[j * slots : (j + 1) * slots].astype(BF16)
    for copy in weights:
        copy.wait()


def select_kernel(station, *refs, blocks, peers, cap, slots, width):
    payloads = refs[:blocks]
    own, tables = refs[blocks : blocks + 2]
    chosen = refs[blocks + 2 :]
    rows = payloads[0].shape[0]
    gathered = jnp.concatenate([ref[...].astype(F32) for ref in payloads], axis=0)
    table = gathered[:, width:]
    body = gathered[:, :width].astype(BF16)
    own[...] = body
    tables[...] = table
    shared = slot_weights(table[rows:], station[0], peers, slots, cap, rows)
    placed = picked_rows(jnp.where(shared > 0.0, 1.0, 0.0).astype(BF16), body[rows:])
    for j, ref in enumerate(chosen):
        ref[...] = placed[j * slots : (j + 1) * slots].astype(BF16)


def weigh_kernel(station, tables, shares, weights, *, peers, cap, rows_each):
    table = tables[...]
    lane = lax.broadcasted_iota(jnp.int32, table.shape, 1)
    share = jnp.sum(jnp.where(lane == station[0], table, 0.0), axis=1, keepdims=True)
    shares[...] = jnp.broadcast_to(share, shares.shape)
    folds, _, lanes = weights.shape
    back = lanes // peers // folds
    for s in range(folds):
        shared = slot_weights(table, station[0], peers, folds * back, cap, rows_each, 1)
        if s:
            shared = jnp.concatenate(
                [jnp.zeros((table.shape[0], s * back), F32), shared[:, : lanes - s * back]], axis=1
            )
        weights[s] = shared.astype(BF16)


def activate(projected):
    half = projected.shape[1] // 2
    gate = projected[:, :half]
    return (gate / (1.0 + jnp.exp(-gate)) * projected[:, half:]).astype(BF16)


def pieces_of(weights, loaded, sems, start):
    steps = sems.shape[0]
    size = loaded.shape[0] // steps
    return [
        pltpu.make_async_copy(
            weights.at[0, pl.ds(start + s * size, size)],
            loaded.at[pl.ds(s * size, size)],
            sems.at[s],
        )
        for s in range(steps)
    ]


def load_kernel(*refs, starts):
    count = len(starts)
    copies = []
    for n, start in enumerate(starts):
        copies += pieces_of(refs[n], refs[count + n], refs[2 * count + n], start)
    for copy in copies:
        copy.start()
    for copy in copies:
        copy.wait()


def hidden_of(stacked, inward):
    total = None
    start = 0
    for ref in inward:
        end = start + ref.shape[0]
        part = jnp.dot(stacked[:, start:end], ref[...], preferred_element_type=F32)
        total = part if total is None else total + part
        start = end
    return activate(total)


def peer_kernel(*refs, peers, parts, held, counts, folds, steps):
    arrived, swapped = refs[:peers], refs[peers : 2 * peers]
    own, other = refs[2 * peers : 2 * peers + 2]
    inward = refs[2 * peers + 2 : 2 * peers + 2 + parts]
    outward = refs[2 * peers + 2 + parts]
    results = refs[2 * peers + 3 + parts : -1]
    stacked = refs[-1]
    width = own.shape[1]
    slots = arrived[0].shape[0]
    for p, ref in enumerate(arrived + swapped):
        stacked[p * slots : (p + 1) * slots] = ref[...]
    base = 2 * peers * slots
    extra = own.shape[0] - held
    stacked[base : base + extra] = own[held:]
    stacked[base + extra :] = other[held:]
    hidden = hidden_of(stacked, inward)
    first = extra // peers
    later, early = counts
    n_len = width // folds // steps
    for c in range(steps):
        values = []
        for f in range(folds):
            start = f * (width // folds) + c * n_len
            values.append(
                jnp.dot(hidden, outward[:, start : start + n_len], preferred_element_type=F32)
            )
        for p, ref in enumerate(results):
            rows = []
            for value in values:
                rows.append(value[p * slots : p * slots + later])
                rows.append(value[base + p * first : base + p * first + early])
            ref[:, c * n_len : (c + 1) * n_len] = jnp.concatenate(rows, axis=0).astype(ref.dtype)


def own_kernel(*refs, parts, steps):
    own, other = refs[:2]
    inward, outward = refs[2 : 2 + parts], refs[2 + parts]
    keep, give = refs[3 + parts : 5 + parts]
    stacked = refs[-1]
    held, width = keep.shape
    stacked[:held] = own[:held]
    stacked[held:] = other[:held]
    hidden = hidden_of(stacked, inward)
    n_len = width // steps
    for c in range(steps):
        cols = slice(c * n_len, (c + 1) * n_len)
        value = jnp.dot(hidden, outward[:, cols], preferred_element_type=F32)
        keep[:, cols] = value[:held]
        give[:, cols] = value[held:].astype(BF16)


def combine_kernel(shares, weights, keep, got, *refs, peers):
    back = refs[:peers]
    blocks = refs[peers:]
    stacked = jnp.concatenate([ref[...] for ref in back], axis=0)
    folds = weights.shape[0]
    rows = blocks[0].shape[0]
    for f in range(folds):
        cols = slice(f * stacked.shape[1], (f + 1) * stacked.shape[1])
        mixed = jnp.dot(weights[f], stacked, preferred_element_type=F32)
        mixed = mixed + shares[:, :1] * (keep[:, cols] + got[:, cols].astype(F32))
        for b, ref in enumerate(blocks):
            ref[:, cols] = mixed[b * rows : (b + 1) * rows].astype(ref.dtype)


def total_kernel(local, *refs):
    total = local[...]
    for ref in refs[:-1]:
        total = total + ref[...].astype(F32)
    refs[-1][...] = total.astype(BF16)


def call(kernel, ins, outs, scratch=(), limit=6, flops=0, moved=0):
    return pl.pallas_call(
        kernel,
        in_specs=list(ins),
        out_specs=[VMEM] * len(outs),
        out_shape=[jax.ShapeDtypeStruct(*out) for out in outs],
        scratch_shapes=list(scratch),
        cost_estimate=pl.CostEstimate(flops=flops, bytes_accessed=moved, transcendentals=0),
        compiler_params=pltpu.CompilerParams(vmem_limit_bytes=limit << 20),
    )


def load(*wanted):
    kernel = call(
        functools.partial(load_kernel, starts=[start for _, start, _, _ in wanted]),
        [HBM] * len(wanted),
        [((size, weights.shape[2]), weights.dtype) for weights, _, size, _ in wanted],
        [pltpu.SemaphoreType.DMA((steps,)) for _, _, _, steps in wanted],
    )
    return kernel(*[weights for weights, _, _, _ in wanted])


def layer(tokens, norm_gain, expert_ids, route_score, expert_pair, w_in, w_out):
    devices = lax.axis_size("expert")
    blocks, plane, up = shape_of(devices)
    peers = plane - 1
    stations = expert_pair.shape[0]
    rows, top = expert_ids.shape
    width = tokens.shape[1]
    half = w_out.shape[1]
    cap = min(rows, -(-rows * top // stations) + 1)
    slots_first = -(-cap // 8) * 8
    slots = -(-(blocks - 1) * cap // 8) * 8
    count = blocks * cap
    folds = next(f for f in (1, 2, 4, 8) if f * count % 8 == 0)
    packed = (folds * count, width // folds)
    table = -(-stations // LANES) * LANES
    held = blocks * rows
    station = (lax.axis_index("expert") // 2).astype(jnp.int32).reshape(1)
    hbm = functools.partial(pltpu.with_memory_space_constraint, memory_space=pltpu.HBM)
    w_in, w_out = hbm(w_in), hbm(w_out)
    cuts = (width // 4, width * 3 // 8, width * 3 // 8)

    inputs = (
        tokens,
        norm_gain.reshape(1, width),
        expert_ids,
        route_score,
        expert_pair.reshape(1, stations),
    )
    payload, inward0, *first = call(
        functools.partial(prepare_kernel, peers=peers, cap=cap, slots=slots_first, width=width),
        [SMEM] + [HBM] * 6,
        [((rows, width + table), BF16), ((cuts[0], 2 * half), BF16)]
        + [((slots_first, width), BF16)] * peers,
        [pltpu.VMEM(x.shape, x.dtype) for x in inputs]
        + [pltpu.SemaphoreType.DMA((5,)), pltpu.SemaphoreType.DMA((4,))],
    )(station, *[hbm(x) for x in inputs], w_in)
    (inward1,) = load((w_in, cuts[0], cuts[1], 6))
    inward2, outward = load((w_in, cuts[0] + cuts[1], cuts[2], 6), (w_out, 0, half, 6))
    inward = [inward0, inward1, inward2]

    column = [payload] + [swap(payload, k << up) for k in range(1, blocks)]
    first = [swap(first[j], (j + 1) << 1) for j in range(peers)]
    own, tables, *chosen = call(
        functools.partial(
            select_kernel, blocks=blocks, peers=peers, cap=cap, slots=slots, width=width
        ),
        [SMEM] + [VMEM] * blocks,
        [((held, width), BF16), ((held, table), F32)]
        + [((slots, width), BF16)] * peers,
    )(station, *column)

    arrived = [swap(chosen[j], (j + 1) << 1) for j in range(peers)]
    own = jnp.concatenate([own] + first, axis=0)
    other = swap(own, 1)
    swapped = [swap(block, 1) for block in arrived]
    parts = len(inward)
    peer_call = call(
        functools.partial(
            peer_kernel,
            peers=peers,
            parts=parts,
            held=held,
            counts=((blocks - 1) * cap, cap),
            folds=folds,
            steps=2,
        ),
        [VMEM] * (2 * peers + 3 + parts),
        [(packed, F32)] * peers + [(packed, BF16)] * peers,
        [pltpu.VMEM((2 * peers * (slots + slots_first), width), BF16)],
        limit=16,
    )
    results = peer_call(*arrived, *swapped, own, other, *inward, outward)
    back = []
    for j in range(peers):
        halves = swap(results[peers + j], 1)
        done = (results[j] + halves.astype(F32)).astype(BF16)
        back.append(swap(done, (j + 1) << 1))
    own_call = call(
        functools.partial(own_kernel, parts=parts, steps=4),
        [VMEM] * (3 + parts),
        [((held, width), F32), ((held, width), BF16)],
        [pltpu.VMEM((2 * held, width), BF16)],
        limit=12,
    )
    keep, give = own_call(own, other, *inward, outward)
    got = swap(give, 1)
    weigh = call(
        functools.partial(weigh_kernel, peers=peers, cap=cap, rows_each=rows),
        [SMEM, VMEM],
        [((held, LANES), F32), ((folds, held, peers * packed[0]), BF16)],
    )
    shares, weights = weigh(station, tables)

    combine = call(
        functools.partial(combine_kernel, peers=peers),
        [VMEM] * (4 + peers),
        [((rows, width), F32)] + [((rows, width), BF16)] * (blocks - 1),
    )
    summed = combine(shares, weights, keep, got, *back)
    returned = [swap(summed[k], k << up) for k in range(1, blocks)]
    (mixed,) = call(total_kernel, [VMEM] * blocks, [((rows, width), BF16)])(summed[0], *returned)
    return mixed


def shape_of(devices):
    bits = (devices // 2).bit_length() - 1
    low = bits // 2
    return 1 << (bits - low), 1 << low, low + 1


def solution(mesh):
    in_specs = (
        P(("groups", "expert"), None),
        P(),
        P(("groups", "expert"), None),
        P(("groups", "expert"), None),
        P("groups"),
        P(("groups", "expert"), None, None),
        P(("groups", "expert"), None, None),
    )
    out_specs = P(("groups", "expert"), None)
    return jax.shard_map(layer, mesh=mesh, in_specs=in_specs, out_specs=out_specs, check_vma=False)
```

time: 57.2 us -> 57.9 us (1.012)
  starting transfers between devices: 27.6 us -> 22.5 us
  waiting for transfers between devices: 17.9 us -> 22.3 us
  Pallas kernels: 11.3 us -> 12.6 us
    ppermute x26 -> x23, starting transfers between devices: 27.6 us -> 22.5 us  [swap(): return lax.ppermute(block, 'expert', [(i, i ^ mask) for i in range(count)])]
    ppermute x26 -> x23, waiting for transfers between devices: 17.9 us -> 22.3 us  [swap(): return lax.ppermute(block, 'expert', [(i, i ^ mask) for i in range(count)])]
    pallas_call x4 -> x6, Pallas kernels: 8.9 us -> 9.89 us  [the longest x2 4.29 us: load(): return kernel(*[weights for weights, _, _, _ in wanted])]
  transfers between devices with their start and end apart: 26 -> 23, of which waited for: 12 -> 9; matrix products, arithmetic and copies ran while one was open for 0% -> 0% of each run, Pallas kernels for 9% -> 13%
where the time goes in v4:
time: 57.9 us; the launch traced here: 57.8 us
  starting transfers between devices  22.5 us (39%)
  waiting for transfers between devices  22.3 us (39%)
  Pallas kernels  12.6 us (22%)
    ppermute x23, starting transfers between devices, swap(): return lax.ppermute(block, 'expert', [(i, i ^ mask) for i in range(count)])  22.5 us
    ppermute x23, waiting for transfers between devices, swap(): return lax.ppermute(block, 'expert', [(i, i ^ mask) for i in range(count)])  22.3 us
    pallas_call x2, Pallas kernels, load(): return kernel(*[weights for weights, _, _, _ in wanted])  4.29 us
    pallas_call x1, Pallas kernels, layer(): results = peer_call(*arrived, *swapped, own, other, *inward, outward)  2.42 us
    pallas_call x1, Pallas kernels, layer(): keep, give = own_call(own, other, *inward, outward)  2.24 us
    pallas_call x1, Pallas kernels, layer(): call(functools.partial(prepare_kernel, peers=peers, cap=cap, slots=slots_...  1.94 us
  transfers between devices with their start and end apart: 23, of which 9 were waited for; matrix products, arithmetic and copies ran while one was open for 0% of the time, Pallas kernels for 13%

profile of v4, /device:TPU:0, one launch (start us, length us, event | category | flops | bytes accessed | tf_op | source)
XLA Modules:
  0.0 57.8 jit_solution(15716921725011814089)
XLA Ops:
  0.0 1.9 %shard_map.73 = (bf16[8,4224]{1,0:T(8,128)(2,1)S(1)}, bf16[1024,768]{1,0:T(8,128)(2,1)S(1)}, bf16[8,4096]{1,0:T(8,128)(2,1)S(1)}, bf16[8,4096]{1,0:T(8,128)(2,1)S(1)}, bf16[8,4096]{1,0:T(8,128)(2,1)S(1)}) custom-call(s32[1]{0:T(128)} %bitcast.station, bf16[8,4096]{1,0:T(8,128)(2,1)} %refs_0_.3, f32[1,4096]{1,0:T(1,128)} %bitcast.3, s32[8,8]{1,0:T(8,128)} %refs_2_.1, ...), custom_call_target="tpu_custom_call" | custom-call | tf_op jit(solution)/shard_map/pallas_call | solution.py:291
  1.9 3.1 %collective-permute-start = (bf16[8,4224]{1,0:T(8,128)(2,1)S(1)}, bf16[8,4224]{1,0:T(8,128)(2,1)S(1)}, u32[]{:S(2)}, u32[]{:S(2)}) collective-permute-start(bf16[8,4224]{1,0:T(8,128)(2,1)S(1)} %get-tuple-element.31.refs_0_), channel_id=1, source_target_pairs={{0,8},{1,9},{2,10},{3,11},{4,12},{5,13},{6,14},{7,15},{8,0},{9,1},... | collective-permute-start | bytes 202760 | tf_op jit(solution)/shard_map/ppermute | solution.py:21
  5.1 2.6 %collective-permute-start.1 = (bf16[8,4224]{1,0:T(8,128)(2,1)S(1)}, bf16[8,4224]{1,0:T(8,128)(2,1)S(1)}, u32[]{:S(2)}, u32[]{:S(2)}) collective-permute-start(bf16[8,4224]{1,0:T(8,128)(2,1)S(1)} %get-tuple-element.31.refs_0_), channel_id=1, source_target_pairs={{0,16},{1,17},{2,18},{3,19},{4,20},{5,21},{6,22},{7,23},{8,24},{9,... | collective-permute-start | bytes 202760 | tf_op jit(solution)/shard_map/ppermute | solution.py:21
  7.7 0.0 collective-permute-start.2
  7.7 1.7 %collective-permute-start.3 = (bf16[8,4096]{1,0:T(8,128)(2,1)S(1)}, bf16[8,4096]{1,0:T(8,128)(2,1)S(1)}, u32[]{:S(2)}, u32[]{:S(2)}) collective-permute-start(bf16[8,4096]{1,0:T(8,128)(2,1)S(1)} %get-tuple-element.36), channel_id=1, source_target_pairs={{0,2},{1,3},{2,0},{3,1},{4,6},{5,7},{6,4},{7,5},{8,10},{9,11},{10,... | collective-permute-start | bytes 196616 | tf_op jit(solution)/shard_map/ppermute | solution.py:21
  9.4 1.5 %collective-permute-start.4 = (bf16[8,4096]{1,0:T(8,128)(2,1)S(1)}, bf16[8,4096]{1,0:T(8,128)(2,1)S(1)}, u32[]{:S(2)}, u32[]{:S(2)}) collective-permute-start(bf16[8,4096]{1,0:T(8,128)(2,1)S(1)} %get-tuple-element.37), channel_id=1, source_target_pairs={{0,4},{1,5},{2,6},{3,7},{4,0},{5,1},{6,2},{7,3},{8,12},{9,13},{10,... | collective-permute-start | bytes 196616 | tf_op jit(solution)/shard_map/ppermute | solution.py:21
  10.9 0.0 collective-permute-done.refs_1_
  10.9 0.3 collective-permute-start.5
  11.1 1.3 %collective-permute-done.1.refs_2_ = bf16[8,4224]{1,0:T(8,128)(2,1)S(1)} collective-permute-done((bf16[8,4224]{1,0:T(8,128)(2,1)S(1)}, bf16[8,4224]{1,0:T(8,128)(2,1)S(1)}, u32[]{:S(2)}, u32[]{:S(2)}) %collective-permute-start.1) | collective-permute-done | bytes 67616 | tf_op jit(solution)/shard_map/ppermute | solution.py:21
  12.5 1.4 %collective-permute-done.2.refs_3_ = bf16[8,4224]{1,0:T(8,128)(2,1)S(1)} collective-permute-done((bf16[8,4224]{1,0:T(8,128)(2,1)S(1)}, bf16[8,4224]{1,0:T(8,128)(2,1)S(1)}, u32[]{:S(2)}, u32[]{:S(2)}) %collective-permute-start.2) | collective-permute-done | bytes 67616 | tf_op jit(solution)/shard_map/ppermute | solution.py:21
  13.8 0.5 shard_map.74
  14.4 0.0 collective-permute-done.3
  14.4 0.0 collective-permute-done.4
  14.4 1.6 %collective-permute-done.5 = bf16[8,4096]{1,0:T(8,128)(2,1)S(1)} collective-permute-done((bf16[8,4096]{1,0:T(8,128)(2,1)S(1)}, bf16[8,4096]{1,0:T(8,128)(2,1)S(1)}, u32[]{:S(2)}, u32[]{:S(2)}) %collective-permute-start.5) | collective-permute-done | bytes 65568 | tf_op jit(solution)/shard_map/ppermute | solution.py:21
  16.1 0.0 collective-permute-start.6
  16.1 0.6 %collective-permute-start.8 = (bf16[16,4096]{1,0:T(8,128)(2,1)S(1)}, bf16[16,4096]{1,0:T(8,128)(2,1)S(1)}, u32[]{:S(2)}, u32[]{:S(2)}) collective-permute-start(bf16[16,4096]{1,0:T(8,128)(2,1)S(1)} %get-tuple-element.44), channel_id=1, source_target_pairs={{0,2},{1,3},{2,0},{3,1},{4,6},{5,7},{6,4},{7,5},{8,10},{9,11},{10,... | collective-permute-start | bytes 393224 | tf_op jit(solution)/shard_map/ppermute | solution.py:21
  16.7 0.9 %collective-permute-start.9 = (bf16[16,4096]{1,0:T(8,128)(2,1)S(1)}, bf16[16,4096]{1,0:T(8,128)(2,1)S(1)}, u32[]{:S(2)}, u32[]{:S(2)}) collective-permute-start(bf16[16,4096]{1,0:T(8,128)(2,1)S(1)} %get-tuple-element.45), channel_id=1, source_target_pairs={{0,4},{1,5},{2,6},{3,7},{4,0},{5,1},{6,2},{7,3},{8,12},{9,13},{10,... | collective-permute-start | bytes 393224 | tf_op jit(solution)/shard_map/ppermute | solution.py:21
  17.6 2.0 %collective-permute-start.10 = (bf16[16,4096]{1,0:T(8,128)(2,1)S(1)}, bf16[16,4096]{1,0:T(8,128)(2,1)S(1)}, u32[]{:S(2)}, u32[]{:S(2)}) collective-permute-start(bf16[16,4096]{1,0:T(8,128)(2,1)S(1)} %get-tuple-element.46), channel_id=1, source_target_pairs={{0,6},{1,7},{2,4},{3,5},{4,2},{5,3},{6,0},{7,1},{8,14},{9,15},{10,... | collective-permute-start | bytes 393224 | tf_op jit(solution)/shard_map/ppermute | solution.py:21
  19.6 2.9 %collective-permute-done.8.refs_0_ = bf16[16,4096]{1,0:T(8,128)(2,1)S(1)} collective-permute-done((bf16[16,4096]{1,0:T(8,128)(2,1)S(1)}, bf16[16,4096]{1,0:T(8,128)(2,1)S(1)}, u32[]{:S(2)}, u32[]{:S(2)}) %collective-permute-start.8) | collective-permute-done | bytes 131104 | tf_op jit(solution)/shard_map/ppermute | solution.py:21
  22.5 0.0 collective-permute-start.11
  22.5 2.5 %collective-permute-done.9.refs_1_ = bf16[16,4096]{1,0:T(8,128)(2,1)S(1)} collective-permute-done((bf16[16,4096]{1,0:T(8,128)(2,1)S(1)}, bf16[16,4096]{1,0:T(8,128)(2,1)S(1)}, u32[]{:S(2)}, u32[]{:S(2)}) %collective-permute-start.9) | collective-permute-done | bytes 131104 | tf_op jit(solution)/shard_map/ppermute | solution.py:21
  25.0 0.0 collective-permute-start.12
  25.0 0.0 collective-permute-done.10.refs_2_
  25.0 0.5 collective-permute-start.13
  25.5 1.6 %shard_map.76.refs_3_.refs_9_ = bf16[1536,768]{1,0:T(8,128)(2,1)S(1)} custom-call(bf16[1,4096,768]{2,1,0:T(8,128)(2,1)} %refs_0_.5), custom_call_target="tpu_custom_call" | custom-call | tf_op jit(solution)/shard_map/pallas_call | solution.py:260
  27.2 2.7 %shard_map.77 = (bf16[1536,768]{1,0:T(8,128)(2,1)S(1)}, bf16[384,4096]{1,0:T(8,128)(2,1)S(1)}) custom-call(bf16[1,4096,768]{2,1,0:T(8,128)(2,1)} %refs_0_.5, bf16[1,384,4096]{2,1,0:T(8,128)(2,1)} %refs_1_.1), custom_call_target="tpu_custom_call" | custom-call | tf_op jit(solution)/shard_map/pallas_call | solution.py:260
  29.9 0.0 collective-permute-done.11.refs_3_
  29.9 0.0 collective-permute-done.12.refs_4_
  29.9 0.0 collective-permute-done.13.refs_5_
  29.9 0.0 collective-permute-done.6.refs_1_.refs_7_
  29.9 2.4 %shard_map.79 = (f32[40,2048]{1,0:T(8,128)S(1)}, f32[40,2048]{1,0:T(8,128)S(1)}, f32[40,2048]{1,0:T(8,128)S(1)}, bf16[40,2048]{1,0:T(8,128)(2,1)S(1)}, bf16[40,2...) custom-call(bf16[16,4096]{1,0:T(8,128)(2,1)S(1)} %collective-permute-done.8.refs_0_, ...), custom_call_target="tpu_custom_call" | custom-call | tf_op jit(solution)/shard_map/pallas_call | solution.py:334
  32.3 0.1 collective-permute-start.18
  32.4 0.5 collective-permute-start.16
  32.9 0.1 collective-permute-start.14
  33.0 2.2 %shard_map.78 = (f32[32,4096]{1,0:T(8,128)S(1)}, bf16[32,4096]{1,0:T(8,128)(2,1)S(1)}) custom-call(bf16[56,4096]{1,0:T(8,128)(2,1)S(1)} %constant_dynamic-update-slice_fusion.refs_0_.refs_6_, bf16[56,4096]{1,0:T(8,128)(2,1)S(1)} %collective-permute-done.6.refs_1_.refs_7_, bf16[1024,768]{1,0:T(8,128)(2,1)S(1)} %get-tuple-element.39.refs_2_.refs_8_, ...), custom_call_target="tpu_custom_call" | custom-call | tf_op jit(solution)/shard_map/pallas_call | solution.py:347
  35.2 0.5 collective-permute-start.7
  35.7 0.0 collective-permute-done.18
  35.8 1.5 %collective-permute-start.19 = (bf16[40,2048]{1,0:T(8,128)(2,1)S(1)}, bf16[40,2048]{1,0:T(8,128)(2,1)S(1)}, u32[]{:S(2)}, u32[]{:S(2)}) collective-permute-start(bf16[40,2048]{1,0:T(8,128)(2,1)S(1)} %add_convert_fusion), channel_id=1, source_target_pairs={{0,6},{1,7},{2,4},{3,5},{4,2},{5,3},{6,0},{7,1},{8,14},{9,15},{10,... | collective-permute-start | bytes 491528 | tf_op jit(solution)/shard_map/ppermute | solution.py:21
  37.3 0.0 collective-permute-done.16
  37.3 1.6 %collective-permute-start.17 = (bf16[40,2048]{1,0:T(8,128)(2,1)S(1)}, bf16[40,2048]{1,0:T(8,128)(2,1)S(1)}, u32[]{:S(2)}, u32[]{:S(2)}) collective-permute-start(bf16[40,2048]{1,0:T(8,128)(2,1)S(1)} %add_convert_fusion.1), channel_id=1, source_target_pairs={{0,4},{1,5},{2,6},{3,7},{4,0},{5,1},{6,2},{7,3},{8,12},{9,13},{10,... | collective-permute-start | bytes 491528 | tf_op jit(solution)/shard_map/ppermute | solution.py:21
  38.9 0.0 collective-permute-done.14
  38.9 0.6 %collective-permute-start.15 = (bf16[40,2048]{1,0:T(8,128)(2,1)S(1)}, bf16[40,2048]{1,0:T(8,128)(2,1)S(1)}, u32[]{:S(2)}, u32[]{:S(2)}) collective-permute-start(bf16[40,2048]{1,0:T(8,128)(2,1)S(1)} %add_convert_fusion.2), channel_id=1, source_target_pairs={{0,2},{1,3},{2,0},{3,1},{4,6},{5,7},{6,4},{7,5},{8,10},{9,11},{10,... | collective-permute-start | bytes 491528 | tf_op jit(solution)/shard_map/ppermute | solution.py:21
  39.5 0.3 shard_map.75
  39.8 0.0 collective-permute-done.7.got
  39.8 4.0 %collective-permute-done.19.refs_2_ = bf16[40,2048]{1,0:T(8,128)(2,1)S(1)} collective-permute-done((bf16[40,2048]{1,0:T(8,128)(2,1)S(1)}, bf16[40,2048]{1,0:T(8,128)(2,1)S(1)}, u32[]{:S(2)}, u32[]{:S(2)}) %collective-permute-start.19) | collective-permute-done | bytes 163872 | tf_op jit(solution)/shard_map/ppermute | solution.py:21
  43.8 2.6 %collective-permute-done.17.refs_1_ = bf16[40,2048]{1,0:T(8,128)(2,1)S(1)} collective-permute-done((bf16[40,2048]{1,0:T(8,128)(2,1)S(1)}, bf16[40,2048]{1,0:T(8,128)(2,1)S(1)}, u32[]{:S(2)}, u32[]{:S(2)}) %collective-permute-start.17) | collective-permute-done | bytes 163872 | tf_op jit(solution)/shard_map/ppermute | solution.py:21
  46.4 0.0 collective-permute-done.15.refs_0_
  46.4 0.3 shard_map.80
  46.7 0.7 %collective-permute-start.20 = (bf16[8,4096]{1,0:T(8,128)(2,1)S(1)}, bf16[8,4096]{1,0:T(8,128)(2,1)S(1)}, u32[]{:S(2)}, u32[]{:S(2)}) collective-permute-start(bf16[8,4096]{1,0:T(8,128)(2,1)S(1)} %get-tuple-element.54), channel_id=1, source_target_pairs={{0,8},{1,9},{2,10},{3,11},{4,12},{5,13},{6,14},{7,15},{8,0},{9,1},... | collective-permute-start | bytes 196616 | tf_op jit(solution)/shard_map/ppermute | solution.py:21
  47.4 3.5 %collective-permute-start.21 = (bf16[8,4096]{1,0:T(8,128)(2,1)S(1)}, bf16[8,4096]{1,0:T(8,128)(2,1)S(1)}, u32[]{:S(2)}, u32[]{:S(2)}) collective-permute-start(bf16[8,4096]{1,0:T(8,128)(2,1)S(1)} %get-tuple-element.55), channel_id=1, source_target_pairs={{0,16},{1,17},{2,18},{3,19},{4,20},{5,21},{6,22},{7,23},{8,24},{9,... | collective-permute-start | bytes 196616 | tf_op jit(solution)/shard_map/ppermute | solution.py:21
  50.9 0.2 collective-permute-start.22
  51.2 0.0 collective-permute-done.20.refs_0_
  51.2 3.7 %collective-permute-done.21.refs_1_ = bf16[8,4096]{1,0:T(8,128)(2,1)S(1)} collective-permute-done((bf16[8,4096]{1,0:T(8,128)(2,1)S(1)}, bf16[8,4096]{1,0:T(8,128)(2,1)S(1)}, u32[]{:S(2)}, u32[]{:S(2)}) %collective-permute-start.21) | collective-permute-done | bytes 65568 | tf_op jit(solution)/shard_map/ppermute | solution.py:21
  54.9 2.2 %collective-permute-done.22.refs_2_ = bf16[8,4096]{1,0:T(8,128)(2,1)S(1)} collective-permute-done((bf16[8,4096]{1,0:T(8,128)(2,1)S(1)}, bf16[8,4096]{1,0:T(8,128)(2,1)S(1)}, u32[]{:S(2)}, u32[]{:S(2)}) %collective-permute-start.22) | collective-permute-done | bytes 65568 | tf_op jit(solution)/shard_map/ppermute | solution.py:21
  57.1 0.7 %shard_map.81 = bf16[8,4096]{1,0:T(8,128)(2,1)} custom-call(f32[8,4096]{1,0:T(8,128)S(1)} %get-tuple-element.53.local, bf16[8,4096]{1,0:T(8,128)(2,1)S(1)} %collective-permute-done.20.refs_0_, bf16[8,4096]{1,0:T(8,128)(2,1)S(1)} %collective-permute-done.21.refs_1_, bf16[8,4096]{1,0:T(8,128)(2,1)S(1)} %collective-permute-done.22.refs_2_), custom_call_target="tpu_custom_call" | custom-call | tf_op jit(solution)/shard_map/pallas_call | solution.py:363
  (7 shorter events, 0.1 us)
Async XLA Ops:
  1.9 8.9 %collective-permute-start = (bf16[8,4224]{1,0:T(8,128)(2,1)S(1)}, bf16[8,4224]{1,0:T(8,128)(2,1)S(1)}, u32[]{:S(2)}, u32[]{:S(2)}) collective-permute-start(bf16[8,4224]{1,0:T(8,128)(2,1)S(1)} %get-tuple-element.31.refs_0_), channel_id=1, source_target_pairs={{0,8},{1,9},{2,10},{3,11},{4,12},{5,13},{6,14},{7,15},{8,0},{9,1},... | collective-permute-start | bytes 202760 | tf_op jit(solution)/shard_map/ppermute | solution.py:21
  5.1 7.4 %collective-permute-start.1 = (bf16[8,4224]{1,0:T(8,128)(2,1)S(1)}, bf16[8,4224]{1,0:T(8,128)(2,1)S(1)}, u32[]{:S(2)}, u32[]{:S(2)}) collective-permute-start(bf16[8,4224]{1,0:T(8,128)(2,1)S(1)} %get-tuple-element.31.refs_0_), channel_id=1, source_target_pairs={{0,16},{1,17},{2,18},{3,19},{4,20},{5,21},{6,22},{7,23},{8,24},{9,... | collective-permute-start | bytes 202760 | tf_op jit(solution)/shard_map/ppermute | solution.py:21
  7.7 6.2 %collective-permute-start.2 = (bf16[8,4224]{1,0:T(8,128)(2,1)S(1)}, bf16[8,4224]{1,0:T(8,128)(2,1)S(1)}, u32[]{:S(2)}, u32[]{:S(2)}) collective-permute-start(bf16[8,4224]{1,0:T(8,128)(2,1)S(1)} %get-tuple-element.31.refs_0_), channel_id=1, source_target_pairs={{0,24},{1,25},{2,26},{3,27},{4,28},{5,29},{6,30},{7,31},{8,16},{9,... | collective-permute-start | bytes 202760 | tf_op jit(solution)/shard_map/ppermute | solution.py:21
  7.7 6.7 %collective-permute-start.3 = (bf16[8,4096]{1,0:T(8,128)(2,1)S(1)}, bf16[8,4096]{1,0:T(8,128)(2,1)S(1)}, u32[]{:S(2)}, u32[]{:S(2)}) collective-permute-start(bf16[8,4096]{1,0:T(8,128)(2,1)S(1)} %get-tuple-element.36), channel_id=1, source_target_pairs={{0,2},{1,3},{2,0},{3,1},{4,6},{5,7},{6,4},{7,5},{8,10},{9,11},{10,... | collective-permute-start | bytes 196616 | tf_op jit(solution)/shard_map/ppermute | solution.py:21
  9.4 5.0 %collective-permute-start.4 = (bf16[8,4096]{1,0:T(8,128)(2,1)S(1)}, bf16[8,4096]{1,0:T(8,128)(2,1)S(1)}, u32[]{:S(2)}, u32[]{:S(2)}) collective-permute-start(bf16[8,4096]{1,0:T(8,128)(2,1)S(1)} %get-tuple-element.37), channel_id=1, source_target_pairs={{0,4},{1,5},{2,6},{3,7},{4,0},{5,1},{6,2},{7,3},{8,12},{9,13},{10,... | collective-permute-start | bytes 196616 | tf_op jit(solution)/shard_map/ppermute | solution.py:21
  10.9 5.2 %collective-permute-start.5 = (bf16[8,4096]{1,0:T(8,128)(2,1)S(1)}, bf16[8,4096]{1,0:T(8,128)(2,1)S(1)}, u32[]{:S(2)}, u32[]{:S(2)}) collective-permute-start(bf16[8,4096]{1,0:T(8,128)(2,1)S(1)} %get-tuple-element.38), channel_id=1, source_target_pairs={{0,6},{1,7},{2,4},{3,5},{4,2},{5,3},{6,0},{7,1},{8,14},{9,15},{10,... | collective-permute-start | bytes 196616 | tf_op jit(solution)/shard_map/ppermute | solution.py:21
  16.1 13.8 %collective-permute-start.6 = (bf16[56,4096]{1,0:T(8,128)(2,1)S(1)}, bf16[56,4096]{1,0:T(8,128)(2,1)S(1)}, u32[]{:S(2)}, u32[]{:S(2)}) collective-permute-start(bf16[56,4096]{1,0:T(8,128)(2,1)S(1)} %constant_dynamic-update-slice_fusion.refs_0_.refs_6_), channel_id=1, source_target_pairs={{0,1},{1,0},{2,3},{3,2},{4,5},{5,4},{6,7},{7,6},{8,9},{9,8},{10,11... | collective-permute-start | bytes 1376264 | tf_op jit(solution)/shard_map/ppermute | solution.py:21
  16.1 6.4 %collective-permute-start.8 = (bf16[16,4096]{1,0:T(8,128)(2,1)S(1)}, bf16[16,4096]{1,0:T(8,128)(2,1)S(1)}, u32[]{:S(2)}, u32[]{:S(2)}) collective-permute-start(bf16[16,4096]{1,0:T(8,128)(2,1)S(1)} %get-tuple-element.44), channel_id=1, source_target_pairs={{0,2},{1,3},{2,0},{3,1},{4,6},{5,7},{6,4},{7,5},{8,10},{9,11},{10,... | collective-permute-start | bytes 393224 | tf_op jit(solution)/shard_map/ppermute | solution.py:21
  16.7 8.4 %collective-permute-start.9 = (bf16[16,4096]{1,0:T(8,128)(2,1)S(1)}, bf16[16,4096]{1,0:T(8,128)(2,1)S(1)}, u32[]{:S(2)}, u32[]{:S(2)}) collective-permute-start(bf16[16,4096]{1,0:T(8,128)(2,1)S(1)} %get-tuple-element.45), channel_id=1, source_target_pairs={{0,4},{1,5},{2,6},{3,7},{4,0},{5,1},{6,2},{7,3},{8,12},{9,13},{10,... | collective-permute-start | bytes 393224 | tf_op jit(solution)/shard_map/ppermute | solution.py:21
  17.6 7.4 %collective-permute-start.10 = (bf16[16,4096]{1,0:T(8,128)(2,1)S(1)}, bf16[16,4096]{1,0:T(8,128)(2,1)S(1)}, u32[]{:S(2)}, u32[]{:S(2)}) collective-permute-start(bf16[16,4096]{1,0:T(8,128)(2,1)S(1)} %get-tuple-element.46), channel_id=1, source_target_pairs={{0,6},{1,7},{2,4},{3,5},{4,2},{5,3},{6,0},{7,1},{8,14},{9,15},{10,... | collective-permute-start | bytes 393224 | tf_op jit(solution)/shard_map/ppermute | solution.py:21
  22.5 7.4 %collective-permute-start.11 = (bf16[16,4096]{1,0:T(8,128)(2,1)S(1)}, bf16[16,4096]{1,0:T(8,128)(2,1)S(1)}, u32[]{:S(2)}, u32[]{:S(2)}) collective-permute-start(bf16[16,4096]{1,0:T(8,128)(2,1)S(1)} %collective-permute-done.8.refs_0_), channel_id=1, source_target_pairs={{0,1},{1,0},{2,3},{3,2},{4,5},{5,4},{6,7},{7,6},{8,9},{9,8},{10,11... | collective-permute-start | bytes 393224 | tf_op jit(solution)/shard_map/ppermute | solution.py:21
  25.0 4.8 %collective-permute-start.12 = (bf16[16,4096]{1,0:T(8,128)(2,1)S(1)}, bf16[16,4096]{1,0:T(8,128)(2,1)S(1)}, u32[]{:S(2)}, u32[]{:S(2)}) collective-permute-start(bf16[16,4096]{1,0:T(8,128)(2,1)S(1)} %collective-permute-done.9.refs_1_), channel_id=1, source_target_pairs={{0,1},{1,0},{2,3},{3,2},{4,5},{5,4},{6,7},{7,6},{8,9},{9,8},{10,11... | collective-permute-start | bytes 393224 | tf_op jit(solution)/shard_map/ppermute | solution.py:21
  25.0 4.8 %collective-permute-start.13 = (bf16[16,4096]{1,0:T(8,128)(2,1)S(1)}, bf16[16,4096]{1,0:T(8,128)(2,1)S(1)}, u32[]{:S(2)}, u32[]{:S(2)}) collective-permute-start(bf16[16,4096]{1,0:T(8,128)(2,1)S(1)} %collective-permute-done.10.refs_2_), channel_id=1, source_target_pairs={{0,1},{1,0},{2,3},{3,2},{4,5},{5,4},{6,7},{7,6},{8,9},{9,8},{10,11... | collective-permute-start | bytes 393224 | tf_op jit(solution)/shard_map/ppermute | solution.py:21
  32.3 3.4 %collective-permute-start.18 = (bf16[40,2048]{1,0:T(8,128)(2,1)S(1)}, bf16[40,2048]{1,0:T(8,128)(2,1)S(1)}, u32[]{:S(2)}, u32[]{:S(2)}) collective-permute-start(bf16[40,2048]{1,0:T(8,128)(2,1)S(1)} %get-tuple-element.52), channel_id=1, source_target_pairs={{0,1},{1,0},{2,3},{3,2},{4,5},{5,4},{6,7},{7,6},{8,9},{9,8},{10,11... | collective-permute-start | bytes 491528 | tf_op jit(solution)/shard_map/ppermute | solution.py:21
  32.4 4.9 %collective-permute-start.16 = (bf16[40,2048]{1,0:T(8,128)(2,1)S(1)}, bf16[40,2048]{1,0:T(8,128)(2,1)S(1)}, u32[]{:S(2)}, u32[]{:S(2)}) collective-permute-start(bf16[40,2048]{1,0:T(8,128)(2,1)S(1)} %get-tuple-element.50), channel_id=1, source_target_pairs={{0,1},{1,0},{2,3},{3,2},{4,5},{5,4},{6,7},{7,6},{8,9},{9,8},{10,11... | collective-permute-start | bytes 491528 | tf_op jit(solution)/shard_map/ppermute | solution.py:21
  32.9 6.0 %collective-permute-start.14 = (bf16[40,2048]{1,0:T(8,128)(2,1)S(1)}, bf16[40,2048]{1,0:T(8,128)(2,1)S(1)}, u32[]{:S(2)}, u32[]{:S(2)}) collective-permute-start(bf16[40,2048]{1,0:T(8,128)(2,1)S(1)} %get-tuple-element.48), channel_id=1, source_target_pairs={{0,1},{1,0},{2,3},{3,2},{4,5},{5,4},{6,7},{7,6},{8,9},{9,8},{10,11... | collective-permute-start | bytes 491528 | tf_op jit(solution)/shard_map/ppermute | solution.py:21
  35.2 4.6 %collective-permute-start.7 = (bf16[32,4096]{1,0:T(8,128)(2,1)S(1)}, bf16[32,4096]{1,0:T(8,128)(2,1)S(1)}, u32[]{:S(2)}, u32[]{:S(2)}) collective-permute-start(bf16[32,4096]{1,0:T(8,128)(2,1)S(1)} %get-tuple-element.43), channel_id=1, source_target_pairs={{0,1},{1,0},{2,3},{3,2},{4,5},{5,4},{6,7},{7,6},{8,9},{9,8},{10,11... | collective-permute-start | bytes 786440 | tf_op jit(solution)/shard_map/ppermute | solution.py:21
  35.8 8.1 %collective-permute-start.19 = (bf16[40,2048]{1,0:T(8,128)(2,1)S(1)}, bf16[40,2048]{1,0:T(8,128)(2,1)S(1)}, u32[]{:S(2)}, u32[]{:S(2)}) collective-permute-start(bf16[40,2048]{1,0:T(8,128)(2,1)S(1)} %add_convert_fusion), channel_id=1, source_target_pairs={{0,6},{1,7},{2,4},{3,5},{4,2},{5,3},{6,0},{7,1},{8,14},{9,15},{10,... | collective-permute-start | bytes 491528 | tf_op jit(solution)/shard_map/ppermute | solution.py:21
  37.3 9.1 %collective-permute-start.17 = (bf16[40,2048]{1,0:T(8,128)(2,1)S(1)}, bf16[40,2048]{1,0:T(8,128)(2,1)S(1)}, u32[]{:S(2)}, u32[]{:S(2)}) collective-permute-start(bf16[40,2048]{1,0:T(8,128)(2,1)S(1)} %add_convert_fusion.1), channel_id=1, source_target_pairs={{0,4},{1,5},{2,6},{3,7},{4,0},{5,1},{6,2},{7,3},{8,12},{9,13},{10,... | collective-permute-start | bytes 491528 | tf_op jit(solution)/shard_map/ppermute | solution.py:21
  38.9 7.5 %collective-permute-start.15 = (bf16[40,2048]{1,0:T(8,128)(2,1)S(1)}, bf16[40,2048]{1,0:T(8,128)(2,1)S(1)}, u32[]{:S(2)}, u32[]{:S(2)}) collective-permute-start(bf16[40,2048]{1,0:T(8,128)(2,1)S(1)} %add_convert_fusion.2), channel_id=1, source_target_pairs={{0,2},{1,3},{2,0},{3,1},{4,6},{5,7},{6,4},{7,5},{8,10},{9,11},{10,... | collective-permute-start | bytes 491528 | tf_op jit(solution)/shard_map/ppermute | solution.py:21
  46.7 4.5 %collective-permute-start.20 = (bf16[8,4096]{1,0:T(8,128)(2,1)S(1)}, bf16[8,4096]{1,0:T(8,128)(2,1)S(1)}, u32[]{:S(2)}, u32[]{:S(2)}) collective-permute-start(bf16[8,4096]{1,0:T(8,128)(2,1)S(1)} %get-tuple-element.54), channel_id=1, source_target_pairs={{0,8},{1,9},{2,10},{3,11},{4,12},{5,13},{6,14},{7,15},{8,0},{9,1},... | collective-permute-start | bytes 196616 | tf_op jit(solution)/shard_map/ppermute | solution.py:21
  47.4 7.5 %collective-permute-start.21 = (bf16[8,4096]{1,0:T(8,128)(2,1)S(1)}, bf16[8,4096]{1,0:T(8,128)(2,1)S(1)}, u32[]{:S(2)}, u32[]{:S(2)}) collective-permute-start(bf16[8,4096]{1,0:T(8,128)(2,1)S(1)} %get-tuple-element.55), channel_id=1, source_target_pairs={{0,16},{1,17},{2,18},{3,19},{4,20},{5,21},{6,22},{7,23},{8,24},{9,... | collective-permute-start | bytes 196616 | tf_op jit(solution)/shard_map/ppermute | solution.py:21
  50.9 6.2 %collective-permute-start.22 = (bf16[8,4096]{1,0:T(8,128)(2,1)S(1)}, bf16[8,4096]{1,0:T(8,128)(2,1)S(1)}, u32[]{:S(2)}, u32[]{:S(2)}) collective-permute-start(bf16[8,4096]{1,0:T(8,128)(2,1)S(1)} %get-tuple-element.56), channel_id=1, source_target_pairs={{0,24},{1,25},{2,26},{3,27},{4,28},{5,29},{6,30},{7,31},{8,16},{9,... | collective-permute-start | bytes 196616 | tf_op jit(solution)/shard_map/ppermute | solution.py:21

commit v5 on v4

--- a/solution.py
+++ b/solution.py
@@ -25,7 +25,7 @@
     return lax.dot_general(placing, body, (((0,), (0,)), ((), ())), preferred_element_type=F32)
 
 
-def slot_weights(table, station, peers, slots, cap, rows_each, first=0):
+def slot_weights(table, station, peers, slots, cap, rows_each):
     rows = table.shape[0]
     row = lax.broadcasted_iota(jnp.int32, (rows, rows), 0)
     col = lax.broadcasted_iota(jnp.int32, (rows, rows), 1)
@@ -35,8 +35,7 @@
         jnp.where(table > 0.0, 1.0, 0.0).astype(BF16),
         preferred_element_type=F32,
     )
-    block = lax.broadcasted_iota(jnp.int32, (rows, 1), 0) // rows_each
-    base = jnp.where(block < first, block + rows // rows_each, block) * cap - first * cap
+    base = lax.broadcasted_iota(jnp.int32, (rows, 1), 0) // rows_each * cap
     lane = lax.broadcasted_iota(jnp.int32, table.shape, 1)
     target = lax.broadcasted_iota(jnp.int32, (rows, peers * slots), 1)
     weights = jnp.zeros((rows, peers * slots), F32)
@@ -109,20 +108,22 @@
         ref[...] = placed[j * slots : (j + 1) * slots].astype(BF16)
 
 
-def weigh_kernel(station, tables, shares, weights, *, peers, cap, rows_each):
+def weigh_kernel(station, tables, shares, *outs, peers, cap, rows_each):
     table = tables[...]
     lane = lax.broadcasted_iota(jnp.int32, table.shape, 1)
     share = jnp.sum(jnp.where(lane == station[0], table, 0.0), axis=1, keepdims=True)
     shares[...] = jnp.broadcast_to(share, shares.shape)
-    folds, _, lanes = weights.shape
-    back = lanes // peers // folds
-    for s in range(folds):
-        shared = slot_weights(table, station[0], peers, folds * back, cap, rows_each, 1)
-        if s:
+    for h, weights in enumerate(outs):
+        folds, rows, lanes = weights.shape
+        back = lanes // peers // folds
+        part = table[h * rows : (h + 1) * rows]
+        shared = slot_weights(part, station[0], peers, folds * back, cap, rows_each)
+        weights[0] = shared.astype(BF16)
+        for f in range(1, folds):
             shared = jnp.concatenate(
-                [jnp.zeros((table.shape[0], s * back), F32), shared[:, : lanes - s * back]], axis=1
+                [jnp.zeros((rows, back), F32), shared[:, : lanes - back]], axis=1
             )
-        weights[s] = shared.astype(BF16)
+            weights[f] = shared.astype(BF16)
 
 
 def activate(projected):
@@ -166,67 +167,64 @@
     return activate(total)
 
 
-def peer_kernel(*refs, peers, parts, held, counts, folds, steps):
+def expert_kernel(*refs, peers, parts, held, cap, near, far, folds, steps):
     arrived, swapped = refs[:peers], refs[peers : 2 * peers]
     own, other = refs[2 * peers : 2 * peers + 2]
     inward = refs[2 * peers + 2 : 2 * peers + 2 + parts]
     outward = refs[2 * peers + 2 + parts]
     results = refs[2 * peers + 3 + parts : -1]
+    keep_far, give_far = results[:peers], results[peers : 2 * peers]
+    keep_near, give_near, keep, give = results[2 * peers :]
     stacked = refs[-1]
     width = own.shape[1]
     slots = arrived[0].shape[0]
-    for p, ref in enumerate(arrived + swapped):
+    pieces = arrived + swapped
+    for p, ref in enumerate(pieces):
         stacked[p * slots : (p + 1) * slots] = ref[...]
-    base = 2 * peers * slots
-    extra = own.shape[0] - held
-    stacked[base : base + extra] = own[held:]
-    stacked[base + extra :] = other[held:]
+    base = len(pieces) * slots
+    early = own.shape[0]
+    stacked[base : base + early] = own[...]
+    stacked[base + early :] = other[...]
     hidden = hidden_of(stacked, inward)
-    first = extra // peers
-    later, early = counts
+    slots_first = (early - held) // peers
     n_len = width // folds // steps
+    tall = folds * far * cap
     for c in range(steps):
+        cols = slice(c * n_len, (c + 1) * n_len)
         values = []
         for f in range(folds):
             start = f * (width // folds) + c * n_len
-            values.append(
-                jnp.dot(hidden, outward[:, start : start + n_len], preferred_element_type=F32)
-            )
-        for p, ref in enumerate(results):
-            rows = []
+            wide = slice(start, start + n_len)
+            value = jnp.dot(hidden, outward[:, wide], preferred_element_type=F32)
+            keep[:, wide] = value[base : base + held]
+            give[:, wide] = value[base + early : base + early + held].astype(BF16)
+            values.append(value)
+        for p in range(2 * peers):
+            side, j = divmod(p, peers)
+            first = base + side * early + held + j * slots_first
+            distant, close = [], []
             for value in values:
-                rows.append(value[p * slots : p * slots + later])
-                rows.append(value[base + p * first : base + p * first + early])
-            ref[:, c * n_len : (c + 1) * n_len] = jnp.concatenate(rows, axis=0).astype(ref.dtype)
-
-
-def own_kernel(*refs, parts, steps):
-    own, other = refs[:2]
-    inward, outward = refs[2 : 2 + parts], refs[2 + parts]
-    keep, give = refs[3 + parts : 5 + parts]
-    stacked = refs[-1]
-    held, width = keep.shape
-    stacked[:held] = own[:held]
-    stacked[held:] = other[:held]
-    hidden = hidden_of(stacked, inward)
-    n_len = width // steps
-    for c in range(steps):
-        cols = slice(c * n_len, (c + 1) * n_len)
-        value = jnp.dot(hidden, outward[:, cols], preferred_element_type=F32)
-        keep[:, cols] = value[:held]
-        give[:, cols] = value[held:].astype(BF16)
-
-
-def combine_kernel(shares, weights, keep, got, *refs, peers):
+                start = p * slots + (near - 1) * cap
+                distant.append(value[start : start + far * cap])
+                close.append(value[first : first + cap])
+                close.append(value[p * slots : start])
+            ref = (give_far if side else keep_far)[j]
+            ref[:, cols] = jnp.concatenate(distant, axis=0).astype(ref.dtype)
+            ref = give_near if side else keep_near
+            ref[j * tall : (j + 1) * tall, cols] = jnp.concatenate(close, axis=0).astype(ref.dtype)
+
+
+def combine_kernel(shares, weights, keep, got, *refs, peers, start):
     back = refs[:peers]
     blocks = refs[peers:]
     stacked = jnp.concatenate([ref[...] for ref in back], axis=0)
-    folds = weights.shape[0]
+    folds, size, _ = weights.shape
+    span = slice(start, start + size)
     rows = blocks[0].shape[0]
     for f in range(folds):
         cols = slice(f * stacked.shape[1], (f + 1) * stacked.shape[1])
         mixed = jnp.dot(weights[f], stacked, preferred_element_type=F32)
-        mixed = mixed + shares[:, :1] * (keep[:, cols] + got[:, cols].astype(F32))
+        mixed = mixed + shares[span, :1] * (keep[span, cols] + got[span, cols].astype(F32))
         for b, ref in enumerate(blocks):
             ref[:, cols] = mixed[b * rows : (b + 1) * rows].astype(ref.dtype)
 
@@ -271,15 +269,17 @@
     cap = min(rows, -(-rows * top // stations) + 1)
     slots_first = -(-cap // 8) * 8
     slots = -(-(blocks - 1) * cap // 8) * 8
-    count = blocks * cap
-    folds = next(f for f in (1, 2, 4, 8) if f * count % 8 == 0)
-    packed = (folds * count, width // folds)
+    near = blocks // 2
+    far = blocks - near
+    folds = next(f for f in (1, 2, 4, 8) if f * far * cap % 8 == 0)
+    packed = (folds * far * cap, width // folds)
     table = -(-stations // LANES) * LANES
     held = blocks * rows
+    early = held + peers * slots_first
     station = (lax.axis_index("expert") // 2).astype(jnp.int32).reshape(1)
     hbm = functools.partial(pltpu.with_memory_space_constraint, memory_space=pltpu.HBM)
     w_in, w_out = hbm(w_in), hbm(w_out)
-    cuts = (width // 4, width * 3 // 8, width * 3 // 8)
+    cuts = (width // 8, width * 3 // 8, width // 2)
 
     inputs = (
         tokens,
@@ -297,7 +297,7 @@
         + [pltpu.SemaphoreType.DMA((5,)), pltpu.SemaphoreType.DMA((4,))],
     )(station, *[hbm(x) for x in inputs], w_in)
     (inward1,) = load((w_in, cuts[0], cuts[1], 6))
-    inward2, outward = load((w_in, cuts[0] + cuts[1], cuts[2], 6), (w_out, 0, half, 6))
+    inward2, outward = load((w_in, cuts[0] + cuts[1], cuts[2], 8), (w_out, 0, half, 6))
     inward = [inward0, inward1, inward2]
 
     column = [payload] + [swap(payload, k << up) for k in range(1, blocks)]
@@ -316,49 +316,59 @@
     other = swap(own, 1)
     swapped = [swap(block, 1) for block in arrived]
     parts = len(inward)
-    peer_call = call(
+    tall = packed[0]
+    expert_call = call(
         functools.partial(
-            peer_kernel,
+            expert_kernel,
             peers=peers,
             parts=parts,
             held=held,
-            counts=((blocks - 1) * cap, cap),
+            cap=cap,
+            near=near,
+            far=far,
             folds=folds,
-            steps=2,
+            steps=1,
         ),
         [VMEM] * (2 * peers + 3 + parts),
-        [(packed, F32)] * peers + [(packed, BF16)] * peers,
-        [pltpu.VMEM((2 * peers * (slots + slots_first), width), BF16)],
-        limit=16,
-    )
-    results = peer_call(*arrived, *swapped, own, other, *inward, outward)
-    back = []
+        [(packed, F32)] * peers
+        + [(packed, BF16)] * peers
+        + [((peers * tall, packed[1]), kind) for kind in (F32, BF16)]
+        + [((held, width), kind) for kind in (F32, BF16)],
+        [pltpu.VMEM((2 * (peers * slots + early), width), BF16)],
+        limit=20,
+    )
+    results = expert_call(*arrived, *swapped, own, other, *inward, outward)
+    keep_near, give_near, keep, give = results[2 * peers :]
+    back_far = []
     for j in range(peers):
         halves = swap(results[peers + j], 1)
         done = (results[j] + halves.astype(F32)).astype(BF16)
-        back.append(swap(done, (j + 1) << 1))
-    own_call = call(
-        functools.partial(own_kernel, parts=parts, steps=4),
-        [VMEM] * (3 + parts),
-        [((held, width), F32), ((held, width), BF16)],
-        [pltpu.VMEM((2 * held, width), BF16)],
-        limit=12,
-    )
-    keep, give = own_call(own, other, *inward, outward)
+        back_far.append(swap(done, (j + 1) << 1))
+    got_near = swap(give_near, 1)
+    back_near = []
+    for j in range(peers):
+        span = slice(j * tall, (j + 1) * tall)
+        done = (keep_near[span] + got_near[span].astype(F32)).astype(BF16)
+        back_near.append(swap(done, (j + 1) << 1))
     got = swap(give, 1)
     weigh = call(
         functools.partial(weigh_kernel, peers=peers, cap=cap, rows_each=rows),
         [SMEM, VMEM],
-        [((held, LANES), F32), ((folds, held, peers * packed[0]), BF16)],
-    )
-    shares, weights = weigh(station, tables)
-
-    combine = call(
-        functools.partial(combine_kernel, peers=peers),
-        [VMEM] * (4 + peers),
-        [((rows, width), F32)] + [((rows, width), BF16)] * (blocks - 1),
-    )
-    summed = combine(shares, weights, keep, got, *back)
+        [((held, LANES), F32)] + [((folds, far * rows, peers * tall), BF16)] * 2,
+    )
+    shares, weights_near, weights_far = weigh(station, tables)
+
+    def combine(start, weights, back, kinds):
+        kernel = call(
+            functools.partial(combine_kernel, peers=peers, start=start),
+            [VMEM] * (4 + peers),
+            [((rows, width), kind) for kind in kinds],
+        )
+        return kernel(shares, weights, keep, got, *back)
+
+    summed_far = combine(near * rows, weights_far, back_far, [BF16] * far)
+    summed_near = combine(0, weights_near, back_near, [F32] + [BF16] * (near - 1))
+    summed = list(summed_near) + list(summed_far)
     returned = [swap(summed[k], k << up) for k in range(1, blocks)]
     (mixed,) = call(total_kernel, [VMEM] * blocks, [((rows, width), BF16)])(summed[0], *returned)
     return mixed

time: 57.9 us -> 54.4 us (0.940)
  waiting for transfers between devices: 22.3 us -> 15.3 us
  starting transfers between devices: 22.5 us -> 26.8 us
  Pallas kernels: 12.6 us -> 11.8 us
    ppermute x23 -> x27, waiting for transfers between devices: 22.3 us -> 15.3 us  [swap(): return lax.ppermute(block, 'expert', [(i, i ^ mask) for i in range(count)])]
    ppermute x23 -> x27, starting transfers between devices: 22.5 us -> 26.8 us  [swap(): return lax.ppermute(block, 'expert', [(i, i ^ mask) for i in range(count)])]
    pallas_call x4, Pallas kernels: 5.22 us -> 4.28 us  [the longest x1 3.36 us: layer(): results = expert_call(*arrived, *swapped, own, other, *inward, outward)]
  transfers between devices with their start and end apart: 23 -> 27, of which waited for: 9 -> 11; matrix products, arithmetic and copies ran while one was open for 0% -> 0% of each run, Pallas kernels for 13% -> 11%
where the time goes in v5:
time: 54.4 us; the launch traced here: 54.2 us
  starting transfers between devices  26.8 us (49%)
  waiting for transfers between devices  15.3 us (28%)
  Pallas kernels  11.8 us (22%)
    ppermute x27, starting transfers between devices, swap(): return lax.ppermute(block, 'expert', [(i, i ^ mask) for i in range(count)])  26.8 us
    ppermute x27, waiting for transfers between devices, swap(): return lax.ppermute(block, 'expert', [(i, i ^ mask) for i in range(count)])  15.3 us
    pallas_call x2, Pallas kernels, load(): return kernel(*[weights for weights, _, _, _ in wanted])  4.54 us
    pallas_call x1, Pallas kernels, layer(): results = expert_call(*arrived, *swapped, own, other, *inward, outward)  3.36 us
    pallas_call x1, Pallas kernels, layer(): call(functools.partial(prepare_kernel, peers=peers, cap=cap, slots=slots_...  1.86 us
  transfers between devices with their start and end apart: 27, of which 11 were waited for; matrix products, arithmetic and copies ran while one was open for 0% of the time, Pallas kernels for 11%

profile of v5, /device:TPU:0, one launch (start us, length us, event | category | flops | bytes accessed | tf_op | source)
XLA Modules:
  0.0 54.2 jit_solution(11087191723662869352)
XLA Ops:
  0.0 1.9 %shard_map.73 = (bf16[8,4224]{1,0:T(8,128)(2,1)S(1)}, bf16[512,768]{1,0:T(8,128)(2,1)S(1)}, bf16[8,4096]{1,0:T(8,128)(2,1)S(1)}, bf16[8,4096]{1,0:T(8,128)(2,1)S(1)}, bf16[8,4096]{1,0:T(8,128)(2,1)S(1)}) custom-call(s32[1]{0:T(128)} %bitcast.station, bf16[8,4096]{1,0:T(8,128)(2,1)} %refs_0_.3, f32[1,4096]{1,0:T(1,128)} %bitcast.3, s32[8,8]{1,0:T(8,128)} %refs_2_.1, ...), custom_call_target="tpu_custom_call" | custom-call | tf_op jit(solution)/shard_map/pallas_call | solution.py:291
  1.9 3.1 %collective-permute-start = (bf16[8,4224]{1,0:T(8,128)(2,1)S(1)}, bf16[8,4224]{1,0:T(8,128)(2,1)S(1)}, u32[]{:S(2)}, u32[]{:S(2)}) collective-permute-start(bf16[8,4224]{1,0:T(8,128)(2,1)S(1)} %get-tuple-element.34.refs_0_), channel_id=1, source_target_pairs={{0,8},{1,9},{2,10},{3,11},{4,12},{5,13},{6,14},{7,15},{8,0},{9,1},... | collective-permute-start | bytes 202760 | tf_op jit(solution)/shard_map/ppermute | solution.py:21
  5.0 2.6 %collective-permute-start.1 = (bf16[8,4224]{1,0:T(8,128)(2,1)S(1)}, bf16[8,4224]{1,0:T(8,128)(2,1)S(1)}, u32[]{:S(2)}, u32[]{:S(2)}) collective-permute-start(bf16[8,4224]{1,0:T(8,128)(2,1)S(1)} %get-tuple-element.34.refs_0_), channel_id=1, source_target_pairs={{0,16},{1,17},{2,18},{3,19},{4,20},{5,21},{6,22},{7,23},{8,24},{9,... | collective-permute-start | bytes 202760 | tf_op jit(solution)/shard_map/ppermute | solution.py:21
  7.6 0.0 collective-permute-start.2
  7.6 1.7 %collective-permute-start.9 = (bf16[8,4096]{1,0:T(8,128)(2,1)S(1)}, bf16[8,4096]{1,0:T(8,128)(2,1)S(1)}, u32[]{:S(2)}, u32[]{:S(2)}) collective-permute-start(bf16[8,4096]{1,0:T(8,128)(2,1)S(1)} %get-tuple-element.42), channel_id=1, source_target_pairs={{0,2},{1,3},{2,0},{3,1},{4,6},{5,7},{6,4},{7,5},{8,10},{9,11},{10,... | collective-permute-start | bytes 196616 | tf_op jit(solution)/shard_map/ppermute | solution.py:21
  9.3 1.5 %collective-permute-start.10 = (bf16[8,4096]{1,0:T(8,128)(2,1)S(1)}, bf16[8,4096]{1,0:T(8,128)(2,1)S(1)}, u32[]{:S(2)}, u32[]{:S(2)}) collective-permute-start(bf16[8,4096]{1,0:T(8,128)(2,1)S(1)} %get-tuple-element.43), channel_id=1, source_target_pairs={{0,4},{1,5},{2,6},{3,7},{4,0},{5,1},{6,2},{7,3},{8,12},{9,13},{10,... | collective-permute-start | bytes 196616 | tf_op jit(solution)/shard_map/ppermute | solution.py:21
  10.8 0.0 collective-permute-done.refs_1_
  10.8 0.3 collective-permute-start.11
  11.1 1.3 %collective-permute-done.1.refs_2_ = bf16[8,4224]{1,0:T(8,128)(2,1)S(1)} collective-permute-done((bf16[8,4224]{1,0:T(8,128)(2,1)S(1)}, bf16[8,4224]{1,0:T(8,128)(2,1)S(1)}, u32[]{:S(2)}, u32[]{:S(2)}) %collective-permute-start.1) | collective-permute-done | bytes 67616 | tf_op jit(solution)/shard_map/ppermute | solution.py:21
  12.4 1.4 %collective-permute-done.2.refs_3_ = bf16[8,4224]{1,0:T(8,128)(2,1)S(1)} collective-permute-done((bf16[8,4224]{1,0:T(8,128)(2,1)S(1)}, bf16[8,4224]{1,0:T(8,128)(2,1)S(1)}, u32[]{:S(2)}, u32[]{:S(2)}) %collective-permute-start.2) | collective-permute-done | bytes 67616 | tf_op jit(solution)/shard_map/ppermute | solution.py:21
  13.8 0.5 shard_map.74
  14.3 0.0 collective-permute-done.9
  14.3 0.0 collective-permute-done.10
  14.3 1.6 %collective-permute-done.11 = bf16[8,4096]{1,0:T(8,128)(2,1)S(1)} collective-permute-done((bf16[8,4096]{1,0:T(8,128)(2,1)S(1)}, bf16[8,4096]{1,0:T(8,128)(2,1)S(1)}, u32[]{:S(2)}, u32[]{:S(2)}) %collective-permute-start.11) | collective-permute-done | bytes 65568 | tf_op jit(solution)/shard_map/ppermute | solution.py:21
  16.0 0.0 collective-permute-start.12
  16.0 0.6 %collective-permute-start.3 = (bf16[16,4096]{1,0:T(8,128)(2,1)S(1)}, bf16[16,4096]{1,0:T(8,128)(2,1)S(1)}, u32[]{:S(2)}, u32[]{:S(2)}) collective-permute-start(bf16[16,4096]{1,0:T(8,128)(2,1)S(1)} %get-tuple-element.38), channel_id=1, source_target_pairs={{0,2},{1,3},{2,0},{3,1},{4,6},{5,7},{6,4},{7,5},{8,10},{9,11},{10,... | collective-permute-start | bytes 393224 | tf_op jit(solution)/shard_map/ppermute | solution.py:21
  16.6 0.9 %collective-permute-start.4 = (bf16[16,4096]{1,0:T(8,128)(2,1)S(1)}, bf16[16,4096]{1,0:T(8,128)(2,1)S(1)}, u32[]{:S(2)}, u32[]{:S(2)}) collective-permute-start(bf16[16,4096]{1,0:T(8,128)(2,1)S(1)} %get-tuple-element.39), channel_id=1, source_target_pairs={{0,4},{1,5},{2,6},{3,7},{4,0},{5,1},{6,2},{7,3},{8,12},{9,13},{10,... | collective-permute-start | bytes 393224 | tf_op jit(solution)/shard_map/ppermute | solution.py:21
  17.5 2.0 %collective-permute-start.5 = (bf16[16,4096]{1,0:T(8,128)(2,1)S(1)}, bf16[16,4096]{1,0:T(8,128)(2,1)S(1)}, u32[]{:S(2)}, u32[]{:S(2)}) collective-permute-start(bf16[16,4096]{1,0:T(8,128)(2,1)S(1)} %get-tuple-element.40), channel_id=1, source_target_pairs={{0,6},{1,7},{2,4},{3,5},{4,2},{5,3},{6,0},{7,1},{8,14},{9,15},{10,... | collective-permute-start | bytes 393224 | tf_op jit(solution)/shard_map/ppermute | solution.py:21
  19.6 2.9 %collective-permute-done.3.refs_0_ = bf16[16,4096]{1,0:T(8,128)(2,1)S(1)} collective-permute-done((bf16[16,4096]{1,0:T(8,128)(2,1)S(1)}, bf16[16,4096]{1,0:T(8,128)(2,1)S(1)}, u32[]{:S(2)}, u32[]{:S(2)}) %collective-permute-start.3) | collective-permute-done | bytes 131104 | tf_op jit(solution)/shard_map/ppermute | solution.py:21
  22.4 0.0 collective-permute-start.6
  22.4 2.5 %collective-permute-done.4.refs_1_ = bf16[16,4096]{1,0:T(8,128)(2,1)S(1)} collective-permute-done((bf16[16,4096]{1,0:T(8,128)(2,1)S(1)}, bf16[16,4096]{1,0:T(8,128)(2,1)S(1)}, u32[]{:S(2)}, u32[]{:S(2)}) %collective-permute-start.4) | collective-permute-done | bytes 131104 | tf_op jit(solution)/shard_map/ppermute | solution.py:21
  25.0 0.0 collective-permute-start.7
  25.0 0.0 collective-permute-done.5.refs_2_
  25.0 0.5 collective-permute-start.8
  25.5 1.6 %shard_map.76.refs_9_ = bf16[1536,768]{1,0:T(8,128)(2,1)S(1)} custom-call(bf16[1,4096,768]{2,1,0:T(8,128)(2,1)} %refs_0_.5), custom_call_target="tpu_custom_call" | custom-call | tf_op jit(solution)/shard_map/pallas_call | solution.py:258
  27.1 2.9 %shard_map.77 = (bf16[2048,768]{1,0:T(8,128)(2,1)S(1)}, bf16[384,4096]{1,0:T(8,128)(2,1)S(1)}) custom-call(bf16[1,4096,768]{2,1,0:T(8,128)(2,1)} %refs_0_.5, bf16[1,384,4096]{2,1,0:T(8,128)(2,1)} %refs_1_.1), custom_call_target="tpu_custom_call" | custom-call | tf_op jit(solution)/shard_map/pallas_call | solution.py:258
  30.0 0.0 collective-permute-done.6.refs_3_
  30.0 0.0 collective-permute-done.7.refs_4_
  30.1 0.0 collective-permute-done.8.refs_5_
  30.1 0.0 collective-permute-done.12.refs_7_
  30.1 3.4 %shard_map.78 = (f32[40,1024]{1,0:T(8,128)S(1)}, f32[40,1024]{1,0:T(8,128)S(1)}, f32[40,1024]{1,0:T(8,128)S(1)}, bf16[40,1024]{1,0:T(8,128)(2,1)S(1)}, bf16[40,1...) custom-call(bf16[16,4096]{1,0:T(8,128)(2,1)S(1)} %collective-permute, ...), custom_call_target="tpu_custom_call" | custom-call | tf_op jit(solution)/shard_map/pallas_call | solution.py:340
  33.4 0.1 collective-permute-start.23
  33.5 0.5 collective-permute-start.21
  34.0 0.1 collective-permute-start.19
  34.1 0.4 collective-permute-start.13
  34.5 0.1 collective-permute-start.14
  34.6 0.2 collective-permute-done.23
  34.8 1.5 %collective-permute-start.24 = (bf16[40,1024]{1,0:T(8,128)(2,1)S(1)}, bf16[40,1024]{1,0:T(8,128)(2,1)S(1)}, u32[]{:S(2)}, u32[]{:S(2)}) collective-permute-start(bf16[40,1024]{1,0:T(8,128)(2,1)S(1)} %add_convert_fusion), channel_id=1, source_target_pairs={{0,6},{1,7},{2,4},{3,5},{4,2},{5,3},{6,0},{7,1},{8,14},{9,15},{10,... | collective-permute-start | bytes 245768 | tf_op jit(solution)/shard_map/ppermute | solution.py:21
  36.3 0.0 collective-permute-done.21
  36.3 1.6 %collective-permute-start.22 = (bf16[40,1024]{1,0:T(8,128)(2,1)S(1)}, bf16[40,1024]{1,0:T(8,128)(2,1)S(1)}, u32[]{:S(2)}, u32[]{:S(2)}) collective-permute-start(bf16[40,1024]{1,0:T(8,128)(2,1)S(1)} %add_convert_fusion.1), channel_id=1, source_target_pairs={{0,4},{1,5},{2,6},{3,7},{4,0},{5,1},{6,2},{7,3},{8,12},{9,13},{10,... | collective-permute-start | bytes 245768 | tf_op jit(solution)/shard_map/ppermute | solution.py:21
  37.9 0.0 collective-permute-done.19
  37.9 0.6 %collective-permute-start.20 = (bf16[40,1024]{1,0:T(8,128)(2,1)S(1)}, bf16[40,1024]{1,0:T(8,128)(2,1)S(1)}, u32[]{:S(2)}, u32[]{:S(2)}) collective-permute-start(bf16[40,1024]{1,0:T(8,128)(2,1)S(1)} %add_convert_fusion.2), channel_id=1, source_target_pairs={{0,2},{1,3},{2,0},{3,1},{4,6},{5,7},{6,4},{7,5},{8,10},{9,11},{10,... | collective-permute-start | bytes 245768 | tf_op jit(solution)/shard_map/ppermute | solution.py:21
  38.5 0.0 collective-permute-done.14
  38.6 1.6 %collective-permute-start.15 = (bf16[40,1024]{1,0:T(8,128)(2,1)S(1)}, bf16[40,1024]{1,0:T(8,128)(2,1)S(1)}, u32[]{:S(2)}, u32[]{:S(2)}) collective-permute-start(bf16[40,1024]{1,0:T(8,128)(2,1)S(1)} %get-tuple-element.65), channel_id=1, source_target_pairs={{0,2},{1,3},{2,0},{3,1},{4,6},{5,7},{6,4},{7,5},{8,10},{9,11},{10,... | collective-permute-start | bytes 245768 | tf_op jit(solution)/shard_map/ppermute | solution.py:21
  40.2 0.4 collective-permute-done.24.refs_2_
  40.5 0.9 %collective-permute-start.16 = (bf16[40,1024]{1,0:T(8,128)(2,1)S(1)}, bf16[40,1024]{1,0:T(8,128)(2,1)S(1)}, u32[]{:S(2)}, u32[]{:S(2)}) collective-permute-start(bf16[40,1024]{1,0:T(8,128)(2,1)S(1)} %get-tuple-element.64), channel_id=1, source_target_pairs={{0,4},{1,5},{2,6},{3,7},{4,0},{5,1},{6,2},{7,3},{8,12},{9,13},{10,... | collective-permute-start | bytes 245768 | tf_op jit(solution)/shard_map/ppermute | solution.py:21
  41.4 0.7 %collective-permute-done.22.refs_1_ = bf16[40,1024]{1,0:T(8,128)(2,1)S(1)} collective-permute-done((bf16[40,1024]{1,0:T(8,128)(2,1)S(1)}, bf16[40,1024]{1,0:T(8,128)(2,1)S(1)}, u32[]{:S(2)}, u32[]{:S(2)}) %collective-permute-start.22) | collective-permute-done | bytes 81952 | tf_op jit(solution)/shard_map/ppermute | solution.py:21
  42.1 1.9 %collective-permute-start.17 = (bf16[40,1024]{1,0:T(8,128)(2,1)S(1)}, bf16[40,1024]{1,0:T(8,128)(2,1)S(1)}, u32[]{:S(2)}, u32[]{:S(2)}) collective-permute-start(bf16[40,1024]{1,0:T(8,128)(2,1)S(1)} %get-tuple-element.63), channel_id=1, source_target_pairs={{0,6},{1,7},{2,4},{3,5},{4,2},{5,3},{6,0},{7,1},{8,14},{9,15},{10,... | collective-permute-start | bytes 245768 | tf_op jit(solution)/shard_map/ppermute | solution.py:21
  44.1 0.4 shard_map.75
  44.5 0.0 collective-permute-done.20.refs_0_
  44.5 0.0 collective-permute-done.13.got
  44.5 0.3 shard_map.80
  44.8 1.7 %collective-permute-start.25 = (bf16[8,4096]{1,0:T(8,128)(2,1)S(1)}, bf16[8,4096]{1,0:T(8,128)(2,1)S(1)}, u32[]{:S(2)}, u32[]{:S(2)}) collective-permute-start(bf16[8,4096]{1,0:T(8,128)(2,1)S(1)} %get-tuple-element.61), channel_id=1, source_target_pairs={{0,16},{1,17},{2,18},{3,19},{4,20},{5,21},{6,22},{7,23},{8,24},{9,... | collective-permute-start | bytes 196616 | tf_op jit(solution)/shard_map/ppermute | solution.py:21
  46.5 2.0 %collective-permute-start.26 = (bf16[8,4096]{1,0:T(8,128)(2,1)S(1)}, bf16[8,4096]{1,0:T(8,128)(2,1)S(1)}, u32[]{:S(2)}, u32[]{:S(2)}) collective-permute-start(bf16[8,4096]{1,0:T(8,128)(2,1)S(1)} %get-tuple-element.62), channel_id=1, source_target_pairs={{0,24},{1,25},{2,26},{3,27},{4,28},{5,29},{6,30},{7,31},{8,16},{9,... | collective-permute-start | bytes 196616 | tf_op jit(solution)/shard_map/ppermute | solution.py:21
  48.5 0.0 collective-permute-done.15.refs_0_
  48.5 0.0 collective-permute-done.16.refs_1_
  48.5 0.0 collective-permute-done.17.refs_2_
  48.5 0.3 shard_map.79
  48.8 0.5 %collective-permute-start.18 = (bf16[8,4096]{1,0:T(8,128)(2,1)S(1)}, bf16[8,4096]{1,0:T(8,128)(2,1)S(1)}, u32[]{:S(2)}, u32[]{:S(2)}) collective-permute-start(bf16[8,4096]{1,0:T(8,128)(2,1)S(1)} %get-tuple-element.53), channel_id=1, source_target_pairs={{0,8},{1,9},{2,10},{3,11},{4,12},{5,13},{6,14},{7,15},{8,0},{9,1},... | collective-permute-start | bytes 196616 | tf_op jit(solution)/shard_map/ppermute | solution.py:21
  49.3 2.1 %collective-permute-done.25.refs_1_ = bf16[8,4096]{1,0:T(8,128)(2,1)S(1)} collective-permute-done((bf16[8,4096]{1,0:T(8,128)(2,1)S(1)}, bf16[8,4096]{1,0:T(8,128)(2,1)S(1)}, u32[]{:S(2)}, u32[]{:S(2)}) %collective-permute-start.25) | collective-permute-done | bytes 65568 | tf_op jit(solution)/shard_map/ppermute | solution.py:21
  51.4 1.6 %collective-permute-done.26.refs_2_ = bf16[8,4096]{1,0:T(8,128)(2,1)S(1)} collective-permute-done((bf16[8,4096]{1,0:T(8,128)(2,1)S(1)}, bf16[8,4096]{1,0:T(8,128)(2,1)S(1)}, u32[]{:S(2)}, u32[]{:S(2)}) %collective-permute-start.26) | collective-permute-done | bytes 65568 | tf_op jit(solution)/shard_map/ppermute | solution.py:21
  53.0 0.6 %collective-permute-done.18.refs_0_ = bf16[8,4096]{1,0:T(8,128)(2,1)S(1)} collective-permute-done((bf16[8,4096]{1,0:T(8,128)(2,1)S(1)}, bf16[8,4096]{1,0:T(8,128)(2,1)S(1)}, u32[]{:S(2)}, u32[]{:S(2)}) %collective-permute-start.18) | collective-permute-done | bytes 65568 | tf_op jit(solution)/shard_map/ppermute | solution.py:21
  53.5 0.7 %shard_map.81 = bf16[8,4096]{1,0:T(8,128)(2,1)} custom-call(f32[8,4096]{1,0:T(8,128)S(1)} %get-tuple-element.52.local, bf16[8,4096]{1,0:T(8,128)(2,1)S(1)} %collective-permute-done.18.refs_0_, bf16[8,4096]{1,0:T(8,128)(2,1)S(1)} %collective-permute-done.25.refs_1_, bf16[8,4096]{1,0:T(8,128)(2,1)S(1)} %collective-permute-done.26.refs_2_), custom_call_target="tpu_custom_call" | custom-call | tf_op jit(solution)/shard_map/pallas_call | solution.py:373
  (8 shorter events, 0.1 us)
Async XLA Ops:
  1.9 8.9 %collective-permute-start = (bf16[8,4224]{1,0:T(8,128)(2,1)S(1)}, bf16[8,4224]{1,0:T(8,128)(2,1)S(1)}, u32[]{:S(2)}, u32[]{:S(2)}) collective-permute-start(bf16[8,4224]{1,0:T(8,128)(2,1)S(1)} %get-tuple-element.34.refs_0_), channel_id=1, source_target_pairs={{0,8},{1,9},{2,10},{3,11},{4,12},{5,13},{6,14},{7,15},{8,0},{9,1},... | collective-permute-start | bytes 202760 | tf_op jit(solution)/shard_map/ppermute | solution.py:21
  5.0 7.4 %collective-permute-start.1 = (bf16[8,4224]{1,0:T(8,128)(2,1)S(1)}, bf16[8,4224]{1,0:T(8,128)(2,1)S(1)}, u32[]{:S(2)}, u32[]{:S(2)}) collective-permute-start(bf16[8,4224]{1,0:T(8,128)(2,1)S(1)} %get-tuple-element.34.refs_0_), channel_id=1, source_target_pairs={{0,16},{1,17},{2,18},{3,19},{4,20},{5,21},{6,22},{7,23},{8,24},{9,... | collective-permute-start | bytes 202760 | tf_op jit(solution)/shard_map/ppermute | solution.py:21
  7.6 6.2 %collective-permute-start.2 = (bf16[8,4224]{1,0:T(8,128)(2,1)S(1)}, bf16[8,4224]{1,0:T(8,128)(2,1)S(1)}, u32[]{:S(2)}, u32[]{:S(2)}) collective-permute-start(bf16[8,4224]{1,0:T(8,128)(2,1)S(1)} %get-tuple-element.34.refs_0_), channel_id=1, source_target_pairs={{0,24},{1,25},{2,26},{3,27},{4,28},{5,29},{6,30},{7,31},{8,16},{9,... | collective-permute-start | bytes 202760 | tf_op jit(solution)/shard_map/ppermute | solution.py:21
  7.6 6.7 %collective-permute-start.9 = (bf16[8,4096]{1,0:T(8,128)(2,1)S(1)}, bf16[8,4096]{1,0:T(8,128)(2,1)S(1)}, u32[]{:S(2)}, u32[]{:S(2)}) collective-permute-start(bf16[8,4096]{1,0:T(8,128)(2,1)S(1)} %get-tuple-element.42), channel_id=1, source_target_pairs={{0,2},{1,3},{2,0},{3,1},{4,6},{5,7},{6,4},{7,5},{8,10},{9,11},{10,... | collective-permute-start | bytes 196616 | tf_op jit(solution)/shard_map/ppermute | solution.py:21
  9.3 5.0 %collective-permute-start.10 = (bf16[8,4096]{1,0:T(8,128)(2,1)S(1)}, bf16[8,4096]{1,0:T(8,128)(2,1)S(1)}, u32[]{:S(2)}, u32[]{:S(2)}) collective-permute-start(bf16[8,4096]{1,0:T(8,128)(2,1)S(1)} %get-tuple-element.43), channel_id=1, source_target_pairs={{0,4},{1,5},{2,6},{3,7},{4,0},{5,1},{6,2},{7,3},{8,12},{9,13},{10,... | collective-permute-start | bytes 196616 | tf_op jit(solution)/shard_map/ppermute | solution.py:21
  10.8 5.2 %collective-permute-start.11 = (bf16[8,4096]{1,0:T(8,128)(2,1)S(1)}, bf16[8,4096]{1,0:T(8,128)(2,1)S(1)}, u32[]{:S(2)}, u32[]{:S(2)}) collective-permute-start(bf16[8,4096]{1,0:T(8,128)(2,1)S(1)} %get-tuple-element.44), channel_id=1, source_target_pairs={{0,6},{1,7},{2,4},{3,5},{4,2},{5,3},{6,0},{7,1},{8,14},{9,15},{10,... | collective-permute-start | bytes 196616 | tf_op jit(solution)/shard_map/ppermute | solution.py:21
  16.0 14.1 %collective-permute-start.12 = (bf16[56,4096]{1,0:T(8,128)(2,1)S(1)}, bf16[56,4096]{1,0:T(8,128)(2,1)S(1)}, u32[]{:S(2)}, u32[]{:S(2)}) collective-permute-start(bf16[56,4096]{1,0:T(8,128)(2,1)S(1)} %constant_dynamic-update-slice_fusion.refs_6_), channel_id=1, source_target_pairs={{0,1},{1,0},{2,3},{3,2},{4,5},{5,4},{6,7},{7,6},{8,9},{9,8},{10,11... | collective-permute-start | bytes 1376264 | tf_op jit(solution)/shard_map/ppermute | solution.py:21
  16.0 6.4 %collective-permute-start.3 = (bf16[16,4096]{1,0:T(8,128)(2,1)S(1)}, bf16[16,4096]{1,0:T(8,128)(2,1)S(1)}, u32[]{:S(2)}, u32[]{:S(2)}) collective-permute-start(bf16[16,4096]{1,0:T(8,128)(2,1)S(1)} %get-tuple-element.38), channel_id=1, source_target_pairs={{0,2},{1,3},{2,0},{3,1},{4,6},{5,7},{6,4},{7,5},{8,10},{9,11},{10,... | collective-permute-start | bytes 393224 | tf_op jit(solution)/shard_map/ppermute | solution.py:21
  16.6 8.4 %collective-permute-start.4 = (bf16[16,4096]{1,0:T(8,128)(2,1)S(1)}, bf16[16,4096]{1,0:T(8,128)(2,1)S(1)}, u32[]{:S(2)}, u32[]{:S(2)}) collective-permute-start(bf16[16,4096]{1,0:T(8,128)(2,1)S(1)} %get-tuple-element.39), channel_id=1, source_target_pairs={{0,4},{1,5},{2,6},{3,7},{4,0},{5,1},{6,2},{7,3},{8,12},{9,13},{10,... | collective-permute-start | bytes 393224 | tf_op jit(solution)/shard_map/ppermute | solution.py:21
  17.5 7.4 %collective-permute-start.5 = (bf16[16,4096]{1,0:T(8,128)(2,1)S(1)}, bf16[16,4096]{1,0:T(8,128)(2,1)S(1)}, u32[]{:S(2)}, u32[]{:S(2)}) collective-permute-start(bf16[16,4096]{1,0:T(8,128)(2,1)S(1)} %get-tuple-element.40), channel_id=1, source_target_pairs={{0,6},{1,7},{2,4},{3,5},{4,2},{5,3},{6,0},{7,1},{8,14},{9,15},{10,... | collective-permute-start | bytes 393224 | tf_op jit(solution)/shard_map/ppermute | solution.py:21
  22.4 7.6 %collective-permute-start.6 = (bf16[16,4096]{1,0:T(8,128)(2,1)S(1)}, bf16[16,4096]{1,0:T(8,128)(2,1)S(1)}, u32[]{:S(2)}, u32[]{:S(2)}) collective-permute-start(bf16[16,4096]{1,0:T(8,128)(2,1)S(1)} %collective-permute-done.3.refs_0_), channel_id=1, source_target_pairs={{0,1},{1,0},{2,3},{3,2},{4,5},{5,4},{6,7},{7,6},{8,9},{9,8},{10,11... | collective-permute-start | bytes 393224 | tf_op jit(solution)/shard_map/ppermute | solution.py:21
  25.0 5.1 %collective-permute-start.7 = (bf16[16,4096]{1,0:T(8,128)(2,1)S(1)}, bf16[16,4096]{1,0:T(8,128)(2,1)S(1)}, u32[]{:S(2)}, u32[]{:S(2)}) collective-permute-start(bf16[16,4096]{1,0:T(8,128)(2,1)S(1)} %collective-permute-done.4.refs_1_), channel_id=1, source_target_pairs={{0,1},{1,0},{2,3},{3,2},{4,5},{5,4},{6,7},{7,6},{8,9},{9,8},{10,11... | collective-permute-start | bytes 393224 | tf_op jit(solution)/shard_map/ppermute | solution.py:21
  25.0 5.1 %collective-permute-start.8 = (bf16[16,4096]{1,0:T(8,128)(2,1)S(1)}, bf16[16,4096]{1,0:T(8,128)(2,1)S(1)}, u32[]{:S(2)}, u32[]{:S(2)}) collective-permute-start(bf16[16,4096]{1,0:T(8,128)(2,1)S(1)} %collective-permute-done.5.refs_2_), channel_id=1, source_target_pairs={{0,1},{1,0},{2,3},{3,2},{4,5},{5,4},{6,7},{7,6},{8,9},{9,8},{10,11... | collective-permute-start | bytes 393224 | tf_op jit(solution)/shard_map/ppermute | solution.py:21
  33.4 1.3 %collective-permute-start.23 = (bf16[40,1024]{1,0:T(8,128)(2,1)S(1)}, bf16[40,1024]{1,0:T(8,128)(2,1)S(1)}, u32[]{:S(2)}, u32[]{:S(2)}) collective-permute-start(bf16[40,1024]{1,0:T(8,128)(2,1)S(1)} %get-tuple-element.60), channel_id=1, source_target_pairs={{0,1},{1,0},{2,3},{3,2},{4,5},{5,4},{6,7},{7,6},{8,9},{9,8},{10,11... | collective-permute-start | bytes 245768 | tf_op jit(solution)/shard_map/ppermute | solution.py:21
  33.5 2.8 %collective-permute-start.21 = (bf16[40,1024]{1,0:T(8,128)(2,1)S(1)}, bf16[40,1024]{1,0:T(8,128)(2,1)S(1)}, u32[]{:S(2)}, u32[]{:S(2)}) collective-permute-start(bf16[40,1024]{1,0:T(8,128)(2,1)S(1)} %get-tuple-element.58), channel_id=1, source_target_pairs={{0,1},{1,0},{2,3},{3,2},{4,5},{5,4},{6,7},{7,6},{8,9},{9,8},{10,11... | collective-permute-start | bytes 245768 | tf_op jit(solution)/shard_map/ppermute | solution.py:21
  34.0 3.9 %collective-permute-start.19 = (bf16[40,1024]{1,0:T(8,128)(2,1)S(1)}, bf16[40,1024]{1,0:T(8,128)(2,1)S(1)}, u32[]{:S(2)}, u32[]{:S(2)}) collective-permute-start(bf16[40,1024]{1,0:T(8,128)(2,1)S(1)} %get-tuple-element.56), channel_id=1, source_target_pairs={{0,1},{1,0},{2,3},{3,2},{4,5},{5,4},{6,7},{7,6},{8,9},{9,8},{10,11... | collective-permute-start | bytes 245768 | tf_op jit(solution)/shard_map/ppermute | solution.py:21
  34.1 10.4 %collective-permute-start.13 = (bf16[32,4096]{1,0:T(8,128)(2,1)S(1)}, bf16[32,4096]{1,0:T(8,128)(2,1)S(1)}, u32[]{:S(2)}, u32[]{:S(2)}) collective-permute-start(bf16[32,4096]{1,0:T(8,128)(2,1)S(1)} %get-tuple-element.49), channel_id=1, source_target_pairs={{0,1},{1,0},{2,3},{3,2},{4,5},{5,4},{6,7},{7,6},{8,9},{9,8},{10,11... | collective-permute-start | bytes 786440 | tf_op jit(solution)/shard_map/ppermute | solution.py:21
  34.5 4.0 %collective-permute-start.14 = (bf16[120,1024]{1,0:T(8,128)(2,1)S(1)}, bf16[120,1024]{1,0:T(8,128)(2,1)S(1)}, u32[]{:S(2)}, u32[]{:S(2)}) collective-permute-start(bf16[120,1024]{1,0:T(8,128)(2,1)S(1)} %get-tuple-element.51), channel_id=1, source_target_pairs={{0,1},{1,0},{2,3},{3,2},{4,5},{5,4},{6,7},{7,6},{8,9},{9,8},{10,11... | collective-permute-start | bytes 737288 | tf_op jit(solution)/shard_map/ppermute | solution.py:21
  34.8 5.7 %collective-permute-start.24 = (bf16[40,1024]{1,0:T(8,128)(2,1)S(1)}, bf16[40,1024]{1,0:T(8,128)(2,1)S(1)}, u32[]{:S(2)}, u32[]{:S(2)}) collective-permute-start(bf16[40,1024]{1,0:T(8,128)(2,1)S(1)} %add_convert_fusion), channel_id=1, source_target_pairs={{0,6},{1,7},{2,4},{3,5},{4,2},{5,3},{6,0},{7,1},{8,14},{9,15},{10,... | collective-permute-start | bytes 245768 | tf_op jit(solution)/shard_map/ppermute | solution.py:21
  36.3 5.8 %collective-permute-start.22 = (bf16[40,1024]{1,0:T(8,128)(2,1)S(1)}, bf16[40,1024]{1,0:T(8,128)(2,1)S(1)}, u32[]{:S(2)}, u32[]{:S(2)}) collective-permute-start(bf16[40,1024]{1,0:T(8,128)(2,1)S(1)} %add_convert_fusion.1), channel_id=1, source_target_pairs={{0,4},{1,5},{2,6},{3,7},{4,0},{5,1},{6,2},{7,3},{8,12},{9,13},{10,... | collective-permute-start | bytes 245768 | tf_op jit(solution)/shard_map/ppermute | solution.py:21
  37.9 6.5 %collective-permute-start.20 = (bf16[40,1024]{1,0:T(8,128)(2,1)S(1)}, bf16[40,1024]{1,0:T(8,128)(2,1)S(1)}, u32[]{:S(2)}, u32[]{:S(2)}) collective-permute-start(bf16[40,1024]{1,0:T(8,128)(2,1)S(1)} %add_convert_fusion.2), channel_id=1, source_target_pairs={{0,2},{1,3},{2,0},{3,1},{4,6},{5,7},{6,4},{7,5},{8,10},{9,11},{10,... | collective-permute-start | bytes 245768 | tf_op jit(solution)/shard_map/ppermute | solution.py:21
  38.6 9.9 %collective-permute-start.15 = (bf16[40,1024]{1,0:T(8,128)(2,1)S(1)}, bf16[40,1024]{1,0:T(8,128)(2,1)S(1)}, u32[]{:S(2)}, u32[]{:S(2)}) collective-permute-start(bf16[40,1024]{1,0:T(8,128)(2,1)S(1)} %get-tuple-element.65), channel_id=1, source_target_pairs={{0,2},{1,3},{2,0},{3,1},{4,6},{5,7},{6,4},{7,5},{8,10},{9,11},{10,... | collective-permute-start | bytes 245768 | tf_op jit(solution)/shard_map/ppermute | solution.py:21
  40.5 8.0 %collective-permute-start.16 = (bf16[40,1024]{1,0:T(8,128)(2,1)S(1)}, bf16[40,1024]{1,0:T(8,128)(2,1)S(1)}, u32[]{:S(2)}, u32[]{:S(2)}) collective-permute-start(bf16[40,1024]{1,0:T(8,128)(2,1)S(1)} %get-tuple-element.64), channel_id=1, source_target_pairs={{0,4},{1,5},{2,6},{3,7},{4,0},{5,1},{6,2},{7,3},{8,12},{9,13},{10,... | collective-permute-start | bytes 245768 | tf_op jit(solution)/shard_map/ppermute | solution.py:21
  42.1 6.4 %collective-permute-start.17 = (bf16[40,1024]{1,0:T(8,128)(2,1)S(1)}, bf16[40,1024]{1,0:T(8,128)(2,1)S(1)}, u32[]{:S(2)}, u32[]{:S(2)}) collective-permute-start(bf16[40,1024]{1,0:T(8,128)(2,1)S(1)} %get-tuple-element.63), channel_id=1, source_target_pairs={{0,6},{1,7},{2,4},{3,5},{4,2},{5,3},{6,0},{7,1},{8,14},{9,15},{10,... | collective-permute-start | bytes 245768 | tf_op jit(solution)/shard_map/ppermute | solution.py:21
  44.8 6.6 %collective-permute-start.25 = (bf16[8,4096]{1,0:T(8,128)(2,1)S(1)}, bf16[8,4096]{1,0:T(8,128)(2,1)S(1)}, u32[]{:S(2)}, u32[]{:S(2)}) collective-permute-start(bf16[8,4096]{1,0:T(8,128)(2,1)S(1)} %get-tuple-element.61), channel_id=1, source_target_pairs={{0,16},{1,17},{2,18},{3,19},{4,20},{5,21},{6,22},{7,23},{8,24},{9,... | collective-permute-start | bytes 196616 | tf_op jit(solution)/shard_map/ppermute | solution.py:21
  46.5 6.5 %collective-permute-start.26 = (bf16[8,4096]{1,0:T(8,128)(2,1)S(1)}, bf16[8,4096]{1,0:T(8,128)(2,1)S(1)}, u32[]{:S(2)}, u32[]{:S(2)}) collective-permute-start(bf16[8,4096]{1,0:T(8,128)(2,1)S(1)} %get-tuple-element.62), channel_id=1, source_target_pairs={{0,24},{1,25},{2,26},{3,27},{4,28},{5,29},{6,30},{7,31},{8,16},{9,... | collective-permute-start | bytes 196616 | tf_op jit(solution)/shard_map/ppermute | solution.py:21
  48.8 4.8 %collective-permute-start.18 = (bf16[8,4096]{1,0:T(8,128)(2,1)S(1)}, bf16[8,4096]{1,0:T(8,128)(2,1)S(1)}, u32[]{:S(2)}, u32[]{:S(2)}) collective-permute-start(bf16[8,4096]{1,0:T(8,128)(2,1)S(1)} %get-tuple-element.53), channel_id=1, source_target_pairs={{0,8},{1,9},{2,10},{3,11},{4,12},{5,13},{6,14},{7,15},{8,0},{9,1},... | collective-permute-start | bytes 196616 | tf_op jit(solution)/shard_map/ppermute | solution.py:21

commit v6 on v5

--- a/solution.py
+++ b/solution.py
@@ -108,7 +108,7 @@
         ref[...] = placed[j * slots : (j + 1) * slots].astype(BF16)
 
 
-def weigh_kernel(station, tables, shares, *outs, peers, cap, rows_each):
+def weigh(station, tables, shares, *outs, peers, cap, rows_each):
     table = tables[...]
     lane = lax.broadcasted_iota(jnp.int32, table.shape, 1)
     share = jnp.sum(jnp.where(lane == station[0], table, 0.0), axis=1, keepdims=True)
@@ -152,6 +152,18 @@
         copies += pieces_of(refs[n], refs[count + n], refs[2 * count + n], start)
     for copy in copies:
         copy.start()
+    for copy in copies:
+        copy.wait()
+
+
+def load_and_weigh_kernel(station, tables, *refs, starts, **sizes):
+    count = len(starts)
+    copies = []
+    for n, start in enumerate(starts):
+        copies += pieces_of(refs[n], refs[count + n], refs[2 * count + 3 + n], start)
+    for copy in copies:
+        copy.start()
+    weigh(station, tables, *refs[2 * count : 2 * count + 3], **sizes)
     for copy in copies:
         copy.wait()
 
@@ -248,16 +260,6 @@
     )
 
 
-def load(*wanted):
-    kernel = call(
-        functools.partial(load_kernel, starts=[start for _, start, _, _ in wanted]),
-        [HBM] * len(wanted),
-        [((size, weights.shape[2]), weights.dtype) for weights, _, size, _ in wanted],
-        [pltpu.SemaphoreType.DMA((steps,)) for _, _, _, steps in wanted],
-    )
-    return kernel(*[weights for weights, _, _, _ in wanted])
-
-
 def layer(tokens, norm_gain, expert_ids, route_score, expert_pair, w_in, w_out):
     devices = lax.axis_size("expert")
     blocks, plane, up = shape_of(devices)
@@ -296,9 +298,13 @@
         [pltpu.VMEM(x.shape, x.dtype) for x in inputs]
         + [pltpu.SemaphoreType.DMA((5,)), pltpu.SemaphoreType.DMA((4,))],
     )(station, *[hbm(x) for x in inputs], w_in)
-    (inward1,) = load((w_in, cuts[0], cuts[1], 6))
-    inward2, outward = load((w_in, cuts[0] + cuts[1], cuts[2], 8), (w_out, 0, half, 6))
-    inward = [inward0, inward1, inward2]
+    middle = call(
+        functools.partial(load_kernel, starts=[cuts[0]]),
+        [HBM],
+        [((cuts[1], 2 * half), BF16)],
+        [pltpu.SemaphoreType.DMA((6,))],
+    )
+    (inward1,) = middle(w_in)
 
     column = [payload] + [swap(payload, k << up) for k in range(1, blocks)]
     first = [swap(first[j], (j + 1) << 1) for j in range(peers)]
@@ -311,12 +317,27 @@
         + [((slots, width), BF16)] * peers,
     )(station, *column)
 
+    tall = packed[0]
+    last = call(
+        functools.partial(
+            load_and_weigh_kernel,
+            starts=[cuts[0] + cuts[1], 0],
+            peers=peers,
+            cap=cap,
+            rows_each=rows,
+        ),
+        [SMEM, VMEM, HBM, HBM],
+        [((cuts[2], 2 * half), BF16), ((half, width), BF16), ((held, LANES), F32)]
+        + [((folds, far * rows, peers * tall), BF16)] * 2,
+        [pltpu.SemaphoreType.DMA((8,)), pltpu.SemaphoreType.DMA((6,))],
+    )
+    inward2, outward, shares, weights_near, weights_far = last(station, tables, w_in, w_out)
+    inward = [inward0, inward1, inward2]
     arrived = [swap(chosen[j], (j + 1) << 1) for j in range(peers)]
     own = jnp.concatenate([own] + first, axis=0)
     other = swap(own, 1)
     swapped = [swap(block, 1) for block in arrived]
     parts = len(inward)
-    tall = packed[0]
     expert_call = call(
         functools.partial(
             expert_kernel,
@@ -351,13 +372,6 @@
         done = (keep_near[span] + got_near[span].astype(F32)).astype(BF16)
         back_near.append(swap(done, (j + 1) << 1))
     got = swap(give, 1)
-    weigh = call(
-        functools.partial(weigh_kernel, peers=peers, cap=cap, rows_each=rows),
-        [SMEM, VMEM],
-        [((held, LANES), F32)] + [((folds, far * rows, peers * tall), BF16)] * 2,
-    )
-    shares, weights_near, weights_far = weigh(station, tables)
-
     def combine(start, weights, back, kinds):
         kernel = call(
             functools.partial(combine_kernel, peers=peers, start=start),

time: 54.4 us -> 54.8 us (level)
  waiting for transfers between devices: 15.3 us -> 15.9 us
    ppermute x27, waiting for transfers between devices: 15.3 us -> 15.9 us  [swap(): return lax.ppermute(block, 'expert', [(i, i ^ mask) for i in range(count)])]
    pallas_call x3 -> x2, Pallas kernels: 4.94 us -> 4.68 us  [the longest x1 3.05 us: layer(): last(station, tables, w_in, w_out)]
  transfers between devices with their start and end apart: 27 -> 27, of which waited for: 11 -> 10; matrix products, arithmetic and copies ran while one was open for 0% -> 0% of each run, Pallas kernels for 11% -> 10%
where the time goes in v6:
time: 54.8 us; the launch traced here: 54.6 us
  starting transfers between devices  26.8 us (49%)
  waiting for transfers between devices  15.9 us (29%)
  Pallas kernels  11.6 us (21%)
    ppermute x27, starting transfers between devices, swap(): return lax.ppermute(block, 'expert', [(i, i ^ mask) for i in range(count)])  26.8 us
    ppermute x27, waiting for transfers between devices, swap(): return lax.ppermute(block, 'expert', [(i, i ^ mask) for i in range(count)])  15.9 us
    pallas_call x1, Pallas kernels, layer(): results = expert_call(*arrived, *swapped, own, other, *inward, outward)  3.37 us
    pallas_call x1, Pallas kernels, layer(): last(station, tables, w_in, w_out)  3.05 us
    pallas_call x1, Pallas kernels, layer(): call(functools.partial(prepare_kernel, peers=peers, cap=cap, slots=slots_...  1.86 us
    pallas_call x1, Pallas kernels, layer(): inward1, = middle(w_in)  1.64 us
  transfers between devices with their start and end apart: 27, of which 10 were waited for; matrix products, arithmetic and copies ran while one was open for 0% of the time, Pallas kernels for 10%

profile of v6, /device:TPU:0, one launch (start us, length us, event | category | flops | bytes accessed | tf_op | source)
XLA Modules:
  0.0 54.6 jit_solution(15157017923441700293)
XLA Ops:
  0.0 1.9 %shard_map.73 = (bf16[8,4224]{1,0:T(8,128)(2,1)S(1)}, bf16[512,768]{1,0:T(8,128)(2,1)S(1)}, bf16[8,4096]{1,0:T(8,128)(2,1)S(1)}, bf16[8,4096]{1,0:T(8,128)(2,1)S(1)}, bf16[8,4096]{1,0:T(8,128)(2,1)S(1)}) custom-call(s32[1]{0:T(128)} %bitcast.station, bf16[8,4096]{1,0:T(8,128)(2,1)} %refs_0_.3, f32[1,4096]{1,0:T(1,128)} %bitcast.3, s32[8,8]{1,0:T(8,128)} %refs_2_.1, ...), custom_call_target="tpu_custom_call" | custom-call | tf_op jit(solution)/shard_map/pallas_call | solution.py:293
  1.9 5.1 %collective-permute-start.2 = (bf16[8,4224]{1,0:T(8,128)(2,1)S(1)}, bf16[8,4224]{1,0:T(8,128)(2,1)S(1)}, u32[]{:S(2)}, u32[]{:S(2)}) collective-permute-start(bf16[8,4224]{1,0:T(8,128)(2,1)S(1)} %get-tuple-element.34.refs_0_), channel_id=1, source_target_pairs={{0,24},{1,25},{2,26},{3,27},{4,28},{5,29},{6,30},{7,31},{8,16},{9,... | collective-permute-start | bytes 202760 | tf_op jit(solution)/shard_map/ppermute | solution.py:21
  7.0 0.0 collective-permute-start.1
  7.0 0.6 %collective-permute-start = (bf16[8,4224]{1,0:T(8,128)(2,1)S(1)}, bf16[8,4224]{1,0:T(8,128)(2,1)S(1)}, u32[]{:S(2)}, u32[]{:S(2)}) collective-permute-start(bf16[8,4224]{1,0:T(8,128)(2,1)S(1)} %get-tuple-element.34.refs_0_), channel_id=1, source_target_pairs={{0,8},{1,9},{2,10},{3,11},{4,12},{5,13},{6,14},{7,15},{8,0},{9,1},... | collective-permute-start | bytes 202760 | tf_op jit(solution)/shard_map/ppermute | solution.py:21
  7.7 1.6 %collective-permute-start.9 = (bf16[8,4096]{1,0:T(8,128)(2,1)S(1)}, bf16[8,4096]{1,0:T(8,128)(2,1)S(1)}, u32[]{:S(2)}, u32[]{:S(2)}) collective-permute-start(bf16[8,4096]{1,0:T(8,128)(2,1)S(1)} %get-tuple-element.42), channel_id=1, source_target_pairs={{0,2},{1,3},{2,0},{3,1},{4,6},{5,7},{6,4},{7,5},{8,10},{9,11},{10,... | collective-permute-start | bytes 196616 | tf_op jit(solution)/shard_map/ppermute | solution.py:21
  9.3 1.5 %collective-permute-start.10 = (bf16[8,4096]{1,0:T(8,128)(2,1)S(1)}, bf16[8,4096]{1,0:T(8,128)(2,1)S(1)}, u32[]{:S(2)}, u32[]{:S(2)}) collective-permute-start(bf16[8,4096]{1,0:T(8,128)(2,1)S(1)} %get-tuple-element.43), channel_id=1, source_target_pairs={{0,4},{1,5},{2,6},{3,7},{4,0},{5,1},{6,2},{7,3},{8,12},{9,13},{10,... | collective-permute-start | bytes 196616 | tf_op jit(solution)/shard_map/ppermute | solution.py:21
  10.8 0.0 collective-permute-done.2.refs_3_
  10.8 1.6 %collective-permute-start.11 = (bf16[8,4096]{1,0:T(8,128)(2,1)S(1)}, bf16[8,4096]{1,0:T(8,128)(2,1)S(1)}, u32[]{:S(2)}, u32[]{:S(2)}) collective-permute-start(bf16[8,4096]{1,0:T(8,128)(2,1)S(1)} %get-tuple-element.44), channel_id=1, source_target_pairs={{0,6},{1,7},{2,4},{3,5},{4,2},{5,3},{6,0},{7,1},{8,14},{9,15},{10,... | collective-permute-start | bytes 196616 | tf_op jit(solution)/shard_map/ppermute | solution.py:21
  12.4 0.4 collective-permute-done.1.refs_2_
  12.8 0.0 collective-permute-done.refs_1_
  12.8 0.5 shard_map.74
  13.3 0.0 collective-permute-done.9
  13.3 0.9 %collective-permute-done.10 = bf16[8,4096]{1,0:T(8,128)(2,1)S(1)} collective-permute-done((bf16[8,4096]{1,0:T(8,128)(2,1)S(1)}, bf16[8,4096]{1,0:T(8,128)(2,1)S(1)}, u32[]{:S(2)}, u32[]{:S(2)}) %collective-permute-start.10) | collective-permute-done | bytes 65568 | tf_op jit(solution)/shard_map/ppermute | solution.py:21
  14.3 1.7 %collective-permute-done.11 = bf16[8,4096]{1,0:T(8,128)(2,1)S(1)} collective-permute-done((bf16[8,4096]{1,0:T(8,128)(2,1)S(1)}, bf16[8,4096]{1,0:T(8,128)(2,1)S(1)}, u32[]{:S(2)}, u32[]{:S(2)}) %collective-permute-start.11) | collective-permute-done | bytes 65568 | tf_op jit(solution)/shard_map/ppermute | solution.py:21
  16.0 0.0 collective-permute-start.12
  16.0 0.7 %collective-permute-start.3 = (bf16[16,4096]{1,0:T(8,128)(2,1)S(1)}, bf16[16,4096]{1,0:T(8,128)(2,1)S(1)}, u32[]{:S(2)}, u32[]{:S(2)}) collective-permute-start(bf16[16,4096]{1,0:T(8,128)(2,1)S(1)} %get-tuple-element.38), channel_id=1, source_target_pairs={{0,2},{1,3},{2,0},{3,1},{4,6},{5,7},{6,4},{7,5},{8,10},{9,11},{10,... | collective-permute-start | bytes 393224 | tf_op jit(solution)/shard_map/ppermute | solution.py:21
  16.7 1.5 %collective-permute-start.4 = (bf16[16,4096]{1,0:T(8,128)(2,1)S(1)}, bf16[16,4096]{1,0:T(8,128)(2,1)S(1)}, u32[]{:S(2)}, u32[]{:S(2)}) collective-permute-start(bf16[16,4096]{1,0:T(8,128)(2,1)S(1)} %get-tuple-element.39), channel_id=1, source_target_pairs={{0,4},{1,5},{2,6},{3,7},{4,0},{5,1},{6,2},{7,3},{8,12},{9,13},{10,... | collective-permute-start | bytes 393224 | tf_op jit(solution)/shard_map/ppermute | solution.py:21
  18.2 1.3 %collective-permute-start.5 = (bf16[16,4096]{1,0:T(8,128)(2,1)S(1)}, bf16[16,4096]{1,0:T(8,128)(2,1)S(1)}, u32[]{:S(2)}, u32[]{:S(2)}) collective-permute-start(bf16[16,4096]{1,0:T(8,128)(2,1)S(1)} %get-tuple-element.40), channel_id=1, source_target_pairs={{0,6},{1,7},{2,4},{3,5},{4,2},{5,3},{6,0},{7,1},{8,14},{9,15},{10,... | collective-permute-start | bytes 393224 | tf_op jit(solution)/shard_map/ppermute | solution.py:21
  19.6 2.9 %collective-permute-done.3.refs_0_ = bf16[16,4096]{1,0:T(8,128)(2,1)S(1)} collective-permute-done((bf16[16,4096]{1,0:T(8,128)(2,1)S(1)}, bf16[16,4096]{1,0:T(8,128)(2,1)S(1)}, u32[]{:S(2)}, u32[]{:S(2)}) %collective-permute-start.3) | collective-permute-done | bytes 131104 | tf_op jit(solution)/shard_map/ppermute | solution.py:21
  22.4 0.0 collective-permute-start.6
  22.4 2.6 %collective-permute-done.4.refs_1_ = bf16[16,4096]{1,0:T(8,128)(2,1)S(1)} collective-permute-done((bf16[16,4096]{1,0:T(8,128)(2,1)S(1)}, bf16[16,4096]{1,0:T(8,128)(2,1)S(1)}, u32[]{:S(2)}, u32[]{:S(2)}) %collective-permute-start.4) | collective-permute-done | bytes 131104 | tf_op jit(solution)/shard_map/ppermute | solution.py:21
  25.1 0.0 collective-permute-start.7
  25.1 0.0 collective-permute-done.5.refs_2_
  25.1 0.5 collective-permute-start.8
  25.6 1.6 %shard_map.76.refs_9_ = bf16[1536,768]{1,0:T(8,128)(2,1)S(1)} custom-call(bf16[1,4096,768]{2,1,0:T(8,128)(2,1)} %refs_0_.5), custom_call_target="tpu_custom_call" | custom-call | tf_op jit(solution)/shard_map/pallas_call | solution.py:307
  27.2 3.0 %shard_map.75 = (bf16[2048,768]{1,0:T(8,128)(2,1)S(1)}, bf16[384,4096]{1,0:T(8,128)(2,1)S(1)}, f32[32,128]{1,0:T(8,128)S(1)}, bf16[4,16,120]{2,1,0:T(8,128)(2,1)S(1)}, bf16[4,16,120]{2,1,0:T(8,128)(2,1)S(1)}) custom-call(s32[1]{0:T(128)} %bitcast.station, f32[32,128]{1,0:T(8,128)S(1)} %get-tuple-element.35.tables, bf16[1,4096,768]{2,1,0:T(8,128)(2,1)} %refs_0_.5, ...), custom_call_target="tpu_custom_call" | custom-call | tf_op jit(solution)/shard_map/pallas_call | solution.py:334
  30.3 0.0 collective-permute-done.6.refs_3_
  30.3 0.0 collective-permute-done.7.refs_4_
  30.3 0.0 collective-permute-done.8.refs_5_
  30.3 0.0 collective-permute-done.12.refs_7_
  30.3 3.4 %shard_map.77 = (f32[40,1024]{1,0:T(8,128)S(1)}, f32[40,1024]{1,0:T(8,128)S(1)}, f32[40,1024]{1,0:T(8,128)S(1)}, bf16[40,1024]{1,0:T(8,128)(2,1)S(1)}, bf16[40,1...) custom-call(bf16[16,4096]{1,0:T(8,128)(2,1)S(1)} %collective-permute, ...), custom_call_target="tpu_custom_call" | custom-call | tf_op jit(solution)/shard_map/pallas_call | solution.py:361
  33.7 0.1 collective-permute-start.19
  33.8 0.5 collective-permute-start.21
  34.3 0.1 collective-permute-start.23
  34.3 0.4 collective-permute-start.14
  34.8 0.1 collective-permute-start.13
  34.9 0.2 collective-permute-done.19
  35.1 1.5 %collective-permute-start.20 = (bf16[40,1024]{1,0:T(8,128)(2,1)S(1)}, bf16[40,1024]{1,0:T(8,128)(2,1)S(1)}, u32[]{:S(2)}, u32[]{:S(2)}) collective-permute-start(bf16[40,1024]{1,0:T(8,128)(2,1)S(1)} %add_convert_fusion.2), channel_id=1, source_target_pairs={{0,2},{1,3},{2,0},{3,1},{4,6},{5,7},{6,4},{7,5},{8,10},{9,11},{10,... | collective-permute-start | bytes 245768 | tf_op jit(solution)/shard_map/ppermute | solution.py:21
  36.5 0.0 collective-permute-done.21
  36.5 0.7 %collective-permute-start.22 = (bf16[40,1024]{1,0:T(8,128)(2,1)S(1)}, bf16[40,1024]{1,0:T(8,128)(2,1)S(1)}, u32[]{:S(2)}, u32[]{:S(2)}) collective-permute-start(bf16[40,1024]{1,0:T(8,128)(2,1)S(1)} %add_convert_fusion.1), channel_id=1, source_target_pairs={{0,4},{1,5},{2,6},{3,7},{4,0},{5,1},{6,2},{7,3},{8,12},{9,13},{10,... | collective-permute-start | bytes 245768 | tf_op jit(solution)/shard_map/ppermute | solution.py:21
  37.3 0.0 collective-permute-done.23
  37.3 1.5 %collective-permute-start.24 = (bf16[40,1024]{1,0:T(8,128)(2,1)S(1)}, bf16[40,1024]{1,0:T(8,128)(2,1)S(1)}, u32[]{:S(2)}, u32[]{:S(2)}) collective-permute-start(bf16[40,1024]{1,0:T(8,128)(2,1)S(1)} %add_convert_fusion), channel_id=1, source_target_pairs={{0,6},{1,7},{2,4},{3,5},{4,2},{5,3},{6,0},{7,1},{8,14},{9,15},{10,... | collective-permute-start | bytes 245768 | tf_op jit(solution)/shard_map/ppermute | solution.py:21
  38.8 0.0 collective-permute-done.14
  38.9 1.6 %collective-permute-start.17 = (bf16[40,1024]{1,0:T(8,128)(2,1)S(1)}, bf16[40,1024]{1,0:T(8,128)(2,1)S(1)}, u32[]{:S(2)}, u32[]{:S(2)}) collective-permute-start(bf16[40,1024]{1,0:T(8,128)(2,1)S(1)} %get-tuple-element.63), channel_id=1, source_target_pairs={{0,6},{1,7},{2,4},{3,5},{4,2},{5,3},{6,0},{7,1},{8,14},{9,15},{10,... | collective-permute-start | bytes 245768 | tf_op jit(solution)/shard_map/ppermute | solution.py:21
  40.4 0.0 collective-permute-done.20.refs_0_
  40.4 1.4 %collective-permute-start.16 = (bf16[40,1024]{1,0:T(8,128)(2,1)S(1)}, bf16[40,1024]{1,0:T(8,128)(2,1)S(1)}, u32[]{:S(2)}, u32[]{:S(2)}) collective-permute-start(bf16[40,1024]{1,0:T(8,128)(2,1)S(1)} %get-tuple-element.64), channel_id=1, source_target_pairs={{0,4},{1,5},{2,6},{3,7},{4,0},{5,1},{6,2},{7,3},{8,12},{9,13},{10,... | collective-permute-start | bytes 245768 | tf_op jit(solution)/shard_map/ppermute | solution.py:21
  41.8 2.2 %collective-permute-done.22.refs_1_ = bf16[40,1024]{1,0:T(8,128)(2,1)S(1)} collective-permute-done((bf16[40,1024]{1,0:T(8,128)(2,1)S(1)}, bf16[40,1024]{1,0:T(8,128)(2,1)S(1)}, u32[]{:S(2)}, u32[]{:S(2)}) %collective-permute-start.22) | collective-permute-done | bytes 81952 | tf_op jit(solution)/shard_map/ppermute | solution.py:21
  44.0 0.0 collective-permute-start.15
  44.0 0.0 collective-permute-done.24.refs_2_
  44.0 0.0 collective-permute-done.13.got
  44.0 0.3 shard_map.79
  44.3 3.2 %collective-permute-start.25 = (bf16[8,4096]{1,0:T(8,128)(2,1)S(1)}, bf16[8,4096]{1,0:T(8,128)(2,1)S(1)}, u32[]{:S(2)}, u32[]{:S(2)}) collective-permute-start(bf16[8,4096]{1,0:T(8,128)(2,1)S(1)} %get-tuple-element.61), channel_id=1, source_target_pairs={{0,16},{1,17},{2,18},{3,19},{4,20},{5,21},{6,22},{7,23},{8,24},{9,... | collective-permute-start | bytes 196616 | tf_op jit(solution)/shard_map/ppermute | solution.py:21
  47.4 1.2 %collective-permute-start.26 = (bf16[8,4096]{1,0:T(8,128)(2,1)S(1)}, bf16[8,4096]{1,0:T(8,128)(2,1)S(1)}, u32[]{:S(2)}, u32[]{:S(2)}) collective-permute-start(bf16[8,4096]{1,0:T(8,128)(2,1)S(1)} %get-tuple-element.62), channel_id=1, source_target_pairs={{0,24},{1,25},{2,26},{3,27},{4,28},{5,29},{6,30},{7,31},{8,16},{9,... | collective-permute-start | bytes 196616 | tf_op jit(solution)/shard_map/ppermute | solution.py:21
  48.7 0.0 collective-permute-done.17.refs_2_
  48.7 0.0 collective-permute-done.16.refs_1_
  48.7 0.0 collective-permute-done.15.refs_0_
  48.7 0.3 shard_map.78
  48.9 0.1 collective-permute-start.18
  49.0 2.1 %collective-permute-done.25.refs_1_ = bf16[8,4096]{1,0:T(8,128)(2,1)S(1)} collective-permute-done((bf16[8,4096]{1,0:T(8,128)(2,1)S(1)}, bf16[8,4096]{1,0:T(8,128)(2,1)S(1)}, u32[]{:S(2)}, u32[]{:S(2)}) %collective-permute-start.25) | collective-permute-done | bytes 65568 | tf_op jit(solution)/shard_map/ppermute | solution.py:21
  51.1 2.5 %collective-permute-done.26.refs_2_ = bf16[8,4096]{1,0:T(8,128)(2,1)S(1)} collective-permute-done((bf16[8,4096]{1,0:T(8,128)(2,1)S(1)}, bf16[8,4096]{1,0:T(8,128)(2,1)S(1)}, u32[]{:S(2)}, u32[]{:S(2)}) %collective-permute-start.26) | collective-permute-done | bytes 65568 | tf_op jit(solution)/shard_map/ppermute | solution.py:21
  53.6 0.3 collective-permute-done.18.refs_0_
  53.9 0.7 %shard_map.80 = bf16[8,4096]{1,0:T(8,128)(2,1)} custom-call(f32[8,4096]{1,0:T(8,128)S(1)} %get-tuple-element.52.local, bf16[8,4096]{1,0:T(8,128)(2,1)S(1)} %collective-permute-done.18.refs_0_, bf16[8,4096]{1,0:T(8,128)(2,1)S(1)} %collective-permute-done.25.refs_1_, bf16[8,4096]{1,0:T(8,128)(2,1)S(1)} %collective-permute-done.26.refs_2_), custom_call_target="tpu_custom_call" | custom-call | tf_op jit(solution)/shard_map/pallas_call | solution.py:387
  (8 shorter events, 0.1 us)
Async XLA Ops:
  1.9 9.0 %collective-permute-start.2 = (bf16[8,4224]{1,0:T(8,128)(2,1)S(1)}, bf16[8,4224]{1,0:T(8,128)(2,1)S(1)}, u32[]{:S(2)}, u32[]{:S(2)}) collective-permute-start(bf16[8,4224]{1,0:T(8,128)(2,1)S(1)} %get-tuple-element.34.refs_0_), channel_id=1, source_target_pairs={{0,24},{1,25},{2,26},{3,27},{4,28},{5,29},{6,30},{7,31},{8,16},{9,... | collective-permute-start | bytes 202760 | tf_op jit(solution)/shard_map/ppermute | solution.py:21
  7.0 5.8 %collective-permute-start.1 = (bf16[8,4224]{1,0:T(8,128)(2,1)S(1)}, bf16[8,4224]{1,0:T(8,128)(2,1)S(1)}, u32[]{:S(2)}, u32[]{:S(2)}) collective-permute-start(bf16[8,4224]{1,0:T(8,128)(2,1)S(1)} %get-tuple-element.34.refs_0_), channel_id=1, source_target_pairs={{0,16},{1,17},{2,18},{3,19},{4,20},{5,21},{6,22},{7,23},{8,24},{9,... | collective-permute-start | bytes 202760 | tf_op jit(solution)/shard_map/ppermute | solution.py:21
  7.0 5.8 %collective-permute-start = (bf16[8,4224]{1,0:T(8,128)(2,1)S(1)}, bf16[8,4224]{1,0:T(8,128)(2,1)S(1)}, u32[]{:S(2)}, u32[]{:S(2)}) collective-permute-start(bf16[8,4224]{1,0:T(8,128)(2,1)S(1)} %get-tuple-element.34.refs_0_), channel_id=1, source_target_pairs={{0,8},{1,9},{2,10},{3,11},{4,12},{5,13},{6,14},{7,15},{8,0},{9,1},... | collective-permute-start | bytes 202760 | tf_op jit(solution)/shard_map/ppermute | solution.py:21
  7.7 5.7 %collective-permute-start.9 = (bf16[8,4096]{1,0:T(8,128)(2,1)S(1)}, bf16[8,4096]{1,0:T(8,128)(2,1)S(1)}, u32[]{:S(2)}, u32[]{:S(2)}) collective-permute-start(bf16[8,4096]{1,0:T(8,128)(2,1)S(1)} %get-tuple-element.42), channel_id=1, source_target_pairs={{0,2},{1,3},{2,0},{3,1},{4,6},{5,7},{6,4},{7,5},{8,10},{9,11},{10,... | collective-permute-start | bytes 196616 | tf_op jit(solution)/shard_map/ppermute | solution.py:21
  9.3 5.0 %collective-permute-start.10 = (bf16[8,4096]{1,0:T(8,128)(2,1)S(1)}, bf16[8,4096]{1,0:T(8,128)(2,1)S(1)}, u32[]{:S(2)}, u32[]{:S(2)}) collective-permute-start(bf16[8,4096]{1,0:T(8,128)(2,1)S(1)} %get-tuple-element.43), channel_id=1, source_target_pairs={{0,4},{1,5},{2,6},{3,7},{4,0},{5,1},{6,2},{7,3},{8,12},{9,13},{10,... | collective-permute-start | bytes 196616 | tf_op jit(solution)/shard_map/ppermute | solution.py:21
  10.8 5.2 %collective-permute-start.11 = (bf16[8,4096]{1,0:T(8,128)(2,1)S(1)}, bf16[8,4096]{1,0:T(8,128)(2,1)S(1)}, u32[]{:S(2)}, u32[]{:S(2)}) collective-permute-start(bf16[8,4096]{1,0:T(8,128)(2,1)S(1)} %get-tuple-element.44), channel_id=1, source_target_pairs={{0,6},{1,7},{2,4},{3,5},{4,2},{5,3},{6,0},{7,1},{8,14},{9,15},{10,... | collective-permute-start | bytes 196616 | tf_op jit(solution)/shard_map/ppermute | solution.py:21
  16.0 14.3 %collective-permute-start.12 = (bf16[56,4096]{1,0:T(8,128)(2,1)S(1)}, bf16[56,4096]{1,0:T(8,128)(2,1)S(1)}, u32[]{:S(2)}, u32[]{:S(2)}) collective-permute-start(bf16[56,4096]{1,0:T(8,128)(2,1)S(1)} %constant_dynamic-update-slice_fusion.refs_6_), channel_id=1, source_target_pairs={{0,1},{1,0},{2,3},{3,2},{4,5},{5,4},{6,7},{7,6},{8,9},{9,8},{10,11... | collective-permute-start | bytes 1376264 | tf_op jit(solution)/shard_map/ppermute | solution.py:21
  16.0 6.4 %collective-permute-start.3 = (bf16[16,4096]{1,0:T(8,128)(2,1)S(1)}, bf16[16,4096]{1,0:T(8,128)(2,1)S(1)}, u32[]{:S(2)}, u32[]{:S(2)}) collective-permute-start(bf16[16,4096]{1,0:T(8,128)(2,1)S(1)} %get-tuple-element.38), channel_id=1, source_target_pairs={{0,2},{1,3},{2,0},{3,1},{4,6},{5,7},{6,4},{7,5},{8,10},{9,11},{10,... | collective-permute-start | bytes 393224 | tf_op jit(solution)/shard_map/ppermute | solution.py:21
  16.7 8.4 %collective-permute-start.4 = (bf16[16,4096]{1,0:T(8,128)(2,1)S(1)}, bf16[16,4096]{1,0:T(8,128)(2,1)S(1)}, u32[]{:S(2)}, u32[]{:S(2)}) collective-permute-start(bf16[16,4096]{1,0:T(8,128)(2,1)S(1)} %get-tuple-element.39), channel_id=1, source_target_pairs={{0,4},{1,5},{2,6},{3,7},{4,0},{5,1},{6,2},{7,3},{8,12},{9,13},{10,... | collective-permute-start | bytes 393224 | tf_op jit(solution)/shard_map/ppermute | solution.py:21
  18.2 6.8 %collective-permute-start.5 = (bf16[16,4096]{1,0:T(8,128)(2,1)S(1)}, bf16[16,4096]{1,0:T(8,128)(2,1)S(1)}, u32[]{:S(2)}, u32[]{:S(2)}) collective-permute-start(bf16[16,4096]{1,0:T(8,128)(2,1)S(1)} %get-tuple-element.40), channel_id=1, source_target_pairs={{0,6},{1,7},{2,4},{3,5},{4,2},{5,3},{6,0},{7,1},{8,14},{9,15},{10,... | collective-permute-start | bytes 393224 | tf_op jit(solution)/shard_map/ppermute | solution.py:21
  22.4 7.8 %collective-permute-start.6 = (bf16[16,4096]{1,0:T(8,128)(2,1)S(1)}, bf16[16,4096]{1,0:T(8,128)(2,1)S(1)}, u32[]{:S(2)}, u32[]{:S(2)}) collective-permute-start(bf16[16,4096]{1,0:T(8,128)(2,1)S(1)} %collective-permute-done.3.refs_0_), channel_id=1, source_target_pairs={{0,1},{1,0},{2,3},{3,2},{4,5},{5,4},{6,7},{7,6},{8,9},{9,8},{10,11... | collective-permute-start | bytes 393224 | tf_op jit(solution)/shard_map/ppermute | solution.py:21
  25.1 5.2 %collective-permute-start.7 = (bf16[16,4096]{1,0:T(8,128)(2,1)S(1)}, bf16[16,4096]{1,0:T(8,128)(2,1)S(1)}, u32[]{:S(2)}, u32[]{:S(2)}) collective-permute-start(bf16[16,4096]{1,0:T(8,128)(2,1)S(1)} %collective-permute-done.4.refs_1_), channel_id=1, source_target_pairs={{0,1},{1,0},{2,3},{3,2},{4,5},{5,4},{6,7},{7,6},{8,9},{9,8},{10,11... | collective-permute-start | bytes 393224 | tf_op jit(solution)/shard_map/ppermute | solution.py:21
  25.1 5.2 %collective-permute-start.8 = (bf16[16,4096]{1,0:T(8,128)(2,1)S(1)}, bf16[16,4096]{1,0:T(8,128)(2,1)S(1)}, u32[]{:S(2)}, u32[]{:S(2)}) collective-permute-start(bf16[16,4096]{1,0:T(8,128)(2,1)S(1)} %collective-permute-done.5.refs_2_), channel_id=1, source_target_pairs={{0,1},{1,0},{2,3},{3,2},{4,5},{5,4},{6,7},{7,6},{8,9},{9,8},{10,11... | collective-permute-start | bytes 393224 | tf_op jit(solution)/shard_map/ppermute | solution.py:21
  33.7 1.3 %collective-permute-start.19 = (bf16[40,1024]{1,0:T(8,128)(2,1)S(1)}, bf16[40,1024]{1,0:T(8,128)(2,1)S(1)}, u32[]{:S(2)}, u32[]{:S(2)}) collective-permute-start(bf16[40,1024]{1,0:T(8,128)(2,1)S(1)} %get-tuple-element.56), channel_id=1, source_target_pairs={{0,1},{1,0},{2,3},{3,2},{4,5},{5,4},{6,7},{7,6},{8,9},{9,8},{10,11... | collective-permute-start | bytes 245768 | tf_op jit(solution)/shard_map/ppermute | solution.py:21
  33.8 2.8 %collective-permute-start.21 = (bf16[40,1024]{1,0:T(8,128)(2,1)S(1)}, bf16[40,1024]{1,0:T(8,128)(2,1)S(1)}, u32[]{:S(2)}, u32[]{:S(2)}) collective-permute-start(bf16[40,1024]{1,0:T(8,128)(2,1)S(1)} %get-tuple-element.58), channel_id=1, source_target_pairs={{0,1},{1,0},{2,3},{3,2},{4,5},{5,4},{6,7},{7,6},{8,9},{9,8},{10,11... | collective-permute-start | bytes 245768 | tf_op jit(solution)/shard_map/ppermute | solution.py:21
  34.3 3.0 %collective-permute-start.23 = (bf16[40,1024]{1,0:T(8,128)(2,1)S(1)}, bf16[40,1024]{1,0:T(8,128)(2,1)S(1)}, u32[]{:S(2)}, u32[]{:S(2)}) collective-permute-start(bf16[40,1024]{1,0:T(8,128)(2,1)S(1)} %get-tuple-element.60), channel_id=1, source_target_pairs={{0,1},{1,0},{2,3},{3,2},{4,5},{5,4},{6,7},{7,6},{8,9},{9,8},{10,11... | collective-permute-start | bytes 245768 | tf_op jit(solution)/shard_map/ppermute | solution.py:21
  34.3 4.4 %collective-permute-start.14 = (bf16[120,1024]{1,0:T(8,128)(2,1)S(1)}, bf16[120,1024]{1,0:T(8,128)(2,1)S(1)}, u32[]{:S(2)}, u32[]{:S(2)}) collective-permute-start(bf16[120,1024]{1,0:T(8,128)(2,1)S(1)} %get-tuple-element.51), channel_id=1, source_target_pairs={{0,1},{1,0},{2,3},{3,2},{4,5},{5,4},{6,7},{7,6},{8,9},{9,8},{10,11... | collective-permute-start | bytes 737288 | tf_op jit(solution)/shard_map/ppermute | solution.py:21
  34.8 9.2 %collective-permute-start.13 = (bf16[32,4096]{1,0:T(8,128)(2,1)S(1)}, bf16[32,4096]{1,0:T(8,128)(2,1)S(1)}, u32[]{:S(2)}, u32[]{:S(2)}) collective-permute-start(bf16[32,4096]{1,0:T(8,128)(2,1)S(1)} %get-tuple-element.49), channel_id=1, source_target_pairs={{0,1},{1,0},{2,3},{3,2},{4,5},{5,4},{6,7},{7,6},{8,9},{9,8},{10,11... | collective-permute-start | bytes 786440 | tf_op jit(solution)/shard_map/ppermute | solution.py:21
  35.1 5.4 %collective-permute-start.20 = (bf16[40,1024]{1,0:T(8,128)(2,1)S(1)}, bf16[40,1024]{1,0:T(8,128)(2,1)S(1)}, u32[]{:S(2)}, u32[]{:S(2)}) collective-permute-start(bf16[40,1024]{1,0:T(8,128)(2,1)S(1)} %add_convert_fusion.2), channel_id=1, source_target_pairs={{0,2},{1,3},{2,0},{3,1},{4,6},{5,7},{6,4},{7,5},{8,10},{9,11},{10,... | collective-permute-start | bytes 245768 | tf_op jit(solution)/shard_map/ppermute | solution.py:21
  36.5 7.5 %collective-permute-start.22 = (bf16[40,1024]{1,0:T(8,128)(2,1)S(1)}, bf16[40,1024]{1,0:T(8,128)(2,1)S(1)}, u32[]{:S(2)}, u32[]{:S(2)}) collective-permute-start(bf16[40,1024]{1,0:T(8,128)(2,1)S(1)} %add_convert_fusion.1), channel_id=1, source_target_pairs={{0,4},{1,5},{2,6},{3,7},{4,0},{5,1},{6,2},{7,3},{8,12},{9,13},{10,... | collective-permute-start | bytes 245768 | tf_op jit(solution)/shard_map/ppermute | solution.py:21
  37.3 6.7 %collective-permute-start.24 = (bf16[40,1024]{1,0:T(8,128)(2,1)S(1)}, bf16[40,1024]{1,0:T(8,128)(2,1)S(1)}, u32[]{:S(2)}, u32[]{:S(2)}) collective-permute-start(bf16[40,1024]{1,0:T(8,128)(2,1)S(1)} %add_convert_fusion), channel_id=1, source_target_pairs={{0,6},{1,7},{2,4},{3,5},{4,2},{5,3},{6,0},{7,1},{8,14},{9,15},{10,... | collective-permute-start | bytes 245768 | tf_op jit(solution)/shard_map/ppermute | solution.py:21
  38.9 9.8 %collective-permute-start.17 = (bf16[40,1024]{1,0:T(8,128)(2,1)S(1)}, bf16[40,1024]{1,0:T(8,128)(2,1)S(1)}, u32[]{:S(2)}, u32[]{:S(2)}) collective-permute-start(bf16[40,1024]{1,0:T(8,128)(2,1)S(1)} %get-tuple-element.63), channel_id=1, source_target_pairs={{0,6},{1,7},{2,4},{3,5},{4,2},{5,3},{6,0},{7,1},{8,14},{9,15},{10,... | collective-permute-start | bytes 245768 | tf_op jit(solution)/shard_map/ppermute | solution.py:21
  40.4 8.2 %collective-permute-start.16 = (bf16[40,1024]{1,0:T(8,128)(2,1)S(1)}, bf16[40,1024]{1,0:T(8,128)(2,1)S(1)}, u32[]{:S(2)}, u32[]{:S(2)}) collective-permute-start(bf16[40,1024]{1,0:T(8,128)(2,1)S(1)} %get-tuple-element.64), channel_id=1, source_target_pairs={{0,4},{1,5},{2,6},{3,7},{4,0},{5,1},{6,2},{7,3},{8,12},{9,13},{10,... | collective-permute-start | bytes 245768 | tf_op jit(solution)/shard_map/ppermute | solution.py:21
  44.0 4.7 %collective-permute-start.15 = (bf16[40,1024]{1,0:T(8,128)(2,1)S(1)}, bf16[40,1024]{1,0:T(8,128)(2,1)S(1)}, u32[]{:S(2)}, u32[]{:S(2)}) collective-permute-start(bf16[40,1024]{1,0:T(8,128)(2,1)S(1)} %get-tuple-element.65), channel_id=1, source_target_pairs={{0,2},{1,3},{2,0},{3,1},{4,6},{5,7},{6,4},{7,5},{8,10},{9,11},{10,... | collective-permute-start | bytes 245768 | tf_op jit(solution)/shard_map/ppermute | solution.py:21
  44.3 6.8 %collective-permute-start.25 = (bf16[8,4096]{1,0:T(8,128)(2,1)S(1)}, bf16[8,4096]{1,0:T(8,128)(2,1)S(1)}, u32[]{:S(2)}, u32[]{:S(2)}) collective-permute-start(bf16[8,4096]{1,0:T(8,128)(2,1)S(1)} %get-tuple-element.61), channel_id=1, source_target_pairs={{0,16},{1,17},{2,18},{3,19},{4,20},{5,21},{6,22},{7,23},{8,24},{9,... | collective-permute-start | bytes 196616 | tf_op jit(solution)/shard_map/ppermute | solution.py:21
  47.4 6.2 %collective-permute-start.26 = (bf16[8,4096]{1,0:T(8,128)(2,1)S(1)}, bf16[8,4096]{1,0:T(8,128)(2,1)S(1)}, u32[]{:S(2)}, u32[]{:S(2)}) collective-permute-start(bf16[8,4096]{1,0:T(8,128)(2,1)S(1)} %get-tuple-element.62), channel_id=1, source_target_pairs={{0,24},{1,25},{2,26},{3,27},{4,28},{5,29},{6,30},{7,31},{8,16},{9,... | collective-permute-start | bytes 196616 | tf_op jit(solution)/shard_map/ppermute | solution.py:21
  48.9 5.0 %collective-permute-start.18 = (bf16[8,4096]{1,0:T(8,128)(2,1)S(1)}, bf16[8,4096]{1,0:T(8,128)(2,1)S(1)}, u32[]{:S(2)}, u32[]{:S(2)}) collective-permute-start(bf16[8,4096]{1,0:T(8,128)(2,1)S(1)} %get-tuple-element.53), channel_id=1, source_target_pairs={{0,8},{1,9},{2,10},{3,11},{4,12},{5,13},{6,14},{7,15},{8,0},{9,1},... | collective-permute-start | bytes 196616 | tf_op jit(solution)/shard_map/ppermute | solution.py:21

commit v7 on v6

--- a/solution.py
+++ b/solution.py
@@ -25,7 +25,7 @@
     return lax.dot_general(placing, body, (((0,), (0,)), ((), ())), preferred_element_type=F32)
 
 
-def slot_weights(table, station, peers, slots, cap, rows_each):
+def slot_weights(table, station, masks, slots, cap, rows_each):
     rows = table.shape[0]
     row = lax.broadcasted_iota(jnp.int32, (rows, rows), 0)
     col = lax.broadcasted_iota(jnp.int32, (rows, rows), 1)
@@ -37,10 +37,10 @@
     )
     base = lax.broadcasted_iota(jnp.int32, (rows, 1), 0) // rows_each * cap
     lane = lax.broadcasted_iota(jnp.int32, table.shape, 1)
-    target = lax.broadcasted_iota(jnp.int32, (rows, peers * slots), 1)
-    weights = jnp.zeros((rows, peers * slots), F32)
-    for j in range(peers):
-        pick = lane == (station ^ (j + 1))
+    target = lax.broadcasted_iota(jnp.int32, (rows, len(masks) * slots), 1)
+    weights = jnp.zeros((rows, len(masks) * slots), F32)
+    for j, mask in enumerate(masks):
+        pick = lane == (station ^ mask)
         share = jnp.sum(jnp.where(pick, table, 0.0), axis=1, keepdims=True)
         ranked = jnp.sum(jnp.where(pick, rank, 0.0), axis=1, keepdims=True)
         slot = base + ranked.astype(jnp.int32) + j * slots
@@ -84,7 +84,7 @@
         named.astype(BF16), moved, (((1,), (1,)), ((), ())), preferred_element_type=F32
     )
     payload[:, width:] = table.astype(BF16)
-    shared = slot_weights(table, station[0], peers, slots, cap, rows)
+    shared = slot_weights(table, station[0], range(1, peers + 1), slots, cap, rows)
     placed = picked_rows(jnp.where(shared > 0.0, 1.0, 0.0).astype(BF16), normed)
     for j, ref in enumerate(chosen):
         ref[...] = placed[j * slots : (j + 1) * slots].astype(BF16)
@@ -100,24 +100,29 @@
     gathered = jnp.concatenate([ref[...].astype(F32) for ref in payloads], axis=0)
     table = gathered[:, width:]
     body = gathered[:, :width].astype(BF16)
-    own[...] = body
     tables[...] = table
-    shared = slot_weights(table[rows:], station[0], peers, slots, cap, rows)
-    placed = picked_rows(jnp.where(shared > 0.0, 1.0, 0.0).astype(BF16), body[rows:])
+    held = own.shape[0]
+    here = slot_weights(table, station[0], [0], held, cap, rows)
+    away = slot_weights(table[rows:], station[0], range(1, peers + 1), slots, cap, rows)
+    away = jnp.concatenate([jnp.zeros((rows, away.shape[1]), F32), away], axis=0)
+    shared = jnp.concatenate([here, away], axis=1)
+    placed = picked_rows(jnp.where(shared > 0.0, 1.0, 0.0).astype(BF16), body)
+    own[...] = placed[:held].astype(BF16)
     for j, ref in enumerate(chosen):
-        ref[...] = placed[j * slots : (j + 1) * slots].astype(BF16)
+        ref[...] = placed[held + j * slots : held + (j + 1) * slots].astype(BF16)
 
 
 def weigh(station, tables, shares, *outs, peers, cap, rows_each):
     table = tables[...]
-    lane = lax.broadcasted_iota(jnp.int32, table.shape, 1)
-    share = jnp.sum(jnp.where(lane == station[0], table, 0.0), axis=1, keepdims=True)
-    shares[...] = jnp.broadcast_to(share, shares.shape)
+    held = shares.shape[1]
+    shares[...] = slot_weights(table, station[0], [0], held, cap, rows_each).astype(BF16)
     for h, weights in enumerate(outs):
         folds, rows, lanes = weights.shape
         back = lanes // peers // folds
         part = table[h * rows : (h + 1) * rows]
-        shared = slot_weights(part, station[0], peers, folds * back, cap, rows_each)
+        shared = slot_weights(
+            part, station[0], range(1, peers + 1), folds * back, cap, rows_each
+        )
         weights[0] = shared.astype(BF16)
         for f in range(1, folds):
             shared = jnp.concatenate(
@@ -194,11 +199,18 @@
     for p, ref in enumerate(pieces):
         stacked[p * slots : (p + 1) * slots] = ref[...]
     base = len(pieces) * slots
-    early = own.shape[0]
-    stacked[base : base + early] = own[...]
-    stacked[base + early :] = other[...]
+    early = (stacked.shape[0] - base) // 2
+    slots_first = (own.shape[0] - held) // peers
+    for side, ref in enumerate((own, other)):
+        offset = base + side * early
+        stacked[offset : offset + held] = ref[:held]
+        loose = ref[held:].astype(F32)
+        tight = [loose[j * slots_first : j * slots_first + cap] for j in range(peers)]
+        spare = early - held - peers * cap
+        if spare:
+            tight.append(jnp.zeros((spare, width), F32))
+        stacked[offset + held : offset + early] = jnp.concatenate(tight, axis=0).astype(BF16)
     hidden = hidden_of(stacked, inward)
-    slots_first = (early - held) // peers
     n_len = width // folds // steps
     tall = folds * far * cap
     for c in range(steps):
@@ -213,7 +225,7 @@
             values.append(value)
         for p in range(2 * peers):
             side, j = divmod(p, peers)
-            first = base + side * early + held + j * slots_first
+            first = base + side * early + held + j * cap
             distant, close = [], []
             for value in values:
                 start = p * slots + (near - 1) * cap
@@ -236,7 +248,8 @@
     for f in range(folds):
         cols = slice(f * stacked.shape[1], (f + 1) * stacked.shape[1])
         mixed = jnp.dot(weights[f], stacked, preferred_element_type=F32)
-        mixed = mixed + shares[span, :1] * (keep[span, cols] + got[span, cols].astype(F32))
+        local = (keep[:, cols] + got[:, cols].astype(F32)).astype(BF16)
+        mixed = mixed + jnp.dot(shares[span], local, preferred_element_type=F32)
         for b, ref in enumerate(blocks):
             ref[:, cols] = mixed[b * rows : (b + 1) * rows].astype(ref.dtype)
 
@@ -276,8 +289,8 @@
     folds = next(f for f in (1, 2, 4, 8) if f * far * cap % 8 == 0)
     packed = (folds * far * cap, width // folds)
     table = -(-stations // LANES) * LANES
-    held = blocks * rows
-    early = held + peers * slots_first
+    held = -(-blocks * cap // 8) * 8
+    early = held + -(-peers * cap // 8) * 8
     station = (lax.axis_index("expert") // 2).astype(jnp.int32).reshape(1)
     hbm = functools.partial(pltpu.with_memory_space_constraint, memory_space=pltpu.HBM)
     w_in, w_out = hbm(w_in), hbm(w_out)
@@ -313,7 +326,7 @@
             select_kernel, blocks=blocks, peers=peers, cap=cap, slots=slots, width=width
         ),
         [SMEM] + [VMEM] * blocks,
-        [((held, width), BF16), ((held, table), F32)]
+        [((held, width), BF16), ((blocks * rows, table), F32)]
         + [((slots, width), BF16)] * peers,
     )(station, *column)
 
@@ -327,7 +340,7 @@
             rows_each=rows,
         ),
         [SMEM, VMEM, HBM, HBM],
-        [((cuts[2], 2 * half), BF16), ((half, width), BF16), ((held, LANES), F32)]
+        [((cuts[2], 2 * half), BF16), ((half, width), BF16), ((blocks * rows, held), BF16)]
         + [((folds, far * rows, peers * tall), BF16)] * 2,
         [pltpu.SemaphoreType.DMA((8,)), pltpu.SemaphoreType.DMA((6,))],
     )

time: 54.8 us -> 54.4 us (level)
  transfers between devices with their start and end apart: 27 -> 27, of which waited for: 10 -> 10; matrix products, arithmetic and copies ran while one was open for 0% -> 0% of each run, Pallas kernels for 10% -> 11%
where the time goes in v7:
time: 54.4 us; the launch traced here: 54.2 us
  starting transfers between devices  26.8 us (49%)
  waiting for transfers between devices  15.7 us (29%)
  Pallas kernels  11.3 us (21%)
    ppermute x27, starting transfers between devices, swap(): return lax.ppermute(block, 'expert', [(i, i ^ mask) for i in range(count)])  26.8 us
    ppermute x27, waiting for transfers between devices, swap(): return lax.ppermute(block, 'expert', [(i, i ^ mask) for i in range(count)])  15.7 us
    pallas_call x1, Pallas kernels, layer(): last(station, tables, w_in, w_out)  2.99 us
    pallas_call x1, Pallas kernels, layer(): results = expert_call(*arrived, *swapped, own, other, *inward, outward)  2.9 us
    pallas_call x1, Pallas kernels, layer(): call(functools.partial(prepare_kernel, peers=peers, cap=cap, slots=slots_...  1.86 us
    pallas_call x1, Pallas kernels, layer(): inward1, = middle(w_in)  1.64 us
  transfers between devices with their start and end apart: 27, of which 10 were waited for; matrix products, arithmetic and copies ran while one was open for 0% of the time, Pallas kernels for 11%

profile of v7, /device:TPU:0, one launch (start us, length us, event | category | flops | bytes accessed | tf_op | source)
XLA Modules:
  0.0 54.2 jit_solution(10122603619097894581)
XLA Ops:
  0.0 1.9 %shard_map.73 = (bf16[8,4224]{1,0:T(8,128)(2,1)S(1)}, bf16[512,768]{1,0:T(8,128)(2,1)S(1)}, bf16[8,4096]{1,0:T(8,128)(2,1)S(1)}, bf16[8,4096]{1,0:T(8,128)(2,1)S(1)}, bf16[8,4096]{1,0:T(8,128)(2,1)S(1)}) custom-call(s32[1]{0:T(128)} %bitcast.station, bf16[8,4096]{1,0:T(8,128)(2,1)} %refs_0_.3, f32[1,4096]{1,0:T(1,128)} %bitcast.3, s32[8,8]{1,0:T(8,128)} %refs_2_.1, ...), custom_call_target="tpu_custom_call" | custom-call | tf_op jit(solution)/shard_map/pallas_call | solution.py:306
  1.9 5.1 %collective-permute-start.2 = (bf16[8,4224]{1,0:T(8,128)(2,1)S(1)}, bf16[8,4224]{1,0:T(8,128)(2,1)S(1)}, u32[]{:S(2)}, u32[]{:S(2)}) collective-permute-start(bf16[8,4224]{1,0:T(8,128)(2,1)S(1)} %get-tuple-element.34.refs_0_), channel_id=1, source_target_pairs={{0,24},{1,25},{2,26},{3,27},{4,28},{5,29},{6,30},{7,31},{8,16},{9,... | collective-permute-start | bytes 202760 | tf_op jit(solution)/shard_map/ppermute | solution.py:21
  7.0 0.0 collective-permute-start.1
  7.0 0.6 %collective-permute-start = (bf16[8,4224]{1,0:T(8,128)(2,1)S(1)}, bf16[8,4224]{1,0:T(8,128)(2,1)S(1)}, u32[]{:S(2)}, u32[]{:S(2)}) collective-permute-start(bf16[8,4224]{1,0:T(8,128)(2,1)S(1)} %get-tuple-element.34.refs_0_), channel_id=1, source_target_pairs={{0,8},{1,9},{2,10},{3,11},{4,12},{5,13},{6,14},{7,15},{8,0},{9,1},... | collective-permute-start | bytes 202760 | tf_op jit(solution)/shard_map/ppermute | solution.py:21
  7.7 1.6 %collective-permute-start.9 = (bf16[8,4096]{1,0:T(8,128)(2,1)S(1)}, bf16[8,4096]{1,0:T(8,128)(2,1)S(1)}, u32[]{:S(2)}, u32[]{:S(2)}) collective-permute-start(bf16[8,4096]{1,0:T(8,128)(2,1)S(1)} %get-tuple-element.42), channel_id=1, source_target_pairs={{0,2},{1,3},{2,0},{3,1},{4,6},{5,7},{6,4},{7,5},{8,10},{9,11},{10,... | collective-permute-start | bytes 196616 | tf_op jit(solution)/shard_map/ppermute | solution.py:21
  9.3 1.5 %collective-permute-start.10 = (bf16[8,4096]{1,0:T(8,128)(2,1)S(1)}, bf16[8,4096]{1,0:T(8,128)(2,1)S(1)}, u32[]{:S(2)}, u32[]{:S(2)}) collective-permute-start(bf16[8,4096]{1,0:T(8,128)(2,1)S(1)} %get-tuple-element.43), channel_id=1, source_target_pairs={{0,4},{1,5},{2,6},{3,7},{4,0},{5,1},{6,2},{7,3},{8,12},{9,13},{10,... | collective-permute-start | bytes 196616 | tf_op jit(solution)/shard_map/ppermute | solution.py:21
  10.8 0.0 collective-permute-done.2.refs_3_
  10.8 1.6 %collective-permute-start.11 = (bf16[8,4096]{1,0:T(8,128)(2,1)S(1)}, bf16[8,4096]{1,0:T(8,128)(2,1)S(1)}, u32[]{:S(2)}, u32[]{:S(2)}) collective-permute-start(bf16[8,4096]{1,0:T(8,128)(2,1)S(1)} %get-tuple-element.44), channel_id=1, source_target_pairs={{0,6},{1,7},{2,4},{3,5},{4,2},{5,3},{6,0},{7,1},{8,14},{9,15},{10,... | collective-permute-start | bytes 196616 | tf_op jit(solution)/shard_map/ppermute | solution.py:21
  12.4 0.4 collective-permute-done.1.refs_2_
  12.8 0.0 collective-permute-done.refs_1_
  12.8 0.6 %shard_map.74 = (bf16[24,4096]{1,0:T(8,128)(2,1)S(1)}, f32[32,128]{1,0:T(8,128)S(1)}, bf16[16,4096]{1,0:T(8,128)(2,1)S(1)}, bf16[16,4096]{1,0:T(8,128)(2,1)S(1)}, bf16[16,4096]{1,0:T(8,128)(2,1)S(1)}) custom-call(s32[1]{0:T(128)} %bitcast.station, bf16[8,4224]{1,0:T(8,128)(2,1)S(1)} %get-tuple-element.34.refs_0_, ...), custom_call_target="tpu_custom_call" | custom-call | tf_op jit(solution)/shard_map/pallas_call | solution.py:324
  13.4 0.0 collective-permute-done.9
  13.5 0.8 %collective-permute-done.10 = bf16[8,4096]{1,0:T(8,128)(2,1)S(1)} collective-permute-done((bf16[8,4096]{1,0:T(8,128)(2,1)S(1)}, bf16[8,4096]{1,0:T(8,128)(2,1)S(1)}, u32[]{:S(2)}, u32[]{:S(2)}) %collective-permute-start.10) | collective-permute-done | bytes 65568 | tf_op jit(solution)/shard_map/ppermute | solution.py:21
  14.3 1.7 %collective-permute-done.11 = bf16[8,4096]{1,0:T(8,128)(2,1)S(1)} collective-permute-done((bf16[8,4096]{1,0:T(8,128)(2,1)S(1)}, bf16[8,4096]{1,0:T(8,128)(2,1)S(1)}, u32[]{:S(2)}, u32[]{:S(2)}) %collective-permute-start.11) | collective-permute-done | bytes 65568 | tf_op jit(solution)/shard_map/ppermute | solution.py:21
  16.0 0.0 collective-permute-start.12
  16.0 0.7 %collective-permute-start.3 = (bf16[16,4096]{1,0:T(8,128)(2,1)S(1)}, bf16[16,4096]{1,0:T(8,128)(2,1)S(1)}, u32[]{:S(2)}, u32[]{:S(2)}) collective-permute-start(bf16[16,4096]{1,0:T(8,128)(2,1)S(1)} %get-tuple-element.38), channel_id=1, source_target_pairs={{0,2},{1,3},{2,0},{3,1},{4,6},{5,7},{6,4},{7,5},{8,10},{9,11},{10,... | collective-permute-start | bytes 393224 | tf_op jit(solution)/shard_map/ppermute | solution.py:21
  16.7 1.5 %collective-permute-start.4 = (bf16[16,4096]{1,0:T(8,128)(2,1)S(1)}, bf16[16,4096]{1,0:T(8,128)(2,1)S(1)}, u32[]{:S(2)}, u32[]{:S(2)}) collective-permute-start(bf16[16,4096]{1,0:T(8,128)(2,1)S(1)} %get-tuple-element.39), channel_id=1, source_target_pairs={{0,4},{1,5},{2,6},{3,7},{4,0},{5,1},{6,2},{7,3},{8,12},{9,13},{10,... | collective-permute-start | bytes 393224 | tf_op jit(solution)/shard_map/ppermute | solution.py:21
  18.2 1.3 %collective-permute-start.5 = (bf16[16,4096]{1,0:T(8,128)(2,1)S(1)}, bf16[16,4096]{1,0:T(8,128)(2,1)S(1)}, u32[]{:S(2)}, u32[]{:S(2)}) collective-permute-start(bf16[16,4096]{1,0:T(8,128)(2,1)S(1)} %get-tuple-element.40), channel_id=1, source_target_pairs={{0,6},{1,7},{2,4},{3,5},{4,2},{5,3},{6,0},{7,1},{8,14},{9,15},{10,... | collective-permute-start | bytes 393224 | tf_op jit(solution)/shard_map/ppermute | solution.py:21
  19.6 2.9 %collective-permute-done.3.refs_0_ = bf16[16,4096]{1,0:T(8,128)(2,1)S(1)} collective-permute-done((bf16[16,4096]{1,0:T(8,128)(2,1)S(1)}, bf16[16,4096]{1,0:T(8,128)(2,1)S(1)}, u32[]{:S(2)}, u32[]{:S(2)}) %collective-permute-start.3) | collective-permute-done | bytes 131104 | tf_op jit(solution)/shard_map/ppermute | solution.py:21
  22.4 0.0 collective-permute-start.6
  22.4 2.6 %collective-permute-done.4.refs_1_ = bf16[16,4096]{1,0:T(8,128)(2,1)S(1)} collective-permute-done((bf16[16,4096]{1,0:T(8,128)(2,1)S(1)}, bf16[16,4096]{1,0:T(8,128)(2,1)S(1)}, u32[]{:S(2)}, u32[]{:S(2)}) %collective-permute-start.4) | collective-permute-done | bytes 131104 | tf_op jit(solution)/shard_map/ppermute | solution.py:21
  25.1 0.0 collective-permute-start.7
  25.1 0.0 collective-permute-done.5.refs_2_
  25.1 0.5 collective-permute-start.8
  25.6 1.6 %shard_map.76.refs_9_ = bf16[1536,768]{1,0:T(8,128)(2,1)S(1)} custom-call(bf16[1,4096,768]{2,1,0:T(8,128)(2,1)} %refs_0_.5), custom_call_target="tpu_custom_call" | custom-call | tf_op jit(solution)/shard_map/pallas_call | solution.py:320
  27.2 3.0 %shard_map.75 = (bf16[2048,768]{1,0:T(8,128)(2,1)S(1)}, bf16[384,4096]{1,0:T(8,128)(2,1)S(1)}, bf16[32,24]{1,0:T(8,128)(2,1)S(1)}, bf16[4,16,120]{2,1,0:T(8,128)(2,1)S(1)}, bf16[4,16,120]{2,1,0:T(8,128)(2,1)S(1)}) custom-call(s32[1]{0:T(128)} %bitcast.station, f32[32,128]{1,0:T(8,128)S(1)} %get-tuple-element.35.tables, bf16[1,4096,768]{2,1,0:T(8,128)(2,1)} %refs_0_.5, ...), custom_call_target="tpu_custom_call" | custom-call | tf_op jit(solution)/shard_map/pallas_call | solution.py:347
  30.2 0.0 collective-permute-done.6.refs_3_
  30.2 0.0 collective-permute-done.7.refs_4_
  30.2 0.0 collective-permute-done.8.refs_5_
  30.2 0.0 collective-permute-done.12.refs_7_
  30.3 2.9 %shard_map.77 = (f32[40,1024]{1,0:T(8,128)S(1)}, f32[40,1024]{1,0:T(8,128)S(1)}, f32[40,1024]{1,0:T(8,128)S(1)}, bf16[40,1024]{1,0:T(8,128)(2,1)S(1)}, bf16[40,1...) custom-call(bf16[16,4096]{1,0:T(8,128)(2,1)S(1)} %collective-permute, ...), custom_call_target="tpu_custom_call" | custom-call | tf_op jit(solution)/shard_map/pallas_call | solution.py:374
  33.2 0.1 collective-permute-start.19
  33.2 0.5 collective-permute-start.21
  33.7 0.1 collective-permute-start.23
  33.8 0.4 collective-permute-start.13
  34.2 0.1 collective-permute-start.14
  34.3 0.2 collective-permute-done.19
  34.5 1.5 %collective-permute-start.20 = (bf16[40,1024]{1,0:T(8,128)(2,1)S(1)}, bf16[40,1024]{1,0:T(8,128)(2,1)S(1)}, u32[]{:S(2)}, u32[]{:S(2)}) collective-permute-start(bf16[40,1024]{1,0:T(8,128)(2,1)S(1)} %add_convert_fusion.2), channel_id=1, source_target_pairs={{0,2},{1,3},{2,0},{3,1},{4,6},{5,7},{6,4},{7,5},{8,10},{9,11},{10,... | collective-permute-start | bytes 245768 | tf_op jit(solution)/shard_map/ppermute | solution.py:21
  36.0 0.0 collective-permute-done.21
  36.0 0.7 %collective-permute-start.22 = (bf16[40,1024]{1,0:T(8,128)(2,1)S(1)}, bf16[40,1024]{1,0:T(8,128)(2,1)S(1)}, u32[]{:S(2)}, u32[]{:S(2)}) collective-permute-start(bf16[40,1024]{1,0:T(8,128)(2,1)S(1)} %add_convert_fusion.1), channel_id=1, source_target_pairs={{0,4},{1,5},{2,6},{3,7},{4,0},{5,1},{6,2},{7,3},{8,12},{9,13},{10,... | collective-permute-start | bytes 245768 | tf_op jit(solution)/shard_map/ppermute | solution.py:21
  36.8 0.0 collective-permute-done.23
  36.8 1.5 %collective-permute-start.24 = (bf16[40,1024]{1,0:T(8,128)(2,1)S(1)}, bf16[40,1024]{1,0:T(8,128)(2,1)S(1)}, u32[]{:S(2)}, u32[]{:S(2)}) collective-permute-start(bf16[40,1024]{1,0:T(8,128)(2,1)S(1)} %add_convert_fusion), channel_id=1, source_target_pairs={{0,6},{1,7},{2,4},{3,5},{4,2},{5,3},{6,0},{7,1},{8,14},{9,15},{10,... | collective-permute-start | bytes 245768 | tf_op jit(solution)/shard_map/ppermute | solution.py:21
  38.3 0.0 collective-permute-done.14
  38.3 1.6 %collective-permute-start.17 = (bf16[40,1024]{1,0:T(8,128)(2,1)S(1)}, bf16[40,1024]{1,0:T(8,128)(2,1)S(1)}, u32[]{:S(2)}, u32[]{:S(2)}) collective-permute-start(bf16[40,1024]{1,0:T(8,128)(2,1)S(1)} %get-tuple-element.63), channel_id=1, source_target_pairs={{0,6},{1,7},{2,4},{3,5},{4,2},{5,3},{6,0},{7,1},{8,14},{9,15},{10,... | collective-permute-start | bytes 245768 | tf_op jit(solution)/shard_map/ppermute | solution.py:21
  39.9 0.0 collective-permute-done.20.refs_0_
  39.9 1.4 %collective-permute-start.16 = (bf16[40,1024]{1,0:T(8,128)(2,1)S(1)}, bf16[40,1024]{1,0:T(8,128)(2,1)S(1)}, u32[]{:S(2)}, u32[]{:S(2)}) collective-permute-start(bf16[40,1024]{1,0:T(8,128)(2,1)S(1)} %get-tuple-element.64), channel_id=1, source_target_pairs={{0,4},{1,5},{2,6},{3,7},{4,0},{5,1},{6,2},{7,3},{8,12},{9,13},{10,... | collective-permute-start | bytes 245768 | tf_op jit(solution)/shard_map/ppermute | solution.py:21
  41.3 2.2 %collective-permute-done.22.refs_1_ = bf16[40,1024]{1,0:T(8,128)(2,1)S(1)} collective-permute-done((bf16[40,1024]{1,0:T(8,128)(2,1)S(1)}, bf16[40,1024]{1,0:T(8,128)(2,1)S(1)}, u32[]{:S(2)}, u32[]{:S(2)}) %collective-permute-start.22) | collective-permute-done | bytes 81952 | tf_op jit(solution)/shard_map/ppermute | solution.py:21
  43.4 0.0 collective-permute-start.15
  43.4 0.0 collective-permute-done.24.refs_2_
  43.5 0.0 collective-permute-done.13.got
  43.5 0.3 shard_map.79
  43.8 3.2 %collective-permute-start.25 = (bf16[8,4096]{1,0:T(8,128)(2,1)S(1)}, bf16[8,4096]{1,0:T(8,128)(2,1)S(1)}, u32[]{:S(2)}, u32[]{:S(2)}) collective-permute-start(bf16[8,4096]{1,0:T(8,128)(2,1)S(1)} %get-tuple-element.61), channel_id=1, source_target_pairs={{0,16},{1,17},{2,18},{3,19},{4,20},{5,21},{6,22},{7,23},{8,24},{9,... | collective-permute-start | bytes 196616 | tf_op jit(solution)/shard_map/ppermute | solution.py:21
  47.0 1.2 %collective-permute-start.26 = (bf16[8,4096]{1,0:T(8,128)(2,1)S(1)}, bf16[8,4096]{1,0:T(8,128)(2,1)S(1)}, u32[]{:S(2)}, u32[]{:S(2)}) collective-permute-start(bf16[8,4096]{1,0:T(8,128)(2,1)S(1)} %get-tuple-element.62), channel_id=1, source_target_pairs={{0,24},{1,25},{2,26},{3,27},{4,28},{5,29},{6,30},{7,31},{8,16},{9,... | collective-permute-start | bytes 196616 | tf_op jit(solution)/shard_map/ppermute | solution.py:21
  48.2 0.0 collective-permute-done.17.refs_2_
  48.2 0.0 collective-permute-done.16.refs_1_
  48.2 0.0 collective-permute-done.15.refs_0_
  48.2 0.3 shard_map.78
  48.5 0.0 collective-permute-start.18
  48.6 2.0 %collective-permute-done.25.refs_1_ = bf16[8,4096]{1,0:T(8,128)(2,1)S(1)} collective-permute-done((bf16[8,4096]{1,0:T(8,128)(2,1)S(1)}, bf16[8,4096]{1,0:T(8,128)(2,1)S(1)}, u32[]{:S(2)}, u32[]{:S(2)}) %collective-permute-start.25) | collective-permute-done | bytes 65568 | tf_op jit(solution)/shard_map/ppermute | solution.py:21
  50.6 2.5 %collective-permute-done.26.refs_2_ = bf16[8,4096]{1,0:T(8,128)(2,1)S(1)} collective-permute-done((bf16[8,4096]{1,0:T(8,128)(2,1)S(1)}, bf16[8,4096]{1,0:T(8,128)(2,1)S(1)}, u32[]{:S(2)}, u32[]{:S(2)}) %collective-permute-start.26) | collective-permute-done | bytes 65568 | tf_op jit(solution)/shard_map/ppermute | solution.py:21
  53.2 0.4 collective-permute-done.18.refs_0_
  53.5 0.7 %shard_map.80 = bf16[8,4096]{1,0:T(8,128)(2,1)} custom-call(f32[8,4096]{1,0:T(8,128)S(1)} %get-tuple-element.52.local, bf16[8,4096]{1,0:T(8,128)(2,1)S(1)} %collective-permute-done.18.refs_0_, bf16[8,4096]{1,0:T(8,128)(2,1)S(1)} %collective-permute-done.25.refs_1_, bf16[8,4096]{1,0:T(8,128)(2,1)S(1)} %collective-permute-done.26.refs_2_), custom_call_target="tpu_custom_call" | custom-call | tf_op jit(solution)/shard_map/pallas_call | solution.py:400
  (8 shorter events, 0.2 us)
Async XLA Ops:
  1.9 9.0 %collective-permute-start.2 = (bf16[8,4224]{1,0:T(8,128)(2,1)S(1)}, bf16[8,4224]{1,0:T(8,128)(2,1)S(1)}, u32[]{:S(2)}, u32[]{:S(2)}) collective-permute-start(bf16[8,4224]{1,0:T(8,128)(2,1)S(1)} %get-tuple-element.34.refs_0_), channel_id=1, source_target_pairs={{0,24},{1,25},{2,26},{3,27},{4,28},{5,29},{6,30},{7,31},{8,16},{9,... | collective-permute-start | bytes 202760 | tf_op jit(solution)/shard_map/ppermute | solution.py:21
  7.0 5.8 %collective-permute-start.1 = (bf16[8,4224]{1,0:T(8,128)(2,1)S(1)}, bf16[8,4224]{1,0:T(8,128)(2,1)S(1)}, u32[]{:S(2)}, u32[]{:S(2)}) collective-permute-start(bf16[8,4224]{1,0:T(8,128)(2,1)S(1)} %get-tuple-element.34.refs_0_), channel_id=1, source_target_pairs={{0,16},{1,17},{2,18},{3,19},{4,20},{5,21},{6,22},{7,23},{8,24},{9,... | collective-permute-start | bytes 202760 | tf_op jit(solution)/shard_map/ppermute | solution.py:21
  7.0 5.8 %collective-permute-start = (bf16[8,4224]{1,0:T(8,128)(2,1)S(1)}, bf16[8,4224]{1,0:T(8,128)(2,1)S(1)}, u32[]{:S(2)}, u32[]{:S(2)}) collective-permute-start(bf16[8,4224]{1,0:T(8,128)(2,1)S(1)} %get-tuple-element.34.refs_0_), channel_id=1, source_target_pairs={{0,8},{1,9},{2,10},{3,11},{4,12},{5,13},{6,14},{7,15},{8,0},{9,1},... | collective-permute-start | bytes 202760 | tf_op jit(solution)/shard_map/ppermute | solution.py:21
  7.7 5.8 %collective-permute-start.9 = (bf16[8,4096]{1,0:T(8,128)(2,1)S(1)}, bf16[8,4096]{1,0:T(8,128)(2,1)S(1)}, u32[]{:S(2)}, u32[]{:S(2)}) collective-permute-start(bf16[8,4096]{1,0:T(8,128)(2,1)S(1)} %get-tuple-element.42), channel_id=1, source_target_pairs={{0,2},{1,3},{2,0},{3,1},{4,6},{5,7},{6,4},{7,5},{8,10},{9,11},{10,... | collective-permute-start | bytes 196616 | tf_op jit(solution)/shard_map/ppermute | solution.py:21
  9.3 5.0 %collective-permute-start.10 = (bf16[8,4096]{1,0:T(8,128)(2,1)S(1)}, bf16[8,4096]{1,0:T(8,128)(2,1)S(1)}, u32[]{:S(2)}, u32[]{:S(2)}) collective-permute-start(bf16[8,4096]{1,0:T(8,128)(2,1)S(1)} %get-tuple-element.43), channel_id=1, source_target_pairs={{0,4},{1,5},{2,6},{3,7},{4,0},{5,1},{6,2},{7,3},{8,12},{9,13},{10,... | collective-permute-start | bytes 196616 | tf_op jit(solution)/shard_map/ppermute | solution.py:21
  10.8 5.2 %collective-permute-start.11 = (bf16[8,4096]{1,0:T(8,128)(2,1)S(1)}, bf16[8,4096]{1,0:T(8,128)(2,1)S(1)}, u32[]{:S(2)}, u32[]{:S(2)}) collective-permute-start(bf16[8,4096]{1,0:T(8,128)(2,1)S(1)} %get-tuple-element.44), channel_id=1, source_target_pairs={{0,6},{1,7},{2,4},{3,5},{4,2},{5,3},{6,0},{7,1},{8,14},{9,15},{10,... | collective-permute-start | bytes 196616 | tf_op jit(solution)/shard_map/ppermute | solution.py:21
  16.0 14.3 %collective-permute-start.12 = (bf16[48,4096]{1,0:T(8,128)(2,1)S(1)}, bf16[48,4096]{1,0:T(8,128)(2,1)S(1)}, u32[]{:S(2)}, u32[]{:S(2)}) collective-permute-start(bf16[48,4096]{1,0:T(8,128)(2,1)S(1)} %constant_dynamic-update-slice_fusion.refs_6_), channel_id=1, source_target_pairs={{0,1},{1,0},{2,3},{3,2},{4,5},{5,4},{6,7},{7,6},{8,9},{9,8},{10,11... | collective-permute-start | bytes 1179656 | tf_op jit(solution)/shard_map/ppermute | solution.py:21
  16.0 6.4 %collective-permute-start.3 = (bf16[16,4096]{1,0:T(8,128)(2,1)S(1)}, bf16[16,4096]{1,0:T(8,128)(2,1)S(1)}, u32[]{:S(2)}, u32[]{:S(2)}) collective-permute-start(bf16[16,4096]{1,0:T(8,128)(2,1)S(1)} %get-tuple-element.38), channel_id=1, source_target_pairs={{0,2},{1,3},{2,0},{3,1},{4,6},{5,7},{6,4},{7,5},{8,10},{9,11},{10,... | collective-permute-start | bytes 393224 | tf_op jit(solution)/shard_map/ppermute | solution.py:21
  16.7 8.4 %collective-permute-start.4 = (bf16[16,4096]{1,0:T(8,128)(2,1)S(1)}, bf16[16,4096]{1,0:T(8,128)(2,1)S(1)}, u32[]{:S(2)}, u32[]{:S(2)}) collective-permute-start(bf16[16,4096]{1,0:T(8,128)(2,1)S(1)} %get-tuple-element.39), channel_id=1, source_target_pairs={{0,4},{1,5},{2,6},{3,7},{4,0},{5,1},{6,2},{7,3},{8,12},{9,13},{10,... | collective-permute-start | bytes 393224 | tf_op jit(solution)/shard_map/ppermute | solution.py:21
  18.2 6.8 %collective-permute-start.5 = (bf16[16,4096]{1,0:T(8,128)(2,1)S(1)}, bf16[16,4096]{1,0:T(8,128)(2,1)S(1)}, u32[]{:S(2)}, u32[]{:S(2)}) collective-permute-start(bf16[16,4096]{1,0:T(8,128)(2,1)S(1)} %get-tuple-element.40), channel_id=1, source_target_pairs={{0,6},{1,7},{2,4},{3,5},{4,2},{5,3},{6,0},{7,1},{8,14},{9,15},{10,... | collective-permute-start | bytes 393224 | tf_op jit(solution)/shard_map/ppermute | solution.py:21
  22.4 7.8 %collective-permute-start.6 = (bf16[16,4096]{1,0:T(8,128)(2,1)S(1)}, bf16[16,4096]{1,0:T(8,128)(2,1)S(1)}, u32[]{:S(2)}, u32[]{:S(2)}) collective-permute-start(bf16[16,4096]{1,0:T(8,128)(2,1)S(1)} %collective-permute-done.3.refs_0_), channel_id=1, source_target_pairs={{0,1},{1,0},{2,3},{3,2},{4,5},{5,4},{6,7},{7,6},{8,9},{9,8},{10,11... | collective-permute-start | bytes 393224 | tf_op jit(solution)/shard_map/ppermute | solution.py:21
  25.1 5.2 %collective-permute-start.7 = (bf16[16,4096]{1,0:T(8,128)(2,1)S(1)}, bf16[16,4096]{1,0:T(8,128)(2,1)S(1)}, u32[]{:S(2)}, u32[]{:S(2)}) collective-permute-start(bf16[16,4096]{1,0:T(8,128)(2,1)S(1)} %collective-permute-done.4.refs_1_), channel_id=1, source_target_pairs={{0,1},{1,0},{2,3},{3,2},{4,5},{5,4},{6,7},{7,6},{8,9},{9,8},{10,11... | collective-permute-start | bytes 393224 | tf_op jit(solution)/shard_map/ppermute | solution.py:21
  25.1 5.2 %collective-permute-start.8 = (bf16[16,4096]{1,0:T(8,128)(2,1)S(1)}, bf16[16,4096]{1,0:T(8,128)(2,1)S(1)}, u32[]{:S(2)}, u32[]{:S(2)}) collective-permute-start(bf16[16,4096]{1,0:T(8,128)(2,1)S(1)} %collective-permute-done.5.refs_2_), channel_id=1, source_target_pairs={{0,1},{1,0},{2,3},{3,2},{4,5},{5,4},{6,7},{7,6},{8,9},{9,8},{10,11... | collective-permute-start | bytes 393224 | tf_op jit(solution)/shard_map/ppermute | solution.py:21
  33.2 1.3 %collective-permute-start.19 = (bf16[40,1024]{1,0:T(8,128)(2,1)S(1)}, bf16[40,1024]{1,0:T(8,128)(2,1)S(1)}, u32[]{:S(2)}, u32[]{:S(2)}) collective-permute-start(bf16[40,1024]{1,0:T(8,128)(2,1)S(1)} %get-tuple-element.56), channel_id=1, source_target_pairs={{0,1},{1,0},{2,3},{3,2},{4,5},{5,4},{6,7},{7,6},{8,9},{9,8},{10,11... | collective-permute-start | bytes 245768 | tf_op jit(solution)/shard_map/ppermute | solution.py:21
  33.2 2.8 %collective-permute-start.21 = (bf16[40,1024]{1,0:T(8,128)(2,1)S(1)}, bf16[40,1024]{1,0:T(8,128)(2,1)S(1)}, u32[]{:S(2)}, u32[]{:S(2)}) collective-permute-start(bf16[40,1024]{1,0:T(8,128)(2,1)S(1)} %get-tuple-element.58), channel_id=1, source_target_pairs={{0,1},{1,0},{2,3},{3,2},{4,5},{5,4},{6,7},{7,6},{8,9},{9,8},{10,11... | collective-permute-start | bytes 245768 | tf_op jit(solution)/shard_map/ppermute | solution.py:21
  33.7 3.0 %collective-permute-start.23 = (bf16[40,1024]{1,0:T(8,128)(2,1)S(1)}, bf16[40,1024]{1,0:T(8,128)(2,1)S(1)}, u32[]{:S(2)}, u32[]{:S(2)}) collective-permute-start(bf16[40,1024]{1,0:T(8,128)(2,1)S(1)} %get-tuple-element.60), channel_id=1, source_target_pairs={{0,1},{1,0},{2,3},{3,2},{4,5},{5,4},{6,7},{7,6},{8,9},{9,8},{10,11... | collective-permute-start | bytes 245768 | tf_op jit(solution)/shard_map/ppermute | solution.py:21
  33.8 9.6 %collective-permute-start.13 = (bf16[24,4096]{1,0:T(8,128)(2,1)S(1)}, bf16[24,4096]{1,0:T(8,128)(2,1)S(1)}, u32[]{:S(2)}, u32[]{:S(2)}) collective-permute-start(bf16[24,4096]{1,0:T(8,128)(2,1)S(1)} %get-tuple-element.49), channel_id=1, source_target_pairs={{0,1},{1,0},{2,3},{3,2},{4,5},{5,4},{6,7},{7,6},{8,9},{9,8},{10,11... | collective-permute-start | bytes 589832 | tf_op jit(solution)/shard_map/ppermute | solution.py:21
  34.2 4.0 %collective-permute-start.14 = (bf16[120,1024]{1,0:T(8,128)(2,1)S(1)}, bf16[120,1024]{1,0:T(8,128)(2,1)S(1)}, u32[]{:S(2)}, u32[]{:S(2)}) collective-permute-start(bf16[120,1024]{1,0:T(8,128)(2,1)S(1)} %get-tuple-element.51), channel_id=1, source_target_pairs={{0,1},{1,0},{2,3},{3,2},{4,5},{5,4},{6,7},{7,6},{8,9},{9,8},{10,11... | collective-permute-start | bytes 737288 | tf_op jit(solution)/shard_map/ppermute | solution.py:21
  34.5 5.4 %collective-permute-start.20 = (bf16[40,1024]{1,0:T(8,128)(2,1)S(1)}, bf16[40,1024]{1,0:T(8,128)(2,1)S(1)}, u32[]{:S(2)}, u32[]{:S(2)}) collective-permute-start(bf16[40,1024]{1,0:T(8,128)(2,1)S(1)} %add_convert_fusion.2), channel_id=1, source_target_pairs={{0,2},{1,3},{2,0},{3,1},{4,6},{5,7},{6,4},{7,5},{8,10},{9,11},{10,... | collective-permute-start | bytes 245768 | tf_op jit(solution)/shard_map/ppermute | solution.py:21
  36.0 7.4 %collective-permute-start.22 = (bf16[40,1024]{1,0:T(8,128)(2,1)S(1)}, bf16[40,1024]{1,0:T(8,128)(2,1)S(1)}, u32[]{:S(2)}, u32[]{:S(2)}) collective-permute-start(bf16[40,1024]{1,0:T(8,128)(2,1)S(1)} %add_convert_fusion.1), channel_id=1, source_target_pairs={{0,4},{1,5},{2,6},{3,7},{4,0},{5,1},{6,2},{7,3},{8,12},{9,13},{10,... | collective-permute-start | bytes 245768 | tf_op jit(solution)/shard_map/ppermute | solution.py:21
  36.8 6.7 %collective-permute-start.24 = (bf16[40,1024]{1,0:T(8,128)(2,1)S(1)}, bf16[40,1024]{1,0:T(8,128)(2,1)S(1)}, u32[]{:S(2)}, u32[]{:S(2)}) collective-permute-start(bf16[40,1024]{1,0:T(8,128)(2,1)S(1)} %add_convert_fusion), channel_id=1, source_target_pairs={{0,6},{1,7},{2,4},{3,5},{4,2},{5,3},{6,0},{7,1},{8,14},{9,15},{10,... | collective-permute-start | bytes 245768 | tf_op jit(solution)/shard_map/ppermute | solution.py:21
  38.3 9.9 %collective-permute-start.17 = (bf16[40,1024]{1,0:T(8,128)(2,1)S(1)}, bf16[40,1024]{1,0:T(8,128)(2,1)S(1)}, u32[]{:S(2)}, u32[]{:S(2)}) collective-permute-start(bf16[40,1024]{1,0:T(8,128)(2,1)S(1)} %get-tuple-element.63), channel_id=1, source_target_pairs={{0,6},{1,7},{2,4},{3,5},{4,2},{5,3},{6,0},{7,1},{8,14},{9,15},{10,... | collective-permute-start | bytes 245768 | tf_op jit(solution)/shard_map/ppermute | solution.py:21
  39.9 8.3 %collective-permute-start.16 = (bf16[40,1024]{1,0:T(8,128)(2,1)S(1)}, bf16[40,1024]{1,0:T(8,128)(2,1)S(1)}, u32[]{:S(2)}, u32[]{:S(2)}) collective-permute-start(bf16[40,1024]{1,0:T(8,128)(2,1)S(1)} %get-tuple-element.64), channel_id=1, source_target_pairs={{0,4},{1,5},{2,6},{3,7},{4,0},{5,1},{6,2},{7,3},{8,12},{9,13},{10,... | collective-permute-start | bytes 245768 | tf_op jit(solution)/shard_map/ppermute | solution.py:21
  43.4 4.8 %collective-permute-start.15 = (bf16[40,1024]{1,0:T(8,128)(2,1)S(1)}, bf16[40,1024]{1,0:T(8,128)(2,1)S(1)}, u32[]{:S(2)}, u32[]{:S(2)}) collective-permute-start(bf16[40,1024]{1,0:T(8,128)(2,1)S(1)} %get-tuple-element.65), channel_id=1, source_target_pairs={{0,2},{1,3},{2,0},{3,1},{4,6},{5,7},{6,4},{7,5},{8,10},{9,11},{10,... | collective-permute-start | bytes 245768 | tf_op jit(solution)/shard_map/ppermute | solution.py:21
  43.8 6.9 %collective-permute-start.25 = (bf16[8,4096]{1,0:T(8,128)(2,1)S(1)}, bf16[8,4096]{1,0:T(8,128)(2,1)S(1)}, u32[]{:S(2)}, u32[]{:S(2)}) collective-permute-start(bf16[8,4096]{1,0:T(8,128)(2,1)S(1)} %get-tuple-element.61), channel_id=1, source_target_pairs={{0,16},{1,17},{2,18},{3,19},{4,20},{5,21},{6,22},{7,23},{8,24},{9,... | collective-permute-start | bytes 196616 | tf_op jit(solution)/shard_map/ppermute | solution.py:21
  47.0 6.2 %collective-permute-start.26 = (bf16[8,4096]{1,0:T(8,128)(2,1)S(1)}, bf16[8,4096]{1,0:T(8,128)(2,1)S(1)}, u32[]{:S(2)}, u32[]{:S(2)}) collective-permute-start(bf16[8,4096]{1,0:T(8,128)(2,1)S(1)} %get-tuple-element.62), channel_id=1, source_target_pairs={{0,24},{1,25},{2,26},{3,27},{4,28},{5,29},{6,30},{7,31},{8,16},{9,... | collective-permute-start | bytes 196616 | tf_op jit(solution)/shard_map/ppermute | solution.py:21
  48.5 5.0 %collective-permute-start.18 = (bf16[8,4096]{1,0:T(8,128)(2,1)S(1)}, bf16[8,4096]{1,0:T(8,128)(2,1)S(1)}, u32[]{:S(2)}, u32[]{:S(2)}) collective-permute-start(bf16[8,4096]{1,0:T(8,128)(2,1)S(1)} %get-tuple-element.53), channel_id=1, source_target_pairs={{0,8},{1,9},{2,10},{3,11},{4,12},{5,13},{6,14},{7,15},{8,0},{9,1},... | collective-permute-start | bytes 196616 | tf_op jit(solution)/shard_map/ppermute | solution.py:21

commit v8 on v7

--- a/solution.py
+++ b/solution.py
@@ -294,7 +294,7 @@
     station = (lax.axis_index("expert") // 2).astype(jnp.int32).reshape(1)
     hbm = functools.partial(pltpu.with_memory_space_constraint, memory_space=pltpu.HBM)
     w_in, w_out = hbm(w_in), hbm(w_out)
-    cuts = (width // 8, width * 3 // 8, width // 2)
+    cuts = (width // 16, width // 4, width * 11 // 16)
 
     inputs = (
         tokens,
@@ -315,7 +315,7 @@
         functools.partial(load_kernel, starts=[cuts[0]]),
         [HBM],
         [((cuts[1], 2 * half), BF16)],
-        [pltpu.SemaphoreType.DMA((6,))],
+        [pltpu.SemaphoreType.DMA((4,))],
     )
     (inward1,) = middle(w_in)
 
@@ -361,7 +361,7 @@
             near=near,
             far=far,
             folds=folds,
-            steps=1,
+            steps=4,
         ),
         [VMEM] * (2 * peers + 3 + parts),
         [(packed, F32)] * peers

time: 54.4 us -> 54.3 us (level)
  no operation moved by 1% of the time
where the time goes in v8:
time: 54.3 us; the launch traced here: 54.2 us
  starting transfers between devices  26.8 us (49%)
  waiting for transfers between devices  15.8 us (29%)
  Pallas kernels  11.3 us (21%)
    ppermute x27, starting transfers between devices, swap(): return lax.ppermute(block, 'expert', [(i, i ^ mask) for i in range(count)])  26.8 us
    ppermute x27, waiting for transfers between devices, swap(): return lax.ppermute(block, 'expert', [(i, i ^ mask) for i in range(count)])  15.8 us
    pallas_call x1, Pallas kernels, layer(): last(station, tables, w_in, w_out)  3.33 us
    pallas_call x1, Pallas kernels, layer(): results = expert_call(*arrived, *swapped, own, other, *inward, outward)  2.9 us
    pallas_call x1, Pallas kernels, layer(): call(functools.partial(prepare_kernel, peers=peers, cap=cap, slots=slots_...  1.72 us
    pallas_call x1, Pallas kernels, layer(): inward1, = middle(w_in)  1.38 us
  transfers between devices with their start and end apart: 27, of which 10 were waited for; matrix products, arithmetic and copies ran while one was open for 0% of the time, Pallas kernels for 11%

profile of v8, /device:TPU:0, one launch (start us, length us, event | category | flops | bytes accessed | tf_op | source)
XLA Modules:
  0.0 54.2 jit_solution(4661615205270658548)
XLA Ops:
  0.0 1.7 %shard_map.73 = (bf16[8,4224]{1,0:T(8,128)(2,1)S(1)}, bf16[256,768]{1,0:T(8,128)(2,1)S(1)}, bf16[8,4096]{1,0:T(8,128)(2,1)S(1)}, bf16[8,4096]{1,0:T(8,128)(2,1)S(1)}, bf16[8,4096]{1,0:T(8,128)(2,1)S(1)}) custom-call(s32[1]{0:T(128)} %bitcast.station, bf16[8,4096]{1,0:T(8,128)(2,1)} %refs_0_.3, f32[1,4096]{1,0:T(1,128)} %bitcast.3, s32[8,8]{1,0:T(8,128)} %refs_2_.1, ...), custom_call_target="tpu_custom_call" | custom-call | tf_op jit(solution)/shard_map/pallas_call | solution.py:306
  1.7 5.1 %collective-permute-start.2 = (bf16[8,4224]{1,0:T(8,128)(2,1)S(1)}, bf16[8,4224]{1,0:T(8,128)(2,1)S(1)}, u32[]{:S(2)}, u32[]{:S(2)}) collective-permute-start(bf16[8,4224]{1,0:T(8,128)(2,1)S(1)} %get-tuple-element.34.refs_0_), channel_id=1, source_target_pairs={{0,24},{1,25},{2,26},{3,27},{4,28},{5,29},{6,30},{7,31},{8,16},{9,... | collective-permute-start | bytes 202760 | tf_op jit(solution)/shard_map/ppermute | solution.py:21
  6.9 0.0 collective-permute-start.1
  6.9 0.6 %collective-permute-start = (bf16[8,4224]{1,0:T(8,128)(2,1)S(1)}, bf16[8,4224]{1,0:T(8,128)(2,1)S(1)}, u32[]{:S(2)}, u32[]{:S(2)}) collective-permute-start(bf16[8,4224]{1,0:T(8,128)(2,1)S(1)} %get-tuple-element.34.refs_0_), channel_id=1, source_target_pairs={{0,8},{1,9},{2,10},{3,11},{4,12},{5,13},{6,14},{7,15},{8,0},{9,1},... | collective-permute-start | bytes 202760 | tf_op jit(solution)/shard_map/ppermute | solution.py:21
  7.5 1.6 %collective-permute-start.9 = (bf16[8,4096]{1,0:T(8,128)(2,1)S(1)}, bf16[8,4096]{1,0:T(8,128)(2,1)S(1)}, u32[]{:S(2)}, u32[]{:S(2)}) collective-permute-start(bf16[8,4096]{1,0:T(8,128)(2,1)S(1)} %get-tuple-element.42), channel_id=1, source_target_pairs={{0,2},{1,3},{2,0},{3,1},{4,6},{5,7},{6,4},{7,5},{8,10},{9,11},{10,... | collective-permute-start | bytes 196616 | tf_op jit(solution)/shard_map/ppermute | solution.py:21
  9.1 1.5 %collective-permute-start.10 = (bf16[8,4096]{1,0:T(8,128)(2,1)S(1)}, bf16[8,4096]{1,0:T(8,128)(2,1)S(1)}, u32[]{:S(2)}, u32[]{:S(2)}) collective-permute-start(bf16[8,4096]{1,0:T(8,128)(2,1)S(1)} %get-tuple-element.43), channel_id=1, source_target_pairs={{0,4},{1,5},{2,6},{3,7},{4,0},{5,1},{6,2},{7,3},{8,12},{9,13},{10,... | collective-permute-start | bytes 196616 | tf_op jit(solution)/shard_map/ppermute | solution.py:21
  10.7 0.0 collective-permute-done.2.refs_3_
  10.7 1.6 %collective-permute-start.11 = (bf16[8,4096]{1,0:T(8,128)(2,1)S(1)}, bf16[8,4096]{1,0:T(8,128)(2,1)S(1)}, u32[]{:S(2)}, u32[]{:S(2)}) collective-permute-start(bf16[8,4096]{1,0:T(8,128)(2,1)S(1)} %get-tuple-element.44), channel_id=1, source_target_pairs={{0,6},{1,7},{2,4},{3,5},{4,2},{5,3},{6,0},{7,1},{8,14},{9,15},{10,... | collective-permute-start | bytes 196616 | tf_op jit(solution)/shard_map/ppermute | solution.py:21
  12.2 0.4 collective-permute-done.1.refs_2_
  12.6 0.0 collective-permute-done.refs_1_
  12.6 0.6 %shard_map.74 = (bf16[24,4096]{1,0:T(8,128)(2,1)S(1)}, f32[32,128]{1,0:T(8,128)S(1)}, bf16[16,4096]{1,0:T(8,128)(2,1)S(1)}, bf16[16,4096]{1,0:T(8,128)(2,1)S(1)}, bf16[16,4096]{1,0:T(8,128)(2,1)S(1)}) custom-call(s32[1]{0:T(128)} %bitcast.station, bf16[8,4224]{1,0:T(8,128)(2,1)S(1)} %get-tuple-element.34.refs_0_, ...), custom_call_target="tpu_custom_call" | custom-call | tf_op jit(solution)/shard_map/pallas_call | solution.py:324
  13.3 0.0 collective-permute-done.9
  13.3 0.8 %collective-permute-done.10 = bf16[8,4096]{1,0:T(8,128)(2,1)S(1)} collective-permute-done((bf16[8,4096]{1,0:T(8,128)(2,1)S(1)}, bf16[8,4096]{1,0:T(8,128)(2,1)S(1)}, u32[]{:S(2)}, u32[]{:S(2)}) %collective-permute-start.10) | collective-permute-done | bytes 65568 | tf_op jit(solution)/shard_map/ppermute | solution.py:21
  14.1 1.7 %collective-permute-done.11 = bf16[8,4096]{1,0:T(8,128)(2,1)S(1)} collective-permute-done((bf16[8,4096]{1,0:T(8,128)(2,1)S(1)}, bf16[8,4096]{1,0:T(8,128)(2,1)S(1)}, u32[]{:S(2)}, u32[]{:S(2)}) %collective-permute-start.11) | collective-permute-done | bytes 65568 | tf_op jit(solution)/shard_map/ppermute | solution.py:21
  15.8 0.0 collective-permute-start.12
  15.8 0.7 %collective-permute-start.3 = (bf16[16,4096]{1,0:T(8,128)(2,1)S(1)}, bf16[16,4096]{1,0:T(8,128)(2,1)S(1)}, u32[]{:S(2)}, u32[]{:S(2)}) collective-permute-start(bf16[16,4096]{1,0:T(8,128)(2,1)S(1)} %get-tuple-element.38), channel_id=1, source_target_pairs={{0,2},{1,3},{2,0},{3,1},{4,6},{5,7},{6,4},{7,5},{8,10},{9,11},{10,... | collective-permute-start | bytes 393224 | tf_op jit(solution)/shard_map/ppermute | solution.py:21
  16.5 1.5 %collective-permute-start.4 = (bf16[16,4096]{1,0:T(8,128)(2,1)S(1)}, bf16[16,4096]{1,0:T(8,128)(2,1)S(1)}, u32[]{:S(2)}, u32[]{:S(2)}) collective-permute-start(bf16[16,4096]{1,0:T(8,128)(2,1)S(1)} %get-tuple-element.39), channel_id=1, source_target_pairs={{0,4},{1,5},{2,6},{3,7},{4,0},{5,1},{6,2},{7,3},{8,12},{9,13},{10,... | collective-permute-start | bytes 393224 | tf_op jit(solution)/shard_map/ppermute | solution.py:21
  18.1 1.4 %collective-permute-start.5 = (bf16[16,4096]{1,0:T(8,128)(2,1)S(1)}, bf16[16,4096]{1,0:T(8,128)(2,1)S(1)}, u32[]{:S(2)}, u32[]{:S(2)}) collective-permute-start(bf16[16,4096]{1,0:T(8,128)(2,1)S(1)} %get-tuple-element.40), channel_id=1, source_target_pairs={{0,6},{1,7},{2,4},{3,5},{4,2},{5,3},{6,0},{7,1},{8,14},{9,15},{10,... | collective-permute-start | bytes 393224 | tf_op jit(solution)/shard_map/ppermute | solution.py:21
  19.4 2.9 %collective-permute-done.3.refs_0_ = bf16[16,4096]{1,0:T(8,128)(2,1)S(1)} collective-permute-done((bf16[16,4096]{1,0:T(8,128)(2,1)S(1)}, bf16[16,4096]{1,0:T(8,128)(2,1)S(1)}, u32[]{:S(2)}, u32[]{:S(2)}) %collective-permute-start.3) | collective-permute-done | bytes 131104 | tf_op jit(solution)/shard_map/ppermute | solution.py:21
  22.3 0.0 collective-permute-start.6
  22.3 2.6 %collective-permute-done.4.refs_1_ = bf16[16,4096]{1,0:T(8,128)(2,1)S(1)} collective-permute-done((bf16[16,4096]{1,0:T(8,128)(2,1)S(1)}, bf16[16,4096]{1,0:T(8,128)(2,1)S(1)}, u32[]{:S(2)}, u32[]{:S(2)}) %collective-permute-start.4) | collective-permute-done | bytes 131104 | tf_op jit(solution)/shard_map/ppermute | solution.py:21
  24.9 0.0 collective-permute-start.7
  24.9 0.0 collective-permute-done.5.refs_2_
  24.9 0.5 collective-permute-start.8
  25.4 1.4 %shard_map.76.refs_9_ = bf16[1024,768]{1,0:T(8,128)(2,1)S(1)} custom-call(bf16[1,4096,768]{2,1,0:T(8,128)(2,1)} %refs_0_.5), custom_call_target="tpu_custom_call" | custom-call | tf_op jit(solution)/shard_map/pallas_call | solution.py:320
  26.8 3.3 %shard_map.75 = (bf16[2816,768]{1,0:T(8,128)(2,1)S(1)}, bf16[384,4096]{1,0:T(8,128)(2,1)S(1)}, bf16[32,24]{1,0:T(8,128)(2,1)S(1)}, bf16[4,16,120]{2,1,0:T(8,128)(2,1)S(1)}, bf16[4,16,120]{2,1,0:T(8,128)(2,1)S(1)}) custom-call(s32[1]{0:T(128)} %bitcast.station, f32[32,128]{1,0:T(8,128)S(1)} %get-tuple-element.35.tables, bf16[1,4096,768]{2,1,0:T(8,128)(2,1)} %refs_0_.5, ...), custom_call_target="tpu_custom_call" | custom-call | tf_op jit(solution)/shard_map/pallas_call | solution.py:347
  30.1 0.0 collective-permute-done.6.refs_3_
  30.1 0.0 collective-permute-done.7.refs_4_
  30.2 0.0 collective-permute-done.8.refs_5_
  30.2 0.0 collective-permute-done.12.refs_7_
  30.2 2.9 %shard_map.77 = (f32[40,1024]{1,0:T(8,128)S(1)}, f32[40,1024]{1,0:T(8,128)S(1)}, f32[40,1024]{1,0:T(8,128)S(1)}, bf16[40,1024]{1,0:T(8,128)(2,1)S(1)}, bf16[40,1...) custom-call(bf16[16,4096]{1,0:T(8,128)(2,1)S(1)} %collective-permute, ...), custom_call_target="tpu_custom_call" | custom-call | tf_op jit(solution)/shard_map/pallas_call | solution.py:374
  33.1 0.1 collective-permute-start.19
  33.2 0.5 collective-permute-start.21
  33.7 0.1 collective-permute-start.23
  33.7 0.4 collective-permute-start.13
  34.2 0.1 collective-permute-start.14
  34.3 0.2 collective-permute-done.19
  34.5 1.5 %collective-permute-start.20 = (bf16[40,1024]{1,0:T(8,128)(2,1)S(1)}, bf16[40,1024]{1,0:T(8,128)(2,1)S(1)}, u32[]{:S(2)}, u32[]{:S(2)}) collective-permute-start(bf16[40,1024]{1,0:T(8,128)(2,1)S(1)} %add_convert_fusion.2), channel_id=1, source_target_pairs={{0,2},{1,3},{2,0},{3,1},{4,6},{5,7},{6,4},{7,5},{8,10},{9,11},{10,... | collective-permute-start | bytes 245768 | tf_op jit(solution)/shard_map/ppermute | solution.py:21
  35.9 0.0 collective-permute-done.21
  36.0 0.7 %collective-permute-start.22 = (bf16[40,1024]{1,0:T(8,128)(2,1)S(1)}, bf16[40,1024]{1,0:T(8,128)(2,1)S(1)}, u32[]{:S(2)}, u32[]{:S(2)}) collective-permute-start(bf16[40,1024]{1,0:T(8,128)(2,1)S(1)} %add_convert_fusion.1), channel_id=1, source_target_pairs={{0,4},{1,5},{2,6},{3,7},{4,0},{5,1},{6,2},{7,3},{8,12},{9,13},{10,... | collective-permute-start | bytes 245768 | tf_op jit(solution)/shard_map/ppermute | solution.py:21
  36.7 0.0 collective-permute-done.23
  36.7 1.5 %collective-permute-start.24 = (bf16[40,1024]{1,0:T(8,128)(2,1)S(1)}, bf16[40,1024]{1,0:T(8,128)(2,1)S(1)}, u32[]{:S(2)}, u32[]{:S(2)}) collective-permute-start(bf16[40,1024]{1,0:T(8,128)(2,1)S(1)} %add_convert_fusion), channel_id=1, source_target_pairs={{0,6},{1,7},{2,4},{3,5},{4,2},{5,3},{6,0},{7,1},{8,14},{9,15},{10,... | collective-permute-start | bytes 245768 | tf_op jit(solution)/shard_map/ppermute | solution.py:21
  38.2 0.0 collective-permute-done.14
  38.3 1.6 %collective-permute-start.17 = (bf16[40,1024]{1,0:T(8,128)(2,1)S(1)}, bf16[40,1024]{1,0:T(8,128)(2,1)S(1)}, u32[]{:S(2)}, u32[]{:S(2)}) collective-permute-start(bf16[40,1024]{1,0:T(8,128)(2,1)S(1)} %get-tuple-element.63), channel_id=1, source_target_pairs={{0,6},{1,7},{2,4},{3,5},{4,2},{5,3},{6,0},{7,1},{8,14},{9,15},{10,... | collective-permute-start | bytes 245768 | tf_op jit(solution)/shard_map/ppermute | solution.py:21
  39.8 0.0 collective-permute-done.20.refs_0_
  39.8 1.4 %collective-permute-start.16 = (bf16[40,1024]{1,0:T(8,128)(2,1)S(1)}, bf16[40,1024]{1,0:T(8,128)(2,1)S(1)}, u32[]{:S(2)}, u32[]{:S(2)}) collective-permute-start(bf16[40,1024]{1,0:T(8,128)(2,1)S(1)} %get-tuple-element.64), channel_id=1, source_target_pairs={{0,4},{1,5},{2,6},{3,7},{4,0},{5,1},{6,2},{7,3},{8,12},{9,13},{10,... | collective-permute-start | bytes 245768 | tf_op jit(solution)/shard_map/ppermute | solution.py:21
  41.2 2.2 %collective-permute-done.22.refs_1_ = bf16[40,1024]{1,0:T(8,128)(2,1)S(1)} collective-permute-done((bf16[40,1024]{1,0:T(8,128)(2,1)S(1)}, bf16[40,1024]{1,0:T(8,128)(2,1)S(1)}, u32[]{:S(2)}, u32[]{:S(2)}) %collective-permute-start.22) | collective-permute-done | bytes 81952 | tf_op jit(solution)/shard_map/ppermute | solution.py:21
  43.4 0.0 collective-permute-start.15
  43.4 0.0 collective-permute-done.24.refs_2_
  43.4 0.0 collective-permute-done.13.got
  43.4 0.3 shard_map.79
  43.8 3.1 %collective-permute-start.25 = (bf16[8,4096]{1,0:T(8,128)(2,1)S(1)}, bf16[8,4096]{1,0:T(8,128)(2,1)S(1)}, u32[]{:S(2)}, u32[]{:S(2)}) collective-permute-start(bf16[8,4096]{1,0:T(8,128)(2,1)S(1)} %get-tuple-element.61), channel_id=1, source_target_pairs={{0,16},{1,17},{2,18},{3,19},{4,20},{5,21},{6,22},{7,23},{8,24},{9,... | collective-permute-start | bytes 196616 | tf_op jit(solution)/shard_map/ppermute | solution.py:21
  46.9 1.3 %collective-permute-start.26 = (bf16[8,4096]{1,0:T(8,128)(2,1)S(1)}, bf16[8,4096]{1,0:T(8,128)(2,1)S(1)}, u32[]{:S(2)}, u32[]{:S(2)}) collective-permute-start(bf16[8,4096]{1,0:T(8,128)(2,1)S(1)} %get-tuple-element.62), channel_id=1, source_target_pairs={{0,24},{1,25},{2,26},{3,27},{4,28},{5,29},{6,30},{7,31},{8,16},{9,... | collective-permute-start | bytes 196616 | tf_op jit(solution)/shard_map/ppermute | solution.py:21
  48.2 0.0 collective-permute-done.17.refs_2_
  48.2 0.0 collective-permute-done.16.refs_1_
  48.2 0.0 collective-permute-done.15.refs_0_
  48.2 0.3 shard_map.78
  48.5 0.0 collective-permute-start.18
  48.5 2.0 %collective-permute-done.25.refs_1_ = bf16[8,4096]{1,0:T(8,128)(2,1)S(1)} collective-permute-done((bf16[8,4096]{1,0:T(8,128)(2,1)S(1)}, bf16[8,4096]{1,0:T(8,128)(2,1)S(1)}, u32[]{:S(2)}, u32[]{:S(2)}) %collective-permute-start.25) | collective-permute-done | bytes 65568 | tf_op jit(solution)/shard_map/ppermute | solution.py:21
  50.5 2.5 %collective-permute-done.26.refs_2_ = bf16[8,4096]{1,0:T(8,128)(2,1)S(1)} collective-permute-done((bf16[8,4096]{1,0:T(8,128)(2,1)S(1)}, bf16[8,4096]{1,0:T(8,128)(2,1)S(1)}, u32[]{:S(2)}, u32[]{:S(2)}) %collective-permute-start.26) | collective-permute-done | bytes 65568 | tf_op jit(solution)/shard_map/ppermute | solution.py:21
  53.1 0.4 collective-permute-done.18.refs_0_
  53.5 0.7 %shard_map.80 = bf16[8,4096]{1,0:T(8,128)(2,1)} custom-call(f32[8,4096]{1,0:T(8,128)S(1)} %get-tuple-element.52.local, bf16[8,4096]{1,0:T(8,128)(2,1)S(1)} %collective-permute-done.18.refs_0_, bf16[8,4096]{1,0:T(8,128)(2,1)S(1)} %collective-permute-done.25.refs_1_, bf16[8,4096]{1,0:T(8,128)(2,1)S(1)} %collective-permute-done.26.refs_2_), custom_call_target="tpu_custom_call" | custom-call | tf_op jit(solution)/shard_map/pallas_call | solution.py:400
  (8 shorter events, 0.2 us)
Async XLA Ops:
  1.7 8.9 %collective-permute-start.2 = (bf16[8,4224]{1,0:T(8,128)(2,1)S(1)}, bf16[8,4224]{1,0:T(8,128)(2,1)S(1)}, u32[]{:S(2)}, u32[]{:S(2)}) collective-permute-start(bf16[8,4224]{1,0:T(8,128)(2,1)S(1)} %get-tuple-element.34.refs_0_), channel_id=1, source_target_pairs={{0,24},{1,25},{2,26},{3,27},{4,28},{5,29},{6,30},{7,31},{8,16},{9,... | collective-permute-start | bytes 202760 | tf_op jit(solution)/shard_map/ppermute | solution.py:21
  6.9 5.8 %collective-permute-start.1 = (bf16[8,4224]{1,0:T(8,128)(2,1)S(1)}, bf16[8,4224]{1,0:T(8,128)(2,1)S(1)}, u32[]{:S(2)}, u32[]{:S(2)}) collective-permute-start(bf16[8,4224]{1,0:T(8,128)(2,1)S(1)} %get-tuple-element.34.refs_0_), channel_id=1, source_target_pairs={{0,16},{1,17},{2,18},{3,19},{4,20},{5,21},{6,22},{7,23},{8,24},{9,... | collective-permute-start | bytes 202760 | tf_op jit(solution)/shard_map/ppermute | solution.py:21
  6.9 5.8 %collective-permute-start = (bf16[8,4224]{1,0:T(8,128)(2,1)S(1)}, bf16[8,4224]{1,0:T(8,128)(2,1)S(1)}, u32[]{:S(2)}, u32[]{:S(2)}) collective-permute-start(bf16[8,4224]{1,0:T(8,128)(2,1)S(1)} %get-tuple-element.34.refs_0_), channel_id=1, source_target_pairs={{0,8},{1,9},{2,10},{3,11},{4,12},{5,13},{6,14},{7,15},{8,0},{9,1},... | collective-permute-start | bytes 202760 | tf_op jit(solution)/shard_map/ppermute | solution.py:21
  7.5 5.8 %collective-permute-start.9 = (bf16[8,4096]{1,0:T(8,128)(2,1)S(1)}, bf16[8,4096]{1,0:T(8,128)(2,1)S(1)}, u32[]{:S(2)}, u32[]{:S(2)}) collective-permute-start(bf16[8,4096]{1,0:T(8,128)(2,1)S(1)} %get-tuple-element.42), channel_id=1, source_target_pairs={{0,2},{1,3},{2,0},{3,1},{4,6},{5,7},{6,4},{7,5},{8,10},{9,11},{10,... | collective-permute-start | bytes 196616 | tf_op jit(solution)/shard_map/ppermute | solution.py:21
  9.1 5.0 %collective-permute-start.10 = (bf16[8,4096]{1,0:T(8,128)(2,1)S(1)}, bf16[8,4096]{1,0:T(8,128)(2,1)S(1)}, u32[]{:S(2)}, u32[]{:S(2)}) collective-permute-start(bf16[8,4096]{1,0:T(8,128)(2,1)S(1)} %get-tuple-element.43), channel_id=1, source_target_pairs={{0,4},{1,5},{2,6},{3,7},{4,0},{5,1},{6,2},{7,3},{8,12},{9,13},{10,... | collective-permute-start | bytes 196616 | tf_op jit(solution)/shard_map/ppermute | solution.py:21
  10.7 5.2 %collective-permute-start.11 = (bf16[8,4096]{1,0:T(8,128)(2,1)S(1)}, bf16[8,4096]{1,0:T(8,128)(2,1)S(1)}, u32[]{:S(2)}, u32[]{:S(2)}) collective-permute-start(bf16[8,4096]{1,0:T(8,128)(2,1)S(1)} %get-tuple-element.44), channel_id=1, source_target_pairs={{0,6},{1,7},{2,4},{3,5},{4,2},{5,3},{6,0},{7,1},{8,14},{9,15},{10,... | collective-permute-start | bytes 196616 | tf_op jit(solution)/shard_map/ppermute | solution.py:21
  15.8 14.3 %collective-permute-start.12 = (bf16[48,4096]{1,0:T(8,128)(2,1)S(1)}, bf16[48,4096]{1,0:T(8,128)(2,1)S(1)}, u32[]{:S(2)}, u32[]{:S(2)}) collective-permute-start(bf16[48,4096]{1,0:T(8,128)(2,1)S(1)} %constant_dynamic-update-slice_fusion.refs_6_), channel_id=1, source_target_pairs={{0,1},{1,0},{2,3},{3,2},{4,5},{5,4},{6,7},{7,6},{8,9},{9,8},{10,11... | collective-permute-start | bytes 1179656 | tf_op jit(solution)/shard_map/ppermute | solution.py:21
  15.8 6.4 %collective-permute-start.3 = (bf16[16,4096]{1,0:T(8,128)(2,1)S(1)}, bf16[16,4096]{1,0:T(8,128)(2,1)S(1)}, u32[]{:S(2)}, u32[]{:S(2)}) collective-permute-start(bf16[16,4096]{1,0:T(8,128)(2,1)S(1)} %get-tuple-element.38), channel_id=1, source_target_pairs={{0,2},{1,3},{2,0},{3,1},{4,6},{5,7},{6,4},{7,5},{8,10},{9,11},{10,... | collective-permute-start | bytes 393224 | tf_op jit(solution)/shard_map/ppermute | solution.py:21
  16.5 8.4 %collective-permute-start.4 = (bf16[16,4096]{1,0:T(8,128)(2,1)S(1)}, bf16[16,4096]{1,0:T(8,128)(2,1)S(1)}, u32[]{:S(2)}, u32[]{:S(2)}) collective-permute-start(bf16[16,4096]{1,0:T(8,128)(2,1)S(1)} %get-tuple-element.39), channel_id=1, source_target_pairs={{0,4},{1,5},{2,6},{3,7},{4,0},{5,1},{6,2},{7,3},{8,12},{9,13},{10,... | collective-permute-start | bytes 393224 | tf_op jit(solution)/shard_map/ppermute | solution.py:21
  18.1 6.9 %collective-permute-start.5 = (bf16[16,4096]{1,0:T(8,128)(2,1)S(1)}, bf16[16,4096]{1,0:T(8,128)(2,1)S(1)}, u32[]{:S(2)}, u32[]{:S(2)}) collective-permute-start(bf16[16,4096]{1,0:T(8,128)(2,1)S(1)} %get-tuple-element.40), channel_id=1, source_target_pairs={{0,6},{1,7},{2,4},{3,5},{4,2},{5,3},{6,0},{7,1},{8,14},{9,15},{10,... | collective-permute-start | bytes 393224 | tf_op jit(solution)/shard_map/ppermute | solution.py:21
  22.3 7.9 %collective-permute-start.6 = (bf16[16,4096]{1,0:T(8,128)(2,1)S(1)}, bf16[16,4096]{1,0:T(8,128)(2,1)S(1)}, u32[]{:S(2)}, u32[]{:S(2)}) collective-permute-start(bf16[16,4096]{1,0:T(8,128)(2,1)S(1)} %collective-permute-done.3.refs_0_), channel_id=1, source_target_pairs={{0,1},{1,0},{2,3},{3,2},{4,5},{5,4},{6,7},{7,6},{8,9},{9,8},{10,11... | collective-permute-start | bytes 393224 | tf_op jit(solution)/shard_map/ppermute | solution.py:21
  24.9 5.3 %collective-permute-start.7 = (bf16[16,4096]{1,0:T(8,128)(2,1)S(1)}, bf16[16,4096]{1,0:T(8,128)(2,1)S(1)}, u32[]{:S(2)}, u32[]{:S(2)}) collective-permute-start(bf16[16,4096]{1,0:T(8,128)(2,1)S(1)} %collective-permute-done.4.refs_1_), channel_id=1, source_target_pairs={{0,1},{1,0},{2,3},{3,2},{4,5},{5,4},{6,7},{7,6},{8,9},{9,8},{10,11... | collective-permute-start | bytes 393224 | tf_op jit(solution)/shard_map/ppermute | solution.py:21
  24.9 5.3 %collective-permute-start.8 = (bf16[16,4096]{1,0:T(8,128)(2,1)S(1)}, bf16[16,4096]{1,0:T(8,128)(2,1)S(1)}, u32[]{:S(2)}, u32[]{:S(2)}) collective-permute-start(bf16[16,4096]{1,0:T(8,128)(2,1)S(1)} %collective-permute-done.5.refs_2_), channel_id=1, source_target_pairs={{0,1},{1,0},{2,3},{3,2},{4,5},{5,4},{6,7},{7,6},{8,9},{9,8},{10,11... | collective-permute-start | bytes 393224 | tf_op jit(solution)/shard_map/ppermute | solution.py:21
  33.1 1.3 %collective-permute-start.19 = (bf16[40,1024]{1,0:T(8,128)(2,1)S(1)}, bf16[40,1024]{1,0:T(8,128)(2,1)S(1)}, u32[]{:S(2)}, u32[]{:S(2)}) collective-permute-start(bf16[40,1024]{1,0:T(8,128)(2,1)S(1)} %get-tuple-element.56), channel_id=1, source_target_pairs={{0,1},{1,0},{2,3},{3,2},{4,5},{5,4},{6,7},{7,6},{8,9},{9,8},{10,11... | collective-permute-start | bytes 245768 | tf_op jit(solution)/shard_map/ppermute | solution.py:21
  33.2 2.8 %collective-permute-start.21 = (bf16[40,1024]{1,0:T(8,128)(2,1)S(1)}, bf16[40,1024]{1,0:T(8,128)(2,1)S(1)}, u32[]{:S(2)}, u32[]{:S(2)}) collective-permute-start(bf16[40,1024]{1,0:T(8,128)(2,1)S(1)} %get-tuple-element.58), channel_id=1, source_target_pairs={{0,1},{1,0},{2,3},{3,2},{4,5},{5,4},{6,7},{7,6},{8,9},{9,8},{10,11... | collective-permute-start | bytes 245768 | tf_op jit(solution)/shard_map/ppermute | solution.py:21
  33.7 3.0 %collective-permute-start.23 = (bf16[40,1024]{1,0:T(8,128)(2,1)S(1)}, bf16[40,1024]{1,0:T(8,128)(2,1)S(1)}, u32[]{:S(2)}, u32[]{:S(2)}) collective-permute-start(bf16[40,1024]{1,0:T(8,128)(2,1)S(1)} %get-tuple-element.60), channel_id=1, source_target_pairs={{0,1},{1,0},{2,3},{3,2},{4,5},{5,4},{6,7},{7,6},{8,9},{9,8},{10,11... | collective-permute-start | bytes 245768 | tf_op jit(solution)/shard_map/ppermute | solution.py:21
  33.7 9.7 %collective-permute-start.13 = (bf16[24,4096]{1,0:T(8,128)(2,1)S(1)}, bf16[24,4096]{1,0:T(8,128)(2,1)S(1)}, u32[]{:S(2)}, u32[]{:S(2)}) collective-permute-start(bf16[24,4096]{1,0:T(8,128)(2,1)S(1)} %get-tuple-element.49), channel_id=1, source_target_pairs={{0,1},{1,0},{2,3},{3,2},{4,5},{5,4},{6,7},{7,6},{8,9},{9,8},{10,11... | collective-permute-start | bytes 589832 | tf_op jit(solution)/shard_map/ppermute | solution.py:21
  34.2 4.0 %collective-permute-start.14 = (bf16[120,1024]{1,0:T(8,128)(2,1)S(1)}, bf16[120,1024]{1,0:T(8,128)(2,1)S(1)}, u32[]{:S(2)}, u32[]{:S(2)}) collective-permute-start(bf16[120,1024]{1,0:T(8,128)(2,1)S(1)} %get-tuple-element.51), channel_id=1, source_target_pairs={{0,1},{1,0},{2,3},{3,2},{4,5},{5,4},{6,7},{7,6},{8,9},{9,8},{10,11... | collective-permute-start | bytes 737288 | tf_op jit(solution)/shard_map/ppermute | solution.py:21
  34.5 5.4 %collective-permute-start.20 = (bf16[40,1024]{1,0:T(8,128)(2,1)S(1)}, bf16[40,1024]{1,0:T(8,128)(2,1)S(1)}, u32[]{:S(2)}, u32[]{:S(2)}) collective-permute-start(bf16[40,1024]{1,0:T(8,128)(2,1)S(1)} %add_convert_fusion.2), channel_id=1, source_target_pairs={{0,2},{1,3},{2,0},{3,1},{4,6},{5,7},{6,4},{7,5},{8,10},{9,11},{10,... | collective-permute-start | bytes 245768 | tf_op jit(solution)/shard_map/ppermute | solution.py:21
  36.0 7.5 %collective-permute-start.22 = (bf16[40,1024]{1,0:T(8,128)(2,1)S(1)}, bf16[40,1024]{1,0:T(8,128)(2,1)S(1)}, u32[]{:S(2)}, u32[]{:S(2)}) collective-permute-start(bf16[40,1024]{1,0:T(8,128)(2,1)S(1)} %add_convert_fusion.1), channel_id=1, source_target_pairs={{0,4},{1,5},{2,6},{3,7},{4,0},{5,1},{6,2},{7,3},{8,12},{9,13},{10,... | collective-permute-start | bytes 245768 | tf_op jit(solution)/shard_map/ppermute | solution.py:21
  36.7 6.7 %collective-permute-start.24 = (bf16[40,1024]{1,0:T(8,128)(2,1)S(1)}, bf16[40,1024]{1,0:T(8,128)(2,1)S(1)}, u32[]{:S(2)}, u32[]{:S(2)}) collective-permute-start(bf16[40,1024]{1,0:T(8,128)(2,1)S(1)} %add_convert_fusion), channel_id=1, source_target_pairs={{0,6},{1,7},{2,4},{3,5},{4,2},{5,3},{6,0},{7,1},{8,14},{9,15},{10,... | collective-permute-start | bytes 245768 | tf_op jit(solution)/shard_map/ppermute | solution.py:21
  38.3 9.9 %collective-permute-start.17 = (bf16[40,1024]{1,0:T(8,128)(2,1)S(1)}, bf16[40,1024]{1,0:T(8,128)(2,1)S(1)}, u32[]{:S(2)}, u32[]{:S(2)}) collective-permute-start(bf16[40,1024]{1,0:T(8,128)(2,1)S(1)} %get-tuple-element.63), channel_id=1, source_target_pairs={{0,6},{1,7},{2,4},{3,5},{4,2},{5,3},{6,0},{7,1},{8,14},{9,15},{10,... | collective-permute-start | bytes 245768 | tf_op jit(solution)/shard_map/ppermute | solution.py:21
  39.8 8.3 %collective-permute-start.16 = (bf16[40,1024]{1,0:T(8,128)(2,1)S(1)}, bf16[40,1024]{1,0:T(8,128)(2,1)S(1)}, u32[]{:S(2)}, u32[]{:S(2)}) collective-permute-start(bf16[40,1024]{1,0:T(8,128)(2,1)S(1)} %get-tuple-element.64), channel_id=1, source_target_pairs={{0,4},{1,5},{2,6},{3,7},{4,0},{5,1},{6,2},{7,3},{8,12},{9,13},{10,... | collective-permute-start | bytes 245768 | tf_op jit(solution)/shard_map/ppermute | solution.py:21
  43.4 4.7 %collective-permute-start.15 = (bf16[40,1024]{1,0:T(8,128)(2,1)S(1)}, bf16[40,1024]{1,0:T(8,128)(2,1)S(1)}, u32[]{:S(2)}, u32[]{:S(2)}) collective-permute-start(bf16[40,1024]{1,0:T(8,128)(2,1)S(1)} %get-tuple-element.65), channel_id=1, source_target_pairs={{0,2},{1,3},{2,0},{3,1},{4,6},{5,7},{6,4},{7,5},{8,10},{9,11},{10,... | collective-permute-start | bytes 245768 | tf_op jit(solution)/shard_map/ppermute | solution.py:21
  43.8 6.8 %collective-permute-start.25 = (bf16[8,4096]{1,0:T(8,128)(2,1)S(1)}, bf16[8,4096]{1,0:T(8,128)(2,1)S(1)}, u32[]{:S(2)}, u32[]{:S(2)}) collective-permute-start(bf16[8,4096]{1,0:T(8,128)(2,1)S(1)} %get-tuple-element.61), channel_id=1, source_target_pairs={{0,16},{1,17},{2,18},{3,19},{4,20},{5,21},{6,22},{7,23},{8,24},{9,... | collective-permute-start | bytes 196616 | tf_op jit(solution)/shard_map/ppermute | solution.py:21
  46.9 6.2 %collective-permute-start.26 = (bf16[8,4096]{1,0:T(8,128)(2,1)S(1)}, bf16[8,4096]{1,0:T(8,128)(2,1)S(1)}, u32[]{:S(2)}, u32[]{:S(2)}) collective-permute-start(bf16[8,4096]{1,0:T(8,128)(2,1)S(1)} %get-tuple-element.62), channel_id=1, source_target_pairs={{0,24},{1,25},{2,26},{3,27},{4,28},{5,29},{6,30},{7,31},{8,16},{9,... | collective-permute-start | bytes 196616 | tf_op jit(solution)/shard_map/ppermute | solution.py:21
  48.5 5.0 %collective-permute-start.18 = (bf16[8,4096]{1,0:T(8,128)(2,1)S(1)}, bf16[8,4096]{1,0:T(8,128)(2,1)S(1)}, u32[]{:S(2)}, u32[]{:S(2)}) collective-permute-start(bf16[8,4096]{1,0:T(8,128)(2,1)S(1)} %get-tuple-element.53), channel_id=1, source_target_pairs={{0,8},{1,9},{2,10},{3,11},{4,12},{5,13},{6,14},{7,15},{8,0},{9,1},... | collective-permute-start | bytes 196616 | tf_op jit(solution)/shard_map/ppermute | solution.py:21
